TPU v7x, 128 devices: a whole 4x4x4 slice. The times are simulated.
128 devices in a mesh: group: 32 (over y, z, core), rep: 4 (over x).
Axes of the slice: x: 4, y: 4, z: 4, core: 2. Of those that a mesh axis runs over, the one named last changes fastest.
Arguments:
- grad_parts: bfloat16 [4, 96, 1024, 1024], P('rep', None, 'group'), may hold values from -40 to 40
- params: bfloat16 [96, 1024, 1024], P('rep', 'group'), may hold values from -6 to 6
- accum: float32 [96, 1024, 1024], P('rep', 'group'), may hold values from 1 to 50
- left_pre: bfloat16 [4, 32, 1, 1024, 1024], P('rep', 'group'), may hold values from -1 to 4
- right_pre: bfloat16 [4, 32, 1, 1024, 1024], P('rep', 'group'), may hold values from -1 to 4
- slot_block: int32 [4, 32, 1], replicated, may hold values from -1 to 23, as said below
- layer_of: int32 [96], replicated, may hold values from 0 to 7
Outputs:
- new_params: bfloat16 [96, 1024, 1024], P(None, 'group')
- new_accum: float32 [96, 1024, 1024], P('rep', 'group')
Inputs may be any that keep to these rules, and one draw needn't show every extreme that they name: For every replica q each of its 24 blocks is named by exactly one slot of slot_block[q]; a device's used slots come first and the others hold -1; in every replica some device has all 1 slots used.
All inputs are finite; a program needn't handle non-finite values.
Results may differ from a plain program's by a relative error of at most 0.018.
Values may be sent and summed in bfloat16 or wider, within the bound.
No kernel may reach another device: no remote copies, remote signals or barrier semaphores. Data moves between devices by JAX's collectives and lax.ppermute only.
A program may use at most 128 MiB of HBM per device.

v0:
```python
import jax
import jax.numpy as jnp
from jax import lax
from jax.experimental import pallas as pl
from jax.experimental.pallas import tpu as pltpu
from jax.sharding import Mesh
from jax.sharding import PartitionSpec as P


LAYERS = 8
GROUP = ("group_0", "group_1", "group_2")
EVERY = ("group_0", "group_1", "group_2", "rep")
LANES = 128
SENT = (512, 512)
RETURNED = (512, 512)


step_rate = 0.5
f32 = jnp.float32
bf16 = jnp.bfloat16


def ring(count, step):
    return [(i, (i + step) % count) for i in range(count)]


def starts(widths):
    return [sum(widths[:i]) for i in range(len(widths))]


def merge(who, parts, far_up, far_down, start, cols):
    _, blocks, rows, _ = parts.shape
    half = blocks // 2
    first = start // LANES

    def body(who_ref, above, below, from_down, from_up, out_up, out_down):
        low = above[0, :half].astype(f32) + from_down[...].astype(f32)
        out_up[:half] = low.astype(bf16)
        out_up[half:] = above[0, half:]
        out_down[:half] = below[0, :half]
        high = below[0, half:].astype(f32) + from_up[...].astype(f32)
        out_down[half:] = high.astype(bf16)

    piece = pl.BlockSpec((half, rows, LANES), lambda i, w: (0, 0, i))
    whole = pl.BlockSpec((blocks, rows, LANES), lambda i, w: (0, 0, i))
    shape = jax.ShapeDtypeStruct((blocks, rows, cols), bf16)
    return pl.pallas_call(
        body,
        grid_spec=pltpu.PrefetchScalarGridSpec(
            num_scalar_prefetch=1,
            grid=(cols // LANES,),
            in_specs=[
                pl.BlockSpec((1, blocks, rows, LANES), lambda i, w: (w[1], 0, 0, first + i)),
                pl.BlockSpec((1, blocks, rows, LANES), lambda i, w: (w[3], 0, 0, first + i)),
                piece,
                piece,
            ],
            out_specs=[whole, whole],
        ),
        out_shape=[shape, shape],
        name="merge",
    )(who, parts, parts, far_up, far_down)


def finish(who, table, parts, up, down, start, cols):
    _, blocks, rows, _ = parts.shape
    slots = table.shape[0]
    first = start // LANES

    def body(who_ref, table_ref, own, one, two, gradient, slotted):
        total = own[0].astype(f32) + one[...].astype(f32) + two[...].astype(f32)
        gradient[...] = total.astype(bf16)
        for slot in range(slots):
            slotted[slot] = gradient[table_ref[slot]]

    block = pl.BlockSpec((blocks, rows, LANES), lambda i, w, t: (0, 0, i))
    return pl.pallas_call(
        body,
        grid_spec=pltpu.PrefetchScalarGridSpec(
            num_scalar_prefetch=2,
            grid=(cols // LANES,),
            in_specs=[
                pl.BlockSpec((1, blocks, rows, LANES), lambda i, w, t: (w[0], 0, 0, first + i)),
                block,
                block,
            ],
            out_specs=[block, pl.BlockSpec((slots, rows, LANES), lambda i, w, t: (0, 0, i))],
        ),
        out_shape=[
            jax.ShapeDtypeStruct((blocks, rows, cols), bf16),
            jax.ShapeDtypeStruct((slots, rows, cols), bf16),
        ],
        name="finish",
    )(who, table, parts, up, down)


def left_times(left, owned):
    order, cols = owned.shape
    tile = order // 4

    def body(left_ref, owned_ref, out):
        out[...] = jnp.dot(left_ref[...], owned_ref[...], preferred_element_type=f32).astype(bf16)

    return pl.pallas_call(
        body,
        grid=(4,),
        in_specs=[
            pl.BlockSpec((tile, order), lambda i: (i, 0)),
            pl.BlockSpec((order, cols), lambda i: (0, 0)),
        ],
        out_specs=pl.BlockSpec((tile, cols), lambda i: (i, 0)),
        out_shape=jax.ShapeDtypeStruct((order, cols), bf16),
        name="left_times",
    )(left, owned)


def products(left, right, owned, earlier):
    order, cols = owned.shape
    tile = order // 4
    offsets = starts(SENT)

    def body(left_ref, right_ref, owned_ref, *rest):
        before, outs, squares = rest[: len(earlier)], rest[len(earlier) : -1], rest[-1]
        last = jnp.dot(left_ref[...], owned_ref[...], preferred_element_type=f32).astype(bf16)
        total = jnp.dot(last, right_ref[offsets[-1] :], preferred_element_type=f32)
        for ref, at, size in zip(before, offsets, SENT):
            total += jnp.dot(ref[...], right_ref[at : at + size], preferred_element_type=f32)
        rounded = total.astype(bf16)
        for out, at, size in zip(outs, starts(RETURNED), RETURNED):
            out[...] = rounded[:, at : at + size]
        wide = rounded.astype(f32)
        part = jnp.sum(jnp.sum(wide * wide, axis=0, keepdims=True), axis=1, keepdims=True)

        @pl.when(pl.program_id(0) == 0)
        def _():
            squares[...] = jnp.zeros_like(squares)

        squares[...] += part

    return pl.pallas_call(
        body,
        grid=(4,),
        in_specs=[
            pl.BlockSpec((tile, order), lambda i: (i, 0)),
            pl.BlockSpec((order, order), lambda i: (0, 0)),
            pl.BlockSpec((order, cols), lambda i: (0, 0)),
            *[pl.BlockSpec((tile, e.shape[1]), lambda i: (i, 0)) for e in earlier],
        ],
        out_specs=[
            *[pl.BlockSpec((tile, size), lambda i: (i, 0)) for size in RETURNED],
            pl.BlockSpec((1, 1), lambda i: (0, 0)),
        ],
        out_shape=[
            *[jax.ShapeDtypeStruct((order, size), bf16) for size in RETURNED],
            jax.ShapeDtypeStruct((1, 1), f32),
        ],
        name="products",
    )(left, right, owned, *earlier)


def update(position, scale, returned, params, start, cols):
    blocks, rows, _ = params.shape
    slots = returned.shape[0]
    first = start // LANES

    def body(position_ref, scale_ref, returned_ref, params_ref, out):
        for block in range(blocks):
            change = scale_ref[block] * returned_ref[position_ref[block]].astype(f32)
            out[block] = (params_ref[block].astype(f32) - change).astype(bf16)

    return pl.pallas_call(
        body,
        grid_spec=pltpu.PrefetchScalarGridSpec(
            num_scalar_prefetch=2,
            grid=(cols // LANES,),
            in_specs=[
                pl.BlockSpec((slots, rows, LANES), lambda i, p, s: (0, 0, i)),
                pl.BlockSpec((blocks, rows, LANES), lambda i, p, s: (0, 0, first + i)),
            ],
            out_specs=pl.BlockSpec((blocks, rows, LANES), lambda i, p, s: (0, 0, i)),
        ),
        out_shape=jax.ShapeDtypeStruct((blocks, rows, cols), bf16),
        name="update",
    )(position, scale, returned, params)


def everywhere(value):
    value = value + lax.ppermute(value, "group_2", [(0, 1), (1, 0)])
    for axis in ("rep", "group_0", "group_1"):
        for pairs in ([(0, 1), (1, 0), (2, 3), (3, 2)], [(0, 3), (3, 0), (1, 2), (2, 1)]):
            value = value + lax.ppermute(value, axis, pairs)
    return value


def local(grad_parts, params, accum, left_pre, right_pre, slot_block, layer_of):
    group_size = lax.axis_size(GROUP)
    reps = lax.axis_size("rep")
    me = lax.axis_index("rep")
    group_index = lax.axis_index(GROUP)
    blocks, rows, width = params.shape
    half = blocks // 2
    up, down = ring(reps, 1), ring(reps, -1)
    parts = grad_parts[0].reshape(reps, blocks, rows, width)
    who = lax.rem(me + jnp.arange(reps, dtype=jnp.int32), reps)
    table = lax.dynamic_index_in_dim(slot_block, me, 0, keepdims=False).reshape(-1)
    wanted = jnp.maximum(table, 0)
    left, right = left_pre[0, 0, 0], right_pre[0, 0, 0]

    far = lax.rem(me + 2, reps)
    gradients, earlier, owned = [], [], None
    for start, cols in zip(starts(SENT), SENT):
        low = lax.dynamic_slice(parts, (far, 0, 0, start), (1, half, rows, cols))[0]
        high = lax.dynamic_slice(parts, (far, half, 0, start), (1, half, rows, cols))[0]
        far_up = lax.ppermute(low, "rep", up)
        far_down = lax.ppermute(high, "rep", down)
        to_up, to_down = merge(who, parts, far_up, far_down, start, cols)
        near_up = lax.ppermute(to_up, "rep", up)
        near_down = lax.ppermute(to_down, "rep", down)
        gradient, outgoing = finish(who, wanted, parts, near_up, near_down, start, cols)
        gradients.append(gradient)
        arrived = lax.all_to_all(outgoing, GROUP, split_axis=0, concat_axis=0, tiled=True)
        if owned is not None:
            earlier.append(left_times(left, owned))
        owned = arrived.reshape(group_size * rows, cols)

    my_layers = lax.dynamic_slice_in_dim(layer_of, me * blocks, blocks)
    onehot = (my_layers[:, None] == jnp.arange(LAYERS, dtype=jnp.int32)[None, :]).astype(f32)
    wide = jnp.concatenate(gradients, axis=2).astype(f32)
    new_accum = accum + wide * wide
    graft = wide * lax.rsqrt(new_accum)
    graft_blocks = jnp.sum(graft * graft, axis=(1, 2))
    graft_layer = jnp.sum(onehot * graft_blocks[:, None], axis=0)
    mine = lax.dynamic_index_in_dim(table, group_index, 0, keepdims=False)
    chosen = (jnp.arange(blocks, dtype=jnp.int32) == mine).astype(f32)
    my_layer = jnp.sum(chosen[:, None] * onehot, axis=0)
    position = jnp.sum(
        jnp.where(
            table[None, :] == jnp.arange(blocks, dtype=jnp.int32)[:, None],
            jnp.arange(group_size, dtype=jnp.int32)[None, :],
            0,
        ),
        axis=1,
    )
    owned, earlier, graft_layer, my_layer, position, onehot, new_accum = lax.optimization_barrier(
        (owned, earlier, graft_layer, my_layer, position, onehot, new_accum)
    )

    *preconds, squares = products(left, right, owned, earlier)
    sums = everywhere(jnp.stack([graft_layer, my_layer * squares[0, 0]]))
    layer_scale = jnp.sqrt(sums[0]) * lax.rsqrt(sums[1] + 1e-06)
    block_scale = step_rate * jnp.sum(onehot * layer_scale[None, :], axis=1)

    new_params = jnp.zeros((reps, blocks, rows, width), bf16)
    for start, cols, precond in zip(starts(RETURNED), RETURNED, preconds):
        outgoing = precond.reshape(group_size, rows, cols)
        returned = lax.all_to_all(outgoing, GROUP, split_axis=0, concat_axis=0, tiled=True)
        updated = update(position, block_scale, returned, params, start, cols)
        from_down = lax.ppermute(updated, "rep", up)
        from_up = lax.ppermute(updated, "rep", down)
        far_low = lax.ppermute(from_down[:half], "rep", up)
        far_high = lax.ppermute(from_up[half:], "rep", down)
        for at, first, piece in (
            (0, 0, updated),
            (3, 0, from_down),
            (1, 0, from_up),
            (2, 0, far_low),
            (2, half, far_high),
        ):
            new_params = lax.dynamic_update_slice(new_params, piece[None], (who[at], first, 0, start))
    return (new_params.reshape(reps * blocks, rows, width), new_accum)


def solution(mesh):
    split = Mesh(mesh.devices.reshape(4, 4, 2, mesh.shape["rep"]), EVERY)
    placed = (
        P("rep", None, GROUP, None),
        P("rep", GROUP, None),
        P("rep", GROUP, None),
        P("rep", GROUP, None, None, None),
        P("rep", GROUP, None, None, None),
        P(),
        P(),
    )
    return jax.shard_map(
        local,
        mesh=split,
        in_specs=placed,
        out_specs=(P(None, GROUP, None), P("rep", GROUP, None)),
        check_vma=False,
    )
```

profile of v0, /device:TPU:0, one launch (start us, length us, event | category | flops | bytes accessed | tf_op | source)
XLA Modules:
  0.0 233.4 jit_solution(17067959653009456939)
XLA Ops:
  6.0 8.2 %collective-permute-done.4.from_down = bf16[12,32,512]{2,1,0:T(8,128)(2,1)S(1)} collective-permute-done((bf16[12,32,512]{2,1,0:T(8,128)(2,1)S(1)}, bf16[12,32,512]{2,1,0:T(8,128)(2,1)S(1)}, u32[]{:S(2)}, u32[]{:S(2)}) %collective-permute-start.4) | collective-permute-done | bytes 393248 | tf_op jit(solution)/shard_map/ppermute | solution.py:214
  15.7 4.5 %merge.3 = (bf16[24,32,512]{2,1,0:T(8,128)(2,1)}, bf16[24,32,512]{2,1,0:T(8,128)(2,1)}) custom-call(s32[4]{0:T(128)} %compare_select_fusion.who_ref, bf16[4,24,32,1024]{3,2,1,0:T(8,128)(2,1)} %bitcast.51, bf16[4,24,32,1024]{3,2,1,0:T(8,128)(2,1)} %bitcast.52, bf16[12,32,512]{2,1,0:T(8,128)(2,1)} %copy-done.14, bf16[12,32,512]{2,1,0:T(8,128)(2,1)} %copy-done.15), custom_call_target="tpu_custom_call" | custom-call | tf_op jit(solution)/shard_map/merge/pallas_call | solution.py:47
  27.1 14.8 %collective-permute-done.6.one = bf16[24,32,512]{2,1,0:T(8,128)(2,1)S(1)} collective-permute-done((bf16[24,32,512]{2,1,0:T(8,128)(2,1)}, bf16[24,32,512]{2,1,0:T(8,128)(2,1)S(1)}, u32[]{:S(2)}, u32[]{:S(2)}) %collective-permute-start.6) | collective-permute-done | bytes 786464 | tf_op jit(solution)/shard_map/ppermute | solution.py:217
  43.1 4.7 %finish.3 = (bf16[24,32,512]{2,1,0:T(8,128)(2,1)}, bf16[32,32,512]{2,1,0:T(8,128)(2,1)}) custom-call(s32[4]{0:T(128)} %compare_select_fusion.who_ref, s32[32]{0:T(128)} %get-tuple-element.40.table_ref, bf16[4,24,32,1024]{3,2,1,0:T(8,128)(2,1)} %bitcast.53, bf16[24,32,512]{2,1,0:T(8,128)(2,1)} %copy-done.7, bf16[24,32,512]{2,1,0:T(8,128)(2,1)} %copy-done.8), custom_call_target="tpu_custom_call" | custom-call | tf_op jit(solution)/shard_map/finish/pallas_call | solution.py:77
  47.8 8.5 %all-to-all-start.1 = ((bf16[32,32,512]{2,1,0:T(8,128)(2,1)}), bf16[32,32,512]{2,1,0:T(8,128)(2,1)S(1)}, u32[]{:S(2)}, u32[]{:S(2)}) async-start(bf16[32,32,512]{2,1,0:T(8,128)(2,1)} %get-tuple-element.25), calls=%async_computation.1 | async-start | bytes 2097152 | tf_op jit(solution)/shard_map/all_to_all | solution.py:221
  57.9 4.5 %merge.2 = (bf16[24,32,512]{2,1,0:T(8,128)(2,1)}, bf16[24,32,512]{2,1,0:T(8,128)(2,1)}) custom-call(s32[4]{0:T(128)} %compare_select_fusion.who_ref, bf16[4,24,32,1024]{3,2,1,0:T(8,128)(2,1)} %bitcast.54, bf16[4,24,32,1024]{3,2,1,0:T(8,128)(2,1)} %bitcast.55, bf16[12,32,512]{2,1,0:T(8,128)(2,1)} %copy-done.12, bf16[12,32,512]{2,1,0:T(8,128)(2,1)} %copy-done.13), custom_call_target="tpu_custom_call" | custom-call | tf_op jit(solution)/shard_map/merge/pallas_call | solution.py:47
  65.7 17.9 %collective-permute-done.2.one = bf16[24,32,512]{2,1,0:T(8,128)(2,1)S(1)} collective-permute-done((bf16[24,32,512]{2,1,0:T(8,128)(2,1)}, bf16[24,32,512]{2,1,0:T(8,128)(2,1)S(1)}, u32[]{:S(2)}, u32[]{:S(2)}) %collective-permute-start.2) | collective-permute-done | bytes 786464 | tf_op jit(solution)/shard_map/ppermute | solution.py:217
  85.4 4.7 %finish.2 = (bf16[24,32,512]{2,1,0:T(8,128)(2,1)}, bf16[32,32,512]{2,1,0:T(8,128)(2,1)}) custom-call(s32[4]{0:T(128)} %compare_select_fusion.who_ref, s32[32]{0:T(128)} %get-tuple-element.40.table_ref, bf16[4,24,32,1024]{3,2,1,0:T(8,128)(2,1)} %bitcast.56, bf16[24,32,512]{2,1,0:T(8,128)(2,1)} %copy-done.9, bf16[24,32,512]{2,1,0:T(8,128)(2,1)} %copy-done.10), custom_call_target="tpu_custom_call" | custom-call | tf_op jit(solution)/shard_map/finish/pallas_call | solution.py:77
  90.1 7.2 %all-to-all-start = ((bf16[32,32,512]{2,1,0:T(8,128)(2,1)}), bf16[32,32,512]{2,1,0:T(8,128)(2,1)S(1)}, u32[]{:S(2)}, u32[]{:S(2)}) async-start(bf16[32,32,512]{2,1,0:T(8,128)(2,1)} %get-tuple-element.22), calls=%async_computation | async-start | bytes 2097152 | tf_op jit(solution)/shard_map/all_to_all | solution.py:221
  99.4 4.5 %fusion = (f32[24,32,1024]{2,1,0:T(8,128)}, f32[24]{0:T(128)S(1)}) fusion(f32[24,32,1024]{2,1,0:T(8,128)} %param.9, bf16[24,32,512]{2,1,0:T(8,128)(2,1)} %get-tuple-element.27, bf16[24,32,512]{2,1,0:T(8,128)(2,1)S(1)} %copy-done.11), kind=kLoop, calls=%fused_computation.2 | loop fusion | flops 7077864 | bytes 7864416 | tf_op jit(solution)/shard_map/add | solution.py:229
  104.0 4.8 %left_times.1.rest_0_ = bf16[1024,512]{1,0:T(8,128)(2,1)} custom-call(bf16[1024,1024]{1,0:T(8,128)(2,1)} %bitcast.57, bf16[1024,512]{1,0:T(8,128)(2,1)} %bitcast.60), custom_call_target="tpu_custom_call" | custom-call | tf_op jit(solution)/shard_map/left_times/pallas_call | solution.py:104
  108.8 5.4 %all-to-all-done = bf16[32,32,512]{2,1,0:T(8,128)(2,1)S(1)} async-done(((bf16[32,32,512]{2,1,0:T(8,128)(2,1)}), bf16[32,32,512]{2,1,0:T(8,128)(2,1)S(1)}, u32[]{:S(2)}, u32[]{:S(2)}) %all-to-all-start) | async-done | bytes 1048608 | tf_op jit(solution)/shard_map/all_to_all | solution.py:221
  115.1 7.5 %products.1 = (bf16[1024,512]{1,0:T(8,128)(2,1)}, bf16[1024,512]{1,0:T(8,128)(2,1)}, f32[1,1]{1,0:T(1,128)}) custom-call(bf16[1024,1024]{1,0:T(8,128)(2,1)} %bitcast.58, bf16[1024,1024]{1,0:T(8,128)(2,1)} %bitcast.62, bf16[1024,512]{1,0:T(8,128)(2,1)} %bitcast.61, bf16[1024,512]{1,0:T(8,128)(2,1)} %left_times.1.rest_0_), custom_call_target="tpu_custom_call" | custom-call | tf_op jit(solution)/shard_map/products/pallas_call | solution.py:140
  122.6 4.2 %all-to-all-start.2 = ((bf16[32,32,512]{2,1,0:T(8,128)(2,1)}), bf16[32,32,512]{2,1,0:T(8,128)(2,1)S(1)}, u32[]{:S(2)}, u32[]{:S(2)}) async-start(bf16[32,32,512]{2,1,0:T(8,128)(2,1)} %bitcast.64), calls=%async_computation.2 | async-start | bytes 2097152 | tf_op jit(solution)/shard_map/all_to_all | solution.py:256
  127.5 16.1 %all-to-all-done.2.returned_ref = bf16[32,32,512]{2,1,0:T(8,128)(2,1)S(1)} async-done(((bf16[32,32,512]{2,1,0:T(8,128)(2,1)}), bf16[32,32,512]{2,1,0:T(8,128)(2,1)S(1)}, u32[]{:S(2)}, u32[]{:S(2)}) %all-to-all-start.2) | async-done | bytes 1048608 | tf_op jit(solution)/shard_map/all_to_all | solution.py:256
  143.6 4.0 %all-to-all-start.3 = ((bf16[32,32,512]{2,1,0:T(8,128)(2,1)}), bf16[32,32,512]{2,1,0:T(8,128)(2,1)S(1)}, u32[]{:S(2)}, u32[]{:S(2)}) async-start(bf16[32,32,512]{2,1,0:T(8,128)(2,1)} %bitcast.63), calls=%async_computation.3 | async-start | bytes 2097152 | tf_op jit(solution)/shard_map/all_to_all | solution.py:256
  149.2 3.3 %collective-permute-done.9 = f32[2,8]{1,0:T(2,128)S(1)} collective-permute-done((f32[2,8]{1,0:T(2,128)S(1)}, f32[2,8]{1,0:T(2,128)S(1)}, u32[]{:S(2)}, u32[]{:S(2)}) %collective-permute-start.9) | collective-permute-done | bytes 96 | tf_op jit(solution)/shard_map/ppermute | solution.py:191
  175.6 4.3 %update.2 = bf16[24,32,512]{2,1,0:T(8,128)(2,1)} custom-call(s32[24]{0:T(128)} %select_reduce_fusion.position_ref, f32[24]{0:T(128)} %broadcast_multiply_fusion.scale_ref, bf16[32,32,512]{2,1,0:T(8,128)(2,1)} %copy-done.2, bf16[24,32,1024]{2,1,0:T(8,128)(2,1)} %params_ref.3), custom_call_target="tpu_custom_call" | custom-call | tf_op jit(solution)/shard_map/update/pallas_call | solution.py:171
  184.1 4.3 %update.3 = bf16[24,32,512]{2,1,0:T(8,128)(2,1)} custom-call(s32[24]{0:T(128)} %select_reduce_fusion.position_ref, f32[24]{0:T(128)} %broadcast_multiply_fusion.scale_ref, bf16[32,32,512]{2,1,0:T(8,128)(2,1)} %copy-done.1, bf16[24,32,1024]{2,1,0:T(8,128)(2,1)} %params_ref.3), custom_call_target="tpu_custom_call" | custom-call | tf_op jit(solution)/shard_map/update/pallas_call | solution.py:171
  188.4 3.2 %collective-permute-start.20 = (bf16[24,32,512]{2,1,0:T(8,128)(2,1)}, bf16[24,32,512]{2,1,0:T(8,128)(2,1)S(1)}, u32[]{:S(2)}, u32[]{:S(2)}) collective-permute-start(bf16[24,32,512]{2,1,0:T(8,128)(2,1)} %update.3), channel_id=1, source_target_pairs={{0,3},{1,0},{2,1},{3,2},{4,7},{5,4},{6,5},{7,6},{8,11},{9,8},{10,9... | collective-permute-start | bytes 2359304 | tf_op jit(solution)/shard_map/ppermute | solution.py:259
  202.9 3.3 %collective-permute-start.18 = (bf16[12,32,512]{2,1,0:T(8,128)(2,1)S(1)}, bf16[12,32,512]{2,1,0:T(8,128)(2,1)S(1)}, u32[]{:S(2)}, u32[]{:S(2)}) collective-permute-start(bf16[12,32,512]{2,1,0:T(8,128)(2,1)S(1)} %slice.47), channel_id=1, source_target_pairs={{0,3},{1,0},{2,1},{3,2},{4,7},{5,4},{6,5},{7,6},{8,11},{9,8},{10,9... | collective-permute-start | bytes 1179656 | tf_op jit(solution)/shard_map/ppermute | solution.py:261
  206.2 12.4 %collective-permute-done.19 = bf16[24,32,512]{2,1,0:T(8,128)(2,1)S(1)} collective-permute-done((bf16[24,32,512]{2,1,0:T(8,128)(2,1)}, bf16[24,32,512]{2,1,0:T(8,128)(2,1)S(1)}, u32[]{:S(2)}, u32[]{:S(2)}) %collective-permute-start.19) | collective-permute-done | bytes 786464 | tf_op jit(solution)/shard_map/ppermute | solution.py:258
  218.7 3.3 %collective-permute-start.22 = (bf16[12,32,512]{2,1,0:T(8,128)(2,1)S(1)}, bf16[12,32,512]{2,1,0:T(8,128)(2,1)S(1)}, u32[]{:S(2)}, u32[]{:S(2)}) collective-permute-start(bf16[12,32,512]{2,1,0:T(8,128)(2,1)S(1)} %slice.49), channel_id=1, source_target_pairs={{0,3},{1,0},{2,1},{3,2},{4,7},{5,4},{6,5},{7,6},{8,11},{9,8},{10,9... | collective-permute-start | bytes 1179656 | tf_op jit(solution)/shard_map/ppermute | solution.py:261
  226.8 3.8 %collective-permute-done.21 = bf16[12,32,512]{2,1,0:T(8,128)(2,1)S(1)} collective-permute-done((bf16[12,32,512]{2,1,0:T(8,128)(2,1)S(1)}, bf16[12,32,512]{2,1,0:T(8,128)(2,1)S(1)}, u32[]{:S(2)}, u32[]{:S(2)}) %collective-permute-start.21) | collective-permute-done | bytes 393248 | tf_op jit(solution)/shard_map/ppermute | solution.py:260
  (114 shorter events, 65.9 us)
Async XLA Ops:
  2.1 12.1 %collective-permute-start.4 = (bf16[12,32,512]{2,1,0:T(8,128)(2,1)S(1)}, bf16[12,32,512]{2,1,0:T(8,128)(2,1)S(1)}, u32[]{:S(2)}, u32[]{:S(2)}) collective-permute-start(bf16[12,32,512]{2,1,0:T(8,128)(2,1)S(1)} %get-tuple-element.43), channel_id=1, source_target_pairs={{0,1},{1,2},{2,3},{3,0},{4,5},{5,6},{6,7},{7,4},{8,9},{9,10},{10,1... | collective-permute-start | bytes 1179656 | tf_op jit(solution)/shard_map/ppermute | solution.py:214
  3.8 10.6 %collective-permute-start.5 = (bf16[12,32,512]{2,1,0:T(8,128)(2,1)S(1)}, bf16[12,32,512]{2,1,0:T(8,128)(2,1)S(1)}, u32[]{:S(2)}, u32[]{:S(2)}) collective-permute-start(bf16[12,32,512]{2,1,0:T(8,128)(2,1)S(1)} %get-tuple-element.42), channel_id=1, source_target_pairs={{0,3},{1,0},{2,1},{3,2},{4,7},{5,4},{6,5},{7,6},{8,11},{9,8},{10,9... | collective-permute-start | bytes 1179656 | tf_op jit(solution)/shard_map/ppermute | solution.py:215
  20.1 21.8 %collective-permute-start.6 = (bf16[24,32,512]{2,1,0:T(8,128)(2,1)}, bf16[24,32,512]{2,1,0:T(8,128)(2,1)S(1)}, u32[]{:S(2)}, u32[]{:S(2)}) collective-permute-start(bf16[24,32,512]{2,1,0:T(8,128)(2,1)} %get-tuple-element.23), channel_id=1, source_target_pairs={{0,1},{1,2},{2,3},{3,0},{4,5},{5,6},{6,7},{7,4},{8,9},{9,10},{10,1... | collective-permute-start | bytes 2359304 | tf_op jit(solution)/shard_map/ppermute | solution.py:217
  21.1 20.9 %collective-permute-start.7 = (bf16[24,32,512]{2,1,0:T(8,128)(2,1)}, bf16[24,32,512]{2,1,0:T(8,128)(2,1)S(1)}, u32[]{:S(2)}, u32[]{:S(2)}) collective-permute-start(bf16[24,32,512]{2,1,0:T(8,128)(2,1)} %get-tuple-element.24), channel_id=1, source_target_pairs={{0,3},{1,0},{2,1},{3,2},{4,7},{5,4},{6,5},{7,6},{8,11},{9,8},{10,9... | collective-permute-start | bytes 2359304 | tf_op jit(solution)/shard_map/ppermute | solution.py:218
  23.4 33.0 %collective-permute-start = (bf16[12,32,512]{2,1,0:T(8,128)(2,1)S(1)}, bf16[12,32,512]{2,1,0:T(8,128)(2,1)S(1)}, u32[]{:S(2)}, u32[]{:S(2)}) collective-permute-start(bf16[12,32,512]{2,1,0:T(8,128)(2,1)S(1)} %get-tuple-element.45), channel_id=1, source_target_pairs={{0,1},{1,2},{2,3},{3,0},{4,5},{5,6},{6,7},{7,4},{8,9},{9,10},{10,1... | collective-permute-start | bytes 1179656 | tf_op jit(solution)/shard_map/ppermute | solution.py:214
  23.4 33.0 %collective-permute-start.1 = (bf16[12,32,512]{2,1,0:T(8,128)(2,1)S(1)}, bf16[12,32,512]{2,1,0:T(8,128)(2,1)S(1)}, u32[]{:S(2)}, u32[]{:S(2)}) collective-permute-start(bf16[12,32,512]{2,1,0:T(8,128)(2,1)S(1)} %get-tuple-element.44), channel_id=1, source_target_pairs={{0,3},{1,0},{2,1},{3,2},{4,7},{5,4},{6,5},{7,6},{8,11},{9,8},{10,9... | collective-permute-start | bytes 1179656 | tf_op jit(solution)/shard_map/ppermute | solution.py:215
  47.8 42.3 %all-to-all-start.1 = ((bf16[32,32,512]{2,1,0:T(8,128)(2,1)}), bf16[32,32,512]{2,1,0:T(8,128)(2,1)S(1)}, u32[]{:S(2)}, u32[]{:S(2)}) async-start(bf16[32,32,512]{2,1,0:T(8,128)(2,1)} %get-tuple-element.25), calls=%async_computation.1 | async-start | bytes 2097152 | tf_op jit(solution)/shard_map/all_to_all | solution.py:221
  62.4 21.2 %collective-permute-start.2 = (bf16[24,32,512]{2,1,0:T(8,128)(2,1)}, bf16[24,32,512]{2,1,0:T(8,128)(2,1)S(1)}, u32[]{:S(2)}, u32[]{:S(2)}) collective-permute-start(bf16[24,32,512]{2,1,0:T(8,128)(2,1)} %get-tuple-element.20), channel_id=1, source_target_pairs={{0,1},{1,2},{2,3},{3,0},{4,5},{5,6},{6,7},{7,4},{8,9},{9,10},{10,1... | collective-permute-start | bytes 2359304 | tf_op jit(solution)/shard_map/ppermute | solution.py:217
  62.9 20.7 %collective-permute-start.3 = (bf16[24,32,512]{2,1,0:T(8,128)(2,1)}, bf16[24,32,512]{2,1,0:T(8,128)(2,1)S(1)}, u32[]{:S(2)}, u32[]{:S(2)}) collective-permute-start(bf16[24,32,512]{2,1,0:T(8,128)(2,1)} %get-tuple-element.21), channel_id=1, source_target_pairs={{0,3},{1,0},{2,1},{3,2},{4,7},{5,4},{6,5},{7,6},{8,11},{9,8},{10,9... | collective-permute-start | bytes 2359304 | tf_op jit(solution)/shard_map/ppermute | solution.py:218
  90.1 24.0 %all-to-all-start = ((bf16[32,32,512]{2,1,0:T(8,128)(2,1)}), bf16[32,32,512]{2,1,0:T(8,128)(2,1)S(1)}, u32[]{:S(2)}, u32[]{:S(2)}) async-start(bf16[32,32,512]{2,1,0:T(8,128)(2,1)} %get-tuple-element.22), calls=%async_computation | async-start | bytes 2097152 | tf_op jit(solution)/shard_map/all_to_all | solution.py:221
  122.6 21.0 %all-to-all-start.2 = ((bf16[32,32,512]{2,1,0:T(8,128)(2,1)}), bf16[32,32,512]{2,1,0:T(8,128)(2,1)S(1)}, u32[]{:S(2)}, u32[]{:S(2)}) async-start(bf16[32,32,512]{2,1,0:T(8,128)(2,1)} %bitcast.64), calls=%async_computation.2 | async-start | bytes 2097152 | tf_op jit(solution)/shard_map/all_to_all | solution.py:256
  143.6 39.5 %all-to-all-start.3 = ((bf16[32,32,512]{2,1,0:T(8,128)(2,1)}), bf16[32,32,512]{2,1,0:T(8,128)(2,1)S(1)}, u32[]{:S(2)}, u32[]{:S(2)}) async-start(bf16[32,32,512]{2,1,0:T(8,128)(2,1)} %bitcast.63), calls=%async_computation.3 | async-start | bytes 2097152 | tf_op jit(solution)/shard_map/all_to_all | solution.py:256
  152.6 4.9 %collective-permute-start.10 = (f32[2,8]{1,0:T(2,128)S(1)}, f32[2,8]{1,0:T(2,128)S(1)}, u32[]{:S(2)}, u32[]{:S(2)}) collective-permute-start(f32[2,8]{1,0:T(2,128)S(1)} %fusion.9), channel_id=1, source_target_pairs={{0,3},{3,0},{1,2},{2,1},{4,7},{7,4},{5,6},{6,5},{8,11},{11,8},{9,1... | collective-permute-start | bytes 200 | tf_op jit(solution)/shard_map/ppermute | solution.py:191
  157.5 4.3 %collective-permute-start.11 = (f32[2,8]{1,0:T(2,128)S(1)}, f32[2,8]{1,0:T(2,128)S(1)}, u32[]{:S(2)}, u32[]{:S(2)}) collective-permute-start(f32[2,8]{1,0:T(2,128)S(1)} %add.93), channel_id=1, source_target_pairs={{0,32},{32,0},{64,96},{96,64},{1,33},{33,1},{65,97},{97,65},{2,34}... | collective-permute-start | bytes 200 | tf_op jit(solution)/shard_map/ppermute | solution.py:191
  161.8 4.8 %collective-permute-start.12 = (f32[2,8]{1,0:T(2,128)S(1)}, f32[2,8]{1,0:T(2,128)S(1)}, u32[]{:S(2)}, u32[]{:S(2)}) collective-permute-start(f32[2,8]{1,0:T(2,128)S(1)} %add.94), channel_id=1, source_target_pairs={{0,96},{96,0},{32,64},{64,32},{1,97},{97,1},{33,65},{65,33},{2,98}... | collective-permute-start | bytes 200 | tf_op jit(solution)/shard_map/ppermute | solution.py:191
  170.1 4.8 %collective-permute-start.14 = (f32[2,8]{1,0:T(2,128)S(1)}, f32[2,8]{1,0:T(2,128)S(1)}, u32[]{:S(2)}, u32[]{:S(2)}) collective-permute-start(f32[2,8]{1,0:T(2,128)S(1)} %add.96), channel_id=1, source_target_pairs={{0,24},{24,0},{8,16},{16,8},{1,25},{25,1},{9,17},{17,9},{2,26},{26... | collective-permute-start | bytes 200 | tf_op jit(solution)/shard_map/ppermute | solution.py:191
  179.9 21.8 %collective-permute-start.15 = (bf16[24,32,512]{2,1,0:T(8,128)(2,1)}, bf16[24,32,512]{2,1,0:T(8,128)(2,1)S(1)}, u32[]{:S(2)}, u32[]{:S(2)}) collective-permute-start(bf16[24,32,512]{2,1,0:T(8,128)(2,1)} %update.2), channel_id=1, source_target_pairs={{0,1},{1,2},{2,3},{3,0},{4,5},{5,6},{6,7},{7,4},{8,9},{9,10},{10,1... | collective-permute-start | bytes 2359304 | tf_op jit(solution)/shard_map/ppermute | solution.py:258
  180.1 21.7 %collective-permute-start.16 = (bf16[24,32,512]{2,1,0:T(8,128)(2,1)}, bf16[24,32,512]{2,1,0:T(8,128)(2,1)}, u32[]{:S(2)}, u32[]{:S(2)}) collective-permute-start(bf16[24,32,512]{2,1,0:T(8,128)(2,1)} %update.2), channel_id=1, source_target_pairs={{0,3},{1,0},{2,1},{3,2},{4,7},{5,4},{6,5},{7,6},{8,11},{9,8},{10,9... | collective-permute-start | bytes 2359304 | tf_op jit(solution)/shard_map/ppermute | solution.py:259
  188.4 30.2 %collective-permute-start.19 = (bf16[24,32,512]{2,1,0:T(8,128)(2,1)}, bf16[24,32,512]{2,1,0:T(8,128)(2,1)S(1)}, u32[]{:S(2)}, u32[]{:S(2)}) collective-permute-start(bf16[24,32,512]{2,1,0:T(8,128)(2,1)} %update.3), channel_id=1, source_target_pairs={{0,1},{1,2},{2,3},{3,0},{4,5},{5,6},{6,7},{7,4},{8,9},{9,10},{10,1... | collective-permute-start | bytes 2359304 | tf_op jit(solution)/shard_map/ppermute | solution.py:258
  188.4 30.3 %collective-permute-start.20 = (bf16[24,32,512]{2,1,0:T(8,128)(2,1)}, bf16[24,32,512]{2,1,0:T(8,128)(2,1)S(1)}, u32[]{:S(2)}, u32[]{:S(2)}) collective-permute-start(bf16[24,32,512]{2,1,0:T(8,128)(2,1)} %update.3), channel_id=1, source_target_pairs={{0,3},{1,0},{2,1},{3,2},{4,7},{5,4},{6,5},{7,6},{8,11},{9,8},{10,9... | collective-permute-start | bytes 2359304 | tf_op jit(solution)/shard_map/ppermute | solution.py:259
  201.8 24.6 %collective-permute-start.17 = (bf16[12,32,512]{2,1,0:T(8,128)(2,1)S(1)}, bf16[12,32,512]{2,1,0:T(8,128)(2,1)S(1)}, u32[]{:S(2)}, u32[]{:S(2)}) collective-permute-start(bf16[12,32,512]{2,1,0:T(8,128)(2,1)S(1)} %slice.46), channel_id=1, source_target_pairs={{0,1},{1,2},{2,3},{3,0},{4,5},{5,6},{6,7},{7,4},{8,9},{9,10},{10,1... | collective-permute-start | bytes 1179656 | tf_op jit(solution)/shard_map/ppermute | solution.py:260
  202.9 23.5 %collective-permute-start.18 = (bf16[12,32,512]{2,1,0:T(8,128)(2,1)S(1)}, bf16[12,32,512]{2,1,0:T(8,128)(2,1)S(1)}, u32[]{:S(2)}, u32[]{:S(2)}) collective-permute-start(bf16[12,32,512]{2,1,0:T(8,128)(2,1)S(1)} %slice.47), channel_id=1, source_target_pairs={{0,3},{1,0},{2,1},{3,2},{4,7},{5,4},{6,5},{7,6},{8,11},{9,8},{10,9... | collective-permute-start | bytes 1179656 | tf_op jit(solution)/shard_map/ppermute | solution.py:261
  218.6 11.9 %collective-permute-start.21 = (bf16[12,32,512]{2,1,0:T(8,128)(2,1)S(1)}, bf16[12,32,512]{2,1,0:T(8,128)(2,1)S(1)}, u32[]{:S(2)}, u32[]{:S(2)}) collective-permute-start(bf16[12,32,512]{2,1,0:T(8,128)(2,1)S(1)} %slice.48), channel_id=1, source_target_pairs={{0,1},{1,2},{2,3},{3,0},{4,5},{5,6},{6,7},{7,4},{8,9},{9,10},{10,1... | collective-permute-start | bytes 1179656 | tf_op jit(solution)/shard_map/ppermute | solution.py:260
  218.7 11.9 %collective-permute-start.22 = (bf16[12,32,512]{2,1,0:T(8,128)(2,1)S(1)}, bf16[12,32,512]{2,1,0:T(8,128)(2,1)S(1)}, u32[]{:S(2)}, u32[]{:S(2)}) collective-permute-start(bf16[12,32,512]{2,1,0:T(8,128)(2,1)S(1)} %slice.49), channel_id=1, source_target_pairs={{0,3},{1,0},{2,1},{3,2},{4,7},{5,4},{6,5},{7,6},{8,11},{9,8},{10,9... | collective-permute-start | bytes 1179656 | tf_op jit(solution)/shard_map/ppermute | solution.py:261
  (22 other events, 274.7 us)
where the time goes:
time: 235 us; the launch traced here: 233 us
  waiting for transfers between devices  99.3 us (42%)
  starting transfers between devices  61.4 us (26%)
  Pallas kernels  39.2 us (17%)
  local copies, waits for them, and re-layouts  16.9 us (7%)
  other arithmetic  8.42 us (4%)
  between operations  8.12 us (3%)
    ppermute x2, waiting for transfers between devices, local(): near_up = lax.ppermute(to_up, 'rep', up)  32.8 us
    all_to_all x4, starting transfers between devices, local(): lax.all_to_all(outgoing, GROUP, split_axis=0, concat_axis=0, tiled=True)  24 us
    all_to_all x4, waiting for transfers between devices, local(): lax.all_to_all(outgoing, GROUP, split_axis=0, concat_axis=0, tiled=True)  21.5 us
    ppermute x6, waiting for transfers between devices, everywhere(): value = value + lax.ppermute(value, axis, pairs)  15.2 us
    ppermute x2, waiting for transfers between devices, local(): from_down = lax.ppermute(updated, 'rep', up)  13.9 us
    ppermute x6, starting transfers between devices, everywhere(): value = value + lax.ppermute(value, axis, pairs)  10.8 us
    unnamed x38, local copies, waits for them, and re-layouts  10.4 us
    pallas_call x2, Pallas kernels, finish(): pl.pallas_call(body, grid_spec=pltpu.PrefetchScalarGridSpec(num_scalar_pr...  9.39 us
  transfers between devices with their start and end apart: 27, of which 17 were waited for; matrix products, arithmetic and copies ran while one was open for 6% of the time, Pallas kernels for 12%

commit v1 on v0

v1 whole, which is shorter than its diff:
```python
import jax
import jax.numpy as jnp
from jax import lax
from jax.experimental import pallas as pl
from jax.experimental.pallas import tpu as pltpu
from jax.sharding import Mesh
from jax.sharding import PartitionSpec as P


LAYERS = 8
GROUP = ("group_0", "group_1", "group_2")
EVERY = ("group_0", "group_1", "group_2", "rep")
SENT = ((0, 512), (512, 512))
RETURNED = ((0, 256), (256, 256), (512, 512))


step_rate = 0.5
f32 = jnp.float32
bf16 = jnp.bfloat16


def ring(count, step):
    return [(i, (i + step) % count) for i in range(count)]


def merge(who, parts, far_up, far_down, start, cols):
    _, blocks, rows, _ = parts.shape
    half = blocks // 2
    at = start // cols

    def body(who_ref, above, below, from_down, from_up, out_up, out_down):
        first = pl.program_id(0) == 0

        @pl.when(first)
        def _():
            out_up[...] = (above[0].astype(f32) + from_down[...].astype(f32)).astype(bf16)
            out_down[...] = below[0]

        @pl.when(jnp.logical_not(first))
        def _():
            out_up[...] = above[0]
            out_down[...] = (below[0].astype(f32) + from_up[...].astype(f32)).astype(bf16)

    piece = pl.BlockSpec((half, rows, cols), lambda i, w: (0, 0, 0))
    out = pl.BlockSpec((half, rows, cols), lambda i, w: (i, 0, 0))
    shape = jax.ShapeDtypeStruct((blocks, rows, cols), bf16)
    return pl.pallas_call(
        body,
        grid_spec=pltpu.PrefetchScalarGridSpec(
            num_scalar_prefetch=1,
            grid=(2,),
            in_specs=[
                pl.BlockSpec((1, half, rows, cols), lambda i, w: (w[1], i, 0, at)),
                pl.BlockSpec((1, half, rows, cols), lambda i, w: (w[3], i, 0, at)),
                piece,
                piece,
            ],
            out_specs=[out, out],
        ),
        out_shape=[shape, shape],
        name="merge",
    )(who, parts, parts, far_up, far_down)


def finish(who, table, parts, up, down, start, cols):
    _, blocks, rows, _ = parts.shape
    slots = table.shape[0]
    at = start // cols

    def body(who_ref, table_ref, own, one, two, gradient, slotted):
        total = own[0].astype(f32) + one[...].astype(f32) + two[...].astype(f32)
        gradient[...] = total.astype(bf16)
        for slot in range(slots):
            slotted[slot] = gradient[table_ref[slot]]

    block = pl.BlockSpec((blocks, rows, cols), lambda i, w, t: (0, 0, 0))
    return pl.pallas_call(
        body,
        grid_spec=pltpu.PrefetchScalarGridSpec(
            num_scalar_prefetch=2,
            grid=(1,),
            in_specs=[
                pl.BlockSpec((1, blocks, rows, cols), lambda i, w, t: (w[0], 0, 0, at)),
                block,
                block,
            ],
            out_specs=[block, pl.BlockSpec((slots, rows, cols), lambda i, w, t: (0, 0, 0))],
        ),
        out_shape=[
            jax.ShapeDtypeStruct((blocks, rows, cols), bf16),
            jax.ShapeDtypeStruct((slots, rows, cols), bf16),
        ],
        name="finish",
    )(who, table, parts, up, down)


def early(left, right, owned, start, so_far, split):
    order, cols = owned.shape
    tile = order // 2
    at = start // cols

    def body(left_ref, right_ref, owned_ref, *rest):
        before, outs = rest[: len(so_far)], rest[len(so_far) :]
        mid = jnp.dot(left_ref[...], owned_ref[...], preferred_element_type=f32).astype(bf16)
        term = jnp.dot(mid, right_ref[...], preferred_element_type=f32)
        pieces = (term[:, :split], term[:, split:])
        for i, (out, piece) in enumerate(zip(outs, pieces)):
            out[...] = piece + before[i][...] if before else piece

    sums = [pl.BlockSpec((tile, split), lambda i: (i, 0)), pl.BlockSpec((tile, order - split), lambda i: (i, 0))]
    return pl.pallas_call(
        body,
        grid=(2,),
        in_specs=[
            pl.BlockSpec((tile, order), lambda i: (i, 0)),
            pl.BlockSpec((cols, order), lambda i: (at, 0)),
            pl.BlockSpec((order, cols), lambda i: (0, 0)),
            *sums[: len(so_far)],
        ],
        out_specs=sums,
        out_shape=[
            jax.ShapeDtypeStruct((order, split), f32),
            jax.ShapeDtypeStruct((order, order - split), f32),
        ],
        name="early",
    )(left, right, owned, *so_far)


def squared(value):
    wide = value.astype(f32)
    return jnp.sum((wide * wide).reshape(-1, 8, value.shape[1]), axis=0)


def accumulate(ref, value):
    @pl.when(pl.program_id(0) == 0)
    def _():
        ref[...] = value

    @pl.when(pl.program_id(0) > 0)
    def _():
        ref[...] += value


def first_product(left, right, owned, so_far, start):
    order, cols = owned.shape
    split = so_far.shape[1]
    tile = order // 2
    at = start // cols

    def body(left_ref, right_ref, owned_ref, before, mid, out, squares):
        mid[...] = jnp.dot(left_ref[...], owned_ref[...], preferred_element_type=f32).astype(bf16)
        total = before[...] + jnp.dot(mid[...], right_ref[...], preferred_element_type=f32)
        out[...] = total.astype(bf16)
        accumulate(squares, squared(out[...]))

    return pl.pallas_call(
        body,
        grid=(2,),
        in_specs=[
            pl.BlockSpec((tile, order), lambda i: (i, 0)),
            pl.BlockSpec((cols, split), lambda i: (at, 0)),
            pl.BlockSpec((order, cols), lambda i: (0, 0)),
            pl.BlockSpec((tile, split), lambda i: (i, 0)),
        ],
        out_specs=[
            pl.BlockSpec((tile, cols), lambda i: (i, 0)),
            pl.BlockSpec((tile, split), lambda i: (i, 0)),
            pl.BlockSpec((8, split), lambda i: (0, 0)),
        ],
        out_shape=[
            jax.ShapeDtypeStruct((order, cols), bf16),
            jax.ShapeDtypeStruct((order, split), bf16),
            jax.ShapeDtypeStruct((8, split), f32),
        ],
        name="first_product",
    )(left, right, owned, so_far)


def other_products(mid, right, so_far, start):
    order, cols = mid.shape
    rest = so_far.shape[1]
    split = order - rest
    tile = order // 2
    at = start // cols
    wanted = RETURNED[1:]

    def body(mid_ref, right_ref, before, *outs):
        squares = outs[-1]
        total = before[...] + jnp.dot(mid_ref[...], right_ref[:, split:], preferred_element_type=f32)
        rounded = total.astype(bf16)
        for out, (first, size) in zip(outs, wanted):
            out[...] = rounded[:, first - split : first - split + size]
        accumulate(squares, squared(rounded))

    return pl.pallas_call(
        body,
        grid=(2,),
        in_specs=[
            pl.BlockSpec((tile, cols), lambda i: (i, 0)),
            pl.BlockSpec((cols, order), lambda i: (at, 0)),
            pl.BlockSpec((tile, rest), lambda i: (i, 0)),
        ],
        out_specs=[
            *[pl.BlockSpec((tile, size), lambda i: (i, 0)) for _, size in wanted],
            pl.BlockSpec((8, rest), lambda i: (0, 0)),
        ],
        out_shape=[
            *[jax.ShapeDtypeStruct((order, size), bf16) for _, size in wanted],
            jax.ShapeDtypeStruct((8, rest), f32),
        ],
        name="other_products",
    )(mid, right, so_far)


def pick(position, returned):
    blocks = position.shape[0]
    slots, rows, cols = returned.shape

    def body(position_ref, returned_ref, out):
        for block in range(blocks):
            out[block] = returned_ref[position_ref[block]]

    return pl.pallas_call(
        body,
        grid_spec=pltpu.PrefetchScalarGridSpec(
            num_scalar_prefetch=1,
            grid=(1,),
            in_specs=[pl.BlockSpec((slots, rows, cols), lambda i, p: (0, 0, 0))],
            out_specs=pl.BlockSpec((blocks, rows, cols), lambda i, p: (0, 0, 0)),
        ),
        out_shape=jax.ShapeDtypeStruct((blocks, rows, cols), bf16),
        name="pick",
    )(position, returned)


def update(position, scale, returned, params, start, cols):
    blocks, rows, _ = params.shape
    slots = returned.shape[0]
    at = start // cols

    def body(position_ref, scale_ref, returned_ref, params_ref, out):
        for block in range(blocks):
            change = scale_ref[block] * returned_ref[position_ref[block]].astype(f32)
            out[block] = (params_ref[block].astype(f32) - change).astype(bf16)

    return pl.pallas_call(
        body,
        grid_spec=pltpu.PrefetchScalarGridSpec(
            num_scalar_prefetch=2,
            grid=(1,),
            in_specs=[
                pl.BlockSpec((slots, rows, cols), lambda i, p, s: (0, 0, 0)),
                pl.BlockSpec((blocks, rows, cols), lambda i, p, s: (0, 0, at)),
            ],
            out_specs=pl.BlockSpec((blocks, rows, cols), lambda i, p, s: (0, 0, 0)),
        ),
        out_shape=jax.ShapeDtypeStruct((blocks, rows, cols), bf16),
        name="update",
    )(position, scale, returned, params)


def everywhere(value):
    swap, near, wrap = [(0, 1), (1, 0)], [(0, 1), (1, 0), (2, 3), (3, 2)], [(0, 3), (3, 0), (1, 2), (2, 1)]
    steps = [("group_2", swap)]
    for axis in ("rep", "group_0", "group_1"):
        steps += [(axis, near), (axis, wrap)]
    for axis, pairs in steps:
        value = value + lax.ppermute(value, axis, pairs)
    return value


def spread(value, reps):
    half = value.shape[0] // 2
    up, down = ring(reps, 1), ring(reps, -1)
    from_down = lax.ppermute(value, "rep", up)
    from_up = lax.ppermute(value, "rep", down)
    far_low = lax.ppermute(from_down[:half], "rep", up)
    far_high = lax.ppermute(from_up[half:], "rep", down)
    return (
        (0, slice(None), value),
        (3, slice(None), from_down),
        (1, slice(None), from_up),
        (2, slice(0, half), far_low),
        (2, slice(half, 2 * half), far_high),
    )


def local(grad_parts, params, accum, left_pre, right_pre, slot_block, layer_of):
    group_size = lax.axis_size(GROUP)
    reps = lax.axis_size("rep")
    me = lax.axis_index("rep")
    group_index = lax.axis_index(GROUP)
    blocks, rows, width = params.shape
    half = blocks // 2
    up, down = ring(reps, 1), ring(reps, -1)
    parts = grad_parts[0].reshape(reps, blocks, rows, width)
    who = lax.rem(me + jnp.arange(reps, dtype=jnp.int32), reps)
    table = lax.dynamic_index_in_dim(slot_block, me, 0, keepdims=False).reshape(-1)
    wanted = jnp.maximum(table, 0)
    left, right = left_pre[0, 0, 0], right_pre[0, 0, 0]
    split = RETURNED[0][1]

    far = lax.rem(me + 2, reps)
    gradients, so_far, owned = [None] * len(SENT), [], None
    for chunk, (start, cols) in enumerate(SENT):
        low = lax.dynamic_slice(parts, (far, 0, 0, start), (1, half, rows, cols))[0]
        high = lax.dynamic_slice(parts, (far, half, 0, start), (1, half, rows, cols))[0]
        far_up = lax.ppermute(low, "rep", up)
        far_down = lax.ppermute(high, "rep", down)
        to_up, to_down = merge(who, parts, far_up, far_down, start, cols)
        near_up = lax.ppermute(to_up, "rep", up)
        near_down = lax.ppermute(to_down, "rep", down)
        gradient, outgoing = finish(who, wanted, parts, near_up, near_down, start, cols)
        gradients[chunk] = gradient
        arrived = lax.all_to_all(outgoing, GROUP, split_axis=0, concat_axis=0, tiled=True)
        if chunk > 0:
            so_far = early(left, right, owned, SENT[chunk - 1][0], so_far, split)
        owned = arrived.reshape(group_size * rows, cols)

    first, size = RETURNED[0]
    ahead = spread(params[:, :, first : first + size], reps)

    onehots = (layer_of[:, None] == jnp.arange(LAYERS, dtype=jnp.int32)[None, :]).astype(f32)
    onehot = lax.dynamic_slice_in_dim(onehots, me * blocks, blocks)
    in_order = sorted(range(len(SENT)), key=lambda c: SENT[c][0])
    wide = jnp.concatenate([gradients[c] for c in in_order], axis=2).astype(f32)
    new_accum = accum + wide * wide
    graft = wide * lax.rsqrt(new_accum)
    graft_blocks = jnp.sum(graft * graft, axis=(1, 2))
    graft_layer = jnp.sum(onehot * graft_blocks[:, None], axis=0)
    mine = lax.dynamic_index_in_dim(table, group_index, 0, keepdims=False)
    chosen = (jnp.arange(blocks, dtype=jnp.int32) == mine).astype(f32)
    my_layer = jnp.sum(chosen[:, None] * onehot, axis=0)
    position = jnp.sum(
        jnp.where(
            table[None, :] == jnp.arange(blocks, dtype=jnp.int32)[:, None],
            jnp.arange(group_size, dtype=jnp.int32)[None, :],
            0,
        ),
        axis=1,
    )
    owned, so_far, graft_layer, my_layer, position, onehots, new_accum = lax.optimization_barrier(
        (owned, so_far, graft_layer, my_layer, position, onehots, new_accum)
    )

    last = SENT[-1][0]
    mid, precond, some = first_product(left, right, owned, so_far[0], last)
    *preconds, others = other_products(mid, right, so_far[1], last)
    preconds = [precond, *preconds]
    squares = jnp.sum(some) + jnp.sum(others)
    sums = everywhere(jnp.stack([graft_layer, my_layer * squares]))
    layer_scale = jnp.sqrt(sums[0]) * lax.rsqrt(sums[1] + 1e-06)
    scales = (step_rate * jnp.sum(onehots * layer_scale[None, :], axis=1)).reshape(reps, blocks)

    new_params = jnp.zeros((reps, blocks, rows, width), bf16)
    for chunk, ((start, cols), precond) in enumerate(zip(RETURNED, preconds)):
        outgoing = precond.reshape(group_size, rows, cols)
        returned = lax.all_to_all(outgoing, GROUP, split_axis=0, concat_axis=0, tiled=True)
        if chunk == 0:
            changes = spread(pick(position, returned), reps)
            pieces = []
            for (offset, part, old), (_, _, change) in zip(ahead, changes):
                scale = scales[who[offset]][part, None, None]
                new = (old.astype(f32) - scale * change.astype(f32)).astype(bf16)
                pieces.append((offset, part, new))
        else:
            pieces = spread(update(position, scales[me], returned, params, start, cols), reps)
        for offset, part, piece in pieces:
            where = (who[offset], part.start or 0, 0, start)
            new_params = lax.dynamic_update_slice(new_params, piece[None], where)
    return (new_params.reshape(reps * blocks, rows, width), new_accum)


def solution(mesh):
    split = Mesh(mesh.devices.reshape(4, 4, 2, mesh.shape["rep"]), EVERY)
    placed = (
        P("rep", None, GROUP, None),
        P("rep", GROUP, None),
        P("rep", GROUP, None),
        P("rep", GROUP, None, None, None),
        P("rep", GROUP, None, None, None),
        P(),
        P(),
    )
    return jax.shard_map(
        local,
        mesh=split,
        in_specs=placed,
        out_specs=(P(None, GROUP, None), P("rep", GROUP, None)),
        check_vma=False,
    )
```

time: 235 us -> 253 us (1.077)
  waiting for transfers between devices: 99.3 us -> 70.1 us
  starting transfers between devices: 61.4 us -> 83.6 us
  local copies, waits for them, and re-layouts: 16.9 us -> 30.3 us
  other arithmetic: 8.42 us -> 18.9 us
    all_to_all x4 -> x5, waiting for transfers between devices: 21.5 us -> 10.9 us  [local(): lax.all_to_all(outgoing, GROUP, split_axis=0, concat_axis=0, tiled=True)]
    all_to_all x4 -> x5, starting transfers between devices: 24 us -> 34.3 us  [local(): lax.all_to_all(outgoing, GROUP, split_axis=0, concat_axis=0, tiled=True)]
    ppermute x9 -> x16, waiting for transfers between devices: 21.5 us -> 11.5 us  [the longest x4 7.18 us: spread(): from_down = lax.ppermute(value, 'rep', up)]
    ppermute x9 -> x16, starting transfers between devices: 13.5 us -> 23.3 us  [the longest x4 12.9 us: spread(): from_up = lax.ppermute(value, 'rep', down)]
    dynamic_update_slice x0 -> x5, other arithmetic: none -> 9.48 us  [local(): new_params = lax.dynamic_update_slice(new_params, piece[None], where)]
    dynamic_update_slice x10, local copies, waits for them, and re-layouts: 1.9 us -> 10.2 us  [local(): new_params = lax.dynamic_update_slice(new_params, piece[None], where)]
    slice x5 -> x10, local copies, waits for them, and re-layouts: 1.7 us -> 7.07 us  [the longest x4 3.02 us: spread(): far_high = lax.ppermute(from_up[half:], 'rep', down)]
    ppermute x6 -> x7, waiting for transfers between devices: 15.2 us -> 10.2 us  [everywhere(): value = value + lax.ppermute(value, axis, pairs)]
  transfers between devices with their start and end apart: 27 -> 36, of which waited for: 17 -> 17; matrix products, arithmetic and copies ran while one was open for 6% -> 16% of each run, Pallas kernels for 12% -> 14%
where the time goes in v1:
time: 253 us; the launch traced here: 250 us
  starting transfers between devices  83.6 us (33%)
  waiting for transfers between devices  70.1 us (28%)
  Pallas kernels  37.5 us (15%)
  local copies, waits for them, and re-layouts  30.3 us (12%)
  other arithmetic  18.9 us (7%)
  between operations  9.64 us (4%)
    all_to_all x5, starting transfers between devices, local(): lax.all_to_all(outgoing, GROUP, split_axis=0, concat_axis=0, tiled=True)  34.3 us
    ppermute x2, waiting for transfers between devices, local(): near_up = lax.ppermute(to_up, 'rep', up)  29.1 us
    ppermute x7, starting transfers between devices, everywhere(): value = value + lax.ppermute(value, axis, pairs)  13 us
    ppermute x4, starting transfers between devices, spread(): from_up = lax.ppermute(value, 'rep', down)  12.9 us
    all_to_all x5, waiting for transfers between devices, local(): lax.all_to_all(outgoing, GROUP, split_axis=0, concat_axis=0, tiled=True)  10.9 us
    ppermute x7, waiting for transfers between devices, everywhere(): value = value + lax.ppermute(value, axis, pairs)  10.2 us
    dynamic_update_slice x10, local copies, waits for them, and re-layouts, local(): new_params = lax.dynamic_update_slice(new_params, piece[None], where)  10.2 us
    dynamic_update_slice x5, other arithmetic, local(): new_params = lax.dynamic_update_slice(new_params, piece[None], where)  9.48 us
  transfers between devices with their start and end apart: 36, of which 17 were waited for; matrix products, arithmetic and copies ran while one was open for 16% of the time, Pallas kernels for 14%

profile of v1, /device:TPU:0, one launch (start us, length us, event | category | flops | bytes accessed | tf_op | source)
XLA Modules:
  0.0 250.1 jit_solution(8388205667599140685)
XLA Ops:
  6.0 8.2 %collective-permute-done.4.from_down = bf16[12,32,512]{2,1,0:T(8,128)(2,1)S(1)} collective-permute-done((bf16[12,32,512]{2,1,0:T(8,128)(2,1)S(1)}, bf16[12,32,512]{2,1,0:T(8,128)(2,1)S(1)}, u32[]{:S(2)}, u32[]{:S(2)}) %collective-permute-start.4) | collective-permute-done | bytes 393248 | tf_op jit(solution)/shard_map/ppermute | solution.py:308
  15.7 3.3 %merge.3 = (bf16[24,32,512]{2,1,0:T(8,128)(2,1)}, bf16[24,32,512]{2,1,0:T(8,128)(2,1)}) custom-call(s32[4]{0:T(128)} %compare_select_fusion.who_ref, bf16[4,24,32,1024]{3,2,1,0:T(8,128)(2,1)} %bitcast.83, bf16[4,24,32,1024]{3,2,1,0:T(8,128)(2,1)} %bitcast.84, bf16[12,32,512]{2,1,0:T(8,128)(2,1)} %copy-done.14, bf16[12,32,512]{2,1,0:T(8,128)(2,1)} %copy-done.15), custom_call_target="tpu_custom_call" | custom-call | tf_op jit(solution)/shard_map/merge/pallas_call | solution.py:47
  22.2 3.2 %collective-permute-start.1 = (bf16[12,32,512]{2,1,0:T(8,128)(2,1)S(1)}, bf16[12,32,512]{2,1,0:T(8,128)(2,1)S(1)}, u32[]{:S(2)}, u32[]{:S(2)}) collective-permute-start(bf16[12,32,512]{2,1,0:T(8,128)(2,1)S(1)} %get-tuple-element.56), channel_id=1, source_target_pairs={{0,3},{1,0},{2,1},{3,2},{4,7},{5,4},{6,5},{7,6},{8,11},{9,8},{10,9... | collective-permute-start | bytes 1179656 | tf_op jit(solution)/shard_map/ppermute | solution.py:309
  26.0 14.8 %collective-permute-done.6.one = bf16[24,32,512]{2,1,0:T(8,128)(2,1)S(1)} collective-permute-done((bf16[24,32,512]{2,1,0:T(8,128)(2,1)}, bf16[24,32,512]{2,1,0:T(8,128)(2,1)S(1)}, u32[]{:S(2)}, u32[]{:S(2)}) %collective-permute-start.6) | collective-permute-done | bytes 786464 | tf_op jit(solution)/shard_map/ppermute | solution.py:311
  41.9 4.1 %finish.3 = (bf16[24,32,512]{2,1,0:T(8,128)(2,1)}, bf16[32,32,512]{2,1,0:T(8,128)(2,1)}) custom-call(s32[4]{0:T(128)} %compare_select_fusion.who_ref, s32[32]{0:T(128)} %get-tuple-element.52.table_ref, bf16[4,24,32,1024]{3,2,1,0:T(8,128)(2,1)} %bitcast.85, bf16[24,32,512]{2,1,0:T(8,128)(2,1)} %copy-done.9, bf16[24,32,512]{2,1,0:T(8,128)(2,1)} %copy-done.10), custom_call_target="tpu_custom_call" | custom-call | tf_op jit(solution)/shard_map/finish/pallas_call | solution.py:77
  46.0 8.5 %all-to-all-start.1 = ((bf16[32,32,512]{2,1,0:T(8,128)(2,1)}), bf16[32,32,512]{2,1,0:T(8,128)(2,1)S(1)}, u32[]{:S(2)}, u32[]{:S(2)}) async-start(bf16[32,32,512]{2,1,0:T(8,128)(2,1)} %get-tuple-element.31), calls=%async_computation.1 | async-start | bytes 2097152 | tf_op jit(solution)/shard_map/all_to_all | solution.py:315
  56.1 3.3 %merge.2 = (bf16[24,32,512]{2,1,0:T(8,128)(2,1)}, bf16[24,32,512]{2,1,0:T(8,128)(2,1)}) custom-call(s32[4]{0:T(128)} %compare_select_fusion.who_ref, bf16[4,24,32,1024]{3,2,1,0:T(8,128)(2,1)} %bitcast.86, bf16[4,24,32,1024]{3,2,1,0:T(8,128)(2,1)} %bitcast.87, bf16[12,32,512]{2,1,0:T(8,128)(2,1)} %copy-done.12, bf16[12,32,512]{2,1,0:T(8,128)(2,1)} %copy-done.13), custom_call_target="tpu_custom_call" | custom-call | tf_op jit(solution)/shard_map/merge/pallas_call | solution.py:47
  67.0 14.3 %collective-permute-done.2.one = bf16[24,32,512]{2,1,0:T(8,128)(2,1)S(1)} collective-permute-done((bf16[24,32,512]{2,1,0:T(8,128)(2,1)}, bf16[24,32,512]{2,1,0:T(8,128)(2,1)S(1)}, u32[]{:S(2)}, u32[]{:S(2)}) %collective-permute-start.2) | collective-permute-done | bytes 786464 | tf_op jit(solution)/shard_map/ppermute | solution.py:311
  82.1 4.1 %finish.2 = (bf16[24,32,512]{2,1,0:T(8,128)(2,1)}, bf16[32,32,512]{2,1,0:T(8,128)(2,1)}) custom-call(s32[4]{0:T(128)} %compare_select_fusion.who_ref, s32[32]{0:T(128)} %get-tuple-element.52.table_ref, bf16[4,24,32,1024]{3,2,1,0:T(8,128)(2,1)} %bitcast.88, bf16[24,32,512]{2,1,0:T(8,128)(2,1)} %copy-done.11, bf16[24,32,512]{2,1,0:T(8,128)(2,1)} %collective-permute-done.3.two), custom_call_target="tpu_custom_call" | custom-call | tf_op jit(solution)/shard_map/finish/pallas_call | solution.py:77
  86.2 7.4 %all-to-all-start = ((bf16[32,32,512]{2,1,0:T(8,128)(2,1)}), bf16[32,32,512]{2,1,0:T(8,128)(2,1)S(1)}, u32[]{:S(2)}, u32[]{:S(2)}) async-start(bf16[32,32,512]{2,1,0:T(8,128)(2,1)} %get-tuple-element.28), calls=%async_computation | async-start | bytes 2097152 | tf_op jit(solution)/shard_map/all_to_all | solution.py:315
  101.2 4.7 %fusion = (f32[24,32,1024]{2,1,0:T(8,128)}, f32[24]{0:T(128)S(1)}) fusion(f32[24,32,1024]{2,1,0:T(8,128)} %param.9, bf16[24,32,512]{2,1,0:T(8,128)(2,1)} %get-tuple-element.35, bf16[24,32,512]{2,1,0:T(8,128)(2,1)} %get-tuple-element.34), kind=kLoop, calls=%fused_computation.2 | loop fusion | flops 7077864 | bytes 7864416 | tf_op jit(solution)/shard_map/add | solution.py:327
  106.1 5.6 %early.1 = (f32[1024,256]{1,0:T(8,128)}, f32[1024,768]{1,0:T(8,128)}) custom-call(bf16[1024,1024]{1,0:T(8,128)(2,1)} %bitcast.92, bf16[1024,1024]{1,0:T(8,128)(2,1)} %bitcast.89, bf16[1024,512]{1,0:T(8,128)(2,1)} %bitcast.94), custom_call_target="tpu_custom_call" | custom-call | tf_op jit(solution)/shard_map/early/pallas_call | solution.py:111
  112.7 4.7 %first_product.1 = (bf16[1024,512]{1,0:T(8,128)(2,1)}, bf16[1024,256]{1,0:T(8,128)(2,1)}, f32[8,256]{1,0:T(8,128)}) custom-call(bf16[1024,1024]{1,0:T(8,128)(2,1)} %bitcast.93, bf16[1024,1024]{1,0:T(8,128)(2,1)} %bitcast.90, bf16[1024,512]{1,0:T(8,128)(2,1)} %bitcast.95, f32[1024,256]{1,0:T(8,128)} %get-tuple-element.40.before), custom_call_target="tpu_custom_call" | custom-call | tf_op jit(solution)/shard_map/first_product/pallas_call | solution.py:156
  117.3 4.1 %other_products.1 = (bf16[1024,256]{1,0:T(8,128)(2,1)}, bf16[1024,512]{1,0:T(8,128)(2,1)}, f32[8,768]{1,0:T(8,128)}) custom-call(bf16[1024,512]{1,0:T(8,128)(2,1)} %get-tuple-element.42.mid_ref, bf16[1024,1024]{1,0:T(8,128)(2,1)} %bitcast.91, f32[1024,768]{1,0:T(8,128)} %get-tuple-element.43.before), custom_call_target="tpu_custom_call" | custom-call | tf_op jit(solution)/shard_map/other_products/pallas_call | solution.py:195
  123.4 7.4 %all-to-all-start.3 = ((bf16[32,32,256]{2,1,0:T(8,128)(2,1)}), bf16[32,32,256]{2,1,0:T(8,128)(2,1)S(1)}, u32[]{:S(2)}, u32[]{:S(2)}) async-start(bf16[32,32,256]{2,1,0:T(8,128)(2,1)} %bitcast.97), calls=%async_computation.3 | async-start | bytes 1048576 | tf_op jit(solution)/shard_map/all_to_all | solution.py:358
  158.5 6.9 %all-to-all-start.2 = ((bf16[32,32,256]{2,1,0:T(8,128)(2,1)}), bf16[32,32,256]{2,1,0:T(8,128)(2,1)S(1)}, u32[]{:S(2)}, u32[]{:S(2)}) async-start(bf16[32,32,256]{2,1,0:T(8,128)(2,1)} %bitcast.16), calls=%async_computation.2 | async-start | bytes 1048576 | tf_op jit(solution)/shard_map/all_to_all | solution.py:358
  165.6 10.9 %all-to-all-done.2.returned_ref = bf16[32,32,256]{2,1,0:T(8,128)(2,1)S(1)} async-done(((bf16[32,32,256]{2,1,0:T(8,128)(2,1)}), bf16[32,32,256]{2,1,0:T(8,128)(2,1)S(1)}, u32[]{:S(2)}, u32[]{:S(2)}) %all-to-all-start.2) | async-done | bytes 524320 | tf_op jit(solution)/shard_map/all_to_all | solution.py:358
  176.5 4.1 %all-to-all-start.4 = ((bf16[32,32,512]{2,1,0:T(8,128)(2,1)}), bf16[32,32,512]{2,1,0:T(8,128)(2,1)S(1)}, u32[]{:S(2)}, u32[]{:S(2)}) async-start(bf16[32,32,512]{2,1,0:T(8,128)(2,1)} %bitcast.96), calls=%async_computation.4 | async-start | bytes 2097152 | tf_op jit(solution)/shard_map/all_to_all | solution.py:358
  183.7 3.2 %collective-permute-start.18 = (bf16[24,32,256]{2,1,0:T(8,128)(2,1)}, bf16[24,32,256]{2,1,0:T(8,128)(2,1)}, u32[]{:S(2)}, u32[]{:S(2)}) collective-permute-start(bf16[24,32,256]{2,1,0:T(8,128)(2,1)} %pick.1), channel_id=1, source_target_pairs={{0,3},{1,0},{2,1},{3,2},{4,7},{5,4},{6,5},{7,6},{8,11},{9,8},{10,9... | collective-permute-start | bytes 1179656 | tf_op jit(solution)/shard_map/ppermute | solution.py:276
  189.6 3.2 %collective-permute-start.24 = (bf16[24,32,256]{2,1,0:T(8,128)(2,1)}, bf16[24,32,256]{2,1,0:T(8,128)(2,1)S(1)}, u32[]{:S(2)}, u32[]{:S(2)}) collective-permute-start(bf16[24,32,256]{2,1,0:T(8,128)(2,1)} %update.2), channel_id=1, source_target_pairs={{0,3},{1,0},{2,1},{3,2},{4,7},{5,4},{6,5},{7,6},{8,11},{9,8},{10,9... | collective-permute-start | bytes 1179656 | tf_op jit(solution)/shard_map/ppermute | solution.py:276
  192.9 3.5 %broadcast_in_dim.69 = bf16[4,24,32,1024]{3,2,1,0:T(8,128)(2,1)} broadcast(bf16[]{:T(256)} %constant.55.clone.1), dimensions={} | broadcast | bytes 6291458 | tf_op jit(solution)/shard_map/broadcast_in_dim | solution.py:355
  213.8 3.3 %update.3 = bf16[24,32,512]{2,1,0:T(8,128)(2,1)} custom-call(s32[24]{0:T(128)} %select_reduce_fusion.position_ref, f32[24]{0:T(128)} %get-tuple-element.60.scale_ref, bf16[32,32,512]{2,1,0:T(8,128)(2,1)} %copy-done.1, bf16[24,32,1024]{2,1,0:T(8,128)(2,1)} %params_ref.3), custom_call_target="tpu_custom_call" | custom-call | tf_op jit(solution)/shard_map/update/pallas_call | solution.py:246
  233.2 5.3 %collective-permute-done.27 = bf16[24,32,512]{2,1,0:T(8,128)(2,1)S(1)} collective-permute-done((bf16[24,32,512]{2,1,0:T(8,128)(2,1)}, bf16[24,32,512]{2,1,0:T(8,128)(2,1)S(1)}, u32[]{:S(2)}, u32[]{:S(2)}) %collective-permute-start.27) | collective-permute-done | bytes 786464 | tf_op jit(solution)/shard_map/ppermute | solution.py:275
  239.9 3.7 %collective-permute-start.30 = (bf16[12,32,512]{2,1,0:T(8,128)(2,1)S(1)}, bf16[12,32,512]{2,1,0:T(8,128)(2,1)S(1)}, u32[]{:S(2)}, u32[]{:S(2)}) collective-permute-start(bf16[12,32,512]{2,1,0:T(8,128)(2,1)S(1)} %slice.93), channel_id=1, source_target_pairs={{0,3},{1,0},{2,1},{3,2},{4,7},{5,4},{6,5},{7,6},{8,11},{9,8},{10,9... | collective-permute-start | bytes 1179656 | tf_op jit(solution)/shard_map/ppermute | solution.py:278
  (150 shorter events, 98.8 us)
Async XLA Ops:
  19.0 21.8 %collective-permute-start.6 = (bf16[24,32,512]{2,1,0:T(8,128)(2,1)}, bf16[24,32,512]{2,1,0:T(8,128)(2,1)S(1)}, u32[]{:S(2)}, u32[]{:S(2)}) collective-permute-start(bf16[24,32,512]{2,1,0:T(8,128)(2,1)} %get-tuple-element.29), channel_id=1, source_target_pairs={{0,1},{1,2},{2,3},{3,0},{4,5},{5,6},{6,7},{7,4},{8,9},{9,10},{10,1... | collective-permute-start | bytes 2359304 | tf_op jit(solution)/shard_map/ppermute | solution.py:311
  19.9 20.9 %collective-permute-start.7 = (bf16[24,32,512]{2,1,0:T(8,128)(2,1)}, bf16[24,32,512]{2,1,0:T(8,128)(2,1)S(1)}, u32[]{:S(2)}, u32[]{:S(2)}) collective-permute-start(bf16[24,32,512]{2,1,0:T(8,128)(2,1)} %get-tuple-element.30), channel_id=1, source_target_pairs={{0,3},{1,0},{2,1},{3,2},{4,7},{5,4},{6,5},{7,6},{8,11},{9,8},{10,9... | collective-permute-start | bytes 2359304 | tf_op jit(solution)/shard_map/ppermute | solution.py:312
  22.2 32.4 %collective-permute-start = (bf16[12,32,512]{2,1,0:T(8,128)(2,1)S(1)}, bf16[12,32,512]{2,1,0:T(8,128)(2,1)S(1)}, u32[]{:S(2)}, u32[]{:S(2)}) collective-permute-start(bf16[12,32,512]{2,1,0:T(8,128)(2,1)S(1)} %get-tuple-element.57), channel_id=1, source_target_pairs={{0,1},{1,2},{2,3},{3,0},{4,5},{5,6},{6,7},{7,4},{8,9},{9,10},{10,1... | collective-permute-start | bytes 1179656 | tf_op jit(solution)/shard_map/ppermute | solution.py:308
  22.2 32.4 %collective-permute-start.1 = (bf16[12,32,512]{2,1,0:T(8,128)(2,1)S(1)}, bf16[12,32,512]{2,1,0:T(8,128)(2,1)S(1)}, u32[]{:S(2)}, u32[]{:S(2)}) collective-permute-start(bf16[12,32,512]{2,1,0:T(8,128)(2,1)S(1)} %get-tuple-element.56), channel_id=1, source_target_pairs={{0,3},{1,0},{2,1},{3,2},{4,7},{5,4},{6,5},{7,6},{8,11},{9,8},{10,9... | collective-permute-start | bytes 1179656 | tf_op jit(solution)/shard_map/ppermute | solution.py:309
  46.0 40.2 %all-to-all-start.1 = ((bf16[32,32,512]{2,1,0:T(8,128)(2,1)}), bf16[32,32,512]{2,1,0:T(8,128)(2,1)S(1)}, u32[]{:S(2)}, u32[]{:S(2)}) async-start(bf16[32,32,512]{2,1,0:T(8,128)(2,1)} %get-tuple-element.31), calls=%async_computation.1 | async-start | bytes 2097152 | tf_op jit(solution)/shard_map/all_to_all | solution.py:315
  59.4 21.9 %collective-permute-start.2 = (bf16[24,32,512]{2,1,0:T(8,128)(2,1)}, bf16[24,32,512]{2,1,0:T(8,128)(2,1)S(1)}, u32[]{:S(2)}, u32[]{:S(2)}) collective-permute-start(bf16[24,32,512]{2,1,0:T(8,128)(2,1)} %get-tuple-element.26), channel_id=1, source_target_pairs={{0,1},{1,2},{2,3},{3,0},{4,5},{5,6},{6,7},{7,4},{8,9},{9,10},{10,1... | collective-permute-start | bytes 2359304 | tf_op jit(solution)/shard_map/ppermute | solution.py:311
  59.9 21.4 %collective-permute-start.3 = (bf16[24,32,512]{2,1,0:T(8,128)(2,1)}, bf16[24,32,512]{2,1,0:T(8,128)(2,1)}, u32[]{:S(2)}, u32[]{:S(2)}) collective-permute-start(bf16[24,32,512]{2,1,0:T(8,128)(2,1)} %get-tuple-element.27), channel_id=1, source_target_pairs={{0,3},{1,0},{2,1},{3,2},{4,7},{5,4},{6,5},{7,6},{8,11},{9,8},{10,9... | collective-permute-start | bytes 2359304 | tf_op jit(solution)/shard_map/ppermute | solution.py:312
  63.7 84.7 %collective-permute-start.15 = (bf16[24,32,256]{2,1,0:T(8,128)(2,1)S(1)}, bf16[24,32,256]{2,1,0:T(8,128)(2,1)S(1)}, u32[]{:S(2)}, u32[]{:S(2)}) collective-permute-start(bf16[24,32,256]{2,1,0:T(8,128)(2,1)S(1)} %slice.69), channel_id=1, source_target_pairs={{0,1},{1,2},{2,3},{3,0},{4,5},{5,6},{6,7},{7,4},{8,9},{9,10},{10,1... | collective-permute-start | bytes 1179656 | tf_op jit(solution)/shard_map/ppermute | solution.py:275
  63.8 93.0 %collective-permute-start.17 = (bf16[24,32,256]{2,1,0:T(8,128)(2,1)S(1)}, bf16[24,32,256]{2,1,0:T(8,128)(2,1)S(1)}, u32[]{:S(2)}, u32[]{:S(2)}) collective-permute-start(bf16[24,32,256]{2,1,0:T(8,128)(2,1)S(1)} %slice.69), channel_id=1, source_target_pairs={{0,3},{1,0},{2,1},{3,2},{4,7},{5,4},{6,5},{7,6},{8,11},{9,8},{10,9... | collective-permute-start | bytes 1179656 | tf_op jit(solution)/shard_map/ppermute | solution.py:276
  86.2 25.5 %all-to-all-start = ((bf16[32,32,512]{2,1,0:T(8,128)(2,1)}), bf16[32,32,512]{2,1,0:T(8,128)(2,1)S(1)}, u32[]{:S(2)}, u32[]{:S(2)}) async-start(bf16[32,32,512]{2,1,0:T(8,128)(2,1)} %get-tuple-element.28), calls=%async_computation | async-start | bytes 2097152 | tf_op jit(solution)/shard_map/all_to_all | solution.py:315
  123.4 35.2 %all-to-all-start.3 = ((bf16[32,32,256]{2,1,0:T(8,128)(2,1)}), bf16[32,32,256]{2,1,0:T(8,128)(2,1)S(1)}, u32[]{:S(2)}, u32[]{:S(2)}) async-start(bf16[32,32,256]{2,1,0:T(8,128)(2,1)} %bitcast.97), calls=%async_computation.3 | async-start | bytes 1048576 | tf_op jit(solution)/shard_map/all_to_all | solution.py:358
  152.0 65.1 %collective-permute-start.19 = (bf16[12,32,256]{2,1,0:T(8,128)(2,1)S(1)}, bf16[12,32,256]{2,1,0:T(8,128)(2,1)}, u32[]{:S(2)}, u32[]{:S(2)}) collective-permute-start(bf16[12,32,256]{2,1,0:T(8,128)(2,1)S(1)} %slice.86), channel_id=1, source_target_pairs={{0,1},{1,2},{2,3},{3,0},{4,5},{5,6},{6,7},{7,4},{8,9},{9,10},{10,1... | collective-permute-start | bytes 589832 | tf_op jit(solution)/shard_map/ppermute | solution.py:277
  158.5 18.0 %all-to-all-start.2 = ((bf16[32,32,256]{2,1,0:T(8,128)(2,1)}), bf16[32,32,256]{2,1,0:T(8,128)(2,1)S(1)}, u32[]{:S(2)}, u32[]{:S(2)}) async-start(bf16[32,32,256]{2,1,0:T(8,128)(2,1)} %bitcast.16), calls=%async_computation.2 | async-start | bytes 1048576 | tf_op jit(solution)/shard_map/all_to_all | solution.py:358
  176.5 36.3 %all-to-all-start.4 = ((bf16[32,32,512]{2,1,0:T(8,128)(2,1)}), bf16[32,32,512]{2,1,0:T(8,128)(2,1)S(1)}, u32[]{:S(2)}, u32[]{:S(2)}) async-start(bf16[32,32,512]{2,1,0:T(8,128)(2,1)} %bitcast.96), calls=%async_computation.4 | async-start | bytes 2097152 | tf_op jit(solution)/shard_map/all_to_all | solution.py:358
  183.7 14.7 %collective-permute-start.16 = (bf16[24,32,256]{2,1,0:T(8,128)(2,1)}, bf16[24,32,256]{2,1,0:T(8,128)(2,1)}, u32[]{:S(2)}, u32[]{:S(2)}) collective-permute-start(bf16[24,32,256]{2,1,0:T(8,128)(2,1)} %pick.1), channel_id=1, source_target_pairs={{0,1},{1,2},{2,3},{3,0},{4,5},{5,6},{6,7},{7,4},{8,9},{9,10},{10,1... | collective-permute-start | bytes 1179656 | tf_op jit(solution)/shard_map/ppermute | solution.py:275
  183.7 16.4 %collective-permute-start.18 = (bf16[24,32,256]{2,1,0:T(8,128)(2,1)}, bf16[24,32,256]{2,1,0:T(8,128)(2,1)}, u32[]{:S(2)}, u32[]{:S(2)}) collective-permute-start(bf16[24,32,256]{2,1,0:T(8,128)(2,1)} %pick.1), channel_id=1, source_target_pairs={{0,3},{1,0},{2,1},{3,2},{4,7},{5,4},{6,5},{7,6},{8,11},{9,8},{10,9... | collective-permute-start | bytes 1179656 | tf_op jit(solution)/shard_map/ppermute | solution.py:276
  189.6 15.9 %collective-permute-start.23 = (bf16[24,32,256]{2,1,0:T(8,128)(2,1)}, bf16[24,32,256]{2,1,0:T(8,128)(2,1)S(1)}, u32[]{:S(2)}, u32[]{:S(2)}) collective-permute-start(bf16[24,32,256]{2,1,0:T(8,128)(2,1)} %update.2), channel_id=1, source_target_pairs={{0,1},{1,2},{2,3},{3,0},{4,5},{5,6},{6,7},{7,4},{8,9},{9,10},{10,1... | collective-permute-start | bytes 1179656 | tf_op jit(solution)/shard_map/ppermute | solution.py:275
  189.6 17.9 %collective-permute-start.24 = (bf16[24,32,256]{2,1,0:T(8,128)(2,1)}, bf16[24,32,256]{2,1,0:T(8,128)(2,1)S(1)}, u32[]{:S(2)}, u32[]{:S(2)}) collective-permute-start(bf16[24,32,256]{2,1,0:T(8,128)(2,1)} %update.2), channel_id=1, source_target_pairs={{0,3},{1,0},{2,1},{3,2},{4,7},{5,4},{6,5},{7,6},{8,11},{9,8},{10,9... | collective-permute-start | bytes 1179656 | tf_op jit(solution)/shard_map/ppermute | solution.py:276
  198.4 23.0 %collective-permute-start.21 = (bf16[12,32,256]{2,1,0:T(8,128)(2,1)}, bf16[12,32,256]{2,1,0:T(8,128)(2,1)}, u32[]{:S(2)}, u32[]{:S(2)}) collective-permute-start(bf16[12,32,256]{2,1,0:T(8,128)(2,1)} %slice.88), channel_id=1, source_target_pairs={{0,3},{1,0},{2,1},{3,2},{4,7},{5,4},{6,5},{7,6},{8,11},{9,8},{10,9... | collective-permute-start | bytes 589832 | tf_op jit(solution)/shard_map/ppermute | solution.py:278
  200.1 19.5 %collective-permute-start.20 = (bf16[12,32,256]{2,1,0:T(8,128)(2,1)}, bf16[12,32,256]{2,1,0:T(8,128)(2,1)}, u32[]{:S(2)}, u32[]{:S(2)}) collective-permute-start(bf16[12,32,256]{2,1,0:T(8,128)(2,1)} %slice.87), channel_id=1, source_target_pairs={{0,1},{1,2},{2,3},{3,0},{4,5},{5,6},{6,7},{7,4},{8,9},{9,10},{10,1... | collective-permute-start | bytes 589832 | tf_op jit(solution)/shard_map/ppermute | solution.py:277
  205.5 19.1 %collective-permute-start.22 = (bf16[12,32,256]{2,1,0:T(8,128)(2,1)}, bf16[12,32,256]{2,1,0:T(8,128)(2,1)}, u32[]{:S(2)}, u32[]{:S(2)}) collective-permute-start(bf16[12,32,256]{2,1,0:T(8,128)(2,1)} %slice.89), channel_id=1, source_target_pairs={{0,3},{1,0},{2,1},{3,2},{4,7},{5,4},{6,5},{7,6},{8,11},{9,8},{10,9... | collective-permute-start | bytes 589832 | tf_op jit(solution)/shard_map/ppermute | solution.py:278
  207.5 21.3 %collective-permute-start.25 = (bf16[12,32,256]{2,1,0:T(8,128)(2,1)}, bf16[12,32,256]{2,1,0:T(8,128)(2,1)}, u32[]{:S(2)}, u32[]{:S(2)}) collective-permute-start(bf16[12,32,256]{2,1,0:T(8,128)(2,1)} %slice.90), channel_id=1, source_target_pairs={{0,1},{1,2},{2,3},{3,0},{4,5},{5,6},{6,7},{7,4},{8,9},{9,10},{10,1... | collective-permute-start | bytes 589832 | tf_op jit(solution)/shard_map/ppermute | solution.py:277
  219.6 18.9 %collective-permute-start.27 = (bf16[24,32,512]{2,1,0:T(8,128)(2,1)}, bf16[24,32,512]{2,1,0:T(8,128)(2,1)S(1)}, u32[]{:S(2)}, u32[]{:S(2)}) collective-permute-start(bf16[24,32,512]{2,1,0:T(8,128)(2,1)} %update.3), channel_id=1, source_target_pairs={{0,1},{1,2},{2,3},{3,0},{4,5},{5,6},{6,7},{7,4},{8,9},{9,10},{10,1... | collective-permute-start | bytes 2359304 | tf_op jit(solution)/shard_map/ppermute | solution.py:275
  221.4 18.5 %collective-permute-start.28 = (bf16[24,32,512]{2,1,0:T(8,128)(2,1)}, bf16[24,32,512]{2,1,0:T(8,128)(2,1)S(1)}, u32[]{:S(2)}, u32[]{:S(2)}) collective-permute-start(bf16[24,32,512]{2,1,0:T(8,128)(2,1)} %update.3), channel_id=1, source_target_pairs={{0,3},{1,0},{2,1},{3,2},{4,7},{5,4},{6,5},{7,6},{8,11},{9,8},{10,9... | collective-permute-start | bytes 2359304 | tf_op jit(solution)/shard_map/ppermute | solution.py:276
  (32 other events, 304.5 us)

commit v2 on v1

--- a/solution.py
+++ b/solution.py
@@ -10,8 +10,8 @@
 LAYERS = 8
 GROUP = ("group_0", "group_1", "group_2")
 EVERY = ("group_0", "group_1", "group_2", "rep")
-SENT = ((0, 512), (512, 512))
-RETURNED = ((0, 256), (256, 256), (512, 512))
+SENT = ((768, 256), (0, 768))
+RETURNED = ((0, 512), (512, 512))
 
 
 step_rate = 0.5
@@ -212,37 +212,48 @@
     )(mid, right, so_far)
 
 
-def pick(position, returned):
+def pick(position, returned, whole):
     blocks = position.shape[0]
+    half = blocks // 2
     slots, rows, cols = returned.shape
 
-    def body(position_ref, returned_ref, out):
-        for block in range(blocks):
-            out[block] = returned_ref[position_ref[block]]
-
+    def body(position_ref, returned_ref, low, high, blank):
+        for block in range(half):
+            low[block] = returned_ref[position_ref[block]]
+            high[block] = returned_ref[position_ref[half + block]]
+
+    out = pl.BlockSpec((half, rows, cols), lambda i, p: (0, 0, 0))
+    shape = jax.ShapeDtypeStruct((half, rows, cols), bf16)
     return pl.pallas_call(
         body,
         grid_spec=pltpu.PrefetchScalarGridSpec(
             num_scalar_prefetch=1,
             grid=(1,),
             in_specs=[pl.BlockSpec((slots, rows, cols), lambda i, p: (0, 0, 0))],
-            out_specs=pl.BlockSpec((blocks, rows, cols), lambda i, p: (0, 0, 0)),
+            out_specs=[out, out, pl.BlockSpec(memory_space=pl.ANY)],
         ),
-        out_shape=jax.ShapeDtypeStruct((blocks, rows, cols), bf16),
+        out_shape=[shape, shape, jax.ShapeDtypeStruct(whole, bf16)],
         name="pick",
     )(position, returned)
 
 
 def update(position, scale, returned, params, start, cols):
     blocks, rows, _ = params.shape
+    half = blocks // 2
     slots = returned.shape[0]
     at = start // cols
 
-    def body(position_ref, scale_ref, returned_ref, params_ref, out):
+    def body(position_ref, scale_ref, returned_ref, params_ref, low, high):
         for block in range(blocks):
             change = scale_ref[block] * returned_ref[position_ref[block]].astype(f32)
-            out[block] = (params_ref[block].astype(f32) - change).astype(bf16)
-
+            new = (params_ref[block].astype(f32) - change).astype(bf16)
+            if block < half:
+                low[block] = new
+            else:
+                high[block - half] = new
+
+    out = pl.BlockSpec((half, rows, cols), lambda i, p, s: (0, 0, 0))
+    shape = jax.ShapeDtypeStruct((half, rows, cols), bf16)
     return pl.pallas_call(
         body,
         grid_spec=pltpu.PrefetchScalarGridSpec(
@@ -252,9 +263,9 @@
                 pl.BlockSpec((slots, rows, cols), lambda i, p, s: (0, 0, 0)),
                 pl.BlockSpec((blocks, rows, cols), lambda i, p, s: (0, 0, at)),
             ],
-            out_specs=pl.BlockSpec((blocks, rows, cols), lambda i, p, s: (0, 0, 0)),
+            out_specs=[out, out],
         ),
-        out_shape=jax.ShapeDtypeStruct((blocks, rows, cols), bf16),
+        out_shape=[shape, shape],
         name="update",
     )(position, scale, returned, params)
 
@@ -269,19 +280,23 @@
     return value
 
 
-def spread(value, reps):
-    half = value.shape[0] // 2
+def spread(low, high, reps):
     up, down = ring(reps, 1), ring(reps, -1)
-    from_down = lax.ppermute(value, "rep", up)
-    from_up = lax.ppermute(value, "rep", down)
-    far_low = lax.ppermute(from_down[:half], "rep", up)
-    far_high = lax.ppermute(from_up[half:], "rep", down)
+    low_up = lax.ppermute(low, "rep", up)
+    high_down = lax.ppermute(high, "rep", down)
+    high_up = lax.ppermute(high, "rep", up)
+    low_down = lax.ppermute(low, "rep", down)
+    far_low = lax.ppermute(low_up, "rep", up)
+    far_high = lax.ppermute(high_down, "rep", down)
     return (
-        (0, slice(None), value),
-        (3, slice(None), from_down),
-        (1, slice(None), from_up),
-        (2, slice(0, half), far_low),
-        (2, slice(half, 2 * half), far_high),
+        (0, 0, low),
+        (0, 1, high),
+        (3, 0, low_up),
+        (1, 1, high_down),
+        (3, 1, high_up),
+        (1, 0, low_down),
+        (2, 0, far_low),
+        (2, 1, far_high),
     )
 
 
@@ -318,7 +333,8 @@
         owned = arrived.reshape(group_size * rows, cols)
 
     first, size = RETURNED[0]
-    ahead = spread(params[:, :, first : first + size], reps)
+    columns = params[:, :, first : first + size]
+    ahead = spread(columns[:half], columns[half:], reps)
 
     onehots = (layer_of[:, None] == jnp.arange(LAYERS, dtype=jnp.int32)[None, :]).astype(f32)
     onehot = lax.dynamic_slice_in_dim(onehots, me * blocks, blocks)
@@ -352,21 +368,21 @@
     layer_scale = jnp.sqrt(sums[0]) * lax.rsqrt(sums[1] + 1e-06)
     scales = (step_rate * jnp.sum(onehots * layer_scale[None, :], axis=1)).reshape(reps, blocks)
 
-    new_params = jnp.zeros((reps, blocks, rows, width), bf16)
     for chunk, ((start, cols), precond) in enumerate(zip(RETURNED, preconds)):
         outgoing = precond.reshape(group_size, rows, cols)
         returned = lax.all_to_all(outgoing, GROUP, split_axis=0, concat_axis=0, tiled=True)
         if chunk == 0:
-            changes = spread(pick(position, returned), reps)
+            low, high, new_params = pick(position, returned, (reps, blocks, rows, width))
             pieces = []
-            for (offset, part, old), (_, _, change) in zip(ahead, changes):
-                scale = scales[who[offset]][part, None, None]
+            for (offset, part, old), (_, _, change) in zip(ahead, spread(low, high, reps)):
+                scale = scales[who[offset]][part * half : (part + 1) * half, None, None]
                 new = (old.astype(f32) - scale * change.astype(f32)).astype(bf16)
                 pieces.append((offset, part, new))
         else:
-            pieces = spread(update(position, scales[me], returned, params, start, cols), reps)
+            low, high = update(position, scales[me], returned, params, start, cols)
+            pieces = spread(low, high, reps)
         for offset, part, piece in pieces:
-            where = (who[offset], part.start or 0, 0, start)
+            where = (who[offset], part * half, 0, start)
             new_params = lax.dynamic_update_slice(new_params, piece[None], where)
     return (new_params.reshape(reps * blocks, rows, width), new_accum)
 

time: 253 us -> 269 us (1.063)
  waiting for transfers between devices: 70.1 us -> 105 us
  starting transfers between devices: 83.6 us -> 72.6 us
  local copies, waits for them, and re-layouts: 30.3 us -> 19.5 us
    ppermute x2, waiting for transfers between devices: 8.17 us -> 37.3 us  [local(): far_up = lax.ppermute(low, 'rep', up)]
    ppermute x16 -> x18, waiting for transfers between devices: 11.5 us -> 34.8 us  [the longest x3 16 us: spread(): far_low = lax.ppermute(low_up, 'rep', up)]
    ppermute x2, waiting for transfers between devices: 29.1 us -> 6.74 us  [local(): near_up = lax.ppermute(to_up, 'rep', up)]
    all_to_all x5 -> x4, starting transfers between devices: 34.3 us -> 23.7 us  [local(): lax.all_to_all(outgoing, GROUP, split_axis=0, concat_axis=0, tiled=True)]
    all_to_all x5 -> x4, waiting for transfers between devices: 10.9 us -> 19.1 us  [local(): lax.all_to_all(outgoing, GROUP, split_axis=0, concat_axis=0, tiled=True)]
    slice x10 -> x2, local copies, waits for them, and re-layouts: 7.07 us -> 1.64 us  [the longest x1 0.97 us: local(): ahead = spread(columns[:half], columns[half:], reps)]
    dynamic_update_slice x10 -> x8, local copies, waits for them, and re-layouts: 10.2 us -> 6.17 us  [local(): new_params = lax.dynamic_update_slice(new_params, piece[None], where)]
    broadcast_in_dim x1 -> x0, local copies, waits for them, and re-layouts: 3.51 us -> none  [local(): new_params = jnp.zeros((reps, blocks, rows, width), bf16)]
  transfers between devices with their start and end apart: 36 -> 37, of which waited for: 17 -> 22; matrix products, arithmetic and copies ran while one was open for 16% -> 12% of each run, Pallas kernels for 14% -> 13%
where the time goes in v2:
time: 269 us; the launch traced here: 267 us
  waiting for transfers between devices  105 us (39%)
  starting transfers between devices  72.6 us (27%)
  Pallas kernels  37.5 us (14%)
  other arithmetic  21.5 us (8%)
  local copies, waits for them, and re-layouts  19.5 us (7%)
  between operations  10 us (4%)
    ppermute x2, waiting for transfers between devices, local(): far_up = lax.ppermute(low, 'rep', up)  37.3 us
    all_to_all x4, starting transfers between devices, local(): lax.all_to_all(outgoing, GROUP, split_axis=0, concat_axis=0, tiled=True)  23.7 us
    all_to_all x4, waiting for transfers between devices, local(): lax.all_to_all(outgoing, GROUP, split_axis=0, concat_axis=0, tiled=True)  19.1 us
    ppermute x3, waiting for transfers between devices, spread(): far_low = lax.ppermute(low_up, 'rep', up)  16 us
    ppermute x7, starting transfers between devices, everywhere(): value = value + lax.ppermute(value, axis, pairs)  14.8 us
    dynamic_update_slice x8, other arithmetic, local(): new_params = lax.dynamic_update_slice(new_params, piece[None], where)  11.6 us
    ppermute x3, starting transfers between devices, spread(): low_down = lax.ppermute(low, 'rep', down)  9.49 us
    pallas_call x2, Pallas kernels, finish(): pl.pallas_call(body, grid_spec=pltpu.PrefetchScalarGridSpec(num_scalar_pr...  8.34 us
  transfers between devices with their start and end apart: 37, of which 22 were waited for; matrix products, arithmetic and copies ran while one was open for 12% of the time, Pallas kernels for 13%

profile of v2, /device:TPU:0, one launch (start us, length us, event | category | flops | bytes accessed | tf_op | source)
XLA Modules:
  0.0 266.6 jit_solution(8405684319083154083)
XLA Ops:
  5.8 12.5 %collective-permute-done.from_down = bf16[12,32,768]{2,1,0:T(8,128)(2,1)S(1)} collective-permute-done((bf16[12,32,768]{2,1,0:T(8,128)(2,1)S(1)}, bf16[12,32,768]{2,1,0:T(8,128)(2,1)S(1)}, u32[]{:S(2)}, u32[]{:S(2)}) %collective-permute-start) | collective-permute-done | bytes 589856 | tf_op jit(solution)/shard_map/ppermute | solution.py:323
  19.9 3.8 %merge.2 = (bf16[24,32,768]{2,1,0:T(8,128)(2,1)}, bf16[24,32,768]{2,1,0:T(8,128)(2,1)}) custom-call(s32[4]{0:T(128)} %compare_select_fusion.who_ref, bf16[4,24,32,1024]{3,2,1,0:T(8,128)(2,1)} %bitcast.96, bf16[4,24,32,1024]{3,2,1,0:T(8,128)(2,1)} %bitcast.97, bf16[12,32,768]{2,1,0:T(8,128)(2,1)} %copy-done.6, bf16[12,32,768]{2,1,0:T(8,128)(2,1)} %copy-done.7), custom_call_target="tpu_custom_call" | custom-call | tf_op jit(solution)/shard_map/merge/pallas_call | solution.py:47
  31.3 24.8 %collective-permute-done.4.from_down = bf16[12,32,256]{2,1,0:T(8,128)(2,1)S(1)} collective-permute-done((bf16[12,32,256]{2,1,0:T(8,128)(2,1)S(1)}, bf16[12,32,256]{2,1,0:T(8,128)(2,1)S(1)}, u32[]{:S(2)}, u32[]{:S(2)}) %collective-permute-start.4) | collective-permute-done | bytes 196640 | tf_op jit(solution)/shard_map/ppermute | solution.py:323
  64.2 6.7 %collective-permute-done.6.one = bf16[24,32,256]{2,1,0:T(8,128)(2,1)S(1)} collective-permute-done((bf16[24,32,256]{2,1,0:T(8,128)(2,1)}, bf16[24,32,256]{2,1,0:T(8,128)(2,1)S(1)}, u32[]{:S(2)}, u32[]{:S(2)}) %collective-permute-start.6) | collective-permute-done | bytes 393248 | tf_op jit(solution)/shard_map/ppermute | solution.py:326
  74.9 8.8 %all-to-all-start.1 = ((bf16[32,32,256]{2,1,0:T(8,128)(2,1)}), bf16[32,32,256]{2,1,0:T(8,128)(2,1)S(1)}, u32[]{:S(2)}, u32[]{:S(2)}) async-start(bf16[32,32,256]{2,1,0:T(8,128)(2,1)} %get-tuple-element.35), calls=%async_computation.1 | async-start | bytes 1048576 | tf_op jit(solution)/shard_map/all_to_all | solution.py:330
  83.8 5.2 %finish.2 = (bf16[24,32,768]{2,1,0:T(8,128)(2,1)}, bf16[32,32,768]{2,1,0:T(8,128)(2,1)}) custom-call(s32[4]{0:T(128)} %compare_select_fusion.who_ref, s32[32]{0:T(128)} %get-tuple-element.60.table_ref, bf16[4,24,32,1024]{3,2,1,0:T(8,128)(2,1)} %bitcast.102, bf16[24,32,768]{2,1,0:T(8,128)(2,1)} %collective-permute-done.2.one, ...), custom_call_target="tpu_custom_call" | custom-call | tf_op jit(solution)/shard_map/finish/pallas_call | solution.py:77
  89.0 5.8 %all-to-all-done.1 = bf16[32,32,256]{2,1,0:T(8,128)(2,1)S(1)} async-done(((bf16[32,32,256]{2,1,0:T(8,128)(2,1)}), bf16[32,32,256]{2,1,0:T(8,128)(2,1)S(1)}, u32[]{:S(2)}, u32[]{:S(2)}) %all-to-all-start.1) | async-done | bytes 524320 | tf_op jit(solution)/shard_map/all_to_all | solution.py:330
  95.6 4.1 %all-to-all-start = ((bf16[32,32,768]{2,1,0:T(8,128)(2,1)}), bf16[32,32,768]{2,1,0:T(8,128)(2,1)S(1)}, u32[]{:S(2)}, u32[]{:S(2)}) async-start(bf16[32,32,768]{2,1,0:T(8,128)(2,1)} %get-tuple-element.32), calls=%async_computation | async-start | bytes 3145728 | tf_op jit(solution)/shard_map/all_to_all | solution.py:330
  109.4 5.0 %early.1 = (f32[1024,512]{1,0:T(8,128)}, f32[1024,512]{1,0:T(8,128)}) custom-call(bf16[1024,1024]{1,0:T(8,128)(2,1)} %bitcast.106, bf16[1024,1024]{1,0:T(8,128)(2,1)} %bitcast.103, bf16[1024,256]{1,0:T(8,128)(2,1)} %bitcast.109), custom_call_target="tpu_custom_call" | custom-call | tf_op jit(solution)/shard_map/early/pallas_call | solution.py:111
  114.4 4.6 %fusion = (f32[24,32,1024]{2,1,0:T(8,128)}, f32[24]{0:T(128)S(1)}) fusion(f32[24,32,1024]{2,1,0:T(8,128)} %param.9, bf16[24,32,256]{2,1,0:T(8,128)(2,1)S(1)} %copy-done.8, bf16[24,32,768]{2,1,0:T(8,128)(2,1)} %get-tuple-element.38), kind=kLoop, calls=%fused_computation.2 | loop fusion | flops 7077864 | bytes 7864416 | tf_op jit(solution)/shard_map/add | solution.py:343
  119.2 3.5 %all-to-all-done = bf16[32,32,768]{2,1,0:T(8,128)(2,1)S(1)} async-done(((bf16[32,32,768]{2,1,0:T(8,128)(2,1)}), bf16[32,32,768]{2,1,0:T(8,128)(2,1)S(1)}, u32[]{:S(2)}, u32[]{:S(2)}) %all-to-all-start) | async-done | bytes 1572896 | tf_op jit(solution)/shard_map/all_to_all | solution.py:330
  123.9 7.2 %first_product.1 = (bf16[1024,768]{1,0:T(8,128)(2,1)}, bf16[1024,512]{1,0:T(8,128)(2,1)}, f32[8,512]{1,0:T(8,128)}) custom-call(bf16[1024,1024]{1,0:T(8,128)(2,1)} %bitcast.107, bf16[1024,1024]{1,0:T(8,128)(2,1)} %bitcast.104, bf16[1024,768]{1,0:T(8,128)(2,1)} %bitcast.108, f32[1024,512]{1,0:T(8,128)} %get-tuple-element.42.before), custom_call_target="tpu_custom_call" | custom-call | tf_op jit(solution)/shard_map/first_product/pallas_call | solution.py:156
  131.1 4.2 %other_products.1 = (bf16[1024,512]{1,0:T(8,128)(2,1)}, f32[8,512]{1,0:T(8,128)}) custom-call(bf16[1024,768]{1,0:T(8,128)(2,1)} %get-tuple-element.49.mid_ref, bf16[1024,1024]{1,0:T(8,128)(2,1)} %bitcast.105, f32[1024,512]{1,0:T(8,128)} %get-tuple-element.50.before), custom_call_target="tpu_custom_call" | custom-call | tf_op jit(solution)/shard_map/other_products/pallas_call | solution.py:195
  138.0 3.9 %all-to-all-start.2 = ((bf16[32,32,512]{2,1,0:T(8,128)(2,1)}), bf16[32,32,512]{2,1,0:T(8,128)(2,1)S(1)}, u32[]{:S(2)}, u32[]{:S(2)}) async-start(bf16[32,32,512]{2,1,0:T(8,128)(2,1)} %bitcast.111), calls=%async_computation.2 | async-start | bytes 2097152 | tf_op jit(solution)/shard_map/all_to_all | solution.py:373
  148.3 3.3 %collective-permute-start.10 = (f32[2,8]{1,0:T(2,128)S(1)}, f32[2,8]{1,0:T(2,128)S(1)}, u32[]{:S(2)}, u32[]{:S(2)}) collective-permute-start(f32[2,8]{1,0:T(2,128)S(1)} %fusion.27), channel_id=1, source_target_pairs={{0,3},{3,0},{1,2},{2,1},{4,7},{7,4},{5,6},{6,5},{8,11},{11,8},{9,1... | collective-permute-start | bytes 200 | tf_op jit(solution)/shard_map/ppermute | solution.py:279
  171.1 6.9 %all-to-all-start.3 = ((bf16[32,32,512]{2,1,0:T(8,128)(2,1)}), bf16[32,32,512]{2,1,0:T(8,128)(2,1)S(1)}, u32[]{:S(2)}, u32[]{:S(2)}) async-start(bf16[32,32,512]{2,1,0:T(8,128)(2,1)} %bitcast.110), calls=%async_computation.3 | async-start | bytes 2097152 | tf_op jit(solution)/shard_map/all_to_all | solution.py:373
  185.0 9.7 %all-to-all-done.3.returned_ref = bf16[32,32,512]{2,1,0:T(8,128)(2,1)S(1)} async-done(((bf16[32,32,512]{2,1,0:T(8,128)(2,1)}), bf16[32,32,512]{2,1,0:T(8,128)(2,1)S(1)}, u32[]{:S(2)}, u32[]{:S(2)}) %all-to-all-start.3) | async-done | bytes 1048608 | tf_op jit(solution)/shard_map/all_to_all | solution.py:373
  214.4 5.2 %collective-permute-done.20 = bf16[12,32,512]{2,1,0:T(8,128)(2,1)S(1)} collective-permute-done((bf16[12,32,512]{2,1,0:T(8,128)(2,1)}, bf16[12,32,512]{2,1,0:T(8,128)(2,1)S(1)}, u32[]{:S(2)}, u32[]{:S(2)}) %collective-permute-start.20) | collective-permute-done | bytes 393248 | tf_op jit(solution)/shard_map/ppermute | solution.py:287
  221.4 6.5 %collective-permute-done.23 = bf16[12,32,512]{2,1,0:T(8,128)(2,1)S(1)} collective-permute-done((bf16[12,32,512]{2,1,0:T(8,128)(2,1)}, bf16[12,32,512]{2,1,0:T(8,128)(2,1)S(1)}, u32[]{:S(2)}, u32[]{:S(2)}) %collective-permute-start.23) | collective-permute-done | bytes 393248 | tf_op jit(solution)/shard_map/ppermute | solution.py:289
  228.9 7.5 %collective-permute-done.24 = bf16[12,32,512]{2,1,0:T(8,128)(2,1)S(1)} collective-permute-done((bf16[12,32,512]{2,1,0:T(8,128)(2,1)}, bf16[12,32,512]{2,1,0:T(8,128)(2,1)S(1)}, u32[]{:S(2)}, u32[]{:S(2)}) %collective-permute-start.24) | collective-permute-done | bytes 393248 | tf_op jit(solution)/shard_map/ppermute | solution.py:289
  240.5 4.3 %collective-permute-done.27 = bf16[12,32,512]{2,1,0:T(8,128)(2,1)S(1)} collective-permute-done((bf16[12,32,512]{2,1,0:T(8,128)(2,1)}, bf16[12,32,512]{2,1,0:T(8,128)(2,1)S(1)}, u32[]{:S(2)}, u32[]{:S(2)}) %collective-permute-start.27) | collective-permute-done | bytes 393248 | tf_op jit(solution)/shard_map/ppermute | solution.py:285
  244.8 3.2 %collective-permute-start.32 = (bf16[12,32,512]{2,1,0:T(8,128)(2,1)S(1)}, bf16[12,32,512]{2,1,0:T(8,128)(2,1)S(1)}, u32[]{:S(2)}, u32[]{:S(2)}) collective-permute-start(bf16[12,32,512]{2,1,0:T(8,128)(2,1)S(1)} %collective-permute-done.28), channel_id=1, source_target_pairs={{0,3},{1,0},{2,1},{3,2},{4,7},{5,4},{6,5},{7,6},{8,11},{9,8},{10,9... | collective-permute-start | bytes 1179656 | tf_op jit(solution)/shard_map/ppermute | solution.py:290
  254.3 3.6 %collective-permute-done.30 = bf16[12,32,512]{2,1,0:T(8,128)(2,1)S(1)} collective-permute-done((bf16[12,32,512]{2,1,0:T(8,128)(2,1)S(1)}, bf16[12,32,512]{2,1,0:T(8,128)(2,1)S(1)}, u32[]{:S(2)}, u32[]{:S(2)}) %collective-permute-start.30) | collective-permute-done | bytes 393248 | tf_op jit(solution)/shard_map/ppermute | solution.py:288
  261.6 4.2 %collective-permute-done.32 = bf16[12,32,512]{2,1,0:T(8,128)(2,1)S(1)} collective-permute-done((bf16[12,32,512]{2,1,0:T(8,128)(2,1)S(1)}, bf16[12,32,512]{2,1,0:T(8,128)(2,1)S(1)}, u32[]{:S(2)}, u32[]{:S(2)}) %collective-permute-start.32) | collective-permute-done | bytes 393248 | tf_op jit(solution)/shard_map/ppermute | solution.py:290
  (143 shorter events, 101.9 us)
Async XLA Ops:
  23.7 60.0 %collective-permute-start.2 = (bf16[24,32,768]{2,1,0:T(8,128)(2,1)}, bf16[24,32,768]{2,1,0:T(8,128)(2,1)}, u32[]{:S(2)}, u32[]{:S(2)}) collective-permute-start(bf16[24,32,768]{2,1,0:T(8,128)(2,1)} %get-tuple-element.30), channel_id=1, source_target_pairs={{0,1},{1,2},{2,3},{3,0},{4,5},{5,6},{6,7},{7,4},{8,9},{9,10},{10,1... | collective-permute-start | bytes 3538952 | tf_op jit(solution)/shard_map/ppermute | solution.py:326
  24.6 59.2 %collective-permute-start.3 = (bf16[24,32,768]{2,1,0:T(8,128)(2,1)}, bf16[24,32,768]{2,1,0:T(8,128)(2,1)}, u32[]{:S(2)}, u32[]{:S(2)}) collective-permute-start(bf16[24,32,768]{2,1,0:T(8,128)(2,1)} %get-tuple-element.31), channel_id=1, source_target_pairs={{0,3},{1,0},{2,1},{3,2},{4,7},{5,4},{6,5},{7,6},{8,11},{9,8},{10,9... | collective-permute-start | bytes 3538952 | tf_op jit(solution)/shard_map/ppermute | solution.py:327
  28.0 28.1 %collective-permute-start.4 = (bf16[12,32,256]{2,1,0:T(8,128)(2,1)S(1)}, bf16[12,32,256]{2,1,0:T(8,128)(2,1)S(1)}, u32[]{:S(2)}, u32[]{:S(2)}) collective-permute-start(bf16[12,32,256]{2,1,0:T(8,128)(2,1)S(1)} %get-tuple-element.63), channel_id=1, source_target_pairs={{0,1},{1,2},{2,3},{3,0},{4,5},{5,6},{6,7},{7,4},{8,9},{9,10},{10,1... | collective-permute-start | bytes 589832 | tf_op jit(solution)/shard_map/ppermute | solution.py:323
  28.1 28.0 %collective-permute-start.5 = (bf16[12,32,256]{2,1,0:T(8,128)(2,1)S(1)}, bf16[12,32,256]{2,1,0:T(8,128)(2,1)S(1)}, u32[]{:S(2)}, u32[]{:S(2)}) collective-permute-start(bf16[12,32,256]{2,1,0:T(8,128)(2,1)S(1)} %get-tuple-element.62), channel_id=1, source_target_pairs={{0,3},{1,0},{2,1},{3,2},{4,7},{5,4},{6,5},{7,6},{8,11},{9,8},{10,9... | collective-permute-start | bytes 589832 | tf_op jit(solution)/shard_map/ppermute | solution.py:324
  74.9 19.9 %all-to-all-start.1 = ((bf16[32,32,256]{2,1,0:T(8,128)(2,1)}), bf16[32,32,256]{2,1,0:T(8,128)(2,1)S(1)}, u32[]{:S(2)}, u32[]{:S(2)}) async-start(bf16[32,32,256]{2,1,0:T(8,128)(2,1)} %get-tuple-element.35), calls=%async_computation.1 | async-start | bytes 1048576 | tf_op jit(solution)/shard_map/all_to_all | solution.py:330
  95.6 27.1 %all-to-all-start = ((bf16[32,32,768]{2,1,0:T(8,128)(2,1)}), bf16[32,32,768]{2,1,0:T(8,128)(2,1)S(1)}, u32[]{:S(2)}, u32[]{:S(2)}) async-start(bf16[32,32,768]{2,1,0:T(8,128)(2,1)} %get-tuple-element.32), calls=%async_computation | async-start | bytes 3145728 | tf_op jit(solution)/shard_map/all_to_all | solution.py:330
  100.7 107.4 %collective-permute-start.17 = (bf16[12,32,512]{2,1,0:T(8,128)(2,1)}, bf16[12,32,512]{2,1,0:T(8,128)(2,1)S(1)}, u32[]{:S(2)}, u32[]{:S(2)}) collective-permute-start(bf16[12,32,512]{2,1,0:T(8,128)(2,1)} %get-tuple-element.68), channel_id=1, source_target_pairs={{0,3},{1,0},{2,1},{3,2},{4,7},{5,4},{6,5},{7,6},{8,11},{9,8},{10,9... | collective-permute-start | bytes 1179656 | tf_op jit(solution)/shard_map/ppermute | solution.py:286
  103.6 108.8 %collective-permute-start.19 = (bf16[12,32,512]{2,1,0:T(8,128)(2,1)}, bf16[12,32,512]{2,1,0:T(8,128)(2,1)}, u32[]{:S(2)}, u32[]{:S(2)}) collective-permute-start(bf16[12,32,512]{2,1,0:T(8,128)(2,1)} %get-tuple-element.68), channel_id=1, source_target_pairs={{0,1},{1,2},{2,3},{3,0},{4,5},{5,6},{6,7},{7,4},{8,9},{9,10},{10,1... | collective-permute-start | bytes 1179656 | tf_op jit(solution)/shard_map/ppermute | solution.py:287
  103.6 99.3 %collective-permute-start.15 = (bf16[12,32,512]{2,1,0:T(8,128)(2,1)}, bf16[12,32,512]{2,1,0:T(8,128)(2,1)}, u32[]{:S(2)}, u32[]{:S(2)}) collective-permute-start(bf16[12,32,512]{2,1,0:T(8,128)(2,1)} %get-tuple-element.69), channel_id=1, source_target_pairs={{0,1},{1,2},{2,3},{3,0},{4,5},{5,6},{6,7},{7,4},{8,9},{9,10},{10,1... | collective-permute-start | bytes 1179656 | tf_op jit(solution)/shard_map/ppermute | solution.py:285
  138.0 32.1 %all-to-all-start.2 = ((bf16[32,32,512]{2,1,0:T(8,128)(2,1)}), bf16[32,32,512]{2,1,0:T(8,128)(2,1)S(1)}, u32[]{:S(2)}, u32[]{:S(2)}) async-start(bf16[32,32,512]{2,1,0:T(8,128)(2,1)} %bitcast.111), calls=%async_computation.2 | async-start | bytes 2097152 | tf_op jit(solution)/shard_map/all_to_all | solution.py:373
  171.1 23.7 %all-to-all-start.3 = ((bf16[32,32,512]{2,1,0:T(8,128)(2,1)}), bf16[32,32,512]{2,1,0:T(8,128)(2,1)S(1)}, u32[]{:S(2)}, u32[]{:S(2)}) async-start(bf16[32,32,512]{2,1,0:T(8,128)(2,1)} %bitcast.110), calls=%async_computation.3 | async-start | bytes 2097152 | tf_op jit(solution)/shard_map/all_to_all | solution.py:373
  181.8 24.3 %collective-permute-start.16 = (bf16[12,32,512]{2,1,0:T(8,128)(2,1)}, bf16[12,32,512]{2,1,0:T(8,128)(2,1)}, u32[]{:S(2)}, u32[]{:S(2)}) collective-permute-start(bf16[12,32,512]{2,1,0:T(8,128)(2,1)} %get-tuple-element.52), channel_id=1, source_target_pairs={{0,1},{1,2},{2,3},{3,0},{4,5},{5,6},{6,7},{7,4},{8,9},{9,10},{10,1... | collective-permute-start | bytes 1179656 | tf_op jit(solution)/shard_map/ppermute | solution.py:285
  183.1 25.3 %collective-permute-start.18 = (bf16[12,32,512]{2,1,0:T(8,128)(2,1)}, bf16[12,32,512]{2,1,0:T(8,128)(2,1)S(1)}, u32[]{:S(2)}, u32[]{:S(2)}) collective-permute-start(bf16[12,32,512]{2,1,0:T(8,128)(2,1)} %get-tuple-element.53), channel_id=1, source_target_pairs={{0,3},{1,0},{2,1},{3,2},{4,7},{5,4},{6,5},{7,6},{8,11},{9,8},{10,9... | collective-permute-start | bytes 1179656 | tf_op jit(solution)/shard_map/ppermute | solution.py:286
  202.9 18.6 %collective-permute-start.21 = (bf16[12,32,512]{2,1,0:T(8,128)(2,1)}, bf16[12,32,512]{2,1,0:T(8,128)(2,1)S(1)}, u32[]{:S(2)}, u32[]{:S(2)}) collective-permute-start(bf16[12,32,512]{2,1,0:T(8,128)(2,1)} %get-tuple-element.69), channel_id=1, source_target_pairs={{0,3},{1,0},{2,1},{3,2},{4,7},{5,4},{6,5},{7,6},{8,11},{9,8},{10,9... | collective-permute-start | bytes 1179656 | tf_op jit(solution)/shard_map/ppermute | solution.py:288
  208.2 19.8 %collective-permute-start.23 = (bf16[12,32,512]{2,1,0:T(8,128)(2,1)}, bf16[12,32,512]{2,1,0:T(8,128)(2,1)S(1)}, u32[]{:S(2)}, u32[]{:S(2)}) collective-permute-start(bf16[12,32,512]{2,1,0:T(8,128)(2,1)} %collective-permute-done.15), channel_id=1, source_target_pairs={{0,1},{1,2},{2,3},{3,0},{4,5},{5,6},{6,7},{7,4},{8,9},{9,10},{10,1... | collective-permute-start | bytes 1179656 | tf_op jit(solution)/shard_map/ppermute | solution.py:289
  208.4 19.5 %collective-permute-start.22 = (bf16[12,32,512]{2,1,0:T(8,128)(2,1)}, bf16[12,32,512]{2,1,0:T(8,128)(2,1)S(1)}, u32[]{:S(2)}, u32[]{:S(2)}) collective-permute-start(bf16[12,32,512]{2,1,0:T(8,128)(2,1)} %get-tuple-element.52), channel_id=1, source_target_pairs={{0,3},{1,0},{2,1},{3,2},{4,7},{5,4},{6,5},{7,6},{8,11},{9,8},{10,9... | collective-permute-start | bytes 1179656 | tf_op jit(solution)/shard_map/ppermute | solution.py:288
  212.4 24.9 %collective-permute-start.25 = (bf16[12,32,512]{2,1,0:T(8,128)(2,1)S(1)}, bf16[12,32,512]{2,1,0:T(8,128)(2,1)S(1)}, u32[]{:S(2)}, u32[]{:S(2)}) collective-permute-start(bf16[12,32,512]{2,1,0:T(8,128)(2,1)S(1)} %collective-permute-done.17), channel_id=1, source_target_pairs={{0,3},{1,0},{2,1},{3,2},{4,7},{5,4},{6,5},{7,6},{8,11},{9,8},{10,9... | collective-permute-start | bytes 1179656 | tf_op jit(solution)/shard_map/ppermute | solution.py:290
  219.5 16.9 %collective-permute-start.24 = (bf16[12,32,512]{2,1,0:T(8,128)(2,1)}, bf16[12,32,512]{2,1,0:T(8,128)(2,1)S(1)}, u32[]{:S(2)}, u32[]{:S(2)}) collective-permute-start(bf16[12,32,512]{2,1,0:T(8,128)(2,1)} %collective-permute-done.16), channel_id=1, source_target_pairs={{0,1},{1,2},{2,3},{3,0},{4,5},{5,6},{6,7},{7,4},{8,9},{9,10},{10,1... | collective-permute-start | bytes 1179656 | tf_op jit(solution)/shard_map/ppermute | solution.py:289
  221.4 23.3 %collective-permute-start.27 = (bf16[12,32,512]{2,1,0:T(8,128)(2,1)}, bf16[12,32,512]{2,1,0:T(8,128)(2,1)S(1)}, u32[]{:S(2)}, u32[]{:S(2)}) collective-permute-start(bf16[12,32,512]{2,1,0:T(8,128)(2,1)} %get-tuple-element.55), channel_id=1, source_target_pairs={{0,1},{1,2},{2,3},{3,0},{4,5},{5,6},{6,7},{7,4},{8,9},{9,10},{10,1... | collective-permute-start | bytes 1179656 | tf_op jit(solution)/shard_map/ppermute | solution.py:285
  227.9 16.9 %collective-permute-start.28 = (bf16[12,32,512]{2,1,0:T(8,128)(2,1)}, bf16[12,32,512]{2,1,0:T(8,128)(2,1)S(1)}, u32[]{:S(2)}, u32[]{:S(2)}) collective-permute-start(bf16[12,32,512]{2,1,0:T(8,128)(2,1)} %get-tuple-element.56), channel_id=1, source_target_pairs={{0,3},{1,0},{2,1},{3,2},{4,7},{5,4},{6,5},{7,6},{8,11},{9,8},{10,9... | collective-permute-start | bytes 1179656 | tf_op jit(solution)/shard_map/ppermute | solution.py:286
  227.9 21.6 %collective-permute-start.26 = (bf16[12,32,512]{2,1,0:T(8,128)(2,1)S(1)}, bf16[12,32,512]{2,1,0:T(8,128)(2,1)S(1)}, u32[]{:S(2)}, u32[]{:S(2)}) collective-permute-start(bf16[12,32,512]{2,1,0:T(8,128)(2,1)S(1)} %collective-permute-done.18), channel_id=1, source_target_pairs={{0,3},{1,0},{2,1},{3,2},{4,7},{5,4},{6,5},{7,6},{8,11},{9,8},{10,9... | collective-permute-start | bytes 1179656 | tf_op jit(solution)/shard_map/ppermute | solution.py:290
  236.4 17.2 %collective-permute-start.29 = (bf16[12,32,512]{2,1,0:T(8,128)(2,1)S(1)}, bf16[12,32,512]{2,1,0:T(8,128)(2,1)S(1)}, u32[]{:S(2)}, u32[]{:S(2)}) collective-permute-start(bf16[12,32,512]{2,1,0:T(8,128)(2,1)S(1)} %copy-done.10), channel_id=1, source_target_pairs={{0,1},{1,2},{2,3},{3,0},{4,5},{5,6},{6,7},{7,4},{8,9},{9,10},{10,1... | collective-permute-start | bytes 1179656 | tf_op jit(solution)/shard_map/ppermute | solution.py:287
  237.3 20.6 %collective-permute-start.30 = (bf16[12,32,512]{2,1,0:T(8,128)(2,1)S(1)}, bf16[12,32,512]{2,1,0:T(8,128)(2,1)S(1)}, u32[]{:S(2)}, u32[]{:S(2)}) collective-permute-start(bf16[12,32,512]{2,1,0:T(8,128)(2,1)S(1)} %copy-done.9), channel_id=1, source_target_pairs={{0,3},{1,0},{2,1},{3,2},{4,7},{5,4},{6,5},{7,6},{8,11},{9,8},{10,9... | collective-permute-start | bytes 1179656 | tf_op jit(solution)/shard_map/ppermute | solution.py:288
  244.8 21.0 %collective-permute-start.32 = (bf16[12,32,512]{2,1,0:T(8,128)(2,1)S(1)}, bf16[12,32,512]{2,1,0:T(8,128)(2,1)S(1)}, u32[]{:S(2)}, u32[]{:S(2)}) collective-permute-start(bf16[12,32,512]{2,1,0:T(8,128)(2,1)S(1)} %collective-permute-done.28), channel_id=1, source_target_pairs={{0,3},{1,0},{2,1},{3,2},{4,7},{5,4},{6,5},{7,6},{8,11},{9,8},{10,9... | collective-permute-start | bytes 1179656 | tf_op jit(solution)/shard_map/ppermute | solution.py:290
  (31 other events, 391.7 us)

commit v3 on v0

v3 whole, which is shorter than its diff:
```python
import jax
import jax.numpy as jnp
from jax import lax
from jax.experimental import pallas as pl
from jax.experimental.pallas import tpu as pltpu
from jax.sharding import Mesh
from jax.sharding import PartitionSpec as P


LAYERS = 8
LANES = 128
GROUP = ("group_0", "group_1", "group_2")
EVERY = ("group_0", "group_1", "group_2", "rep")
SENT = ((768, 256), (0, 768))


step_rate = 0.5
f32 = jnp.float32
bf16 = jnp.bfloat16


def ring(count, step):
    return [(i, (i + step) % count) for i in range(count)]


def merge(who, parts, far_up, far_down, start, cols):
    _, blocks, rows, _ = parts.shape
    half = blocks // 2
    at = start // cols

    def body(who_ref, above, below, from_down, from_up, out_up, out_down):
        first = pl.program_id(0) == 0

        @pl.when(first)
        def _():
            out_up[...] = (above[0].astype(f32) + from_down[...].astype(f32)).astype(bf16)
            out_down[...] = below[0]

        @pl.when(jnp.logical_not(first))
        def _():
            out_up[...] = above[0]
            out_down[...] = (below[0].astype(f32) + from_up[...].astype(f32)).astype(bf16)

    piece = pl.BlockSpec((half, rows, cols), lambda i, w: (0, 0, 0))
    out = pl.BlockSpec((half, rows, cols), lambda i, w: (i, 0, 0))
    shape = jax.ShapeDtypeStruct((blocks, rows, cols), bf16)
    return pl.pallas_call(
        body,
        grid_spec=pltpu.PrefetchScalarGridSpec(
            num_scalar_prefetch=1,
            grid=(2,),
            in_specs=[
                pl.BlockSpec((1, half, rows, cols), lambda i, w: (w[1], i, 0, at)),
                pl.BlockSpec((1, half, rows, cols), lambda i, w: (w[3], i, 0, at)),
                piece,
                piece,
            ],
            out_specs=[out, out],
        ),
        out_shape=[shape, shape],
        name="merge",
    )(who, parts, parts, far_up, far_down)


def finish(who, table, parts, up, down, start, cols):
    _, blocks, rows, _ = parts.shape
    slots = table.shape[0]
    at = start // cols

    def body(who_ref, table_ref, own, one, two, gradient, slotted):
        total = own[0].astype(f32) + one[...].astype(f32) + two[...].astype(f32)
        gradient[...] = total.astype(bf16)
        for slot in range(slots):
            slotted[slot] = gradient[table_ref[slot]]

    block = pl.BlockSpec((blocks, rows, cols), lambda i, w, t: (0, 0, 0))
    return pl.pallas_call(
        body,
        grid_spec=pltpu.PrefetchScalarGridSpec(
            num_scalar_prefetch=2,
            grid=(1,),
            in_specs=[
                pl.BlockSpec((1, blocks, rows, cols), lambda i, w, t: (w[0], 0, 0, at)),
                block,
                block,
            ],
            out_specs=[block, pl.BlockSpec((slots, rows, cols), lambda i, w, t: (0, 0, 0))],
        ),
        out_shape=[
            jax.ShapeDtypeStruct((blocks, rows, cols), bf16),
            jax.ShapeDtypeStruct((slots, rows, cols), bf16),
        ],
        name="finish",
    )(who, table, parts, up, down)


def left_times(left, owned):
    order, cols = owned.shape
    tile = order // 2

    def body(left_ref, owned_ref, out):
        out[...] = jnp.dot(left_ref[...], owned_ref[...], preferred_element_type=f32).astype(bf16)

    return pl.pallas_call(
        body,
        grid=(2,),
        in_specs=[
            pl.BlockSpec((tile, order), lambda i: (i, 0)),
            pl.BlockSpec((order, cols), lambda i: (0, 0)),
        ],
        out_specs=pl.BlockSpec((tile, cols), lambda i: (i, 0)),
        out_shape=jax.ShapeDtypeStruct((order, cols), bf16),
        name="left_times",
    )(left, owned)


def products(left, right, owned, earlier, graft_row, layer_row):
    order, cols = owned.shape
    steps = 2
    tile = order // steps
    last = SENT[-1][0]

    def body(left_ref, right_ref, owned_ref, graft_ref, layer_ref, *rest):
        before, (out, sums, mid) = rest[: len(earlier)], rest[len(earlier) :]
        mid[:, last : last + cols] = jnp.dot(
            left_ref[...], owned_ref[...], preferred_element_type=f32
        ).astype(bf16)
        for ref, (start, size) in zip(before, SENT):
            mid[:, start : start + size] = ref[...]
        out[...] = jnp.dot(mid[...], right_ref[...], preferred_element_type=f32).astype(bf16)
        wide = out[...].astype(f32)
        squares = jnp.sum(jnp.sum(wide * wide, axis=0, keepdims=True), axis=1, keepdims=True)

        @pl.when(pl.program_id(0) == 0)
        def _():
            sums[0:1] = graft_ref[...]
            sums[1:2] = layer_ref[...] * squares

        @pl.when(pl.program_id(0) > 0)
        def _():
            sums[1:2] += layer_ref[...] * squares

    row = pl.BlockSpec((1, LANES), lambda i: (0, 0))
    return pl.pallas_call(
        body,
        grid=(steps,),
        in_specs=[
            pl.BlockSpec((tile, order), lambda i: (i, 0)),
            pl.BlockSpec((order, order), lambda i: (0, 0)),
            pl.BlockSpec((order, cols), lambda i: (0, 0)),
            row,
            row,
            *[pl.BlockSpec((tile, e.shape[1]), lambda i: (i, 0)) for e in earlier],
        ],
        out_specs=[pl.BlockSpec((tile, order), lambda i: (i, 0)), pl.BlockSpec((2, LANES), lambda i: (0, 0))],
        out_shape=[jax.ShapeDtypeStruct((order, order), bf16), jax.ShapeDtypeStruct((2, LANES), f32)],
        scratch_shapes=[pltpu.VMEM((tile, order), bf16)],
        name="products",
    )(left, right, owned, graft_row, layer_row, *earlier)


def update(who, position, scale, returned, params, reps):
    blocks, rows, cols = params.shape
    half = blocks // 2
    slots = returned.shape[0]

    def body(who_ref, position_ref, scale_ref, returned_ref, params_ref, low, high, whole):
        for block in range(blocks):
            change = scale_ref[block] * returned_ref[position_ref[block]].astype(f32)
            new = (params_ref[block].astype(f32) - change).astype(bf16)
            whole[0, block] = new
            if block < half:
                low[block] = new
            else:
                high[block - half] = new

    out = pl.BlockSpec((half, rows, cols), lambda i, w, p, s: (0, 0, 0))
    shape = jax.ShapeDtypeStruct((half, rows, cols), bf16)
    return pl.pallas_call(
        body,
        grid_spec=pltpu.PrefetchScalarGridSpec(
            num_scalar_prefetch=3,
            grid=(1,),
            in_specs=[
                pl.BlockSpec((slots, rows, cols), lambda i, w, p, s: (0, 0, 0)),
                pl.BlockSpec((blocks, rows, cols), lambda i, w, p, s: (0, 0, 0)),
            ],
            out_specs=[out, out, pl.BlockSpec((1, blocks, rows, cols), lambda i, w, p, s: (w[0], 0, 0, 0))],
        ),
        out_shape=[shape, shape, jax.ShapeDtypeStruct((reps, blocks, rows, cols), bf16)],
        name="update",
    )(who, position, scale, returned, params)


def everywhere(value):
    swap, near, wrap = [(0, 1), (1, 0)], [(0, 1), (1, 0), (2, 3), (3, 2)], [(0, 3), (3, 0), (1, 2), (2, 1)]
    steps = [("group_2", swap)]
    for axis in ("rep", "group_0", "group_1"):
        steps += [(axis, near), (axis, wrap)]
    for axis, pairs in steps:
        value = value + lax.ppermute(value, axis, pairs)
    return value


def spread(low, high, reps):
    up, down = ring(reps, 1), ring(reps, -1)
    low_up = lax.ppermute(low, "rep", up)
    high_down = lax.ppermute(high, "rep", down)
    high_up = lax.ppermute(high, "rep", up)
    low_down = lax.ppermute(low, "rep", down)
    far_low = lax.ppermute(low_up, "rep", up)
    far_high = lax.ppermute(high_down, "rep", down)
    return (
        (3, 0, low_up),
        (1, 1, high_down),
        (3, 1, high_up),
        (1, 0, low_down),
        (2, 0, far_low),
        (2, 1, far_high),
    )


def local(grad_parts, params, accum, left_pre, right_pre, slot_block, layer_of):
    group_size = lax.axis_size(GROUP)
    reps = lax.axis_size("rep")
    me = lax.axis_index("rep")
    group_index = lax.axis_index(GROUP)
    blocks, rows, width = params.shape
    half = blocks // 2
    up, down = ring(reps, 1), ring(reps, -1)
    parts = grad_parts[0].reshape(reps, blocks, rows, width)
    who = lax.rem(me + jnp.arange(reps, dtype=jnp.int32), reps)
    table = lax.dynamic_index_in_dim(slot_block, me, 0, keepdims=False).reshape(-1)
    wanted = jnp.maximum(table, 0)
    left, right = left_pre[0, 0, 0], right_pre[0, 0, 0]

    far = lax.rem(me + 2, reps)
    gradients, earlier, owned = [None] * len(SENT), [], None
    for chunk, (start, cols) in enumerate(SENT):
        low = lax.dynamic_slice(parts, (far, 0, 0, start), (1, half, rows, cols))[0]
        high = lax.dynamic_slice(parts, (far, half, 0, start), (1, half, rows, cols))[0]
        far_up = lax.ppermute(low, "rep", up)
        far_down = lax.ppermute(high, "rep", down)
        to_up, to_down = merge(who, parts, far_up, far_down, start, cols)
        near_up = lax.ppermute(to_up, "rep", up)
        near_down = lax.ppermute(to_down, "rep", down)
        gradient, outgoing = finish(who, wanted, parts, near_up, near_down, start, cols)
        gradients[chunk] = gradient
        arrived = lax.all_to_all(outgoing, GROUP, split_axis=0, concat_axis=0, tiled=True)
        if chunk > 0:
            earlier.append(left_times(left, owned))
        owned = arrived.reshape(group_size * rows, cols)

    my_layers = lax.dynamic_slice_in_dim(layer_of, me * blocks, blocks)
    onehot = (my_layers[:, None] == jnp.arange(LAYERS, dtype=jnp.int32)[None, :]).astype(f32)
    in_order = sorted(range(len(SENT)), key=lambda c: SENT[c][0])
    wide = jnp.concatenate([gradients[c] for c in in_order], axis=2).astype(f32)
    new_accum = accum + wide * wide
    graft = wide * lax.rsqrt(new_accum)
    graft_blocks = jnp.sum(graft * graft, axis=(1, 2))
    graft_layer = jnp.sum(onehot * graft_blocks[:, None], axis=0)
    mine = lax.dynamic_index_in_dim(table, group_index, 0, keepdims=False)
    chosen = (jnp.arange(blocks, dtype=jnp.int32) == mine).astype(f32)
    my_layer = jnp.sum(chosen[:, None] * onehot, axis=0)
    position = jnp.sum(
        jnp.where(
            table[None, :] == jnp.arange(blocks, dtype=jnp.int32)[:, None],
            jnp.arange(group_size, dtype=jnp.int32)[None, :],
            0,
        ),
        axis=1,
    )
    to_lanes = ((0, 0), (0, LANES - LAYERS))
    graft_row = jnp.pad(graft_layer[None, :], to_lanes)
    layer_row = jnp.pad(my_layer[None, :], to_lanes)
    owned, earlier, graft_row, layer_row, position, onehot, new_accum = lax.optimization_barrier(
        (owned, earlier, graft_row, layer_row, position, onehot, new_accum)
    )

    precond, sums = products(left, right, owned, earlier, graft_row, layer_row)
    outgoing = precond.reshape(group_size, rows, width)
    returned = lax.all_to_all(outgoing, GROUP, split_axis=0, concat_axis=0, tiled=True)
    sums = everywhere(sums)
    layer_scale = jnp.sqrt(sums[0, :LAYERS]) * lax.rsqrt(sums[1, :LAYERS] + 1e-06)
    scale = step_rate * jnp.sum(onehot * layer_scale[None, :], axis=1)

    low, high, new_params = update(who, position, scale, returned, params, reps)
    for offset, part, piece in spread(low, high, reps):
        new_params = lax.dynamic_update_slice(new_params, piece[None], (who[offset], part * half, 0, 0))
    return (new_params.reshape(reps * blocks, rows, width), new_accum)


def solution(mesh):
    split = Mesh(mesh.devices.reshape(4, 4, 2, mesh.shape["rep"]), EVERY)
    placed = (
        P("rep", None, GROUP, None),
        P("rep", GROUP, None),
        P("rep", GROUP, None),
        P("rep", GROUP, None, None, None),
        P("rep", GROUP, None, None, None),
        P(),
        P(),
    )
    return jax.shard_map(
        local,
        mesh=split,
        in_specs=placed,
        out_specs=(P(None, GROUP, None), P("rep", GROUP, None)),
        check_vma=False,
    )
```

time: 235 us -> 235 us (level)
  waiting for transfers between devices: 99.3 us -> 122 us
  starting transfers between devices: 61.4 us -> 49.8 us
  Pallas kernels: 39.2 us -> 30.4 us
    ppermute x2, waiting for transfers between devices: 0.19 us -> 37.1 us  [local(): far_down = lax.ppermute(high, 'rep', down)]
    ppermute x2, waiting for transfers between devices: 32.8 us -> 6.44 us  [local(): near_up = lax.ppermute(to_up, 'rep', up)]
    ppermute x6 -> x7, waiting for transfers between devices: 15.2 us -> 27.5 us  [everywhere(): value = value + lax.ppermute(value, axis, pairs)]
    ppermute x9 -> x6, waiting for transfers between devices: 21.5 us -> 30.9 us  [the longest x1 11.7 us: spread(): high_up = lax.ppermute(high, 'rep', up)]
    all_to_all x4 -> x3, starting transfers between devices: 24 us -> 16.6 us  [local(): lax.all_to_all(outgoing, GROUP, split_axis=0, concat_axis=0, tiled=True)]
    all_to_all x4 -> x3, waiting for transfers between devices: 21.5 us -> 16.3 us  [local(): lax.all_to_all(outgoing, GROUP, split_axis=0, concat_axis=0, tiled=True)]
    ppermute x2, waiting for transfers between devices: 8.2 us -> 4.14 us  [local(): far_up = lax.ppermute(low, 'rep', up)]
    pallas_call x2 -> x1, Pallas kernels: 8.57 us -> 4.66 us  [update(): pl.pallas_call(body, grid_spec=pltpu.PrefetchScalarGridSpec(num_scalar_pr...]
  transfers between devices with their start and end apart: 27 -> 24, of which waited for: 17 -> 17; matrix products, arithmetic and copies ran while one was open for 6% -> 7% of each run, Pallas kernels for 12% -> 6%
where the time goes in v3:
time: 235 us; the launch traced here: 234 us
  waiting for transfers between devices  122 us (52%)
  starting transfers between devices  49.8 us (21%)
  Pallas kernels  30.4 us (13%)
  local copies, waits for them, and re-layouts  17.5 us (7%)
  other arithmetic  7.48 us (3%)
  between operations  6.3 us (3%)
    ppermute x2, waiting for transfers between devices, local(): far_down = lax.ppermute(high, 'rep', down)  37.1 us
    ppermute x7, waiting for transfers between devices, everywhere(): value = value + lax.ppermute(value, axis, pairs)  27.5 us
    all_to_all x3, starting transfers between devices, local(): lax.all_to_all(outgoing, GROUP, split_axis=0, concat_axis=0, tiled=True)  16.6 us
    all_to_all x3, waiting for transfers between devices, local(): lax.all_to_all(outgoing, GROUP, split_axis=0, concat_axis=0, tiled=True)  16.3 us
    ppermute x1, waiting for transfers between devices, spread(): high_up = lax.ppermute(high, 'rep', up)  11.7 us
    ppermute x7, starting transfers between devices, everywhere(): value = value + lax.ppermute(value, axis, pairs)  11.4 us
    ppermute x1, waiting for transfers between devices, spread(): far_low = lax.ppermute(low_up, 'rep', up)  10.1 us
    ppermute x1, waiting for transfers between devices, spread(): low_up = lax.ppermute(low, 'rep', up)  9.15 us
  transfers between devices with their start and end apart: 24, of which 17 were waited for; matrix products, arithmetic and copies ran while one was open for 7% of the time, Pallas kernels for 6%

profile of v3, /device:TPU:0, one launch (start us, length us, event | category | flops | bytes accessed | tf_op | source)
XLA Modules:
  0.0 233.9 jit_solution(17476536619545427732)
XLA Ops:
  5.4 12.1 %collective-permute-done.1.from_up = bf16[12,32,768]{2,1,0:T(8,128)(2,1)S(1)} collective-permute-done((bf16[12,32,768]{2,1,0:T(8,128)(2,1)S(1)}, bf16[12,32,768]{2,1,0:T(8,128)(2,1)S(1)}, u32[]{:S(2)}, u32[]{:S(2)}) %collective-permute-start.1) | collective-permute-done | bytes 589856 | tf_op jit(solution)/shard_map/ppermute | solution.py:243
  17.5 3.4 %collective-permute-done.from_down = bf16[12,32,768]{2,1,0:T(8,128)(2,1)S(1)} collective-permute-done((bf16[12,32,768]{2,1,0:T(8,128)(2,1)S(1)}, bf16[12,32,768]{2,1,0:T(8,128)(2,1)S(1)}, u32[]{:S(2)}, u32[]{:S(2)}) %collective-permute-start) | collective-permute-done | bytes 589856 | tf_op jit(solution)/shard_map/ppermute | solution.py:242
  21.7 3.8 %merge.2 = (bf16[24,32,768]{2,1,0:T(8,128)(2,1)}, bf16[24,32,768]{2,1,0:T(8,128)(2,1)}) custom-call(s32[4]{0:T(128)} %compare_select_fusion.who_ref, bf16[4,24,32,1024]{3,2,1,0:T(8,128)(2,1)} %bitcast.39, bf16[4,24,32,1024]{3,2,1,0:T(8,128)(2,1)} %bitcast.40, bf16[12,32,768]{2,1,0:T(8,128)(2,1)} %copy-done.7, bf16[12,32,768]{2,1,0:T(8,128)(2,1)} %copy-done.6), custom_call_target="tpu_custom_call" | custom-call | tf_op jit(solution)/shard_map/merge/pallas_call | solution.py:47
  25.6 3.2 %collective-permute-start.3 = (bf16[24,32,768]{2,1,0:T(8,128)(2,1)}, bf16[24,32,768]{2,1,0:T(8,128)(2,1)S(1)}, u32[]{:S(2)}, u32[]{:S(2)}) collective-permute-start(bf16[24,32,768]{2,1,0:T(8,128)(2,1)} %get-tuple-element.23), channel_id=1, source_target_pairs={{0,3},{1,0},{2,1},{3,2},{4,7},{5,4},{6,5},{7,6},{8,11},{9,8},{10,9... | collective-permute-start | bytes 3538952 | tf_op jit(solution)/shard_map/ppermute | solution.py:246
  32.0 25.1 %collective-permute-done.5.from_up = bf16[12,32,256]{2,1,0:T(8,128)(2,1)S(1)} collective-permute-done((bf16[12,32,256]{2,1,0:T(8,128)(2,1)S(1)}, bf16[12,32,256]{2,1,0:T(8,128)(2,1)S(1)}, u32[]{:S(2)}, u32[]{:S(2)}) %collective-permute-start.5) | collective-permute-done | bytes 196640 | tf_op jit(solution)/shard_map/ppermute | solution.py:243
  61.6 3.4 %collective-permute-start.7 = (bf16[24,32,256]{2,1,0:T(8,128)(2,1)}, bf16[24,32,256]{2,1,0:T(8,128)(2,1)S(1)}, u32[]{:S(2)}, u32[]{:S(2)}) collective-permute-start(bf16[24,32,256]{2,1,0:T(8,128)(2,1)} %get-tuple-element.26), channel_id=1, source_target_pairs={{0,3},{1,0},{2,1},{3,2},{4,7},{5,4},{6,5},{7,6},{8,11},{9,8},{10,9... | collective-permute-start | bytes 1179656 | tf_op jit(solution)/shard_map/ppermute | solution.py:246
  65.6 6.4 %collective-permute-done.6.one = bf16[24,32,256]{2,1,0:T(8,128)(2,1)S(1)} collective-permute-done((bf16[24,32,256]{2,1,0:T(8,128)(2,1)}, bf16[24,32,256]{2,1,0:T(8,128)(2,1)S(1)}, u32[]{:S(2)}, u32[]{:S(2)}) %collective-permute-start.6) | collective-permute-done | bytes 393248 | tf_op jit(solution)/shard_map/ppermute | solution.py:245
  73.0 3.1 %finish.3 = (bf16[24,32,256]{2,1,0:T(8,128)(2,1)}, bf16[32,32,256]{2,1,0:T(8,128)(2,1)}) custom-call(s32[4]{0:T(128)} %compare_select_fusion.who_ref, s32[32]{0:T(128)} %get-tuple-element.44.table_ref, bf16[4,24,32,1024]{3,2,1,0:T(8,128)(2,1)} %bitcast.44, bf16[24,32,256]{2,1,0:T(8,128)(2,1)} %copy-done.8, bf16[24,32,256]{2,1,0:T(8,128)(2,1)} %copy-done.9), custom_call_target="tpu_custom_call" | custom-call | tf_op jit(solution)/shard_map/finish/pallas_call | solution.py:77
  76.1 8.3 %all-to-all-start.1 = ((bf16[32,32,256]{2,1,0:T(8,128)(2,1)}), bf16[32,32,256]{2,1,0:T(8,128)(2,1)S(1)}, u32[]{:S(2)}, u32[]{:S(2)}) async-start(bf16[32,32,256]{2,1,0:T(8,128)(2,1)} %get-tuple-element.27), calls=%async_computation.1 | async-start | bytes 1048576 | tf_op jit(solution)/shard_map/all_to_all | solution.py:249
  86.5 5.2 %finish.2 = (bf16[24,32,768]{2,1,0:T(8,128)(2,1)}, bf16[32,32,768]{2,1,0:T(8,128)(2,1)}) custom-call(s32[4]{0:T(128)} %compare_select_fusion.who_ref, s32[32]{0:T(128)} %get-tuple-element.44.table_ref, bf16[4,24,32,1024]{3,2,1,0:T(8,128)(2,1)} %bitcast.45, bf16[24,32,768]{2,1,0:T(8,128)(2,1)} %copy-done.3, bf16[24,32,768]{2,1,0:T(8,128)(2,1)} %copy-done.4), custom_call_target="tpu_custom_call" | custom-call | tf_op jit(solution)/shard_map/finish/pallas_call | solution.py:77
  91.6 3.9 %all-to-all-done.1 = bf16[32,32,256]{2,1,0:T(8,128)(2,1)S(1)} async-done(((bf16[32,32,256]{2,1,0:T(8,128)(2,1)}), bf16[32,32,256]{2,1,0:T(8,128)(2,1)S(1)}, u32[]{:S(2)}, u32[]{:S(2)}) %all-to-all-start.1) | async-done | bytes 524320 | tf_op jit(solution)/shard_map/all_to_all | solution.py:249
  95.5 4.3 %all-to-all-start = ((bf16[32,32,768]{2,1,0:T(8,128)(2,1)}), bf16[32,32,768]{2,1,0:T(8,128)(2,1)S(1)}, u32[]{:S(2)}, u32[]{:S(2)}) async-start(bf16[32,32,768]{2,1,0:T(8,128)(2,1)} %get-tuple-element.24), calls=%async_computation | async-start | bytes 3145728 | tf_op jit(solution)/shard_map/all_to_all | solution.py:249
  101.7 3.0 %left_times.1.rest_0_ = bf16[1024,256]{1,0:T(8,128)(2,1)} custom-call(bf16[1024,1024]{1,0:T(8,128)(2,1)} %bitcast.46, bf16[1024,256]{1,0:T(8,128)(2,1)} %bitcast.51), custom_call_target="tpu_custom_call" | custom-call | tf_op jit(solution)/shard_map/left_times/pallas_call | solution.py:104
  104.7 4.3 %fusion = (f32[24,32,1024]{2,1,0:T(8,128)}, f32[24]{0:T(128)S(1)}) fusion(f32[24,32,1024]{2,1,0:T(8,128)} %param.9, bf16[24,32,256]{2,1,0:T(8,128)(2,1)} %get-tuple-element.29, bf16[24,32,768]{2,1,0:T(8,128)(2,1)S(1)} %copy-done.5), kind=kLoop, calls=%fused_computation.2 | loop fusion | flops 7077864 | bytes 7864416 | tf_op jit(solution)/shard_map/add | solution.py:258
  110.3 12.4 %all-to-all-done = bf16[32,32,768]{2,1,0:T(8,128)(2,1)S(1)} async-done(((bf16[32,32,768]{2,1,0:T(8,128)(2,1)}), bf16[32,32,768]{2,1,0:T(8,128)(2,1)S(1)}, u32[]{:S(2)}, u32[]{:S(2)}) %all-to-all-start) | async-done | bytes 1572896 | tf_op jit(solution)/shard_map/all_to_all | solution.py:249
  123.9 7.8 %products.1 = (bf16[1024,1024]{1,0:T(8,128)(2,1)}, f32[2,128]{1,0:T(2,128)}) custom-call(bf16[1024,1024]{1,0:T(8,128)(2,1)} %bitcast.47, bf16[1024,1024]{1,0:T(8,128)(2,1)} %bitcast.49, bf16[1024,768]{1,0:T(8,128)(2,1)} %bitcast.48, f32[1,128]{1,0:T(1,128)} %pad.7.graft_ref, f32[1,128]{1,0:T(1,128)} %pad.8.layer_ref, bf16[1024,256]{1,0:T(8,128)(2,1)} %left_times.1.rest_0_), custom_call_target="tpu_custom_call" | custom-call | tf_op jit(solution)/shard_map/products/pallas_call | solution.py:144
  131.7 4.0 %all-to-all-start.2 = ((bf16[32,32,1024]{2,1,0:T(8,128)(2,1)}), bf16[32,32,1024]{2,1,0:T(8,128)(2,1)S(1)}, u32[]{:S(2)}, u32[]{:S(2)}) async-start(bf16[32,32,1024]{2,1,0:T(8,128)(2,1)} %bitcast.50), calls=%async_computation.2 | async-start | bytes 4194304 | tf_op jit(solution)/shard_map/all_to_all | solution.py:282
  147.1 14.4 %collective-permute-done.11 = f32[2,128]{1,0:T(2,128)S(1)} collective-permute-done((f32[2,128]{1,0:T(2,128)S(1)}, f32[2,128]{1,0:T(2,128)S(1)}, u32[]{:S(2)}, u32[]{:S(2)}) %collective-permute-start.11) | collective-permute-done | bytes 1056 | tf_op jit(solution)/shard_map/ppermute | solution.py:201
  176.7 4.7 %update.1 = (bf16[12,32,1024]{2,1,0:T(8,128)(2,1)}, bf16[12,32,1024]{2,1,0:T(8,128)(2,1)}, bf16[4,24,32,1024]{3,2,1,0:T(8,128)(2,1)}) custom-call(s32[4]{0:T(128)} %compare_select_fusion.who_ref, s32[24]{0:T(128)} %select_reduce_fusion.position_ref, f32[24]{0:T(128)} %broadcast_multiply_fusion.scale_ref, bf16[32,32,1024]{2,1,0:T(8,128)(2,1)} %copy-done, ...), custom_call_target="tpu_custom_call" | custom-call | tf_op jit(solution)/shard_map/update/pallas_call | solution.py:179
  190.7 3.3 %collective-permute-start.18 = (bf16[12,32,1024]{2,1,0:T(8,128)(2,1)}, bf16[12,32,1024]{2,1,0:T(8,128)(2,1)S(1)}, u32[]{:S(2)}, u32[]{:S(2)}) collective-permute-start(bf16[12,32,1024]{2,1,0:T(8,128)(2,1)} %get-tuple-element.39), channel_id=1, source_target_pairs={{0,3},{1,0},{2,1},{3,2},{4,7},{5,4},{6,5},{7,6},{8,11},{9,8},{10,9... | collective-permute-start | bytes 2359304 | tf_op jit(solution)/shard_map/ppermute | solution.py:210
  194.0 9.1 %collective-permute-done.15 = bf16[12,32,1024]{2,1,0:T(8,128)(2,1)S(1)} collective-permute-done((bf16[12,32,1024]{2,1,0:T(8,128)(2,1)}, bf16[12,32,1024]{2,1,0:T(8,128)(2,1)S(1)}, u32[]{:S(2)}, u32[]{:S(2)}) %collective-permute-start.15) | collective-permute-done | bytes 786464 | tf_op jit(solution)/shard_map/ppermute | solution.py:207
  203.2 3.2 %collective-permute-start.20 = (bf16[12,32,1024]{2,1,0:T(8,128)(2,1)S(1)}, bf16[12,32,1024]{2,1,0:T(8,128)(2,1)S(1)}, u32[]{:S(2)}, u32[]{:S(2)}) collective-permute-start(bf16[12,32,1024]{2,1,0:T(8,128)(2,1)S(1)} %collective-permute-done.16), channel_id=1, source_target_pairs={{0,3},{1,0},{2,1},{3,2},{4,7},{5,4},{6,5},{7,6},{8,11},{9,8},{10,9... | collective-permute-start | bytes 2359304 | tf_op jit(solution)/shard_map/ppermute | solution.py:212
  208.3 11.7 %collective-permute-done.17 = bf16[12,32,1024]{2,1,0:T(8,128)(2,1)S(1)} collective-permute-done((bf16[12,32,1024]{2,1,0:T(8,128)(2,1)}, bf16[12,32,1024]{2,1,0:T(8,128)(2,1)S(1)}, u32[]{:S(2)}, u32[]{:S(2)}) %collective-permute-start.17) | collective-permute-done | bytes 786464 | tf_op jit(solution)/shard_map/ppermute | solution.py:209
  221.9 10.1 %collective-permute-done.19 = bf16[12,32,1024]{2,1,0:T(8,128)(2,1)S(1)} collective-permute-done((bf16[12,32,1024]{2,1,0:T(8,128)(2,1)S(1)}, bf16[12,32,1024]{2,1,0:T(8,128)(2,1)S(1)}, u32[]{:S(2)}, u32[]{:S(2)}) %collective-permute-start.19) | collective-permute-done | bytes 786464 | tf_op jit(solution)/shard_map/ppermute | solution.py:211
  (93 shorter events, 57.3 us)
Async XLA Ops:
  2.0 15.5 %collective-permute-start.1 = (bf16[12,32,768]{2,1,0:T(8,128)(2,1)S(1)}, bf16[12,32,768]{2,1,0:T(8,128)(2,1)S(1)}, u32[]{:S(2)}, u32[]{:S(2)}) collective-permute-start(bf16[12,32,768]{2,1,0:T(8,128)(2,1)S(1)} %get-tuple-element.48), channel_id=1, source_target_pairs={{0,3},{1,0},{2,1},{3,2},{4,7},{5,4},{6,5},{7,6},{8,11},{9,8},{10,9... | collective-permute-start | bytes 1769480 | tf_op jit(solution)/shard_map/ppermute | solution.py:243
  4.9 16.0 %collective-permute-start = (bf16[12,32,768]{2,1,0:T(8,128)(2,1)S(1)}, bf16[12,32,768]{2,1,0:T(8,128)(2,1)S(1)}, u32[]{:S(2)}, u32[]{:S(2)}) collective-permute-start(bf16[12,32,768]{2,1,0:T(8,128)(2,1)S(1)} %get-tuple-element.49), channel_id=1, source_target_pairs={{0,1},{1,2},{2,3},{3,0},{4,5},{5,6},{6,7},{7,4},{8,9},{9,10},{10,1... | collective-permute-start | bytes 1769480 | tf_op jit(solution)/shard_map/ppermute | solution.py:242
  25.6 58.8 %collective-permute-start.2 = (bf16[24,32,768]{2,1,0:T(8,128)(2,1)}, bf16[24,32,768]{2,1,0:T(8,128)(2,1)S(1)}, u32[]{:S(2)}, u32[]{:S(2)}) collective-permute-start(bf16[24,32,768]{2,1,0:T(8,128)(2,1)} %get-tuple-element.22), channel_id=1, source_target_pairs={{0,1},{1,2},{2,3},{3,0},{4,5},{5,6},{6,7},{7,4},{8,9},{9,10},{10,1... | collective-permute-start | bytes 3538952 | tf_op jit(solution)/shard_map/ppermute | solution.py:245
  25.6 58.9 %collective-permute-start.3 = (bf16[24,32,768]{2,1,0:T(8,128)(2,1)}, bf16[24,32,768]{2,1,0:T(8,128)(2,1)S(1)}, u32[]{:S(2)}, u32[]{:S(2)}) collective-permute-start(bf16[24,32,768]{2,1,0:T(8,128)(2,1)} %get-tuple-element.23), channel_id=1, source_target_pairs={{0,3},{1,0},{2,1},{3,2},{4,7},{5,4},{6,5},{7,6},{8,11},{9,8},{10,9... | collective-permute-start | bytes 3538952 | tf_op jit(solution)/shard_map/ppermute | solution.py:246
  29.9 27.2 %collective-permute-start.5 = (bf16[12,32,256]{2,1,0:T(8,128)(2,1)S(1)}, bf16[12,32,256]{2,1,0:T(8,128)(2,1)S(1)}, u32[]{:S(2)}, u32[]{:S(2)}) collective-permute-start(bf16[12,32,256]{2,1,0:T(8,128)(2,1)S(1)} %get-tuple-element.46), channel_id=1, source_target_pairs={{0,3},{1,0},{2,1},{3,2},{4,7},{5,4},{6,5},{7,6},{8,11},{9,8},{10,9... | collective-permute-start | bytes 589832 | tf_op jit(solution)/shard_map/ppermute | solution.py:243
  30.0 27.8 %collective-permute-start.4 = (bf16[12,32,256]{2,1,0:T(8,128)(2,1)S(1)}, bf16[12,32,256]{2,1,0:T(8,128)(2,1)S(1)}, u32[]{:S(2)}, u32[]{:S(2)}) collective-permute-start(bf16[12,32,256]{2,1,0:T(8,128)(2,1)S(1)} %get-tuple-element.47), channel_id=1, source_target_pairs={{0,1},{1,2},{2,3},{3,0},{4,5},{5,6},{6,7},{7,4},{8,9},{9,10},{10,1... | collective-permute-start | bytes 589832 | tf_op jit(solution)/shard_map/ppermute | solution.py:242
  61.4 10.7 %collective-permute-start.6 = (bf16[24,32,256]{2,1,0:T(8,128)(2,1)}, bf16[24,32,256]{2,1,0:T(8,128)(2,1)S(1)}, u32[]{:S(2)}, u32[]{:S(2)}) collective-permute-start(bf16[24,32,256]{2,1,0:T(8,128)(2,1)} %get-tuple-element.25), channel_id=1, source_target_pairs={{0,1},{1,2},{2,3},{3,0},{4,5},{5,6},{6,7},{7,4},{8,9},{9,10},{10,1... | collective-permute-start | bytes 1179656 | tf_op jit(solution)/shard_map/ppermute | solution.py:245
  61.6 10.4 %collective-permute-start.7 = (bf16[24,32,256]{2,1,0:T(8,128)(2,1)}, bf16[24,32,256]{2,1,0:T(8,128)(2,1)S(1)}, u32[]{:S(2)}, u32[]{:S(2)}) collective-permute-start(bf16[24,32,256]{2,1,0:T(8,128)(2,1)} %get-tuple-element.26), channel_id=1, source_target_pairs={{0,3},{1,0},{2,1},{3,2},{4,7},{5,4},{6,5},{7,6},{8,11},{9,8},{10,9... | collective-permute-start | bytes 1179656 | tf_op jit(solution)/shard_map/ppermute | solution.py:246
  76.1 19.4 %all-to-all-start.1 = ((bf16[32,32,256]{2,1,0:T(8,128)(2,1)}), bf16[32,32,256]{2,1,0:T(8,128)(2,1)S(1)}, u32[]{:S(2)}, u32[]{:S(2)}) async-start(bf16[32,32,256]{2,1,0:T(8,128)(2,1)} %get-tuple-element.27), calls=%async_computation.1 | async-start | bytes 1048576 | tf_op jit(solution)/shard_map/all_to_all | solution.py:249
  95.5 27.2 %all-to-all-start = ((bf16[32,32,768]{2,1,0:T(8,128)(2,1)}), bf16[32,32,768]{2,1,0:T(8,128)(2,1)S(1)}, u32[]{:S(2)}, u32[]{:S(2)}) async-start(bf16[32,32,768]{2,1,0:T(8,128)(2,1)} %get-tuple-element.24), calls=%async_computation | async-start | bytes 3145728 | tf_op jit(solution)/shard_map/all_to_all | solution.py:249
  131.7 43.6 %all-to-all-start.2 = ((bf16[32,32,1024]{2,1,0:T(8,128)(2,1)}), bf16[32,32,1024]{2,1,0:T(8,128)(2,1)S(1)}, u32[]{:S(2)}, u32[]{:S(2)}) async-start(bf16[32,32,1024]{2,1,0:T(8,128)(2,1)} %bitcast.50), calls=%async_computation.2 | async-start | bytes 4194304 | tf_op jit(solution)/shard_map/all_to_all | solution.py:282
  135.8 1.2 collective-permute-start.8
  137.0 3.6 %collective-permute-start.9 = (f32[2,128]{1,0:T(2,128)S(1)}, f32[2,128]{1,0:T(2,128)S(1)}, u32[]{:S(2)}, u32[]{:S(2)}) collective-permute-start(f32[2,128]{1,0:T(2,128)S(1)} %add.89), channel_id=1, source_target_pairs={{0,1},{1,0},{2,3},{3,2},{4,5},{5,4},{6,7},{7,6},{8,9},{9,8},{10,11... | collective-permute-start | bytes 3080 | tf_op jit(solution)/shard_map/ppermute | solution.py:201
  140.6 4.8 %collective-permute-start.10 = (f32[2,128]{1,0:T(2,128)S(1)}, f32[2,128]{1,0:T(2,128)S(1)}, u32[]{:S(2)}, u32[]{:S(2)}) collective-permute-start(f32[2,128]{1,0:T(2,128)S(1)} %add.90), channel_id=1, source_target_pairs={{0,3},{3,0},{1,2},{2,1},{4,7},{7,4},{5,6},{6,5},{8,11},{11,8},{9,1... | collective-permute-start | bytes 3080 | tf_op jit(solution)/shard_map/ppermute | solution.py:201
  145.4 16.1 %collective-permute-start.11 = (f32[2,128]{1,0:T(2,128)S(1)}, f32[2,128]{1,0:T(2,128)S(1)}, u32[]{:S(2)}, u32[]{:S(2)}) collective-permute-start(f32[2,128]{1,0:T(2,128)S(1)} %add.91), channel_id=1, source_target_pairs={{0,32},{32,0},{64,96},{96,64},{1,33},{33,1},{65,97},{97,65},{2,34}... | collective-permute-start | bytes 3080 | tf_op jit(solution)/shard_map/ppermute | solution.py:201
  161.5 4.8 %collective-permute-start.12 = (f32[2,128]{1,0:T(2,128)S(1)}, f32[2,128]{1,0:T(2,128)S(1)}, u32[]{:S(2)}, u32[]{:S(2)}) collective-permute-start(f32[2,128]{1,0:T(2,128)S(1)} %add.92), channel_id=1, source_target_pairs={{0,96},{96,0},{32,64},{64,32},{1,97},{97,1},{33,65},{65,33},{2,98}... | collective-permute-start | bytes 3080 | tf_op jit(solution)/shard_map/ppermute | solution.py:201
  166.3 3.6 %collective-permute-start.13 = (f32[2,128]{1,0:T(2,128)S(1)}, f32[2,128]{1,0:T(2,128)S(1)}, u32[]{:S(2)}, u32[]{:S(2)}) collective-permute-start(f32[2,128]{1,0:T(2,128)S(1)} %add.93), channel_id=1, source_target_pairs={{0,8},{8,0},{16,24},{24,16},{1,9},{9,1},{17,25},{25,17},{2,10},{10... | collective-permute-start | bytes 3080 | tf_op jit(solution)/shard_map/ppermute | solution.py:201
  169.8 4.8 %collective-permute-start.14 = (f32[2,128]{1,0:T(2,128)S(1)}, f32[2,128]{1,0:T(2,128)S(1)}, u32[]{:S(2)}, u32[]{:S(2)}) collective-permute-start(f32[2,128]{1,0:T(2,128)S(1)} %add.94), channel_id=1, source_target_pairs={{0,24},{24,0},{8,16},{16,8},{1,25},{25,1},{9,17},{17,9},{2,26},{26... | collective-permute-start | bytes 3080 | tf_op jit(solution)/shard_map/ppermute | solution.py:201
  181.3 21.8 %collective-permute-start.15 = (bf16[12,32,1024]{2,1,0:T(8,128)(2,1)}, bf16[12,32,1024]{2,1,0:T(8,128)(2,1)S(1)}, u32[]{:S(2)}, u32[]{:S(2)}) collective-permute-start(bf16[12,32,1024]{2,1,0:T(8,128)(2,1)} %get-tuple-element.39), channel_id=1, source_target_pairs={{0,1},{1,2},{2,3},{3,0},{4,5},{5,6},{6,7},{7,4},{8,9},{9,10},{10,1... | collective-permute-start | bytes 2359304 | tf_op jit(solution)/shard_map/ppermute | solution.py:207
  182.3 20.9 %collective-permute-start.16 = (bf16[12,32,1024]{2,1,0:T(8,128)(2,1)}, bf16[12,32,1024]{2,1,0:T(8,128)(2,1)S(1)}, u32[]{:S(2)}, u32[]{:S(2)}) collective-permute-start(bf16[12,32,1024]{2,1,0:T(8,128)(2,1)} %get-tuple-element.40), channel_id=1, source_target_pairs={{0,3},{1,0},{2,1},{3,2},{4,7},{5,4},{6,5},{7,6},{8,11},{9,8},{10,9... | collective-permute-start | bytes 2359304 | tf_op jit(solution)/shard_map/ppermute | solution.py:208
  184.6 35.5 %collective-permute-start.17 = (bf16[12,32,1024]{2,1,0:T(8,128)(2,1)}, bf16[12,32,1024]{2,1,0:T(8,128)(2,1)S(1)}, u32[]{:S(2)}, u32[]{:S(2)}) collective-permute-start(bf16[12,32,1024]{2,1,0:T(8,128)(2,1)} %get-tuple-element.40), channel_id=1, source_target_pairs={{0,1},{1,2},{2,3},{3,0},{4,5},{5,6},{6,7},{7,4},{8,9},{9,10},{10,1... | collective-permute-start | bytes 2359304 | tf_op jit(solution)/shard_map/ppermute | solution.py:209
  190.7 30.3 %collective-permute-start.18 = (bf16[12,32,1024]{2,1,0:T(8,128)(2,1)}, bf16[12,32,1024]{2,1,0:T(8,128)(2,1)S(1)}, u32[]{:S(2)}, u32[]{:S(2)}) collective-permute-start(bf16[12,32,1024]{2,1,0:T(8,128)(2,1)} %get-tuple-element.39), channel_id=1, source_target_pairs={{0,3},{1,0},{2,1},{3,2},{4,7},{5,4},{6,5},{7,6},{8,11},{9,8},{10,9... | collective-permute-start | bytes 2359304 | tf_op jit(solution)/shard_map/ppermute | solution.py:210
  203.2 28.8 %collective-permute-start.19 = (bf16[12,32,1024]{2,1,0:T(8,128)(2,1)S(1)}, bf16[12,32,1024]{2,1,0:T(8,128)(2,1)S(1)}, u32[]{:S(2)}, u32[]{:S(2)}) collective-permute-start(bf16[12,32,1024]{2,1,0:T(8,128)(2,1)S(1)} %collective-permute-done.15), channel_id=1, source_target_pairs={{0,1},{1,2},{2,3},{3,0},{4,5},{5,6},{6,7},{7,4},{8,9},{9,10},{10,1... | collective-permute-start | bytes 2359304 | tf_op jit(solution)/shard_map/ppermute | solution.py:211
  203.2 29.8 %collective-permute-start.20 = (bf16[12,32,1024]{2,1,0:T(8,128)(2,1)S(1)}, bf16[12,32,1024]{2,1,0:T(8,128)(2,1)S(1)}, u32[]{:S(2)}, u32[]{:S(2)}) collective-permute-start(bf16[12,32,1024]{2,1,0:T(8,128)(2,1)S(1)} %collective-permute-done.16), channel_id=1, source_target_pairs={{0,3},{1,0},{2,1},{3,2},{4,7},{5,4},{6,5},{7,6},{8,11},{9,8},{10,9... | collective-permute-start | bytes 2359304 | tf_op jit(solution)/shard_map/ppermute | solution.py:212
  (16 other events, 128.2 us)

commit v4 on v3

--- a/solution.py
+++ b/solution.py
@@ -11,7 +11,7 @@
 LANES = 128
 GROUP = ("group_0", "group_1", "group_2")
 EVERY = ("group_0", "group_1", "group_2", "rep")
-SENT = ((768, 256), (0, 768))
+SENT = ((0, 384), (384, 640))
 
 
 step_rate = 0.5
@@ -23,10 +23,13 @@
     return [(i, (i + step) % count) for i in range(count)]
 
 
+def elements(*sizes):
+    return tuple(pl.Element(size) for size in sizes)
+
+
 def merge(who, parts, far_up, far_down, start, cols):
     _, blocks, rows, _ = parts.shape
     half = blocks // 2
-    at = start // cols
 
     def body(who_ref, above, below, from_down, from_up, out_up, out_down):
         first = pl.program_id(0) == 0
@@ -50,8 +53,8 @@
             num_scalar_prefetch=1,
             grid=(2,),
             in_specs=[
-                pl.BlockSpec((1, half, rows, cols), lambda i, w: (w[1], i, 0, at)),
-                pl.BlockSpec((1, half, rows, cols), lambda i, w: (w[3], i, 0, at)),
+                pl.BlockSpec(elements(1, half, rows, cols), lambda i, w: (w[1], i * half, 0, start)),
+                pl.BlockSpec(elements(1, half, rows, cols), lambda i, w: (w[3], i * half, 0, start)),
                 piece,
                 piece,
             ],
@@ -65,7 +68,6 @@
 def finish(who, table, parts, up, down, start, cols):
     _, blocks, rows, _ = parts.shape
     slots = table.shape[0]
-    at = start // cols
 
     def body(who_ref, table_ref, own, one, two, gradient, slotted):
         total = own[0].astype(f32) + one[...].astype(f32) + two[...].astype(f32)
@@ -80,7 +82,7 @@
             num_scalar_prefetch=2,
             grid=(1,),
             in_specs=[
-                pl.BlockSpec((1, blocks, rows, cols), lambda i, w, t: (w[0], 0, 0, at)),
+                pl.BlockSpec(elements(1, blocks, rows, cols), lambda i, w, t: (w[0], 0, 0, start)),
                 block,
                 block,
             ],
@@ -159,23 +161,39 @@
     )(left, right, owned, graft_row, layer_row, *earlier)
 
 
+def pick(position, returned, count):
+    slots, rows, cols = returned.shape
+
+    def body(position_ref, returned_ref, out):
+        for block in range(count):
+            out[block] = returned_ref[position_ref[block]]
+
+    return pl.pallas_call(
+        body,
+        grid_spec=pltpu.PrefetchScalarGridSpec(
+            num_scalar_prefetch=1,
+            grid=(1,),
+            in_specs=[pl.BlockSpec((slots, rows, cols), lambda i, p: (0, 0, 0))],
+            out_specs=pl.BlockSpec((count, rows, cols), lambda i, p: (0, 0, 0)),
+        ),
+        out_shape=jax.ShapeDtypeStruct((count, rows, cols), bf16),
+        name="pick",
+    )(position, returned)
+
+
 def update(who, position, scale, returned, params, reps):
     blocks, rows, cols = params.shape
     half = blocks // 2
     slots = returned.shape[0]
 
-    def body(who_ref, position_ref, scale_ref, returned_ref, params_ref, low, high, whole):
+    def body(who_ref, position_ref, scale_ref, returned_ref, params_ref, high, whole):
         for block in range(blocks):
             change = scale_ref[block] * returned_ref[position_ref[block]].astype(f32)
             new = (params_ref[block].astype(f32) - change).astype(bf16)
             whole[0, block] = new
-            if block < half:
-                low[block] = new
-            else:
+            if block >= half:
                 high[block - half] = new
 
-    out = pl.BlockSpec((half, rows, cols), lambda i, w, p, s: (0, 0, 0))
-    shape = jax.ShapeDtypeStruct((half, rows, cols), bf16)
     return pl.pallas_call(
         body,
         grid_spec=pltpu.PrefetchScalarGridSpec(
@@ -185,9 +203,15 @@
                 pl.BlockSpec((slots, rows, cols), lambda i, w, p, s: (0, 0, 0)),
                 pl.BlockSpec((blocks, rows, cols), lambda i, w, p, s: (0, 0, 0)),
             ],
-            out_specs=[out, out, pl.BlockSpec((1, blocks, rows, cols), lambda i, w, p, s: (w[0], 0, 0, 0))],
-        ),
-        out_shape=[shape, shape, jax.ShapeDtypeStruct((reps, blocks, rows, cols), bf16)],
+            out_specs=[
+                pl.BlockSpec((half, rows, cols), lambda i, w, p, s: (0, 0, 0)),
+                pl.BlockSpec((1, blocks, rows, cols), lambda i, w, p, s: (w[0], 0, 0, 0)),
+            ],
+        ),
+        out_shape=[
+            jax.ShapeDtypeStruct((half, rows, cols), bf16),
+            jax.ShapeDtypeStruct((reps, blocks, rows, cols), bf16),
+        ],
         name="update",
     )(who, position, scale, returned, params)
 
@@ -202,22 +226,12 @@
     return value
 
 
-def spread(low, high, reps):
+def spread(value, reps, onward):
     up, down = ring(reps, 1), ring(reps, -1)
-    low_up = lax.ppermute(low, "rep", up)
-    high_down = lax.ppermute(high, "rep", down)
-    high_up = lax.ppermute(high, "rep", up)
-    low_down = lax.ppermute(low, "rep", down)
-    far_low = lax.ppermute(low_up, "rep", up)
-    far_high = lax.ppermute(high_down, "rep", down)
-    return (
-        (3, 0, low_up),
-        (1, 1, high_down),
-        (3, 1, high_up),
-        (1, 0, low_down),
-        (2, 0, far_low),
-        (2, 1, far_high),
-    )
+    from_down = lax.ppermute(value, "rep", up)
+    from_up = lax.ppermute(value, "rep", down)
+    far = lax.ppermute(from_down, "rep", up) if onward > 0 else lax.ppermute(from_up, "rep", down)
+    return ((3, from_down), (1, from_up), (2, far))
 
 
 def local(grad_parts, params, accum, left_pre, right_pre, slot_block, layer_of):
@@ -251,8 +265,10 @@
             earlier.append(left_times(left, owned))
         owned = arrived.reshape(group_size * rows, cols)
 
-    my_layers = lax.dynamic_slice_in_dim(layer_of, me * blocks, blocks)
-    onehot = (my_layers[:, None] == jnp.arange(LAYERS, dtype=jnp.int32)[None, :]).astype(f32)
+    ahead = spread(params[:half], reps, 1)
+
+    onehots = (layer_of[:, None] == jnp.arange(LAYERS, dtype=jnp.int32)[None, :]).astype(f32)
+    onehot = lax.dynamic_slice_in_dim(onehots, me * blocks, blocks)
     in_order = sorted(range(len(SENT)), key=lambda c: SENT[c][0])
     wide = jnp.concatenate([gradients[c] for c in in_order], axis=2).astype(f32)
     new_accum = accum + wide * wide
@@ -273,8 +289,8 @@
     to_lanes = ((0, 0), (0, LANES - LAYERS))
     graft_row = jnp.pad(graft_layer[None, :], to_lanes)
     layer_row = jnp.pad(my_layer[None, :], to_lanes)
-    owned, earlier, graft_row, layer_row, position, onehot, new_accum = lax.optimization_barrier(
-        (owned, earlier, graft_row, layer_row, position, onehot, new_accum)
+    owned, earlier, graft_row, layer_row, position, onehots, new_accum = lax.optimization_barrier(
+        (owned, earlier, graft_row, layer_row, position, onehots, new_accum)
     )
 
     precond, sums = products(left, right, owned, earlier, graft_row, layer_row)
@@ -282,11 +298,17 @@
     returned = lax.all_to_all(outgoing, GROUP, split_axis=0, concat_axis=0, tiled=True)
     sums = everywhere(sums)
     layer_scale = jnp.sqrt(sums[0, :LAYERS]) * lax.rsqrt(sums[1, :LAYERS] + 1e-06)
-    scale = step_rate * jnp.sum(onehot * layer_scale[None, :], axis=1)
-
-    low, high, new_params = update(who, position, scale, returned, params, reps)
-    for offset, part, piece in spread(low, high, reps):
-        new_params = lax.dynamic_update_slice(new_params, piece[None], (who[offset], part * half, 0, 0))
+    scales = (step_rate * jnp.sum(onehots * layer_scale[None, :], axis=1)).reshape(reps, blocks)
+
+    changes = spread(pick(position, returned, half), reps, 1)
+    high, new_params = update(who, position, scales[me], returned, params, reps)
+    finished = spread(high, reps, -1)
+    for (offset, old), (_, change) in zip(ahead, changes):
+        scale = scales[who[offset]][:half, None, None]
+        new = (old.astype(f32) - scale * change.astype(f32)).astype(bf16)
+        new_params = lax.dynamic_update_slice(new_params, new[None], (who[offset], 0, 0, 0))
+    for offset, piece in finished:
+        new_params = lax.dynamic_update_slice(new_params, piece[None], (who[offset], half, 0, 0))
     return (new_params.reshape(reps * blocks, rows, width), new_accum)
 
 

time: 235 us -> 227 us (0.966)
  waiting for transfers between devices: 122 us -> 100 us
  starting transfers between devices: 49.8 us -> 56.2 us
  other arithmetic: 7.48 us -> 13.2 us
  Pallas kernels: 30.4 us -> 34 us
    ppermute x2, waiting for transfers between devices: 37.1 us -> 0.78 us  [local(): far_down = lax.ppermute(high, 'rep', down)]
    ppermute x6 -> x9, waiting for transfers between devices: 30.9 us -> 49.2 us  [the longest x3 24.3 us: spread(): from_down = lax.ppermute(value, 'rep', up)]
    all_to_all x3, waiting for transfers between devices: 16.3 us -> 8.91 us  [local(): lax.all_to_all(outgoing, GROUP, split_axis=0, concat_axis=0, tiled=True)]
    dynamic_update_slice x0 -> x3, other arithmetic: none -> 6.15 us  [local(): lax.dynamic_update_slice(new_params, new[None], (who[offset], 0, 0, 0))]
    ppermute x2, waiting for transfers between devices: 6.44 us -> 10.8 us  [local(): near_up = lax.ppermute(to_up, 'rep', up)]
    all_to_all x3, starting transfers between devices: 16.6 us -> 20.8 us  [local(): lax.all_to_all(outgoing, GROUP, split_axis=0, concat_axis=0, tiled=True)]
    ppermute x7, waiting for transfers between devices: 27.5 us -> 24.1 us  [everywhere(): value = value + lax.ppermute(value, axis, pairs)]
    pallas_call x0 -> x1, Pallas kernels: none -> 3.22 us  [pick(): pl.pallas_call(body, grid_spec=pltpu.PrefetchScalarGridSpec(num_scalar_pr...]
  transfers between devices with their start and end apart: 24 -> 27, of which waited for: 17 -> 20; matrix products, arithmetic and copies ran while one was open for 7% -> 9% of each run, Pallas kernels for 6% -> 12%
where the time goes in v4:
time: 227 us; the launch traced here: 226 us
  waiting for transfers between devices  100 us (44%)
  starting transfers between devices  56.2 us (25%)
  Pallas kernels  34 us (15%)
  local copies, waits for them, and re-layouts  16.1 us (7%)
  other arithmetic  13.2 us (6%)
  between operations  6.22 us (3%)
    ppermute x3, waiting for transfers between devices, spread(): from_down = lax.ppermute(value, 'rep', up)  24.3 us
    ppermute x7, waiting for transfers between devices, everywhere(): value = value + lax.ppermute(value, axis, pairs)  24.1 us
    all_to_all x3, starting transfers between devices, local(): lax.all_to_all(outgoing, GROUP, split_axis=0, concat_axis=0, tiled=True)  20.8 us
    ppermute x3, waiting for transfers between devices, spread(): from_up = lax.ppermute(value, 'rep', down)  15.3 us
    ppermute x2, waiting for transfers between devices, local(): near_up = lax.ppermute(to_up, 'rep', up)  10.8 us
    ppermute x7, starting transfers between devices, everywhere(): value = value + lax.ppermute(value, axis, pairs)  9.62 us
    ppermute x2, waiting for transfers between devices, spread(): lax.ppermute(from_down, 'rep', up)  9.58 us
    all_to_all x3, waiting for transfers between devices, local(): lax.all_to_all(outgoing, GROUP, split_axis=0, concat_axis=0, tiled=True)  8.91 us
  transfers between devices with their start and end apart: 27, of which 20 were waited for; matrix products, arithmetic and copies ran while one was open for 9% of the time, Pallas kernels for 12%

profile of v4, /device:TPU:0, one launch (start us, length us, event | category | flops | bytes accessed | tf_op | source)
XLA Modules:
  0.0 225.7 jit_solution(9457770794780436096)
XLA Ops:
  14.4 3.1 %merge.3 = (bf16[24,32,384]{2,1,0:T(8,128)(2,1)}, bf16[24,32,384]{2,1,0:T(8,128)(2,1)}) custom-call(s32[4]{0:T(128)} %compare_select_fusion.who_ref, bf16[4,24,32,1024]{3,2,1,0:T(8,128)(2,1)} %bitcast.54, bf16[4,24,32,1024]{3,2,1,0:T(8,128)(2,1)} %bitcast.55, bf16[12,32,384]{2,1,0:T(8,128)(2,1)} %copy-done.10, bf16[12,32,384]{2,1,0:T(8,128)(2,1)} %copy-done.11), custom_call_target="tpu_custom_call" | custom-call | tf_op jit(solution)/shard_map/merge/pallas_call | solution.py:50
  25.0 3.6 %merge.2 = (bf16[24,32,640]{2,1,0:T(8,128)(2,1)}, bf16[24,32,640]{2,1,0:T(8,128)(2,1)}) custom-call(s32[4]{0:T(128)} %compare_select_fusion.who_ref, bf16[4,24,32,1024]{3,2,1,0:T(8,128)(2,1)} %bitcast.56, bf16[4,24,32,1024]{3,2,1,0:T(8,128)(2,1)} %bitcast.57, bf16[12,32,640]{2,1,0:T(8,128)(2,1)} %copy-done.8, bf16[12,32,640]{2,1,0:T(8,128)(2,1)} %copy-done.9), custom_call_target="tpu_custom_call" | custom-call | tf_op jit(solution)/shard_map/merge/pallas_call | solution.py:50
  32.3 3.8 %collective-permute-done.6.one = bf16[24,32,384]{2,1,0:T(8,128)(2,1)S(1)} collective-permute-done((bf16[24,32,384]{2,1,0:T(8,128)(2,1)}, bf16[24,32,384]{2,1,0:T(8,128)(2,1)S(1)}, u32[]{:S(2)}, u32[]{:S(2)}) %collective-permute-start.6) | collective-permute-done | bytes 589856 | tf_op jit(solution)/shard_map/ppermute | solution.py:259
  36.9 3.6 %finish.3 = (bf16[24,32,384]{2,1,0:T(8,128)(2,1)}, bf16[32,32,384]{2,1,0:T(8,128)(2,1)}) custom-call(s32[4]{0:T(128)} %compare_select_fusion.who_ref, s32[32]{0:T(128)} %get-tuple-element.42.table_ref, bf16[4,24,32,1024]{3,2,1,0:T(8,128)(2,1)} %bitcast.58, bf16[24,32,384]{2,1,0:T(8,128)(2,1)} %copy-done.7, bf16[24,32,384]{2,1,0:T(8,128)(2,1)} %collective-permute-done.7.two), custom_call_target="tpu_custom_call" | custom-call | tf_op jit(solution)/shard_map/finish/pallas_call | solution.py:79
  40.5 8.4 %all-to-all-start.1 = ((bf16[32,32,384]{2,1,0:T(8,128)(2,1)}), bf16[32,32,384]{2,1,0:T(8,128)(2,1)S(1)}, u32[]{:S(2)}, u32[]{:S(2)}) async-start(bf16[32,32,384]{2,1,0:T(8,128)(2,1)} %get-tuple-element.26), calls=%async_computation.1 | async-start | bytes 1572864 | tf_op jit(solution)/shard_map/all_to_all | solution.py:263
  48.9 7.0 %collective-permute-done.2.one = bf16[24,32,640]{2,1,0:T(8,128)(2,1)S(1)} collective-permute-done((bf16[24,32,640]{2,1,0:T(8,128)(2,1)}, bf16[24,32,640]{2,1,0:T(8,128)(2,1)S(1)}, u32[]{:S(2)}, u32[]{:S(2)}) %collective-permute-start.2) | collective-permute-done | bytes 983072 | tf_op jit(solution)/shard_map/ppermute | solution.py:259
  57.8 4.6 %finish.2 = (bf16[24,32,640]{2,1,0:T(8,128)(2,1)}, bf16[32,32,640]{2,1,0:T(8,128)(2,1)}) custom-call(s32[4]{0:T(128)} %compare_select_fusion.who_ref, s32[32]{0:T(128)} %get-tuple-element.42.table_ref, bf16[4,24,32,1024]{3,2,1,0:T(8,128)(2,1)} %bitcast.59, bf16[24,32,640]{2,1,0:T(8,128)(2,1)} %copy-done.4, bf16[24,32,640]{2,1,0:T(8,128)(2,1)} %copy-done.5), custom_call_target="tpu_custom_call" | custom-call | tf_op jit(solution)/shard_map/finish/pallas_call | solution.py:79
  62.8 8.3 %all-to-all-start = ((bf16[32,32,640]{2,1,0:T(8,128)(2,1)}), bf16[32,32,640]{2,1,0:T(8,128)(2,1)S(1)}, u32[]{:S(2)}, u32[]{:S(2)}) async-start(bf16[32,32,640]{2,1,0:T(8,128)(2,1)} %get-tuple-element.23), calls=%async_computation | async-start | bytes 2621440 | tf_op jit(solution)/shard_map/all_to_all | solution.py:263
  73.1 4.4 %fusion = (f32[24,32,1024]{2,1,0:T(8,128)}, f32[24]{0:T(128)S(1)}) fusion(f32[24,32,1024]{2,1,0:T(8,128)} %param.9, bf16[24,32,640]{2,1,0:T(8,128)(2,1)S(1)} %copy-done.3, bf16[24,32,384]{2,1,0:T(8,128)(2,1)} %get-tuple-element.27), kind=kLoop, calls=%fused_computation.2 | loop fusion | flops 7077864 | bytes 7864416 | tf_op jit(solution)/shard_map/add | solution.py:274
  78.7 3.6 %left_times.1.rest_0_ = bf16[1024,384]{1,0:T(8,128)(2,1)} custom-call(bf16[1024,1024]{1,0:T(8,128)(2,1)} %bitcast.60, bf16[1024,384]{1,0:T(8,128)(2,1)} %bitcast.63), custom_call_target="tpu_custom_call" | custom-call | tf_op jit(solution)/shard_map/left_times/pallas_call | solution.py:106
  82.4 8.5 %all-to-all-done = bf16[32,32,640]{2,1,0:T(8,128)(2,1)S(1)} async-done(((bf16[32,32,640]{2,1,0:T(8,128)(2,1)}), bf16[32,32,640]{2,1,0:T(8,128)(2,1)S(1)}, u32[]{:S(2)}, u32[]{:S(2)}) %all-to-all-start) | async-done | bytes 1310752 | tf_op jit(solution)/shard_map/all_to_all | solution.py:263
  92.0 7.7 %products.1 = (bf16[1024,1024]{1,0:T(8,128)(2,1)}, f32[2,128]{1,0:T(2,128)}) custom-call(bf16[1024,1024]{1,0:T(8,128)(2,1)} %bitcast.61, bf16[1024,1024]{1,0:T(8,128)(2,1)} %bitcast.64, bf16[1024,640]{1,0:T(8,128)(2,1)} %bitcast.62, f32[1,128]{1,0:T(1,128)} %pad.7.graft_ref, f32[1,128]{1,0:T(1,128)} %pad.8.layer_ref, bf16[1024,384]{1,0:T(8,128)(2,1)} %left_times.1.rest_0_), custom_call_target="tpu_custom_call" | custom-call | tf_op jit(solution)/shard_map/products/pallas_call | solution.py:146
  99.8 4.0 %all-to-all-start.2 = ((bf16[32,32,1024]{2,1,0:T(8,128)(2,1)}), bf16[32,32,1024]{2,1,0:T(8,128)(2,1)S(1)}, u32[]{:S(2)}, u32[]{:S(2)}) async-start(bf16[32,32,1024]{2,1,0:T(8,128)(2,1)} %bitcast.65), calls=%async_computation.2 | async-start | bytes 4194304 | tf_op jit(solution)/shard_map/all_to_all | solution.py:298
  105.6 3.0 %collective-permute-done.9 = f32[2,128]{1,0:T(2,128)S(1)} collective-permute-done((f32[2,128]{1,0:T(2,128)S(1)}, f32[2,128]{1,0:T(2,128)S(1)}, u32[]{:S(2)}, u32[]{:S(2)}) %collective-permute-start.9) | collective-permute-done | bytes 1056 | tf_op jit(solution)/shard_map/ppermute | solution.py:225
  115.2 14.4 %collective-permute-done.11 = f32[2,128]{1,0:T(2,128)S(1)} collective-permute-done((f32[2,128]{1,0:T(2,128)S(1)}, f32[2,128]{1,0:T(2,128)S(1)}, u32[]{:S(2)}, u32[]{:S(2)}) %collective-permute-start.11) | collective-permute-done | bytes 1056 | tf_op jit(solution)/shard_map/ppermute | solution.py:225
  131.4 2.9 %collective-permute-done.12 = f32[2,128]{1,0:T(2,128)S(1)} collective-permute-done((f32[2,128]{1,0:T(2,128)S(1)}, f32[2,128]{1,0:T(2,128)S(1)}, u32[]{:S(2)}, u32[]{:S(2)}) %collective-permute-start.12) | collective-permute-done | bytes 1056 | tf_op jit(solution)/shard_map/ppermute | solution.py:225
  149.7 3.2 %pick.1 = bf16[12,32,1024]{2,1,0:T(8,128)(2,1)} custom-call(s32[24]{0:T(128)} %select_reduce_fusion.position_ref, bf16[32,32,1024]{2,1,0:T(8,128)(2,1)} %copy-done), custom_call_target="tpu_custom_call" | custom-call | tf_op jit(solution)/shard_map/pick/pallas_call | solution.py:171
  153.7 4.6 %update.1 = (bf16[12,32,1024]{2,1,0:T(8,128)(2,1)}, bf16[4,24,32,1024]{3,2,1,0:T(8,128)(2,1)}) custom-call(s32[4]{0:T(128)} %compare_select_fusion.who_ref, s32[24]{0:T(128)} %select_reduce_fusion.position_ref, f32[24]{0:T(128)} %get-tuple-element.53.scale_ref, bf16[32,32,1024]{2,1,0:T(8,128)(2,1)} %copy-done, bf16[24,32,1024]{2,1,0:T(8,128)(2,1)} %params_ref.1), custom_call_target="tpu_custom_call" | custom-call | tf_op jit(solution)/shard_map/update/pallas_call | solution.py:197
  158.2 3.2 %collective-permute-start.22 = (bf16[12,32,1024]{2,1,0:T(8,128)(2,1)}, bf16[12,32,1024]{2,1,0:T(8,128)(2,1)S(1)}, u32[]{:S(2)}, u32[]{:S(2)}) collective-permute-start(bf16[12,32,1024]{2,1,0:T(8,128)(2,1)} %get-tuple-element.38), channel_id=1, source_target_pairs={{0,3},{1,0},{2,1},{3,2},{4,7},{5,4},{6,5},{7,6},{8,11},{9,8},{10,9... | collective-permute-start | bytes 2359304 | tf_op jit(solution)/shard_map/ppermute | solution.py:232
  163.5 11.3 %collective-permute-done.16 = bf16[12,32,1024]{2,1,0:T(8,128)(2,1)S(1)} collective-permute-done((bf16[12,32,1024]{2,1,0:T(8,128)(2,1)}, bf16[12,32,1024]{2,1,0:T(8,128)(2,1)S(1)}, u32[]{:S(2)}, u32[]{:S(2)}) %collective-permute-start.16) | collective-permute-done | bytes 786464 | tf_op jit(solution)/shard_map/ppermute | solution.py:231
  179.7 3.6 %collective-permute-start.23 = (bf16[12,32,1024]{2,1,0:T(8,128)(2,1)S(1)}, bf16[12,32,1024]{2,1,0:T(8,128)(2,1)S(1)}, u32[]{:S(2)}, u32[]{:S(2)}) collective-permute-start(bf16[12,32,1024]{2,1,0:T(8,128)(2,1)S(1)} %collective-permute-done.22), channel_id=1, source_target_pairs={{0,3},{1,0},{2,1},{3,2},{4,7},{5,4},{6,5},{7,6},{8,11},{9,8},{10,9... | collective-permute-start | bytes 2359304 | tf_op jit(solution)/shard_map/ppermute | solution.py:233
  183.3 13.2 %collective-permute-done.18 = bf16[12,32,1024]{2,1,0:T(8,128)(2,1)S(1)} collective-permute-done((bf16[12,32,1024]{2,1,0:T(8,128)(2,1)S(1)}, bf16[12,32,1024]{2,1,0:T(8,128)(2,1)S(1)}, u32[]{:S(2)}, u32[]{:S(2)}) %collective-permute-start.18) | collective-permute-done | bytes 786464 | tf_op jit(solution)/shard_map/ppermute | solution.py:232
  198.9 9.6 %collective-permute-done.20 = bf16[12,32,1024]{2,1,0:T(8,128)(2,1)S(1)} collective-permute-done((bf16[12,32,1024]{2,1,0:T(8,128)(2,1)S(1)}, bf16[12,32,1024]{2,1,0:T(8,128)(2,1)S(1)}, u32[]{:S(2)}, u32[]{:S(2)}) %collective-permute-start.20) | collective-permute-done | bytes 786464 | tf_op jit(solution)/shard_map/ppermute | solution.py:233
  209.8 13.0 %collective-permute-done.21 = bf16[12,32,1024]{2,1,0:T(8,128)(2,1)S(1)} collective-permute-done((bf16[12,32,1024]{2,1,0:T(8,128)(2,1)}, bf16[12,32,1024]{2,1,0:T(8,128)(2,1)S(1)}, u32[]{:S(2)}, u32[]{:S(2)}) %collective-permute-start.21) | collective-permute-done | bytes 786464 | tf_op jit(solution)/shard_map/ppermute | solution.py:231
  (104 shorter events, 66.8 us)
Async XLA Ops:
  1.8 11.2 %collective-permute-start.4 = (bf16[12,32,384]{2,1,0:T(8,128)(2,1)S(1)}, bf16[12,32,384]{2,1,0:T(8,128)(2,1)S(1)}, u32[]{:S(2)}, u32[]{:S(2)}) collective-permute-start(bf16[12,32,384]{2,1,0:T(8,128)(2,1)S(1)} %get-tuple-element.45), channel_id=1, source_target_pairs={{0,1},{1,2},{2,3},{3,0},{4,5},{5,6},{6,7},{7,4},{8,9},{9,10},{10,1... | collective-permute-start | bytes 884744 | tf_op jit(solution)/shard_map/ppermute | solution.py:256
  3.4 9.9 %collective-permute-start.5 = (bf16[12,32,384]{2,1,0:T(8,128)(2,1)S(1)}, bf16[12,32,384]{2,1,0:T(8,128)(2,1)S(1)}, u32[]{:S(2)}, u32[]{:S(2)}) collective-permute-start(bf16[12,32,384]{2,1,0:T(8,128)(2,1)S(1)} %get-tuple-element.44), channel_id=1, source_target_pairs={{0,3},{1,0},{2,1},{3,2},{4,7},{5,4},{6,5},{7,6},{8,11},{9,8},{10,9... | collective-permute-start | bytes 884744 | tf_op jit(solution)/shard_map/ppermute | solution.py:257
  6.3 17.1 %collective-permute-start = (bf16[12,32,640]{2,1,0:T(8,128)(2,1)S(1)}, bf16[12,32,640]{2,1,0:T(8,128)(2,1)S(1)}, u32[]{:S(2)}, u32[]{:S(2)}) collective-permute-start(bf16[12,32,640]{2,1,0:T(8,128)(2,1)S(1)} %get-tuple-element.47), channel_id=1, source_target_pairs={{0,1},{1,2},{2,3},{3,0},{4,5},{5,6},{6,7},{7,4},{8,9},{9,10},{10,1... | collective-permute-start | bytes 1474568 | tf_op jit(solution)/shard_map/ppermute | solution.py:256
  6.8 17.0 %collective-permute-start.1 = (bf16[12,32,640]{2,1,0:T(8,128)(2,1)S(1)}, bf16[12,32,640]{2,1,0:T(8,128)(2,1)S(1)}, u32[]{:S(2)}, u32[]{:S(2)}) collective-permute-start(bf16[12,32,640]{2,1,0:T(8,128)(2,1)S(1)} %get-tuple-element.46), channel_id=1, source_target_pairs={{0,3},{1,0},{2,1},{3,2},{4,7},{5,4},{6,5},{7,6},{8,11},{9,8},{10,9... | collective-permute-start | bytes 1474568 | tf_op jit(solution)/shard_map/ppermute | solution.py:257
  17.4 18.7 %collective-permute-start.6 = (bf16[24,32,384]{2,1,0:T(8,128)(2,1)}, bf16[24,32,384]{2,1,0:T(8,128)(2,1)S(1)}, u32[]{:S(2)}, u32[]{:S(2)}) collective-permute-start(bf16[24,32,384]{2,1,0:T(8,128)(2,1)} %get-tuple-element.24), channel_id=1, source_target_pairs={{0,1},{1,2},{2,3},{3,0},{4,5},{5,6},{6,7},{7,4},{8,9},{9,10},{10,1... | collective-permute-start | bytes 1769480 | tf_op jit(solution)/shard_map/ppermute | solution.py:259
  18.6 18.0 %collective-permute-start.7 = (bf16[24,32,384]{2,1,0:T(8,128)(2,1)}, bf16[24,32,384]{2,1,0:T(8,128)(2,1)}, u32[]{:S(2)}, u32[]{:S(2)}) collective-permute-start(bf16[24,32,384]{2,1,0:T(8,128)(2,1)} %get-tuple-element.25), channel_id=1, source_target_pairs={{0,3},{1,0},{2,1},{3,2},{4,7},{5,4},{6,5},{7,6},{8,11},{9,8},{10,9... | collective-permute-start | bytes 1769480 | tf_op jit(solution)/shard_map/ppermute | solution.py:260
  28.6 27.4 %collective-permute-start.2 = (bf16[24,32,640]{2,1,0:T(8,128)(2,1)}, bf16[24,32,640]{2,1,0:T(8,128)(2,1)S(1)}, u32[]{:S(2)}, u32[]{:S(2)}) collective-permute-start(bf16[24,32,640]{2,1,0:T(8,128)(2,1)} %get-tuple-element.21), channel_id=1, source_target_pairs={{0,1},{1,2},{2,3},{3,0},{4,5},{5,6},{6,7},{7,4},{8,9},{9,10},{10,1... | collective-permute-start | bytes 2949128 | tf_op jit(solution)/shard_map/ppermute | solution.py:259
  29.7 26.4 %collective-permute-start.3 = (bf16[24,32,640]{2,1,0:T(8,128)(2,1)}, bf16[24,32,640]{2,1,0:T(8,128)(2,1)S(1)}, u32[]{:S(2)}, u32[]{:S(2)}) collective-permute-start(bf16[24,32,640]{2,1,0:T(8,128)(2,1)} %get-tuple-element.22), channel_id=1, source_target_pairs={{0,3},{1,0},{2,1},{3,2},{4,7},{5,4},{6,5},{7,6},{8,11},{9,8},{10,9... | collective-permute-start | bytes 2949128 | tf_op jit(solution)/shard_map/ppermute | solution.py:260
  40.5 22.4 %all-to-all-start.1 = ((bf16[32,32,384]{2,1,0:T(8,128)(2,1)}), bf16[32,32,384]{2,1,0:T(8,128)(2,1)S(1)}, u32[]{:S(2)}, u32[]{:S(2)}) async-start(bf16[32,32,384]{2,1,0:T(8,128)(2,1)} %get-tuple-element.26), calls=%async_computation.1 | async-start | bytes 1572864 | tf_op jit(solution)/shard_map/all_to_all | solution.py:263
  62.8 28.1 %all-to-all-start = ((bf16[32,32,640]{2,1,0:T(8,128)(2,1)}), bf16[32,32,640]{2,1,0:T(8,128)(2,1)S(1)}, u32[]{:S(2)}, u32[]{:S(2)}) async-start(bf16[32,32,640]{2,1,0:T(8,128)(2,1)} %get-tuple-element.23), calls=%async_computation | async-start | bytes 2621440 | tf_op jit(solution)/shard_map/all_to_all | solution.py:263
  99.8 48.6 %all-to-all-start.2 = ((bf16[32,32,1024]{2,1,0:T(8,128)(2,1)}), bf16[32,32,1024]{2,1,0:T(8,128)(2,1)S(1)}, u32[]{:S(2)}, u32[]{:S(2)}) async-start(bf16[32,32,1024]{2,1,0:T(8,128)(2,1)} %bitcast.65), calls=%async_computation.2 | async-start | bytes 4194304 | tf_op jit(solution)/shard_map/all_to_all | solution.py:298
  108.7 4.8 %collective-permute-start.10 = (f32[2,128]{1,0:T(2,128)S(1)}, f32[2,128]{1,0:T(2,128)S(1)}, u32[]{:S(2)}, u32[]{:S(2)}) collective-permute-start(f32[2,128]{1,0:T(2,128)S(1)} %add.94), channel_id=1, source_target_pairs={{0,3},{3,0},{1,2},{2,1},{4,7},{7,4},{5,6},{6,5},{8,11},{11,8},{9,1... | collective-permute-start | bytes 3080 | tf_op jit(solution)/shard_map/ppermute | solution.py:225
  113.4 16.1 %collective-permute-start.11 = (f32[2,128]{1,0:T(2,128)S(1)}, f32[2,128]{1,0:T(2,128)S(1)}, u32[]{:S(2)}, u32[]{:S(2)}) collective-permute-start(f32[2,128]{1,0:T(2,128)S(1)} %add.95), channel_id=1, source_target_pairs={{0,32},{32,0},{64,96},{96,64},{1,33},{33,1},{65,97},{97,65},{2,34}... | collective-permute-start | bytes 3080 | tf_op jit(solution)/shard_map/ppermute | solution.py:225
  134.3 5.8 %collective-permute-start.13 = (f32[2,128]{1,0:T(2,128)S(1)}, f32[2,128]{1,0:T(2,128)S(1)}, u32[]{:S(2)}, u32[]{:S(2)}) collective-permute-start(f32[2,128]{1,0:T(2,128)S(1)} %add.97), channel_id=1, source_target_pairs={{0,8},{8,0},{16,24},{24,16},{1,9},{9,1},{17,25},{25,17},{2,10},{10... | collective-permute-start | bytes 3080 | tf_op jit(solution)/shard_map/ppermute | solution.py:225
  136.6 24.9 %collective-permute-start.15 = (bf16[12,32,1024]{2,1,0:T(8,128)(2,1)S(1)}, bf16[12,32,1024]{2,1,0:T(8,128)(2,1)}, u32[]{:S(2)}, u32[]{:S(2)}) collective-permute-start(bf16[12,32,1024]{2,1,0:T(8,128)(2,1)S(1)} %slice.38), channel_id=1, source_target_pairs={{0,1},{1,2},{2,3},{3,0},{4,5},{5,6},{6,7},{7,4},{8,9},{9,10},{10,1... | collective-permute-start | bytes 2359304 | tf_op jit(solution)/shard_map/ppermute | solution.py:231
  137.4 37.3 %collective-permute-start.17 = (bf16[12,32,1024]{2,1,0:T(8,128)(2,1)S(1)}, bf16[12,32,1024]{2,1,0:T(8,128)(2,1)}, u32[]{:S(2)}, u32[]{:S(2)}) collective-permute-start(bf16[12,32,1024]{2,1,0:T(8,128)(2,1)S(1)} %slice.38), channel_id=1, source_target_pairs={{0,3},{1,0},{2,1},{3,2},{4,7},{5,4},{6,5},{7,6},{8,11},{9,8},{10,9... | collective-permute-start | bytes 2359304 | tf_op jit(solution)/shard_map/ppermute | solution.py:232
  140.1 8.2 %collective-permute-start.14 = (f32[2,128]{1,0:T(2,128)S(1)}, f32[2,128]{1,0:T(2,128)S(1)}, u32[]{:S(2)}, u32[]{:S(2)}) collective-permute-start(f32[2,128]{1,0:T(2,128)S(1)} %add.98), channel_id=1, source_target_pairs={{0,24},{24,0},{8,16},{16,8},{1,25},{25,1},{9,17},{17,9},{2,26},{26... | collective-permute-start | bytes 3080 | tf_op jit(solution)/shard_map/ppermute | solution.py:225
  152.9 21.8 %collective-permute-start.16 = (bf16[12,32,1024]{2,1,0:T(8,128)(2,1)}, bf16[12,32,1024]{2,1,0:T(8,128)(2,1)S(1)}, u32[]{:S(2)}, u32[]{:S(2)}) collective-permute-start(bf16[12,32,1024]{2,1,0:T(8,128)(2,1)} %pick.1), channel_id=1, source_target_pairs={{0,1},{1,2},{2,3},{3,0},{4,5},{5,6},{6,7},{7,4},{8,9},{9,10},{10,1... | collective-permute-start | bytes 2359304 | tf_op jit(solution)/shard_map/ppermute | solution.py:231
  158.2 21.5 %collective-permute-start.22 = (bf16[12,32,1024]{2,1,0:T(8,128)(2,1)}, bf16[12,32,1024]{2,1,0:T(8,128)(2,1)S(1)}, u32[]{:S(2)}, u32[]{:S(2)}) collective-permute-start(bf16[12,32,1024]{2,1,0:T(8,128)(2,1)} %get-tuple-element.38), channel_id=1, source_target_pairs={{0,3},{1,0},{2,1},{3,2},{4,7},{5,4},{6,5},{7,6},{8,11},{9,8},{10,9... | collective-permute-start | bytes 2359304 | tf_op jit(solution)/shard_map/ppermute | solution.py:232
  161.5 35.0 %collective-permute-start.18 = (bf16[12,32,1024]{2,1,0:T(8,128)(2,1)S(1)}, bf16[12,32,1024]{2,1,0:T(8,128)(2,1)S(1)}, u32[]{:S(2)}, u32[]{:S(2)}) collective-permute-start(bf16[12,32,1024]{2,1,0:T(8,128)(2,1)S(1)} %copy-done.6), channel_id=1, source_target_pairs={{0,3},{1,0},{2,1},{3,2},{4,7},{5,4},{6,5},{7,6},{8,11},{9,8},{10,9... | collective-permute-start | bytes 2359304 | tf_op jit(solution)/shard_map/ppermute | solution.py:232
  161.5 37.4 %collective-permute-start.19 = (bf16[12,32,1024]{2,1,0:T(8,128)(2,1)}, bf16[12,32,1024]{2,1,0:T(8,128)(2,1)S(1)}, u32[]{:S(2)}, u32[]{:S(2)}) collective-permute-start(bf16[12,32,1024]{2,1,0:T(8,128)(2,1)} %collective-permute-done.15), channel_id=1, source_target_pairs={{0,1},{1,2},{2,3},{3,0},{4,5},{5,6},{6,7},{7,4},{8,9},{9,10},{10,1... | collective-permute-start | bytes 2359304 | tf_op jit(solution)/shard_map/ppermute | solution.py:233
  174.8 33.7 %collective-permute-start.20 = (bf16[12,32,1024]{2,1,0:T(8,128)(2,1)S(1)}, bf16[12,32,1024]{2,1,0:T(8,128)(2,1)S(1)}, u32[]{:S(2)}, u32[]{:S(2)}) collective-permute-start(bf16[12,32,1024]{2,1,0:T(8,128)(2,1)S(1)} %collective-permute-done.16), channel_id=1, source_target_pairs={{0,1},{1,2},{2,3},{3,0},{4,5},{5,6},{6,7},{7,4},{8,9},{9,10},{10,1... | collective-permute-start | bytes 2359304 | tf_op jit(solution)/shard_map/ppermute | solution.py:233
  174.8 48.0 %collective-permute-start.21 = (bf16[12,32,1024]{2,1,0:T(8,128)(2,1)}, bf16[12,32,1024]{2,1,0:T(8,128)(2,1)S(1)}, u32[]{:S(2)}, u32[]{:S(2)}) collective-permute-start(bf16[12,32,1024]{2,1,0:T(8,128)(2,1)} %get-tuple-element.38), channel_id=1, source_target_pairs={{0,1},{1,2},{2,3},{3,0},{4,5},{5,6},{6,7},{7,4},{8,9},{9,10},{10,1... | collective-permute-start | bytes 2359304 | tf_op jit(solution)/shard_map/ppermute | solution.py:231
  179.7 45.0 %collective-permute-start.23 = (bf16[12,32,1024]{2,1,0:T(8,128)(2,1)S(1)}, bf16[12,32,1024]{2,1,0:T(8,128)(2,1)S(1)}, u32[]{:S(2)}, u32[]{:S(2)}) collective-permute-start(bf16[12,32,1024]{2,1,0:T(8,128)(2,1)S(1)} %collective-permute-done.22), channel_id=1, source_target_pairs={{0,3},{1,0},{2,1},{3,2},{4,7},{5,4},{6,5},{7,6},{8,11},{9,8},{10,9... | collective-permute-start | bytes 2359304 | tf_op jit(solution)/shard_map/ppermute | solution.py:233
  (19 other events, 135.5 us)

commit v5 on v3

--- a/solution.py
+++ b/solution.py
@@ -11,7 +11,8 @@
 LANES = 128
 GROUP = ("group_0", "group_1", "group_2")
 EVERY = ("group_0", "group_1", "group_2", "rep")
-SENT = ((768, 256), (0, 768))
+SENT = ((0, 384), (384, 640))
+RAW = 16
 
 
 step_rate = 0.5
@@ -23,10 +24,13 @@
     return [(i, (i + step) % count) for i in range(count)]
 
 
+def elements(*sizes):
+    return tuple(pl.Element(size) for size in sizes)
+
+
 def merge(who, parts, far_up, far_down, start, cols):
     _, blocks, rows, _ = parts.shape
     half = blocks // 2
-    at = start // cols
 
     def body(who_ref, above, below, from_down, from_up, out_up, out_down):
         first = pl.program_id(0) == 0
@@ -50,8 +54,8 @@
             num_scalar_prefetch=1,
             grid=(2,),
             in_specs=[
-                pl.BlockSpec((1, half, rows, cols), lambda i, w: (w[1], i, 0, at)),
-                pl.BlockSpec((1, half, rows, cols), lambda i, w: (w[3], i, 0, at)),
+                pl.BlockSpec(elements(1, half, rows, cols), lambda i, w: (w[1], i * half, 0, start)),
+                pl.BlockSpec(elements(1, half, rows, cols), lambda i, w: (w[3], i * half, 0, start)),
                 piece,
                 piece,
             ],
@@ -65,7 +69,6 @@
 def finish(who, table, parts, up, down, start, cols):
     _, blocks, rows, _ = parts.shape
     slots = table.shape[0]
-    at = start // cols
 
     def body(who_ref, table_ref, own, one, two, gradient, slotted):
         total = own[0].astype(f32) + one[...].astype(f32) + two[...].astype(f32)
@@ -80,7 +83,7 @@
             num_scalar_prefetch=2,
             grid=(1,),
             in_specs=[
-                pl.BlockSpec((1, blocks, rows, cols), lambda i, w, t: (w[0], 0, 0, at)),
+                pl.BlockSpec(elements(1, blocks, rows, cols), lambda i, w, t: (w[0], 0, 0, start)),
                 block,
                 block,
             ],
@@ -159,33 +162,70 @@
     )(left, right, owned, graft_row, layer_row, *earlier)
 
 
+def pick(position, returned):
+    _, rows, cols = returned.shape
+    half = RAW // 2
+
+    def body(position_ref, returned_ref, low, high, sems):
+        copies = []
+        for block in range(RAW):
+            out = low.at[block] if block < half else high.at[block - half]
+            copies.append(pltpu.make_async_copy(returned_ref.at[position_ref[block]], out, sems.at[block]))
+        for copy in copies:
+            copy.start()
+        for copy in copies:
+            copy.wait()
+
+    hbm = pl.BlockSpec(memory_space=pltpu.HBM)
+    shape = jax.ShapeDtypeStruct((half, rows, cols), bf16)
+    return pl.pallas_call(
+        body,
+        in_specs=[pl.BlockSpec(memory_space=pltpu.SMEM), hbm],
+        out_specs=[hbm, hbm],
+        out_shape=[shape, shape],
+        scratch_shapes=[pltpu.SemaphoreType.DMA((RAW,))],
+        name="pick",
+    )(position, returned)
+
+
 def update(who, position, scale, returned, params, reps):
     blocks, rows, cols = params.shape
-    half = blocks // 2
-    slots = returned.shape[0]
-
-    def body(who_ref, position_ref, scale_ref, returned_ref, params_ref, low, high, whole):
-        for block in range(blocks):
-            change = scale_ref[block] * returned_ref[position_ref[block]].astype(f32)
+    part = (blocks - RAW) // 2
+
+    def body(who_ref, position_ref, scale_ref, returned_ref, params_ref, low, high, whole, picked, sems):
+        copies = [
+            pltpu.make_async_copy(returned_ref.at[position_ref[block]], picked.at[block], sems.at[block])
+            for block in range(blocks)
+        ]
+        for copy in copies:
+            copy.start()
+        for block, copy in enumerate(copies):
+            copy.wait()
+            change = scale_ref[block] * picked[block].astype(f32)
             new = (params_ref[block].astype(f32) - change).astype(bf16)
             whole[0, block] = new
-            if block < half:
-                low[block] = new
-            else:
-                high[block - half] = new
-
-    out = pl.BlockSpec((half, rows, cols), lambda i, w, p, s: (0, 0, 0))
-    shape = jax.ShapeDtypeStruct((half, rows, cols), bf16)
+            if RAW <= block < RAW + part:
+                low[block - RAW] = new
+            elif block >= RAW + part:
+                high[block - RAW - part] = new
+
+    piece = pl.BlockSpec((part, rows, cols), lambda i, w, p, s: (0, 0, 0))
+    shape = jax.ShapeDtypeStruct((part, rows, cols), bf16)
     return pl.pallas_call(
         body,
         grid_spec=pltpu.PrefetchScalarGridSpec(
             num_scalar_prefetch=3,
             grid=(1,),
             in_specs=[
-                pl.BlockSpec((slots, rows, cols), lambda i, w, p, s: (0, 0, 0)),
+                pl.BlockSpec(memory_space=pltpu.HBM),
                 pl.BlockSpec((blocks, rows, cols), lambda i, w, p, s: (0, 0, 0)),
             ],
-            out_specs=[out, out, pl.BlockSpec((1, blocks, rows, cols), lambda i, w, p, s: (w[0], 0, 0, 0))],
+            out_specs=[
+                piece,
+                piece,
+                pl.BlockSpec((1, blocks, rows, cols), lambda i, w, p, s: (w[0], 0, 0, 0)),
+            ],
+            scratch_shapes=[pltpu.VMEM((blocks, rows, cols), bf16), pltpu.SemaphoreType.DMA((blocks,))],
         ),
         out_shape=[shape, shape, jax.ShapeDtypeStruct((reps, blocks, rows, cols), bf16)],
         name="update",
@@ -251,8 +291,10 @@
             earlier.append(left_times(left, owned))
         owned = arrived.reshape(group_size * rows, cols)
 
-    my_layers = lax.dynamic_slice_in_dim(layer_of, me * blocks, blocks)
-    onehot = (my_layers[:, None] == jnp.arange(LAYERS, dtype=jnp.int32)[None, :]).astype(f32)
+    ahead = spread(params[: RAW // 2], params[RAW // 2 : RAW], reps)
+
+    onehots = (layer_of[:, None] == jnp.arange(LAYERS, dtype=jnp.int32)[None, :]).astype(f32)
+    onehot = lax.dynamic_slice_in_dim(onehots, me * blocks, blocks)
     in_order = sorted(range(len(SENT)), key=lambda c: SENT[c][0])
     wide = jnp.concatenate([gradients[c] for c in in_order], axis=2).astype(f32)
     new_accum = accum + wide * wide
@@ -273,8 +315,8 @@
     to_lanes = ((0, 0), (0, LANES - LAYERS))
     graft_row = jnp.pad(graft_layer[None, :], to_lanes)
     layer_row = jnp.pad(my_layer[None, :], to_lanes)
-    owned, earlier, graft_row, layer_row, position, onehot, new_accum = lax.optimization_barrier(
-        (owned, earlier, graft_row, layer_row, position, onehot, new_accum)
+    owned, earlier, graft_row, layer_row, position, onehots, new_accum = lax.optimization_barrier(
+        (owned, earlier, graft_row, layer_row, position, onehots, new_accum)
     )
 
     precond, sums = products(left, right, owned, earlier, graft_row, layer_row)
@@ -282,11 +324,22 @@
     returned = lax.all_to_all(outgoing, GROUP, split_axis=0, concat_axis=0, tiled=True)
     sums = everywhere(sums)
     layer_scale = jnp.sqrt(sums[0, :LAYERS]) * lax.rsqrt(sums[1, :LAYERS] + 1e-06)
-    scale = step_rate * jnp.sum(onehot * layer_scale[None, :], axis=1)
-
-    low, high, new_params = update(who, position, scale, returned, params, reps)
-    for offset, part, piece in spread(low, high, reps):
-        new_params = lax.dynamic_update_slice(new_params, piece[None], (who[offset], part * half, 0, 0))
+    scales = (step_rate * jnp.sum(onehots * layer_scale[None, :], axis=1)).reshape(reps, blocks)
+
+    def owner(offset):
+        return lax.rem(me + offset, reps)
+
+    changes = spread(*pick(position, returned), reps)
+    low, high, new_params = update(who, position, scales[me], returned, params, reps)
+    finished = spread(low, high, reps)
+    for (offset, part, old), (_, _, change) in zip(ahead, changes):
+        size = RAW // 2
+        scale = lax.dynamic_slice(scales, (owner(offset), part * size), (1, size))[0, :, None, None]
+        new = (old.astype(f32) - scale * change.astype(f32)).astype(bf16)
+        new_params = lax.dynamic_update_slice(new_params, new[None], (owner(offset), part * size, 0, 0))
+    for offset, part, piece in finished:
+        first = RAW + part * piece.shape[0]
+        new_params = lax.dynamic_update_slice(new_params, piece[None], (owner(offset), first, 0, 0))
     return (new_params.reshape(reps * blocks, rows, width), new_accum)
 
 

time: 235 us -> 256 us (1.089)
  waiting for transfers between devices: 122 us -> 86 us
  Pallas kernels: 30.4 us -> 64.9 us
  starting transfers between devices: 49.8 us -> 68.8 us
  other arithmetic: 7.48 us -> 15.5 us
  between operations: 6.3 us -> 0.83 us
    ppermute x2, waiting for transfers between devices: 37.1 us -> 0.78 us  [local(): far_down = lax.ppermute(high, 'rep', down)]
    pallas_call x0 -> x1, Pallas kernels: none -> 33.7 us  [pick(): pl.pallas_call(body, in_specs=[pl.BlockSpec(memory_space=pltpu.SMEM), hbm...]
    dynamic_update_slice x0 -> x6, other arithmetic: none -> 7.66 us  [local(): lax.dynamic_update_slice(new_params, new[None], (owner(offset), part * si...]
    all_to_all x3, waiting for transfers between devices: 16.3 us -> 9.21 us  [local(): lax.all_to_all(outgoing, GROUP, split_axis=0, concat_axis=0, tiled=True)]
    ppermute x1 -> x3, waiting for transfers between devices: 0.01 us -> 5.98 us  [spread(): low_down = lax.ppermute(low, 'rep', down)]
    ppermute x1 -> x3, waiting for transfers between devices: 0.01 us -> 5.61 us  [spread(): far_high = lax.ppermute(high_down, 'rep', down)]
    ppermute x1 -> x3, starting transfers between devices: 2.25 us -> 6.76 us  [spread(): high_down = lax.ppermute(high, 'rep', down)]
    ppermute x2, waiting for transfers between devices: 6.44 us -> 10.4 us  [local(): near_up = lax.ppermute(to_up, 'rep', up)]
  transfers between devices with their start and end apart: 24 -> 36, of which waited for: 17 -> 24; matrix products, arithmetic and copies ran while one was open for 7% -> 10% of each run, Pallas kernels for 6% -> 22%
where the time goes in v5:
time: 256 us; the launch traced here: 255 us
  waiting for transfers between devices  86 us (34%)
  starting transfers between devices  68.8 us (27%)
  Pallas kernels  64.9 us (25%)
  local copies, waits for them, and re-layouts  18.6 us (7%)
  other arithmetic  15.5 us (6%)
    pallas_call x1, Pallas kernels, pick(): pl.pallas_call(body, in_specs=[pl.BlockSpec(memory_space=pltpu.SMEM), hbm...  33.7 us
    ppermute x7, waiting for transfers between devices, everywhere(): value = value + lax.ppermute(value, axis, pairs)  26.1 us
    all_to_all x3, starting transfers between devices, local(): lax.all_to_all(outgoing, GROUP, split_axis=0, concat_axis=0, tiled=True)  20.2 us
    ppermute x2, waiting for transfers between devices, local(): near_up = lax.ppermute(to_up, 'rep', up)  10.4 us
    ppermute x7, starting transfers between devices, everywhere(): value = value + lax.ppermute(value, axis, pairs)  9.62 us
    all_to_all x3, waiting for transfers between devices, local(): lax.all_to_all(outgoing, GROUP, split_axis=0, concat_axis=0, tiled=True)  9.21 us
    pallas_call x2, Pallas kernels, finish(): pl.pallas_call(body, grid_spec=pltpu.PrefetchScalarGridSpec(num_scalar_pr...  8.17 us
    ppermute x3, waiting for transfers between devices, spread(): high_up = lax.ppermute(high, 'rep', up)  7.82 us
  transfers between devices with their start and end apart: 36, of which 24 were waited for; matrix products, arithmetic and copies ran while one was open for 10% of the time, Pallas kernels for 22%

profile of v5, /device:TPU:0, one launch (start us, length us, event | category | flops | bytes accessed | tf_op | source)
XLA Modules:
  0.0 254.6 jit_solution(17792311633115732167)
XLA Ops:
  14.4 3.1 %merge.3 = (bf16[24,32,384]{2,1,0:T(8,128)(2,1)}, bf16[24,32,384]{2,1,0:T(8,128)(2,1)}) custom-call(s32[4]{0:T(128)} %compare_select_fusion.who_ref, bf16[4,24,32,1024]{3,2,1,0:T(8,128)(2,1)} %bitcast.75, bf16[4,24,32,1024]{3,2,1,0:T(8,128)(2,1)} %bitcast.76, bf16[12,32,384]{2,1,0:T(8,128)(2,1)} %copy-done.10, bf16[12,32,384]{2,1,0:T(8,128)(2,1)} %copy-done.11), custom_call_target="tpu_custom_call" | custom-call | tf_op jit(solution)/shard_map/merge/pallas_call | solution.py:51
  25.0 3.6 %merge.2 = (bf16[24,32,640]{2,1,0:T(8,128)(2,1)}, bf16[24,32,640]{2,1,0:T(8,128)(2,1)}) custom-call(s32[4]{0:T(128)} %compare_select_fusion.who_ref, bf16[4,24,32,1024]{3,2,1,0:T(8,128)(2,1)} %bitcast.77, bf16[4,24,32,1024]{3,2,1,0:T(8,128)(2,1)} %bitcast.78, bf16[12,32,640]{2,1,0:T(8,128)(2,1)} %copy-done.8, bf16[12,32,640]{2,1,0:T(8,128)(2,1)} %copy-done.9), custom_call_target="tpu_custom_call" | custom-call | tf_op jit(solution)/shard_map/merge/pallas_call | solution.py:51
  32.3 3.8 %collective-permute-done.6.one = bf16[24,32,384]{2,1,0:T(8,128)(2,1)S(1)} collective-permute-done((bf16[24,32,384]{2,1,0:T(8,128)(2,1)}, bf16[24,32,384]{2,1,0:T(8,128)(2,1)S(1)}, u32[]{:S(2)}, u32[]{:S(2)}) %collective-permute-start.6) | collective-permute-done | bytes 589856 | tf_op jit(solution)/shard_map/ppermute | solution.py:285
  37.3 3.5 %finish.3 = (bf16[24,32,384]{2,1,0:T(8,128)(2,1)}, bf16[32,32,384]{2,1,0:T(8,128)(2,1)}) custom-call(s32[4]{0:T(128)} %compare_select_fusion.who_ref, s32[32]{0:T(128)} %get-tuple-element.48.table_ref, bf16[4,24,32,1024]{3,2,1,0:T(8,128)(2,1)} %bitcast.79, bf16[24,32,384]{2,1,0:T(8,128)(2,1)} %copy-done.6, bf16[24,32,384]{2,1,0:T(8,128)(2,1)} %copy-done.7), custom_call_target="tpu_custom_call" | custom-call | tf_op jit(solution)/shard_map/finish/pallas_call | solution.py:80
  40.9 8.5 %all-to-all-start.1 = ((bf16[32,32,384]{2,1,0:T(8,128)(2,1)}), bf16[32,32,384]{2,1,0:T(8,128)(2,1)S(1)}, u32[]{:S(2)}, u32[]{:S(2)}) async-start(bf16[32,32,384]{2,1,0:T(8,128)(2,1)} %get-tuple-element.29), calls=%async_computation.1 | async-start | bytes 1572864 | tf_op jit(solution)/shard_map/all_to_all | solution.py:289
  49.3 6.6 %collective-permute-done.2.one = bf16[24,32,640]{2,1,0:T(8,128)(2,1)S(1)} collective-permute-done((bf16[24,32,640]{2,1,0:T(8,128)(2,1)}, bf16[24,32,640]{2,1,0:T(8,128)(2,1)S(1)}, u32[]{:S(2)}, u32[]{:S(2)}) %collective-permute-start.2) | collective-permute-done | bytes 983072 | tf_op jit(solution)/shard_map/ppermute | solution.py:285
  57.9 4.6 %finish.2 = (bf16[24,32,640]{2,1,0:T(8,128)(2,1)}, bf16[32,32,640]{2,1,0:T(8,128)(2,1)}) custom-call(s32[4]{0:T(128)} %compare_select_fusion.who_ref, s32[32]{0:T(128)} %get-tuple-element.48.table_ref, bf16[4,24,32,1024]{3,2,1,0:T(8,128)(2,1)} %bitcast.80, bf16[24,32,640]{2,1,0:T(8,128)(2,1)} %copy-done.3, bf16[24,32,640]{2,1,0:T(8,128)(2,1)} %copy-done.4), custom_call_target="tpu_custom_call" | custom-call | tf_op jit(solution)/shard_map/finish/pallas_call | solution.py:80
  63.3 7.7 %all-to-all-start = ((bf16[32,32,640]{2,1,0:T(8,128)(2,1)}), bf16[32,32,640]{2,1,0:T(8,128)(2,1)S(1)}, u32[]{:S(2)}, u32[]{:S(2)}) async-start(bf16[32,32,640]{2,1,0:T(8,128)(2,1)} %get-tuple-element.26), calls=%async_computation | async-start | bytes 2621440 | tf_op jit(solution)/shard_map/all_to_all | solution.py:289
  72.9 4.5 %fusion = (f32[24,32,1024]{2,1,0:T(8,128)}, f32[24]{0:T(128)S(1)}) fusion(f32[24,32,1024]{2,1,0:T(8,128)} %param.9, bf16[24,32,640]{2,1,0:T(8,128)(2,1)} %get-tuple-element.31, bf16[24,32,384]{2,1,0:T(8,128)(2,1)S(1)} %copy-done.5), kind=kLoop, calls=%fused_computation.2 | loop fusion | flops 7077864 | bytes 7864416 | tf_op jit(solution)/shard_map/add | solution.py:300
  78.7 3.6 %left_times.1.rest_0_ = bf16[1024,384]{1,0:T(8,128)(2,1)} custom-call(bf16[1024,1024]{1,0:T(8,128)(2,1)} %bitcast.81, bf16[1024,384]{1,0:T(8,128)(2,1)} %bitcast.84), custom_call_target="tpu_custom_call" | custom-call | tf_op jit(solution)/shard_map/left_times/pallas_call | solution.py:107
  82.4 8.4 %all-to-all-done = bf16[32,32,640]{2,1,0:T(8,128)(2,1)S(1)} async-done(((bf16[32,32,640]{2,1,0:T(8,128)(2,1)}), bf16[32,32,640]{2,1,0:T(8,128)(2,1)S(1)}, u32[]{:S(2)}, u32[]{:S(2)}) %all-to-all-start) | async-done | bytes 1310752 | tf_op jit(solution)/shard_map/all_to_all | solution.py:289
  91.9 7.7 %products.1 = (bf16[1024,1024]{1,0:T(8,128)(2,1)}, f32[2,128]{1,0:T(2,128)}) custom-call(bf16[1024,1024]{1,0:T(8,128)(2,1)} %bitcast.82, bf16[1024,1024]{1,0:T(8,128)(2,1)} %bitcast.85, bf16[1024,640]{1,0:T(8,128)(2,1)} %bitcast.83, f32[1,128]{1,0:T(1,128)} %pad.7.graft_ref, f32[1,128]{1,0:T(1,128)} %pad.8.layer_ref, bf16[1024,384]{1,0:T(8,128)(2,1)} %left_times.1.rest_0_), custom_call_target="tpu_custom_call" | custom-call | tf_op jit(solution)/shard_map/products/pallas_call | solution.py:147
  99.7 4.0 %all-to-all-start.2 = ((bf16[32,32,1024]{2,1,0:T(8,128)(2,1)}), bf16[32,32,1024]{2,1,0:T(8,128)(2,1)S(1)}, u32[]{:S(2)}, u32[]{:S(2)}) async-start(bf16[32,32,1024]{2,1,0:T(8,128)(2,1)} %bitcast.86), calls=%async_computation.2 | async-start | bytes 4194304 | tf_op jit(solution)/shard_map/all_to_all | solution.py:324
  106.4 3.0 %collective-permute-done.9 = f32[2,128]{1,0:T(2,128)S(1)} collective-permute-done((f32[2,128]{1,0:T(2,128)S(1)}, f32[2,128]{1,0:T(2,128)S(1)}, u32[]{:S(2)}, u32[]{:S(2)}) %collective-permute-start.9) | collective-permute-done | bytes 1056 | tf_op jit(solution)/shard_map/ppermute | solution.py:241
  115.9 13.5 %collective-permute-done.11 = f32[2,128]{1,0:T(2,128)S(1)} collective-permute-done((f32[2,128]{1,0:T(2,128)S(1)}, f32[2,128]{1,0:T(2,128)S(1)}, u32[]{:S(2)}, u32[]{:S(2)}) %collective-permute-start.11) | collective-permute-done | bytes 1056 | tf_op jit(solution)/shard_map/ppermute | solution.py:241
  146.3 33.7 %pick.1 = (bf16[8,32,1024]{2,1,0:T(8,128)(2,1)}, bf16[8,32,1024]{2,1,0:T(8,128)(2,1)}) custom-call(s32[24]{0:T(128)} %select_reduce_fusion.position_ref, bf16[32,32,1024]{2,1,0:T(8,128)(2,1)} %copy-done), custom_call_target="tpu_custom_call" | custom-call | tf_op jit(solution)/shard_map/pick/pallas_call | solution.py:181
  184.1 5.1 %update.1 = (bf16[4,32,1024]{2,1,0:T(8,128)(2,1)}, bf16[4,32,1024]{2,1,0:T(8,128)(2,1)}, bf16[4,24,32,1024]{3,2,1,0:T(8,128)(2,1)}) custom-call(s32[4]{0:T(128)} %compare_select_fusion.who_ref, s32[24]{0:T(128)} %select_reduce_fusion.position_ref, f32[24]{0:T(128)} %fusion.21.scale_ref, bf16[32,32,1024]{2,1,0:T(8,128)(2,1)} %copy-done, ...), custom_call_target="tpu_custom_call" | custom-call | tf_op jit(solution)/shard_map/update/pallas_call | solution.py:214
  200.5 7.8 %collective-permute-done.20 = bf16[8,32,1024]{2,1,0:T(8,128)(2,1)S(1)} collective-permute-done((bf16[8,32,1024]{2,1,0:T(8,128)(2,1)}, bf16[8,32,1024]{2,1,0:T(8,128)(2,1)S(1)}, u32[]{:S(2)}, u32[]{:S(2)}) %collective-permute-start.20) | collective-permute-done | bytes 524320 | tf_op jit(solution)/shard_map/ppermute | solution.py:249
  213.7 5.5 %collective-permute-done.22 = bf16[8,32,1024]{2,1,0:T(8,128)(2,1)S(1)} collective-permute-done((bf16[8,32,1024]{2,1,0:T(8,128)(2,1)}, bf16[8,32,1024]{2,1,0:T(8,128)(2,1)S(1)}, u32[]{:S(2)}, u32[]{:S(2)}) %collective-permute-start.22) | collective-permute-done | bytes 524320 | tf_op jit(solution)/shard_map/ppermute | solution.py:250
  222.8 7.8 %collective-permute-done.24 = bf16[8,32,1024]{2,1,0:T(8,128)(2,1)S(1)} collective-permute-done((bf16[8,32,1024]{2,1,0:T(8,128)(2,1)S(1)}, bf16[8,32,1024]{2,1,0:T(8,128)(2,1)S(1)}, u32[]{:S(2)}, u32[]{:S(2)}) %collective-permute-start.24) | collective-permute-done | bytes 524320 | tf_op jit(solution)/shard_map/ppermute | solution.py:251
  232.0 2.9 %collective-permute-start.30 = (bf16[4,32,1024]{2,1,0:T(8,128)(2,1)S(1)}, bf16[4,32,1024]{2,1,0:T(8,128)(2,1)S(1)}, u32[]{:S(2)}, u32[]{:S(2)}) collective-permute-start(bf16[4,32,1024]{2,1,0:T(8,128)(2,1)S(1)} %copy-done.14), channel_id=1, source_target_pairs={{0,3},{1,0},{2,1},{3,2},{4,7},{5,4},{6,5},{7,6},{8,11},{9,8},{10,9... | collective-permute-start | bytes 786440 | tf_op jit(solution)/shard_map/ppermute | solution.py:250
  234.9 4.9 %collective-permute-done.27 = bf16[4,32,1024]{2,1,0:T(8,128)(2,1)S(1)} collective-permute-done((bf16[4,32,1024]{2,1,0:T(8,128)(2,1)S(1)}, bf16[4,32,1024]{2,1,0:T(8,128)(2,1)S(1)}, u32[]{:S(2)}, u32[]{:S(2)}) %collective-permute-start.27) | collective-permute-done | bytes 262176 | tf_op jit(solution)/shard_map/ppermute | solution.py:247
  239.8 3.2 %collective-permute-start.32 = (bf16[4,32,1024]{2,1,0:T(8,128)(2,1)S(1)}, bf16[4,32,1024]{2,1,0:T(8,128)(2,1)S(1)}, u32[]{:S(2)}, u32[]{:S(2)}) collective-permute-start(bf16[4,32,1024]{2,1,0:T(8,128)(2,1)S(1)} %collective-permute-done.28), channel_id=1, source_target_pairs={{0,3},{1,0},{2,1},{3,2},{4,7},{5,4},{6,5},{7,6},{8,11},{9,8},{10,9... | collective-permute-start | bytes 786440 | tf_op jit(solution)/shard_map/ppermute | solution.py:252
  243.0 4.2 %collective-permute-done.26 = bf16[8,32,1024]{2,1,0:T(8,128)(2,1)S(1)} collective-permute-done((bf16[8,32,1024]{2,1,0:T(8,128)(2,1)S(1)}, bf16[8,32,1024]{2,1,0:T(8,128)(2,1)S(1)}, u32[]{:S(2)}, u32[]{:S(2)}) %collective-permute-start.26) | collective-permute-done | bytes 524320 | tf_op jit(solution)/shard_map/ppermute | solution.py:252
  (126 shorter events, 92.3 us)
Async XLA Ops:
  6.3 17.1 %collective-permute-start = (bf16[12,32,640]{2,1,0:T(8,128)(2,1)S(1)}, bf16[12,32,640]{2,1,0:T(8,128)(2,1)S(1)}, u32[]{:S(2)}, u32[]{:S(2)}) collective-permute-start(bf16[12,32,640]{2,1,0:T(8,128)(2,1)S(1)} %get-tuple-element.53), channel_id=1, source_target_pairs={{0,1},{1,2},{2,3},{3,0},{4,5},{5,6},{6,7},{7,4},{8,9},{9,10},{10,1... | collective-permute-start | bytes 1474568 | tf_op jit(solution)/shard_map/ppermute | solution.py:282
  6.8 17.0 %collective-permute-start.1 = (bf16[12,32,640]{2,1,0:T(8,128)(2,1)S(1)}, bf16[12,32,640]{2,1,0:T(8,128)(2,1)S(1)}, u32[]{:S(2)}, u32[]{:S(2)}) collective-permute-start(bf16[12,32,640]{2,1,0:T(8,128)(2,1)S(1)} %get-tuple-element.52), channel_id=1, source_target_pairs={{0,3},{1,0},{2,1},{3,2},{4,7},{5,4},{6,5},{7,6},{8,11},{9,8},{10,9... | collective-permute-start | bytes 1474568 | tf_op jit(solution)/shard_map/ppermute | solution.py:283
  17.4 18.7 %collective-permute-start.6 = (bf16[24,32,384]{2,1,0:T(8,128)(2,1)}, bf16[24,32,384]{2,1,0:T(8,128)(2,1)S(1)}, u32[]{:S(2)}, u32[]{:S(2)}) collective-permute-start(bf16[24,32,384]{2,1,0:T(8,128)(2,1)} %get-tuple-element.27), channel_id=1, source_target_pairs={{0,1},{1,2},{2,3},{3,0},{4,5},{5,6},{6,7},{7,4},{8,9},{9,10},{10,1... | collective-permute-start | bytes 1769480 | tf_op jit(solution)/shard_map/ppermute | solution.py:285
  18.6 17.9 %collective-permute-start.7 = (bf16[24,32,384]{2,1,0:T(8,128)(2,1)}, bf16[24,32,384]{2,1,0:T(8,128)(2,1)S(1)}, u32[]{:S(2)}, u32[]{:S(2)}) collective-permute-start(bf16[24,32,384]{2,1,0:T(8,128)(2,1)} %get-tuple-element.28), channel_id=1, source_target_pairs={{0,3},{1,0},{2,1},{3,2},{4,7},{5,4},{6,5},{7,6},{8,11},{9,8},{10,9... | collective-permute-start | bytes 1769480 | tf_op jit(solution)/shard_map/ppermute | solution.py:286
  28.6 27.3 %collective-permute-start.2 = (bf16[24,32,640]{2,1,0:T(8,128)(2,1)}, bf16[24,32,640]{2,1,0:T(8,128)(2,1)S(1)}, u32[]{:S(2)}, u32[]{:S(2)}) collective-permute-start(bf16[24,32,640]{2,1,0:T(8,128)(2,1)} %get-tuple-element.24), channel_id=1, source_target_pairs={{0,1},{1,2},{2,3},{3,0},{4,5},{5,6},{6,7},{7,4},{8,9},{9,10},{10,1... | collective-permute-start | bytes 2949128 | tf_op jit(solution)/shard_map/ppermute | solution.py:285
  29.7 26.4 %collective-permute-start.3 = (bf16[24,32,640]{2,1,0:T(8,128)(2,1)}, bf16[24,32,640]{2,1,0:T(8,128)(2,1)S(1)}, u32[]{:S(2)}, u32[]{:S(2)}) collective-permute-start(bf16[24,32,640]{2,1,0:T(8,128)(2,1)} %get-tuple-element.25), channel_id=1, source_target_pairs={{0,3},{1,0},{2,1},{3,2},{4,7},{5,4},{6,5},{7,6},{8,11},{9,8},{10,9... | collective-permute-start | bytes 2949128 | tf_op jit(solution)/shard_map/ppermute | solution.py:286
  40.9 22.4 %all-to-all-start.1 = ((bf16[32,32,384]{2,1,0:T(8,128)(2,1)}), bf16[32,32,384]{2,1,0:T(8,128)(2,1)S(1)}, u32[]{:S(2)}, u32[]{:S(2)}) async-start(bf16[32,32,384]{2,1,0:T(8,128)(2,1)} %get-tuple-element.29), calls=%async_computation.1 | async-start | bytes 1572864 | tf_op jit(solution)/shard_map/all_to_all | solution.py:289
  63.3 27.5 %all-to-all-start = ((bf16[32,32,640]{2,1,0:T(8,128)(2,1)}), bf16[32,32,640]{2,1,0:T(8,128)(2,1)S(1)}, u32[]{:S(2)}, u32[]{:S(2)}) async-start(bf16[32,32,640]{2,1,0:T(8,128)(2,1)} %get-tuple-element.26), calls=%async_computation | async-start | bytes 2621440 | tf_op jit(solution)/shard_map/all_to_all | solution.py:289
  99.7 45.3 %all-to-all-start.2 = ((bf16[32,32,1024]{2,1,0:T(8,128)(2,1)}), bf16[32,32,1024]{2,1,0:T(8,128)(2,1)S(1)}, u32[]{:S(2)}, u32[]{:S(2)}) async-start(bf16[32,32,1024]{2,1,0:T(8,128)(2,1)} %bitcast.86), calls=%async_computation.2 | async-start | bytes 4194304 | tf_op jit(solution)/shard_map/all_to_all | solution.py:324
  114.2 15.2 %collective-permute-start.11 = (f32[2,128]{1,0:T(2,128)S(1)}, f32[2,128]{1,0:T(2,128)S(1)}, u32[]{:S(2)}, u32[]{:S(2)}) collective-permute-start(f32[2,128]{1,0:T(2,128)S(1)} %add.124), channel_id=1, source_target_pairs={{0,32},{32,0},{64,96},{96,64},{1,33},{33,1},{65,97},{97,65},{2,34}... | collective-permute-start | bytes 3080 | tf_op jit(solution)/shard_map/ppermute | solution.py:241
  137.5 57.4 %collective-permute-start.17 = (bf16[8,32,1024]{2,1,0:T(8,128)(2,1)}, bf16[8,32,1024]{2,1,0:T(8,128)(2,1)S(1)}, u32[]{:S(2)}, u32[]{:S(2)}) collective-permute-start(bf16[8,32,1024]{2,1,0:T(8,128)(2,1)} %get-tuple-element.56), channel_id=1, source_target_pairs={{0,3},{1,0},{2,1},{3,2},{4,7},{5,4},{6,5},{7,6},{8,11},{9,8},{10,9... | collective-permute-start | bytes 1572872 | tf_op jit(solution)/shard_map/ppermute | solution.py:248
  139.6 59.7 %collective-permute-start.19 = (bf16[8,32,1024]{2,1,0:T(8,128)(2,1)}, bf16[8,32,1024]{2,1,0:T(8,128)(2,1)}, u32[]{:S(2)}, u32[]{:S(2)}) collective-permute-start(bf16[8,32,1024]{2,1,0:T(8,128)(2,1)} %get-tuple-element.56), channel_id=1, source_target_pairs={{0,1},{1,2},{2,3},{3,0},{4,5},{5,6},{6,7},{7,4},{8,9},{9,10},{10,1... | collective-permute-start | bytes 1572872 | tf_op jit(solution)/shard_map/ppermute | solution.py:249
  139.6 49.6 %collective-permute-start.15 = (bf16[8,32,1024]{2,1,0:T(8,128)(2,1)}, bf16[8,32,1024]{2,1,0:T(8,128)(2,1)S(1)}, u32[]{:S(2)}, u32[]{:S(2)}) collective-permute-start(bf16[8,32,1024]{2,1,0:T(8,128)(2,1)} %get-tuple-element.57), channel_id=1, source_target_pairs={{0,1},{1,2},{2,3},{3,0},{4,5},{5,6},{6,7},{7,4},{8,9},{9,10},{10,1... | collective-permute-start | bytes 1572872 | tf_op jit(solution)/shard_map/ppermute | solution.py:247
  181.3 16.0 %collective-permute-start.18 = (bf16[8,32,1024]{2,1,0:T(8,128)(2,1)}, bf16[8,32,1024]{2,1,0:T(8,128)(2,1)S(1)}, u32[]{:S(2)}, u32[]{:S(2)}) collective-permute-start(bf16[8,32,1024]{2,1,0:T(8,128)(2,1)} %get-tuple-element.42), channel_id=1, source_target_pairs={{0,3},{1,0},{2,1},{3,2},{4,7},{5,4},{6,5},{7,6},{8,11},{9,8},{10,9... | collective-permute-start | bytes 1572872 | tf_op jit(solution)/shard_map/ppermute | solution.py:248
  189.2 21.8 %collective-permute-start.21 = (bf16[8,32,1024]{2,1,0:T(8,128)(2,1)}, bf16[8,32,1024]{2,1,0:T(8,128)(2,1)S(1)}, u32[]{:S(2)}, u32[]{:S(2)}) collective-permute-start(bf16[8,32,1024]{2,1,0:T(8,128)(2,1)} %get-tuple-element.57), channel_id=1, source_target_pairs={{0,3},{1,0},{2,1},{3,2},{4,7},{5,4},{6,5},{7,6},{8,11},{9,8},{10,9... | collective-permute-start | bytes 1572872 | tf_op jit(solution)/shard_map/ppermute | solution.py:250
  192.1 16.2 %collective-permute-start.20 = (bf16[8,32,1024]{2,1,0:T(8,128)(2,1)}, bf16[8,32,1024]{2,1,0:T(8,128)(2,1)S(1)}, u32[]{:S(2)}, u32[]{:S(2)}) collective-permute-start(bf16[8,32,1024]{2,1,0:T(8,128)(2,1)} %get-tuple-element.42), channel_id=1, source_target_pairs={{0,1},{1,2},{2,3},{3,0},{4,5},{5,6},{6,7},{7,4},{8,9},{9,10},{10,1... | collective-permute-start | bytes 1572872 | tf_op jit(solution)/shard_map/ppermute | solution.py:249
  194.9 26.8 %collective-permute-start.23 = (bf16[8,32,1024]{2,1,0:T(8,128)(2,1)S(1)}, bf16[8,32,1024]{2,1,0:T(8,128)(2,1)S(1)}, u32[]{:S(2)}, u32[]{:S(2)}) collective-permute-start(bf16[8,32,1024]{2,1,0:T(8,128)(2,1)S(1)} %collective-permute-done.15), channel_id=1, source_target_pairs={{0,1},{1,2},{2,3},{3,0},{4,5},{5,6},{6,7},{7,4},{8,9},{9,10},{10,1... | collective-permute-start | bytes 1572872 | tf_op jit(solution)/shard_map/ppermute | solution.py:251
  197.3 21.9 %collective-permute-start.22 = (bf16[8,32,1024]{2,1,0:T(8,128)(2,1)}, bf16[8,32,1024]{2,1,0:T(8,128)(2,1)S(1)}, u32[]{:S(2)}, u32[]{:S(2)}) collective-permute-start(bf16[8,32,1024]{2,1,0:T(8,128)(2,1)} %get-tuple-element.41), channel_id=1, source_target_pairs={{0,3},{1,0},{2,1},{3,2},{4,7},{5,4},{6,5},{7,6},{8,11},{9,8},{10,9... | collective-permute-start | bytes 1572872 | tf_op jit(solution)/shard_map/ppermute | solution.py:250
  199.3 32.7 %collective-permute-start.25 = (bf16[8,32,1024]{2,1,0:T(8,128)(2,1)S(1)}, bf16[8,32,1024]{2,1,0:T(8,128)(2,1)S(1)}, u32[]{:S(2)}, u32[]{:S(2)}) collective-permute-start(bf16[8,32,1024]{2,1,0:T(8,128)(2,1)S(1)} %collective-permute-done.17), channel_id=1, source_target_pairs={{0,3},{1,0},{2,1},{3,2},{4,7},{5,4},{6,5},{7,6},{8,11},{9,8},{10,9... | collective-permute-start | bytes 1572872 | tf_op jit(solution)/shard_map/ppermute | solution.py:252
  208.3 22.2 %collective-permute-start.24 = (bf16[8,32,1024]{2,1,0:T(8,128)(2,1)S(1)}, bf16[8,32,1024]{2,1,0:T(8,128)(2,1)S(1)}, u32[]{:S(2)}, u32[]{:S(2)}) collective-permute-start(bf16[8,32,1024]{2,1,0:T(8,128)(2,1)S(1)} %collective-permute-done.16), channel_id=1, source_target_pairs={{0,1},{1,2},{2,3},{3,0},{4,5},{5,6},{6,7},{7,4},{8,9},{9,10},{10,1... | collective-permute-start | bytes 1572872 | tf_op jit(solution)/shard_map/ppermute | solution.py:251
  211.0 28.8 %collective-permute-start.28 = (bf16[4,32,1024]{2,1,0:T(8,128)(2,1)}, bf16[4,32,1024]{2,1,0:T(8,128)(2,1)S(1)}, u32[]{:S(2)}, u32[]{:S(2)}) collective-permute-start(bf16[4,32,1024]{2,1,0:T(8,128)(2,1)} %get-tuple-element.44), channel_id=1, source_target_pairs={{0,3},{1,0},{2,1},{3,2},{4,7},{5,4},{6,5},{7,6},{8,11},{9,8},{10,9... | collective-permute-start | bytes 786440 | tf_op jit(solution)/shard_map/ppermute | solution.py:248
  219.2 28.1 %collective-permute-start.26 = (bf16[8,32,1024]{2,1,0:T(8,128)(2,1)S(1)}, bf16[8,32,1024]{2,1,0:T(8,128)(2,1)S(1)}, u32[]{:S(2)}, u32[]{:S(2)}) collective-permute-start(bf16[8,32,1024]{2,1,0:T(8,128)(2,1)S(1)} %collective-permute-done.18), channel_id=1, source_target_pairs={{0,3},{1,0},{2,1},{3,2},{4,7},{5,4},{6,5},{7,6},{8,11},{9,8},{10,9... | collective-permute-start | bytes 1572872 | tf_op jit(solution)/shard_map/ppermute | solution.py:252
  221.8 28.1 %collective-permute-start.29 = (bf16[4,32,1024]{2,1,0:T(8,128)(2,1)S(1)}, bf16[4,32,1024]{2,1,0:T(8,128)(2,1)S(1)}, u32[]{:S(2)}, u32[]{:S(2)}) collective-permute-start(bf16[4,32,1024]{2,1,0:T(8,128)(2,1)S(1)} %copy-done.15), channel_id=1, source_target_pairs={{0,1},{1,2},{2,3},{3,0},{4,5},{5,6},{6,7},{7,4},{8,9},{9,10},{10,1... | collective-permute-start | bytes 786440 | tf_op jit(solution)/shard_map/ppermute | solution.py:249
  232.0 19.1 %collective-permute-start.30 = (bf16[4,32,1024]{2,1,0:T(8,128)(2,1)S(1)}, bf16[4,32,1024]{2,1,0:T(8,128)(2,1)S(1)}, u32[]{:S(2)}, u32[]{:S(2)}) collective-permute-start(bf16[4,32,1024]{2,1,0:T(8,128)(2,1)S(1)} %copy-done.14), channel_id=1, source_target_pairs={{0,3},{1,0},{2,1},{3,2},{4,7},{5,4},{6,5},{7,6},{8,11},{9,8},{10,9... | collective-permute-start | bytes 786440 | tf_op jit(solution)/shard_map/ppermute | solution.py:250
  (28 other events, 269.7 us)

commit v6 on v5

--- a/solution.py
+++ b/solution.py
@@ -12,7 +12,7 @@
 GROUP = ("group_0", "group_1", "group_2")
 EVERY = ("group_0", "group_1", "group_2", "rep")
 SENT = ((0, 384), (384, 640))
-RAW = 16
+RAW = (4, 12)
 
 
 step_rate = 0.5
@@ -162,55 +162,54 @@
     )(left, right, owned, graft_row, layer_row, *earlier)
 
 
+def fetch(position_ref, returned_ref, target, sems, blocks):
+    copies = []
+    for block in blocks:
+        copy = pltpu.make_async_copy(returned_ref.at[position_ref[block]], target(block), sems.at[block])
+        copy.start()
+        copies.append(copy)
+    return copies
+
+
 def pick(position, returned):
     _, rows, cols = returned.shape
-    half = RAW // 2
+    split, total = RAW[0], sum(RAW)
 
     def body(position_ref, returned_ref, low, high, sems):
-        copies = []
-        for block in range(RAW):
-            out = low.at[block] if block < half else high.at[block - half]
-            copies.append(pltpu.make_async_copy(returned_ref.at[position_ref[block]], out, sems.at[block]))
-        for copy in copies:
-            copy.start()
-        for copy in copies:
+        def target(block):
+            return low.at[block] if block < split else high.at[block - split]
+
+        for copy in fetch(position_ref, returned_ref, target, sems, range(total)):
             copy.wait()
 
-    hbm = pl.BlockSpec(memory_space=pltpu.HBM)
-    shape = jax.ShapeDtypeStruct((half, rows, cols), bf16)
-    return pl.pallas_call(
-        body,
-        in_specs=[pl.BlockSpec(memory_space=pltpu.SMEM), hbm],
-        out_specs=[hbm, hbm],
-        out_shape=[shape, shape],
-        scratch_shapes=[pltpu.SemaphoreType.DMA((RAW,))],
+    return pl.pallas_call(
+        body,
+        grid_spec=pltpu.PrefetchScalarGridSpec(
+            num_scalar_prefetch=1,
+            grid=(1,),
+            in_specs=[pl.BlockSpec(memory_space=pltpu.HBM)],
+            out_specs=[pl.BlockSpec((size, rows, cols), lambda i, p: (0, 0, 0)) for size in RAW],
+            scratch_shapes=[pltpu.SemaphoreType.DMA((total,))],
+        ),
+        out_shape=[jax.ShapeDtypeStruct((size, rows, cols), bf16) for size in RAW],
         name="pick",
     )(position, returned)
 
 
 def update(who, position, scale, returned, params, reps):
     blocks, rows, cols = params.shape
-    part = (blocks - RAW) // 2
-
-    def body(who_ref, position_ref, scale_ref, returned_ref, params_ref, low, high, whole, picked, sems):
-        copies = [
-            pltpu.make_async_copy(returned_ref.at[position_ref[block]], picked.at[block], sems.at[block])
-            for block in range(blocks)
-        ]
-        for copy in copies:
-            copy.start()
+    first = sum(RAW)
+
+    def body(who_ref, position_ref, scale_ref, returned_ref, params_ref, last, whole, picked, sems):
+        copies = fetch(position_ref, returned_ref, lambda block: picked.at[block], sems, range(blocks))
         for block, copy in enumerate(copies):
             copy.wait()
             change = scale_ref[block] * picked[block].astype(f32)
             new = (params_ref[block].astype(f32) - change).astype(bf16)
             whole[0, block] = new
-            if RAW <= block < RAW + part:
-                low[block - RAW] = new
-            elif block >= RAW + part:
-                high[block - RAW - part] = new
-
-    piece = pl.BlockSpec((part, rows, cols), lambda i, w, p, s: (0, 0, 0))
-    shape = jax.ShapeDtypeStruct((part, rows, cols), bf16)
+            if block >= first:
+                last[block - first] = new
+
     return pl.pallas_call(
         body,
         grid_spec=pltpu.PrefetchScalarGridSpec(
@@ -221,39 +220,39 @@
                 pl.BlockSpec((blocks, rows, cols), lambda i, w, p, s: (0, 0, 0)),
             ],
             out_specs=[
-                piece,
-                piece,
+                pl.BlockSpec((blocks - first, rows, cols), lambda i, w, p, s: (0, 0, 0)),
                 pl.BlockSpec((1, blocks, rows, cols), lambda i, w, p, s: (w[0], 0, 0, 0)),
             ],
             scratch_shapes=[pltpu.VMEM((blocks, rows, cols), bf16), pltpu.SemaphoreType.DMA((blocks,))],
         ),
-        out_shape=[shape, shape, jax.ShapeDtypeStruct((reps, blocks, rows, cols), bf16)],
+        out_shape=[
+            jax.ShapeDtypeStruct((blocks - first, rows, cols), bf16),
+            jax.ShapeDtypeStruct((reps, blocks, rows, cols), bf16),
+        ],
         name="update",
     )(who, position, scale, returned, params)
 
 
 def everywhere(value):
-    swap, near, wrap = [(0, 1), (1, 0)], [(0, 1), (1, 0), (2, 3), (3, 2)], [(0, 3), (3, 0), (1, 2), (2, 1)]
-    steps = [("group_2", swap)]
+    value = value + lax.ppermute(value, "group_2", [(0, 1), (1, 0)])
     for axis in ("rep", "group_0", "group_1"):
-        steps += [(axis, near), (axis, wrap)]
-    for axis, pairs in steps:
-        value = value + lax.ppermute(value, axis, pairs)
+        one, two, three = [lax.ppermute(value, axis, ring(4, step)) for step in (1, 2, 3)]
+        value = (value + two) + (one + three)
     return value
 
 
 def spread(low, high, reps):
     up, down = ring(reps, 1), ring(reps, -1)
+    high_up = lax.ppermute(high, "rep", up)
+    high_down = lax.ppermute(high, "rep", down)
     low_up = lax.ppermute(low, "rep", up)
-    high_down = lax.ppermute(high, "rep", down)
-    high_up = lax.ppermute(high, "rep", up)
     low_down = lax.ppermute(low, "rep", down)
+    far_high = lax.ppermute(high_down, "rep", down)
     far_low = lax.ppermute(low_up, "rep", up)
-    far_high = lax.ppermute(high_down, "rep", down)
     return (
+        (3, 1, high_up),
+        (1, 1, high_down),
         (3, 0, low_up),
-        (1, 1, high_down),
-        (3, 1, high_up),
         (1, 0, low_down),
         (2, 0, far_low),
         (2, 1, far_high),
@@ -291,7 +290,7 @@
             earlier.append(left_times(left, owned))
         owned = arrived.reshape(group_size * rows, cols)
 
-    ahead = spread(params[: RAW // 2], params[RAW // 2 : RAW], reps)
+    ahead = spread(params[: RAW[0]], params[RAW[0] : sum(RAW)], reps)
 
     onehots = (layer_of[:, None] == jnp.arange(LAYERS, dtype=jnp.int32)[None, :]).astype(f32)
     onehot = lax.dynamic_slice_in_dim(onehots, me * blocks, blocks)
@@ -330,16 +329,17 @@
         return lax.rem(me + offset, reps)
 
     changes = spread(*pick(position, returned), reps)
-    low, high, new_params = update(who, position, scales[me], returned, params, reps)
-    finished = spread(low, high, reps)
+    last, new_params = update(who, position, scales[me], returned, params, reps)
+    from_down = lax.ppermute(last, "rep", up)
+    from_up = lax.ppermute(last, "rep", down)
+    onward = lax.ppermute(from_down, "rep", up)
     for (offset, part, old), (_, _, change) in zip(ahead, changes):
-        size = RAW // 2
-        scale = lax.dynamic_slice(scales, (owner(offset), part * size), (1, size))[0, :, None, None]
+        first = RAW[0] * part
+        scale = lax.dynamic_slice(scales, (owner(offset), first), (1, RAW[part]))[0, :, None, None]
         new = (old.astype(f32) - scale * change.astype(f32)).astype(bf16)
-        new_params = lax.dynamic_update_slice(new_params, new[None], (owner(offset), part * size, 0, 0))
-    for offset, part, piece in finished:
-        first = RAW + part * piece.shape[0]
-        new_params = lax.dynamic_update_slice(new_params, piece[None], (owner(offset), first, 0, 0))
+        new_params = lax.dynamic_update_slice(new_params, new[None], (owner(offset), first, 0, 0))
+    for offset, piece in ((3, from_down), (1, from_up), (2, onward)):
+        new_params = lax.dynamic_update_slice(new_params, piece[None], (owner(offset), sum(RAW), 0, 0))
     return (new_params.reshape(reps * blocks, rows, width), new_accum)
 
 

time: 256 us -> 222 us (0.87)
  Pallas kernels: 64.9 us -> 34.3 us
  waiting for transfers between devices: 86 us -> 81.9 us
    pallas_call x1, Pallas kernels: 33.7 us -> 3 us  [pick(): pl.pallas_call(body, grid_spec=pltpu.PrefetchScalarGridSpec(num_scalar_pr...]
    ppermute x3 -> x2, waiting for transfers between devices: 5.98 us -> 18.2 us  [spread(): low_down = lax.ppermute(low, 'rep', down)]
    ppermute x7 -> x13, starting transfers between devices: 9.62 us -> 20.4 us  [the longest x9 16.5 us: everywhere(): lax.ppermute(value, axis, ring(4, step))]
    ppermute x7 -> x13, waiting for transfers between devices: 26.1 us -> 18.2 us  [the longest x9 11 us: everywhere(): lax.ppermute(value, axis, ring(4, step))]
    ppermute x3 -> x2, waiting for transfers between devices: 6.27 us -> 0.01 us  [spread(): low_up = lax.ppermute(low, 'rep', up)]
    ppermute x3 -> x2, starting transfers between devices: 5.91 us -> 2.38 us  [spread(): far_high = lax.ppermute(high_down, 'rep', down)]
    ppermute x3 -> x2, waiting for transfers between devices: 7.8 us -> 4.98 us  [spread(): far_low = lax.ppermute(low_up, 'rep', up)]
    ppermute x3 -> x2, starting transfers between devices: 6.76 us -> 5.24 us  [spread(): high_down = lax.ppermute(high, 'rep', down)]
  transfers between devices with their start and end apart: 36 -> 36, of which waited for: 24 -> 20; matrix products, arithmetic and copies ran while one was open for 10% -> 11% of each run, Pallas kernels for 22% -> 12%
where the time goes in v6:
time: 222 us; the launch traced here: 220 us
  waiting for transfers between devices  81.9 us (37%)
  starting transfers between devices  70.9 us (32%)
  Pallas kernels  34.3 us (15%)
  local copies, waits for them, and re-layouts  16.2 us (7%)
  other arithmetic  15.9 us (7%)
    all_to_all x3, starting transfers between devices, local(): lax.all_to_all(outgoing, GROUP, split_axis=0, concat_axis=0, tiled=True)  20.9 us
    ppermute x2, waiting for transfers between devices, spread(): low_down = lax.ppermute(low, 'rep', down)  18.2 us
    ppermute x9, starting transfers between devices, everywhere(): lax.ppermute(value, axis, ring(4, step))  16.5 us
    ppermute x9, waiting for transfers between devices, everywhere(): lax.ppermute(value, axis, ring(4, step))  11 us
    ppermute x2, waiting for transfers between devices, local(): near_up = lax.ppermute(to_up, 'rep', up)  10.7 us
    all_to_all x3, waiting for transfers between devices, local(): lax.all_to_all(outgoing, GROUP, split_axis=0, concat_axis=0, tiled=True)  8.8 us
    dynamic_update_slice x6, other arithmetic, local(): lax.dynamic_update_slice(new_params, new[None], (owner(offset), first, 0,...  8.78 us
    ppermute x2, waiting for transfers between devices, spread(): high_up = lax.ppermute(high, 'rep', up)  8.46 us
  transfers between devices with their start and end apart: 36, of which 20 were waited for; matrix products, arithmetic and copies ran while one was open for 11% of the time, Pallas kernels for 12%

profile of v6, /device:TPU:0, one launch (start us, length us, event | category | flops | bytes accessed | tf_op | source)
XLA Modules:
  0.0 220.2 jit_solution(72275224744624510)
XLA Ops:
  14.4 3.1 %merge.3 = (bf16[24,32,384]{2,1,0:T(8,128)(2,1)}, bf16[24,32,384]{2,1,0:T(8,128)(2,1)}) custom-call(s32[4]{0:T(128)} %compare_select_fusion.who_ref, bf16[4,24,32,1024]{3,2,1,0:T(8,128)(2,1)} %bitcast.69, bf16[4,24,32,1024]{3,2,1,0:T(8,128)(2,1)} %bitcast.70, bf16[12,32,384]{2,1,0:T(8,128)(2,1)} %copy-done.9, bf16[12,32,384]{2,1,0:T(8,128)(2,1)} %copy-done.10), custom_call_target="tpu_custom_call" | custom-call | tf_op jit(solution)/shard_map/merge/pallas_call | solution.py:51
  25.0 3.6 %merge.2 = (bf16[24,32,640]{2,1,0:T(8,128)(2,1)}, bf16[24,32,640]{2,1,0:T(8,128)(2,1)}) custom-call(s32[4]{0:T(128)} %compare_select_fusion.who_ref, bf16[4,24,32,1024]{3,2,1,0:T(8,128)(2,1)} %bitcast.71, bf16[4,24,32,1024]{3,2,1,0:T(8,128)(2,1)} %bitcast.72, bf16[12,32,640]{2,1,0:T(8,128)(2,1)} %copy-done.7, bf16[12,32,640]{2,1,0:T(8,128)(2,1)} %copy-done.8), custom_call_target="tpu_custom_call" | custom-call | tf_op jit(solution)/shard_map/merge/pallas_call | solution.py:51
  32.4 3.7 %collective-permute-done.6.one = bf16[24,32,384]{2,1,0:T(8,128)(2,1)S(1)} collective-permute-done((bf16[24,32,384]{2,1,0:T(8,128)(2,1)}, bf16[24,32,384]{2,1,0:T(8,128)(2,1)S(1)}, u32[]{:S(2)}, u32[]{:S(2)}) %collective-permute-start.6) | collective-permute-done | bytes 589856 | tf_op jit(solution)/shard_map/ppermute | solution.py:284
  36.9 3.5 %finish.3 = (bf16[24,32,384]{2,1,0:T(8,128)(2,1)}, bf16[32,32,384]{2,1,0:T(8,128)(2,1)}) custom-call(s32[4]{0:T(128)} %compare_select_fusion.who_ref, s32[32]{0:T(128)} %get-tuple-element.46.table_ref, bf16[4,24,32,1024]{3,2,1,0:T(8,128)(2,1)} %bitcast.73, bf16[24,32,384]{2,1,0:T(8,128)(2,1)} %copy-done.6, bf16[24,32,384]{2,1,0:T(8,128)(2,1)} %collective-permute-done.7.two), custom_call_target="tpu_custom_call" | custom-call | tf_op jit(solution)/shard_map/finish/pallas_call | solution.py:80
  40.5 8.4 %all-to-all-start.1 = ((bf16[32,32,384]{2,1,0:T(8,128)(2,1)}), bf16[32,32,384]{2,1,0:T(8,128)(2,1)S(1)}, u32[]{:S(2)}, u32[]{:S(2)}) async-start(bf16[32,32,384]{2,1,0:T(8,128)(2,1)} %get-tuple-element.28), calls=%async_computation.1 | async-start | bytes 1572864 | tf_op jit(solution)/shard_map/all_to_all | solution.py:288
  48.9 7.0 %collective-permute-done.2.one = bf16[24,32,640]{2,1,0:T(8,128)(2,1)S(1)} collective-permute-done((bf16[24,32,640]{2,1,0:T(8,128)(2,1)}, bf16[24,32,640]{2,1,0:T(8,128)(2,1)S(1)}, u32[]{:S(2)}, u32[]{:S(2)}) %collective-permute-start.2) | collective-permute-done | bytes 983072 | tf_op jit(solution)/shard_map/ppermute | solution.py:284
  57.9 4.6 %finish.2 = (bf16[24,32,640]{2,1,0:T(8,128)(2,1)}, bf16[32,32,640]{2,1,0:T(8,128)(2,1)}) custom-call(s32[4]{0:T(128)} %compare_select_fusion.who_ref, s32[32]{0:T(128)} %get-tuple-element.46.table_ref, bf16[4,24,32,1024]{3,2,1,0:T(8,128)(2,1)} %bitcast.74, bf16[24,32,640]{2,1,0:T(8,128)(2,1)} %copy-done.4, bf16[24,32,640]{2,1,0:T(8,128)(2,1)} %copy-done.5), custom_call_target="tpu_custom_call" | custom-call | tf_op jit(solution)/shard_map/finish/pallas_call | solution.py:80
  62.8 8.3 %all-to-all-start = ((bf16[32,32,640]{2,1,0:T(8,128)(2,1)}), bf16[32,32,640]{2,1,0:T(8,128)(2,1)S(1)}, u32[]{:S(2)}, u32[]{:S(2)}) async-start(bf16[32,32,640]{2,1,0:T(8,128)(2,1)} %get-tuple-element.25), calls=%async_computation | async-start | bytes 2621440 | tf_op jit(solution)/shard_map/all_to_all | solution.py:288
  73.1 4.4 %fusion = (f32[24,32,1024]{2,1,0:T(8,128)}, f32[24]{0:T(128)S(1)}) fusion(f32[24,32,1024]{2,1,0:T(8,128)} %param.9, bf16[24,32,640]{2,1,0:T(8,128)(2,1)S(1)} %copy-done.3, bf16[24,32,384]{2,1,0:T(8,128)(2,1)} %get-tuple-element.29), kind=kLoop, calls=%fused_computation.2 | loop fusion | flops 7077864 | bytes 7864416 | tf_op jit(solution)/shard_map/add | solution.py:299
  78.8 3.6 %left_times.1.rest_0_ = bf16[1024,384]{1,0:T(8,128)(2,1)} custom-call(bf16[1024,1024]{1,0:T(8,128)(2,1)} %bitcast.75, bf16[1024,384]{1,0:T(8,128)(2,1)} %bitcast.78), custom_call_target="tpu_custom_call" | custom-call | tf_op jit(solution)/shard_map/left_times/pallas_call | solution.py:107
  82.5 8.5 %all-to-all-done = bf16[32,32,640]{2,1,0:T(8,128)(2,1)S(1)} async-done(((bf16[32,32,640]{2,1,0:T(8,128)(2,1)}), bf16[32,32,640]{2,1,0:T(8,128)(2,1)S(1)}, u32[]{:S(2)}, u32[]{:S(2)}) %all-to-all-start) | async-done | bytes 1310752 | tf_op jit(solution)/shard_map/all_to_all | solution.py:288
  92.1 7.7 %products.1 = (bf16[1024,1024]{1,0:T(8,128)(2,1)}, f32[2,128]{1,0:T(2,128)}) custom-call(bf16[1024,1024]{1,0:T(8,128)(2,1)} %bitcast.76, bf16[1024,1024]{1,0:T(8,128)(2,1)} %bitcast.79, bf16[1024,640]{1,0:T(8,128)(2,1)} %bitcast.77, f32[1,128]{1,0:T(1,128)} %pad.7.graft_ref, f32[1,128]{1,0:T(1,128)} %pad.8.layer_ref, bf16[1024,384]{1,0:T(8,128)(2,1)} %left_times.1.rest_0_), custom_call_target="tpu_custom_call" | custom-call | tf_op jit(solution)/shard_map/products/pallas_call | solution.py:147
  99.8 4.1 %all-to-all-start.2 = ((bf16[32,32,1024]{2,1,0:T(8,128)(2,1)}), bf16[32,32,1024]{2,1,0:T(8,128)(2,1)S(1)}, u32[]{:S(2)}, u32[]{:S(2)}) async-start(bf16[32,32,1024]{2,1,0:T(8,128)(2,1)} %bitcast.80), calls=%async_computation.2 | async-start | bytes 4194304 | tf_op jit(solution)/shard_map/all_to_all | solution.py:323
  110.0 3.5 %collective-permute-done.9 = f32[2,128]{1,0:T(2,128)S(1)} collective-permute-done((f32[2,128]{1,0:T(2,128)S(1)}, f32[2,128]{1,0:T(2,128)S(1)}, u32[]{:S(2)}, u32[]{:S(2)}) %collective-permute-start.9) | collective-permute-done | bytes 1056 | tf_op jit(solution)/shard_map/ppermute | solution.py:239
  113.5 3.3 %collective-permute-start.12 = (f32[2,128]{1,0:T(2,128)S(1)}, f32[2,128]{1,0:T(2,128)S(1)}, u32[]{:S(2)}, u32[]{:S(2)}) collective-permute-start(f32[2,128]{1,0:T(2,128)S(1)} %add_add_fusion.2), channel_id=1, source_target_pairs={{0,64},{32,96},{64,0},{96,32},{1,65},{33,97},{65,1},{97,33},{2,66}... | collective-permute-start | bytes 3080 | tf_op jit(solution)/shard_map/ppermute | solution.py:239
  121.3 3.2 %collective-permute-start.20 = (bf16[12,32,1024]{2,1,0:T(8,128)(2,1)S(1)}, bf16[12,32,1024]{2,1,0:T(8,128)(2,1)}, u32[]{:S(2)}, u32[]{:S(2)}) collective-permute-start(bf16[12,32,1024]{2,1,0:T(8,128)(2,1)S(1)} %slice.14), channel_id=1, source_target_pairs={{0,3},{1,0},{2,1},{3,2},{4,7},{5,4},{6,5},{7,6},{8,11},{9,8},{10,9... | collective-permute-start | bytes 2359304 | tf_op jit(solution)/shard_map/ppermute | solution.py:247
  124.6 6.5 %collective-permute-done.12 = f32[2,128]{1,0:T(2,128)S(1)} collective-permute-done((f32[2,128]{1,0:T(2,128)S(1)}, f32[2,128]{1,0:T(2,128)S(1)}, u32[]{:S(2)}, u32[]{:S(2)}) %collective-permute-start.12) | collective-permute-done | bytes 1056 | tf_op jit(solution)/shard_map/ppermute | solution.py:239
  147.2 5.1 %update.1 = (bf16[8,32,1024]{2,1,0:T(8,128)(2,1)}, bf16[4,24,32,1024]{3,2,1,0:T(8,128)(2,1)}) custom-call(s32[4]{0:T(128)} %compare_select_fusion.who_ref, s32[24]{0:T(128)} %select_reduce_fusion.position_ref, f32[24]{0:T(128)} %fusion.21.scale_ref, bf16[32,32,1024]{2,1,0:T(8,128)(2,1)} %copy-done, bf16[24,32,1024]{2,1,0:T(8,128)(2,1)} %params_ref.1), custom_call_target="tpu_custom_call" | custom-call | tf_op jit(solution)/shard_map/update/pallas_call | solution.py:213
  154.7 8.5 %collective-permute-done.19 = bf16[12,32,1024]{2,1,0:T(8,128)(2,1)S(1)} collective-permute-done((bf16[12,32,1024]{2,1,0:T(8,128)(2,1)}, bf16[12,32,1024]{2,1,0:T(8,128)(2,1)S(1)}, u32[]{:S(2)}, u32[]{:S(2)}) %collective-permute-start.19) | collective-permute-done | bytes 786464 | tf_op jit(solution)/shard_map/ppermute | solution.py:246
  165.7 3.2 %collective-permute-start.25 = (bf16[4,32,1024]{2,1,0:T(8,128)(2,1)}, bf16[4,32,1024]{2,1,0:T(8,128)(2,1)S(1)}, u32[]{:S(2)}, u32[]{:S(2)}) collective-permute-start(bf16[4,32,1024]{2,1,0:T(8,128)(2,1)} %get-tuple-element.41), channel_id=1, source_target_pairs={{0,3},{1,0},{2,1},{3,2},{4,7},{5,4},{6,5},{7,6},{8,11},{9,8},{10,9... | collective-permute-start | bytes 786440 | tf_op jit(solution)/shard_map/ppermute | solution.py:249
  176.9 16.3 %collective-permute-done.25 = bf16[4,32,1024]{2,1,0:T(8,128)(2,1)S(1)} collective-permute-done((bf16[4,32,1024]{2,1,0:T(8,128)(2,1)}, bf16[4,32,1024]{2,1,0:T(8,128)(2,1)S(1)}, u32[]{:S(2)}, u32[]{:S(2)}) %collective-permute-start.25) | collective-permute-done | bytes 262176 | tf_op jit(solution)/shard_map/ppermute | solution.py:249
  198.7 5.0 %collective-permute-done.27 = bf16[4,32,1024]{2,1,0:T(8,128)(2,1)S(1)} collective-permute-done((bf16[4,32,1024]{2,1,0:T(8,128)(2,1)S(1)}, bf16[4,32,1024]{2,1,0:T(8,128)(2,1)S(1)}, u32[]{:S(2)}, u32[]{:S(2)}) %collective-permute-start.27) | collective-permute-done | bytes 262176 | tf_op jit(solution)/shard_map/ppermute | solution.py:251
  204.5 5.6 %collective-permute-done.29 = bf16[12,32,1024]{2,1,0:T(8,128)(2,1)S(1)} collective-permute-done((bf16[12,32,1024]{2,1,0:T(8,128)(2,1)S(1)}, bf16[12,32,1024]{2,1,0:T(8,128)(2,1)S(1)}, u32[]{:S(2)}, u32[]{:S(2)}) %collective-permute-start.29) | collective-permute-done | bytes 786464 | tf_op jit(solution)/shard_map/ppermute | solution.py:250
  212.3 6.2 %collective-permute-done.31 = bf16[8,32,1024]{2,1,0:T(8,128)(2,1)S(1)} collective-permute-done((bf16[8,32,1024]{2,1,0:T(8,128)(2,1)S(1)}, bf16[8,32,1024]{2,1,0:T(8,128)(2,1)S(1)}, u32[]{:S(2)}, u32[]{:S(2)}) %collective-permute-start.31) | collective-permute-done | bytes 524320 | tf_op jit(solution)/shard_map/ppermute | solution.py:334
  (120 shorter events, 82.2 us)
Async XLA Ops:
  6.3 17.1 %collective-permute-start = (bf16[12,32,640]{2,1,0:T(8,128)(2,1)S(1)}, bf16[12,32,640]{2,1,0:T(8,128)(2,1)S(1)}, u32[]{:S(2)}, u32[]{:S(2)}) collective-permute-start(bf16[12,32,640]{2,1,0:T(8,128)(2,1)S(1)} %get-tuple-element.51), channel_id=1, source_target_pairs={{0,1},{1,2},{2,3},{3,0},{4,5},{5,6},{6,7},{7,4},{8,9},{9,10},{10,1... | collective-permute-start | bytes 1474568 | tf_op jit(solution)/shard_map/ppermute | solution.py:281
  6.8 17.0 %collective-permute-start.1 = (bf16[12,32,640]{2,1,0:T(8,128)(2,1)S(1)}, bf16[12,32,640]{2,1,0:T(8,128)(2,1)S(1)}, u32[]{:S(2)}, u32[]{:S(2)}) collective-permute-start(bf16[12,32,640]{2,1,0:T(8,128)(2,1)S(1)} %get-tuple-element.50), channel_id=1, source_target_pairs={{0,3},{1,0},{2,1},{3,2},{4,7},{5,4},{6,5},{7,6},{8,11},{9,8},{10,9... | collective-permute-start | bytes 1474568 | tf_op jit(solution)/shard_map/ppermute | solution.py:282
  17.4 18.7 %collective-permute-start.6 = (bf16[24,32,384]{2,1,0:T(8,128)(2,1)}, bf16[24,32,384]{2,1,0:T(8,128)(2,1)S(1)}, u32[]{:S(2)}, u32[]{:S(2)}) collective-permute-start(bf16[24,32,384]{2,1,0:T(8,128)(2,1)} %get-tuple-element.26), channel_id=1, source_target_pairs={{0,1},{1,2},{2,3},{3,0},{4,5},{5,6},{6,7},{7,4},{8,9},{9,10},{10,1... | collective-permute-start | bytes 1769480 | tf_op jit(solution)/shard_map/ppermute | solution.py:284
  18.6 18.0 %collective-permute-start.7 = (bf16[24,32,384]{2,1,0:T(8,128)(2,1)}, bf16[24,32,384]{2,1,0:T(8,128)(2,1)}, u32[]{:S(2)}, u32[]{:S(2)}) collective-permute-start(bf16[24,32,384]{2,1,0:T(8,128)(2,1)} %get-tuple-element.27), channel_id=1, source_target_pairs={{0,3},{1,0},{2,1},{3,2},{4,7},{5,4},{6,5},{7,6},{8,11},{9,8},{10,9... | collective-permute-start | bytes 1769480 | tf_op jit(solution)/shard_map/ppermute | solution.py:285
  28.6 27.3 %collective-permute-start.2 = (bf16[24,32,640]{2,1,0:T(8,128)(2,1)}, bf16[24,32,640]{2,1,0:T(8,128)(2,1)S(1)}, u32[]{:S(2)}, u32[]{:S(2)}) collective-permute-start(bf16[24,32,640]{2,1,0:T(8,128)(2,1)} %get-tuple-element.23), channel_id=1, source_target_pairs={{0,1},{1,2},{2,3},{3,0},{4,5},{5,6},{6,7},{7,4},{8,9},{9,10},{10,1... | collective-permute-start | bytes 2949128 | tf_op jit(solution)/shard_map/ppermute | solution.py:284
  29.7 26.5 %collective-permute-start.3 = (bf16[24,32,640]{2,1,0:T(8,128)(2,1)}, bf16[24,32,640]{2,1,0:T(8,128)(2,1)S(1)}, u32[]{:S(2)}, u32[]{:S(2)}) collective-permute-start(bf16[24,32,640]{2,1,0:T(8,128)(2,1)} %get-tuple-element.24), channel_id=1, source_target_pairs={{0,3},{1,0},{2,1},{3,2},{4,7},{5,4},{6,5},{7,6},{8,11},{9,8},{10,9... | collective-permute-start | bytes 2949128 | tf_op jit(solution)/shard_map/ppermute | solution.py:285
  40.5 22.4 %all-to-all-start.1 = ((bf16[32,32,384]{2,1,0:T(8,128)(2,1)}), bf16[32,32,384]{2,1,0:T(8,128)(2,1)S(1)}, u32[]{:S(2)}, u32[]{:S(2)}) async-start(bf16[32,32,384]{2,1,0:T(8,128)(2,1)} %get-tuple-element.28), calls=%async_computation.1 | async-start | bytes 1572864 | tf_op jit(solution)/shard_map/all_to_all | solution.py:288
  62.8 28.1 %all-to-all-start = ((bf16[32,32,640]{2,1,0:T(8,128)(2,1)}), bf16[32,32,640]{2,1,0:T(8,128)(2,1)S(1)}, u32[]{:S(2)}, u32[]{:S(2)}) async-start(bf16[32,32,640]{2,1,0:T(8,128)(2,1)} %get-tuple-element.25), calls=%async_computation | async-start | bytes 2621440 | tf_op jit(solution)/shard_map/all_to_all | solution.py:288
  99.8 39.0 %all-to-all-start.2 = ((bf16[32,32,1024]{2,1,0:T(8,128)(2,1)}), bf16[32,32,1024]{2,1,0:T(8,128)(2,1)S(1)}, u32[]{:S(2)}, u32[]{:S(2)}) async-start(bf16[32,32,1024]{2,1,0:T(8,128)(2,1)} %bitcast.80), calls=%async_computation.2 | async-start | bytes 4194304 | tf_op jit(solution)/shard_map/all_to_all | solution.py:323
  113.5 17.5 %collective-permute-start.12 = (f32[2,128]{1,0:T(2,128)S(1)}, f32[2,128]{1,0:T(2,128)S(1)}, u32[]{:S(2)}, u32[]{:S(2)}) collective-permute-start(f32[2,128]{1,0:T(2,128)S(1)} %add_add_fusion.2), channel_id=1, source_target_pairs={{0,64},{32,96},{64,0},{96,32},{1,65},{33,97},{65,1},{97,33},{2,66}... | collective-permute-start | bytes 3080 | tf_op jit(solution)/shard_map/ppermute | solution.py:239
  116.8 14.2 %collective-permute-start.13 = (f32[2,128]{1,0:T(2,128)S(1)}, f32[2,128]{1,0:T(2,128)S(1)}, u32[]{:S(2)}, u32[]{:S(2)}) collective-permute-start(f32[2,128]{1,0:T(2,128)S(1)} %add_add_fusion.2), channel_id=1, source_target_pairs={{0,32},{32,64},{64,96},{96,0},{1,33},{33,65},{65,97},{97,1},{2,34}... | collective-permute-start | bytes 3080 | tf_op jit(solution)/shard_map/ppermute | solution.py:239
  121.3 31.1 %collective-permute-start.18 = (bf16[12,32,1024]{2,1,0:T(8,128)(2,1)S(1)}, bf16[12,32,1024]{2,1,0:T(8,128)(2,1)}, u32[]{:S(2)}, u32[]{:S(2)}) collective-permute-start(bf16[12,32,1024]{2,1,0:T(8,128)(2,1)S(1)} %slice.14), channel_id=1, source_target_pairs={{0,1},{1,2},{2,3},{3,0},{4,5},{5,6},{6,7},{7,4},{8,9},{9,10},{10,1... | collective-permute-start | bytes 2359304 | tf_op jit(solution)/shard_map/ppermute | solution.py:246
  121.3 32.6 %collective-permute-start.20 = (bf16[12,32,1024]{2,1,0:T(8,128)(2,1)S(1)}, bf16[12,32,1024]{2,1,0:T(8,128)(2,1)}, u32[]{:S(2)}, u32[]{:S(2)}) collective-permute-start(bf16[12,32,1024]{2,1,0:T(8,128)(2,1)S(1)} %slice.14), channel_id=1, source_target_pairs={{0,3},{1,0},{2,1},{3,2},{4,7},{5,4},{6,5},{7,6},{8,11},{9,8},{10,9... | collective-permute-start | bytes 2359304 | tf_op jit(solution)/shard_map/ppermute | solution.py:247
  138.2 27.5 %collective-permute-start.22 = (bf16[4,32,1024]{2,1,0:T(8,128)(2,1)S(1)}, bf16[4,32,1024]{2,1,0:T(8,128)(2,1)S(1)}, u32[]{:S(2)}, u32[]{:S(2)}) collective-permute-start(bf16[4,32,1024]{2,1,0:T(8,128)(2,1)S(1)} %slice.15), channel_id=1, source_target_pairs={{0,1},{1,2},{2,3},{3,0},{4,5},{5,6},{6,7},{7,4},{8,9},{9,10},{10,1... | collective-permute-start | bytes 786440 | tf_op jit(solution)/shard_map/ppermute | solution.py:248
  143.2 20.0 %collective-permute-start.19 = (bf16[12,32,1024]{2,1,0:T(8,128)(2,1)}, bf16[12,32,1024]{2,1,0:T(8,128)(2,1)S(1)}, u32[]{:S(2)}, u32[]{:S(2)}) collective-permute-start(bf16[12,32,1024]{2,1,0:T(8,128)(2,1)} %get-tuple-element.40), channel_id=1, source_target_pairs={{0,1},{1,2},{2,3},{3,0},{4,5},{5,6},{6,7},{7,4},{8,9},{9,10},{10,1... | collective-permute-start | bytes 2359304 | tf_op jit(solution)/shard_map/ppermute | solution.py:246
  144.5 27.9 %collective-permute-start.21 = (bf16[12,32,1024]{2,1,0:T(8,128)(2,1)}, bf16[12,32,1024]{2,1,0:T(8,128)(2,1)S(1)}, u32[]{:S(2)}, u32[]{:S(2)}) collective-permute-start(bf16[12,32,1024]{2,1,0:T(8,128)(2,1)} %get-tuple-element.40), channel_id=1, source_target_pairs={{0,3},{1,0},{2,1},{3,2},{4,7},{5,4},{6,5},{7,6},{8,11},{9,8},{10,9... | collective-permute-start | bytes 2359304 | tf_op jit(solution)/shard_map/ppermute | solution.py:247
  152.4 18.4 %collective-permute-start.24 = (bf16[4,32,1024]{2,1,0:T(8,128)(2,1)S(1)}, bf16[4,32,1024]{2,1,0:T(8,128)(2,1)S(1)}, u32[]{:S(2)}, u32[]{:S(2)}) collective-permute-start(bf16[4,32,1024]{2,1,0:T(8,128)(2,1)S(1)} %slice.15), channel_id=1, source_target_pairs={{0,3},{1,0},{2,1},{3,2},{4,7},{5,4},{6,5},{7,6},{8,11},{9,8},{10,9... | collective-permute-start | bytes 786440 | tf_op jit(solution)/shard_map/ppermute | solution.py:249
  153.9 50.6 %collective-permute-start.28 = (bf16[12,32,1024]{2,1,0:T(8,128)(2,1)}, bf16[12,32,1024]{2,1,0:T(8,128)(2,1)S(1)}, u32[]{:S(2)}, u32[]{:S(2)}) collective-permute-start(bf16[12,32,1024]{2,1,0:T(8,128)(2,1)} %collective-permute-done.20), channel_id=1, source_target_pairs={{0,3},{1,0},{2,1},{3,2},{4,7},{5,4},{6,5},{7,6},{8,11},{9,8},{10,9... | collective-permute-start | bytes 2359304 | tf_op jit(solution)/shard_map/ppermute | solution.py:250
  165.7 27.6 %collective-permute-start.25 = (bf16[4,32,1024]{2,1,0:T(8,128)(2,1)}, bf16[4,32,1024]{2,1,0:T(8,128)(2,1)S(1)}, u32[]{:S(2)}, u32[]{:S(2)}) collective-permute-start(bf16[4,32,1024]{2,1,0:T(8,128)(2,1)} %get-tuple-element.41), channel_id=1, source_target_pairs={{0,3},{1,0},{2,1},{3,2},{4,7},{5,4},{6,5},{7,6},{8,11},{9,8},{10,9... | collective-permute-start | bytes 786440 | tf_op jit(solution)/shard_map/ppermute | solution.py:249
  170.8 27.4 %collective-permute-start.30 = (bf16[8,32,1024]{2,1,0:T(8,128)(2,1)}, bf16[8,32,1024]{2,1,0:T(8,128)(2,1)S(1)}, u32[]{:S(2)}, u32[]{:S(2)}) collective-permute-start(bf16[8,32,1024]{2,1,0:T(8,128)(2,1)} %get-tuple-element.42), channel_id=1, source_target_pairs={{0,1},{1,2},{2,3},{3,0},{4,5},{5,6},{6,7},{7,4},{8,9},{9,10},{10,1... | collective-permute-start | bytes 1572872 | tf_op jit(solution)/shard_map/ppermute | solution.py:333
  172.5 37.7 %collective-permute-start.29 = (bf16[12,32,1024]{2,1,0:T(8,128)(2,1)S(1)}, bf16[12,32,1024]{2,1,0:T(8,128)(2,1)S(1)}, u32[]{:S(2)}, u32[]{:S(2)}) collective-permute-start(bf16[12,32,1024]{2,1,0:T(8,128)(2,1)S(1)} %collective-permute-done.21), channel_id=1, source_target_pairs={{0,3},{1,0},{2,1},{3,2},{4,7},{5,4},{6,5},{7,6},{8,11},{9,8},{10,9... | collective-permute-start | bytes 2359304 | tf_op jit(solution)/shard_map/ppermute | solution.py:250
  176.5 20.2 %collective-permute-start.26 = (bf16[4,32,1024]{2,1,0:T(8,128)(2,1)S(1)}, bf16[4,32,1024]{2,1,0:T(8,128)(2,1)S(1)}, u32[]{:S(2)}, u32[]{:S(2)}) collective-permute-start(bf16[4,32,1024]{2,1,0:T(8,128)(2,1)S(1)} %collective-permute-done.22), channel_id=1, source_target_pairs={{0,1},{1,2},{2,3},{3,0},{4,5},{5,6},{6,7},{7,4},{8,9},{9,10},{10,1... | collective-permute-start | bytes 786440 | tf_op jit(solution)/shard_map/ppermute | solution.py:251
  196.6 21.8 %collective-permute-start.31 = (bf16[8,32,1024]{2,1,0:T(8,128)(2,1)S(1)}, bf16[8,32,1024]{2,1,0:T(8,128)(2,1)S(1)}, u32[]{:S(2)}, u32[]{:S(2)}) collective-permute-start(bf16[8,32,1024]{2,1,0:T(8,128)(2,1)S(1)} %copy-done.14), channel_id=1, source_target_pairs={{0,3},{1,0},{2,1},{3,2},{4,7},{5,4},{6,5},{7,6},{8,11},{9,8},{10,9... | collective-permute-start | bytes 1572872 | tf_op jit(solution)/shard_map/ppermute | solution.py:334
  198.2 21.1 %collective-permute-start.32 = (bf16[8,32,1024]{2,1,0:T(8,128)(2,1)S(1)}, bf16[8,32,1024]{2,1,0:T(8,128)(2,1)S(1)}, u32[]{:S(2)}, u32[]{:S(2)}) collective-permute-start(bf16[8,32,1024]{2,1,0:T(8,128)(2,1)S(1)} %collective-permute-done.30), channel_id=1, source_target_pairs={{0,1},{1,2},{2,3},{3,0},{4,5},{5,6},{6,7},{7,4},{8,9},{9,10},{10,1... | collective-permute-start | bytes 1572872 | tf_op jit(solution)/shard_map/ppermute | solution.py:335
  (27 other events, 198.2 us)

commit v7 on v6

--- a/solution.py
+++ b/solution.py
@@ -93,7 +93,6 @@
             jax.ShapeDtypeStruct((blocks, rows, cols), bf16),
             jax.ShapeDtypeStruct((slots, rows, cols), bf16),
         ],
-        name="finish",
     )(who, table, parts, up, down)
 
 
@@ -117,13 +116,13 @@
     )(left, owned)
 
 
-def products(left, right, owned, earlier, graft_row, layer_row):
+def products(left, right, owned, earlier, layer_row):
     order, cols = owned.shape
     steps = 2
     tile = order // steps
     last = SENT[-1][0]
 
-    def body(left_ref, right_ref, owned_ref, graft_ref, layer_ref, *rest):
+    def body(left_ref, right_ref, owned_ref, layer_ref, *rest):
         before, (out, sums, mid) = rest[: len(earlier)], rest[len(earlier) :]
         mid[:, last : last + cols] = jnp.dot(
             left_ref[...], owned_ref[...], preferred_element_type=f32
@@ -136,7 +135,7 @@
 
         @pl.when(pl.program_id(0) == 0)
         def _():
-            sums[0:1] = graft_ref[...]
+            sums[0:1] = jnp.zeros_like(squares * layer_ref[...])
             sums[1:2] = layer_ref[...] * squares
 
         @pl.when(pl.program_id(0) > 0)
@@ -151,7 +150,6 @@
             pl.BlockSpec((tile, order), lambda i: (i, 0)),
             pl.BlockSpec((order, order), lambda i: (0, 0)),
             pl.BlockSpec((order, cols), lambda i: (0, 0)),
-            row,
             row,
             *[pl.BlockSpec((tile, e.shape[1]), lambda i: (i, 0)) for e in earlier],
         ],
@@ -159,7 +157,7 @@
         out_shape=[jax.ShapeDtypeStruct((order, order), bf16), jax.ShapeDtypeStruct((2, LANES), f32)],
         scratch_shapes=[pltpu.VMEM((tile, order), bf16)],
         name="products",
-    )(left, right, owned, graft_row, layer_row, *earlier)
+    )(left, right, owned, layer_row, *earlier)
 
 
 def fetch(position_ref, returned_ref, target, sems, blocks):
@@ -290,19 +288,15 @@
             earlier.append(left_times(left, owned))
         owned = arrived.reshape(group_size * rows, cols)
 
-    ahead = spread(params[: RAW[0]], params[RAW[0] : sum(RAW)], reps)
+    old_low, old_high = params[: RAW[0]], params[RAW[0] : sum(RAW)]
+    ahead = spread(old_low, old_high, reps)
 
     onehots = (layer_of[:, None] == jnp.arange(LAYERS, dtype=jnp.int32)[None, :]).astype(f32)
     onehot = lax.dynamic_slice_in_dim(onehots, me * blocks, blocks)
-    in_order = sorted(range(len(SENT)), key=lambda c: SENT[c][0])
-    wide = jnp.concatenate([gradients[c] for c in in_order], axis=2).astype(f32)
-    new_accum = accum + wide * wide
-    graft = wide * lax.rsqrt(new_accum)
-    graft_blocks = jnp.sum(graft * graft, axis=(1, 2))
-    graft_layer = jnp.sum(onehot * graft_blocks[:, None], axis=0)
     mine = lax.dynamic_index_in_dim(table, group_index, 0, keepdims=False)
     chosen = (jnp.arange(blocks, dtype=jnp.int32) == mine).astype(f32)
     my_layer = jnp.sum(chosen[:, None] * onehot, axis=0)
+    layer_row = jnp.pad(my_layer[None, :], ((0, 0), (0, LANES - LAYERS)))
     position = jnp.sum(
         jnp.where(
             table[None, :] == jnp.arange(blocks, dtype=jnp.int32)[:, None],
@@ -311,17 +305,21 @@
         ),
         axis=1,
     )
-    to_lanes = ((0, 0), (0, LANES - LAYERS))
-    graft_row = jnp.pad(graft_layer[None, :], to_lanes)
-    layer_row = jnp.pad(my_layer[None, :], to_lanes)
-    owned, earlier, graft_row, layer_row, position, onehots, new_accum = lax.optimization_barrier(
-        (owned, earlier, graft_row, layer_row, position, onehots, new_accum)
-    )
-
-    precond, sums = products(left, right, owned, earlier, graft_row, layer_row)
+
+    owned, earlier, layer_row, onehot, gradients = lax.optimization_barrier(
+        (owned, earlier, layer_row, onehot, gradients)
+    )
+
+    wide = jnp.concatenate(gradients, axis=2).astype(f32)
+    new_accum = accum + wide * wide
+    graft = wide * lax.rsqrt(new_accum)
+    graft_blocks = jnp.sum(graft * graft, axis=(1, 2))
+    graft_layer = jnp.sum(onehot * graft_blocks[:, None], axis=0)
+    graft_row = jnp.pad(graft_layer[None, :], ((0, 1), (0, LANES - LAYERS)))
+    precond, sums = products(left, right, owned, earlier, layer_row)
     outgoing = precond.reshape(group_size, rows, width)
     returned = lax.all_to_all(outgoing, GROUP, split_axis=0, concat_axis=0, tiled=True)
-    sums = everywhere(sums)
+    sums = everywhere(sums + graft_row)
     layer_scale = jnp.sqrt(sums[0, :LAYERS]) * lax.rsqrt(sums[1, :LAYERS] + 1e-06)
     scales = (step_rate * jnp.sum(onehots * layer_scale[None, :], axis=1)).reshape(reps, blocks)
 
@@ -333,13 +331,21 @@
     from_down = lax.ppermute(last, "rep", up)
     from_up = lax.ppermute(last, "rep", down)
     onward = lax.ppermute(from_down, "rep", up)
-    for (offset, part, old), (_, _, change) in zip(ahead, changes):
-        first = RAW[0] * part
-        scale = lax.dynamic_slice(scales, (owner(offset), first), (1, RAW[part]))[0, :, None, None]
-        new = (old.astype(f32) - scale * change.astype(f32)).astype(bf16)
-        new_params = lax.dynamic_update_slice(new_params, new[None], (owner(offset), first, 0, 0))
-    for offset, piece in ((3, from_down), (1, from_up), (2, onward)):
-        new_params = lax.dynamic_update_slice(new_params, piece[None], (owner(offset), sum(RAW), 0, 0))
+
+    def place(whole, offset, first, piece):
+        return lax.dynamic_update_slice(whole, piece[None], (owner(offset), first, 0, 0))
+
+    pairs = list(zip(ahead, changes))
+    for group, name in ((pairs[:4], "place_near"), (pairs[4:], "place_far")):
+        for (offset, part, old), (_, _, change) in group:
+            first = RAW[0] * part
+            scale = lax.dynamic_slice(scales, (owner(offset), first), (1, RAW[part]))[0, :, None, None]
+            new = (old.astype(f32) - scale * change.astype(f32)).astype(bf16)
+            new_params = place(new_params, offset, first, new)
+        if name == "place_near":
+            new_params = place(new_params, 3, sum(RAW), from_down)
+            new_params = place(new_params, 1, sum(RAW), from_up)
+    new_params = place(new_params, 2, sum(RAW), onward)
     return (new_params.reshape(reps * blocks, rows, width), new_accum)
 
 

time: 222 us -> 224 us (level)
  waiting for transfers between devices: 81.9 us -> 89.9 us
  starting transfers between devices: 70.9 us -> 65.9 us
    ppermute x2, waiting for transfers between devices: 18.2 us -> 0.01 us  [spread(): low_down = lax.ppermute(low, 'rep', down)]
    ppermute x2, waiting for transfers between devices: 5.6 us -> 23.3 us  [spread(): far_high = lax.ppermute(high_down, 'rep', down)]
    all_to_all x3, waiting for transfers between devices: 8.8 us -> 14.6 us  [local(): lax.all_to_all(outgoing, GROUP, split_axis=0, concat_axis=0, tiled=True)]
    reduce_sum x0 -> x2, other arithmetic: none -> 4.69 us  [the longest x1 4.57 us: local(): graft_blocks = jnp.sum(graft * graft, axis=(1, 2))]
    ppermute x1, waiting for transfers between devices: 0.01 us -> 4.44 us  [local(): from_down = lax.ppermute(last, 'rep', up)]
    add x1, other arithmetic: 4.4 us -> 0.01 us  [local(): sums = everywhere(sums + graft_row)]
    ppermute x9, waiting for transfers between devices: 11 us -> 6.74 us  [everywhere(): lax.ppermute(value, axis, ring(4, step))]
    ppermute x2, waiting for transfers between devices: 0.01 us -> 3.14 us  [spread(): low_up = lax.ppermute(low, 'rep', up)]
  transfers between devices with their start and end apart: 36 -> 36, of which waited for: 20 -> 20; matrix products, arithmetic and copies ran while one was open for 11% -> 10% of each run, Pallas kernels for 12% -> 12%
where the time goes in v7:
time: 224 us; the launch traced here: 222 us
  waiting for transfers between devices  89.9 us (40%)
  starting transfers between devices  65.9 us (29%)
  Pallas kernels  34.3 us (15%)
  other arithmetic  16.1 us (7%)
  local copies, waits for them, and re-layouts  15 us (7%)
    ppermute x2, waiting for transfers between devices, spread(): far_high = lax.ppermute(high_down, 'rep', down)  23.3 us
    all_to_all x3, starting transfers between devices, local(): lax.all_to_all(outgoing, GROUP, split_axis=0, concat_axis=0, tiled=True)  20.4 us
    ppermute x9, starting transfers between devices, everywhere(): lax.ppermute(value, axis, ring(4, step))  16.5 us
    all_to_all x3, waiting for transfers between devices, local(): lax.all_to_all(outgoing, GROUP, split_axis=0, concat_axis=0, tiled=True)  14.6 us
    ppermute x2, waiting for transfers between devices, spread(): high_up = lax.ppermute(high, 'rep', up)  10.6 us
    ppermute x2, waiting for transfers between devices, local(): near_up = lax.ppermute(to_up, 'rep', up)  10.5 us
    dynamic_update_slice x6, other arithmetic, place(): lax.dynamic_update_slice(whole, piece[None], (owner(offset), first, 0, 0))  8.72 us
    pallas_call x2, Pallas kernels, finish(): pl.pallas_call(body, grid_spec=pltpu.PrefetchScalarGridSpec(num_scalar_pr...  8.17 us
  transfers between devices with their start and end apart: 36, of which 20 were waited for; matrix products, arithmetic and copies ran while one was open for 10% of the time, Pallas kernels for 12%

profile of v7, /device:TPU:0, one launch (start us, length us, event | category | flops | bytes accessed | tf_op | source)
XLA Modules:
  0.0 222.1 jit_solution(1873027410251186143)
XLA Ops:
  14.4 3.1 %merge.3 = (bf16[24,32,384]{2,1,0:T(8,128)(2,1)}, bf16[24,32,384]{2,1,0:T(8,128)(2,1)}) custom-call(s32[4]{0:T(128)} %compare_select_fusion.who_ref, bf16[4,24,32,1024]{3,2,1,0:T(8,128)(2,1)} %bitcast.69, bf16[4,24,32,1024]{3,2,1,0:T(8,128)(2,1)} %bitcast.70, bf16[12,32,384]{2,1,0:T(8,128)(2,1)} %copy-done.11, bf16[12,32,384]{2,1,0:T(8,128)(2,1)} %copy-done.12), custom_call_target="tpu_custom_call" | custom-call | tf_op jit(solution)/shard_map/merge/pallas_call | solution.py:51
  25.0 3.6 %merge.2 = (bf16[24,32,640]{2,1,0:T(8,128)(2,1)}, bf16[24,32,640]{2,1,0:T(8,128)(2,1)}) custom-call(s32[4]{0:T(128)} %compare_select_fusion.who_ref, bf16[4,24,32,1024]{3,2,1,0:T(8,128)(2,1)} %bitcast.71, bf16[4,24,32,1024]{3,2,1,0:T(8,128)(2,1)} %bitcast.72, bf16[12,32,640]{2,1,0:T(8,128)(2,1)} %copy-done.9, bf16[12,32,640]{2,1,0:T(8,128)(2,1)} %copy-done.10), custom_call_target="tpu_custom_call" | custom-call | tf_op jit(solution)/shard_map/merge/pallas_call | solution.py:51
  32.3 3.8 %collective-permute-done.6.one = bf16[24,32,384]{2,1,0:T(8,128)(2,1)S(1)} collective-permute-done((bf16[24,32,384]{2,1,0:T(8,128)(2,1)}, bf16[24,32,384]{2,1,0:T(8,128)(2,1)S(1)}, u32[]{:S(2)}, u32[]{:S(2)}) %collective-permute-start.6) | collective-permute-done | bytes 589856 | tf_op jit(solution)/shard_map/ppermute | solution.py:282
  37.3 3.6 %shard_map.87 = (bf16[24,32,384]{2,1,0:T(8,128)(2,1)}, bf16[32,32,384]{2,1,0:T(8,128)(2,1)}) custom-call(s32[4]{0:T(128)} %compare_select_fusion.who_ref, s32[32]{0:T(128)} %get-tuple-element.46.table_ref, bf16[4,24,32,1024]{3,2,1,0:T(8,128)(2,1)} %bitcast.73, bf16[24,32,384]{2,1,0:T(8,128)(2,1)} %copy-done.7, bf16[24,32,384]{2,1,0:T(8,128)(2,1)} %copy-done.8), custom_call_target="tpu_custom_call" | custom-call | tf_op jit(solution)/shard_map/pallas_call | solution.py:80
  40.9 8.3 %all-to-all-start.1 = ((bf16[32,32,384]{2,1,0:T(8,128)(2,1)}), bf16[32,32,384]{2,1,0:T(8,128)(2,1)S(1)}, u32[]{:S(2)}, u32[]{:S(2)}) async-start(bf16[32,32,384]{2,1,0:T(8,128)(2,1)} %get-tuple-element.27), calls=%async_computation.1 | async-start | bytes 1572864 | tf_op jit(solution)/shard_map/all_to_all | solution.py:286
  49.2 6.7 %collective-permute-done.2.one = bf16[24,32,640]{2,1,0:T(8,128)(2,1)S(1)} collective-permute-done((bf16[24,32,640]{2,1,0:T(8,128)(2,1)}, bf16[24,32,640]{2,1,0:T(8,128)(2,1)S(1)}, u32[]{:S(2)}, u32[]{:S(2)}) %collective-permute-start.2) | collective-permute-done | bytes 983072 | tf_op jit(solution)/shard_map/ppermute | solution.py:282
  57.9 4.6 %shard_map.86 = (bf16[24,32,640]{2,1,0:T(8,128)(2,1)}, bf16[32,32,640]{2,1,0:T(8,128)(2,1)}) custom-call(s32[4]{0:T(128)} %compare_select_fusion.who_ref, s32[32]{0:T(128)} %get-tuple-element.46.table_ref, bf16[4,24,32,1024]{3,2,1,0:T(8,128)(2,1)} %bitcast.74, bf16[24,32,640]{2,1,0:T(8,128)(2,1)} %copy-done.5, bf16[24,32,640]{2,1,0:T(8,128)(2,1)} %copy-done.6), custom_call_target="tpu_custom_call" | custom-call | tf_op jit(solution)/shard_map/pallas_call | solution.py:80
  63.1 7.9 %all-to-all-start = ((bf16[32,32,640]{2,1,0:T(8,128)(2,1)}), bf16[32,32,640]{2,1,0:T(8,128)(2,1)S(1)}, u32[]{:S(2)}, u32[]{:S(2)}) async-start(bf16[32,32,640]{2,1,0:T(8,128)(2,1)} %get-tuple-element.24), calls=%async_computation | async-start | bytes 2621440 | tf_op jit(solution)/shard_map/all_to_all | solution.py:286
  73.2 3.6 %left_times.1.rest_0_ = bf16[1024,384]{1,0:T(8,128)(2,1)} custom-call(bf16[1024,1024]{1,0:T(8,128)(2,1)} %bitcast.75, bf16[1024,384]{1,0:T(8,128)(2,1)} %bitcast.78), custom_call_target="tpu_custom_call" | custom-call | tf_op jit(solution)/shard_map/left_times/pallas_call | solution.py:106
  76.8 14.0 %all-to-all-done = bf16[32,32,640]{2,1,0:T(8,128)(2,1)S(1)} async-done(((bf16[32,32,640]{2,1,0:T(8,128)(2,1)}), bf16[32,32,640]{2,1,0:T(8,128)(2,1)S(1)}, u32[]{:S(2)}, u32[]{:S(2)}) %all-to-all-start) | async-done | bytes 1310752 | tf_op jit(solution)/shard_map/all_to_all | solution.py:286
  91.9 7.7 %products.1 = (bf16[1024,1024]{1,0:T(8,128)(2,1)}, f32[2,128]{1,0:T(2,128)}) custom-call(bf16[1024,1024]{1,0:T(8,128)(2,1)} %bitcast.76, bf16[1024,1024]{1,0:T(8,128)(2,1)} %bitcast.79, bf16[1024,640]{1,0:T(8,128)(2,1)} %bitcast.77, f32[1,128]{1,0:T(1,128)} %pad.8.layer_ref, bf16[1024,384]{1,0:T(8,128)(2,1)} %left_times.1.rest_0_), custom_call_target="tpu_custom_call" | custom-call | tf_op jit(solution)/shard_map/products/pallas_call | solution.py:146
  99.6 4.1 %all-to-all-start.2 = ((bf16[32,32,1024]{2,1,0:T(8,128)(2,1)}), bf16[32,32,1024]{2,1,0:T(8,128)(2,1)S(1)}, u32[]{:S(2)}, u32[]{:S(2)}) async-start(bf16[32,32,1024]{2,1,0:T(8,128)(2,1)} %bitcast.80), calls=%async_computation.2 | async-start | bytes 4194304 | tf_op jit(solution)/shard_map/all_to_all | solution.py:321
  103.8 4.6 %fusion.2 = (f32[24]{0:T(128)S(1)}, f32[24,32,1024]{2,1,0:T(8,128)}) fusion(bf16[24,32,640]{2,1,0:T(8,128)(2,1)S(1)} %copy-done.4, bf16[24,32,384]{2,1,0:T(8,128)(2,1)} %get-tuple-element.35, f32[24,32,1024]{2,1,0:T(8,128)} %param.9), kind=kLoop, calls=%fused_computation.4 | loop fusion | flops 7077864 | bytes 7864416 | tf_op jit(solution)/shard_map/reduce_sum | solution.py:316
  118.1 3.3 %collective-permute-start.12 = (f32[2,128]{1,0:T(2,128)S(1)}, f32[2,128]{1,0:T(2,128)S(1)}, u32[]{:S(2)}, u32[]{:S(2)}) collective-permute-start(f32[2,128]{1,0:T(2,128)S(1)} %add_add_fusion.2), channel_id=1, source_target_pairs={{0,64},{32,96},{64,0},{96,32},{1,65},{33,97},{65,1},{97,33},{2,66}... | collective-permute-start | bytes 3080 | tf_op jit(solution)/shard_map/ppermute | solution.py:237
  125.2 5.6 %collective-permute-done.12 = f32[2,128]{1,0:T(2,128)S(1)} collective-permute-done((f32[2,128]{1,0:T(2,128)S(1)}, f32[2,128]{1,0:T(2,128)S(1)}, u32[]{:S(2)}, u32[]{:S(2)}) %collective-permute-start.12) | collective-permute-done | bytes 1056 | tf_op jit(solution)/shard_map/ppermute | solution.py:237
  147.0 5.1 %update.1 = (bf16[8,32,1024]{2,1,0:T(8,128)(2,1)}, bf16[4,24,32,1024]{3,2,1,0:T(8,128)(2,1)}) custom-call(s32[4]{0:T(128)} %compare_select_fusion.who_ref, s32[24]{0:T(128)} %select_reduce_fusion.position_ref, f32[24]{0:T(128)} %fusion.21.scale_ref, bf16[32,32,1024]{2,1,0:T(8,128)(2,1)} %copy-done, bf16[24,32,1024]{2,1,0:T(8,128)(2,1)} %params_ref.1), custom_call_target="tpu_custom_call" | custom-call | tf_op jit(solution)/shard_map/update/pallas_call | solution.py:211
  154.2 10.6 %collective-permute-done.19 = bf16[12,32,1024]{2,1,0:T(8,128)(2,1)S(1)} collective-permute-done((bf16[12,32,1024]{2,1,0:T(8,128)(2,1)}, bf16[12,32,1024]{2,1,0:T(8,128)(2,1)S(1)}, u32[]{:S(2)}, u32[]{:S(2)}) %collective-permute-start.19) | collective-permute-done | bytes 786464 | tf_op jit(solution)/shard_map/ppermute | solution.py:244
  167.3 3.2 %collective-permute-start.25 = (bf16[4,32,1024]{2,1,0:T(8,128)(2,1)}, bf16[4,32,1024]{2,1,0:T(8,128)(2,1)S(1)}, u32[]{:S(2)}, u32[]{:S(2)}) collective-permute-start(bf16[4,32,1024]{2,1,0:T(8,128)(2,1)} %get-tuple-element.40), channel_id=1, source_target_pairs={{0,3},{1,0},{2,1},{3,2},{4,7},{5,4},{6,5},{7,6},{8,11},{9,8},{10,9... | collective-permute-start | bytes 786440 | tf_op jit(solution)/shard_map/ppermute | solution.py:247
  173.0 3.1 %collective-permute-done.23 = bf16[4,32,1024]{2,1,0:T(8,128)(2,1)S(1)} collective-permute-done((bf16[4,32,1024]{2,1,0:T(8,128)(2,1)}, bf16[4,32,1024]{2,1,0:T(8,128)(2,1)S(1)}, u32[]{:S(2)}, u32[]{:S(2)}) %collective-permute-start.23) | collective-permute-done | bytes 262176 | tf_op jit(solution)/shard_map/ppermute | solution.py:246
  181.0 4.4 %collective-permute-done.26 = bf16[8,32,1024]{2,1,0:T(8,128)(2,1)S(1)} collective-permute-done((bf16[8,32,1024]{2,1,0:T(8,128)(2,1)}, bf16[8,32,1024]{2,1,0:T(8,128)(2,1)S(1)}, u32[]{:S(2)}, u32[]{:S(2)}) %collective-permute-start.26) | collective-permute-done | bytes 524320 | tf_op jit(solution)/shard_map/ppermute | solution.py:331
  186.3 4.6 %collective-permute-done.27 = bf16[8,32,1024]{2,1,0:T(8,128)(2,1)S(1)} collective-permute-done((bf16[8,32,1024]{2,1,0:T(8,128)(2,1)S(1)}, bf16[8,32,1024]{2,1,0:T(8,128)(2,1)S(1)}, u32[]{:S(2)}, u32[]{:S(2)}) %collective-permute-start.27) | collective-permute-done | bytes 524320 | tf_op jit(solution)/shard_map/ppermute | solution.py:332
  191.8 4.0 %collective-permute-done.29 = bf16[4,32,1024]{2,1,0:T(8,128)(2,1)S(1)} collective-permute-done((bf16[4,32,1024]{2,1,0:T(8,128)(2,1)S(1)}, bf16[4,32,1024]{2,1,0:T(8,128)(2,1)S(1)}, u32[]{:S(2)}, u32[]{:S(2)}) %collective-permute-start.29) | collective-permute-done | bytes 262176 | tf_op jit(solution)/shard_map/ppermute | solution.py:249
  196.7 11.1 %collective-permute-done.30 = bf16[12,32,1024]{2,1,0:T(8,128)(2,1)S(1)} collective-permute-done((bf16[12,32,1024]{2,1,0:T(8,128)(2,1)}, bf16[12,32,1024]{2,1,0:T(8,128)(2,1)S(1)}, u32[]{:S(2)}, u32[]{:S(2)}) %collective-permute-start.30) | collective-permute-done | bytes 786464 | tf_op jit(solution)/shard_map/ppermute | solution.py:248
  207.8 12.2 %collective-permute-done.31 = bf16[12,32,1024]{2,1,0:T(8,128)(2,1)S(1)} collective-permute-done((bf16[12,32,1024]{2,1,0:T(8,128)(2,1)S(1)}, bf16[12,32,1024]{2,1,0:T(8,128)(2,1)S(1)}, u32[]{:S(2)}, u32[]{:S(2)}) %collective-permute-start.31) | collective-permute-done | bytes 786464 | tf_op jit(solution)/shard_map/ppermute | solution.py:248
  (125 shorter events, 78.3 us)
Async XLA Ops:
  6.3 17.1 %collective-permute-start = (bf16[12,32,640]{2,1,0:T(8,128)(2,1)S(1)}, bf16[12,32,640]{2,1,0:T(8,128)(2,1)S(1)}, u32[]{:S(2)}, u32[]{:S(2)}) collective-permute-start(bf16[12,32,640]{2,1,0:T(8,128)(2,1)S(1)} %get-tuple-element.51), channel_id=1, source_target_pairs={{0,1},{1,2},{2,3},{3,0},{4,5},{5,6},{6,7},{7,4},{8,9},{9,10},{10,1... | collective-permute-start | bytes 1474568 | tf_op jit(solution)/shard_map/ppermute | solution.py:279
  6.8 17.0 %collective-permute-start.1 = (bf16[12,32,640]{2,1,0:T(8,128)(2,1)S(1)}, bf16[12,32,640]{2,1,0:T(8,128)(2,1)S(1)}, u32[]{:S(2)}, u32[]{:S(2)}) collective-permute-start(bf16[12,32,640]{2,1,0:T(8,128)(2,1)S(1)} %get-tuple-element.50), channel_id=1, source_target_pairs={{0,3},{1,0},{2,1},{3,2},{4,7},{5,4},{6,5},{7,6},{8,11},{9,8},{10,9... | collective-permute-start | bytes 1474568 | tf_op jit(solution)/shard_map/ppermute | solution.py:280
  17.4 18.7 %collective-permute-start.6 = (bf16[24,32,384]{2,1,0:T(8,128)(2,1)}, bf16[24,32,384]{2,1,0:T(8,128)(2,1)S(1)}, u32[]{:S(2)}, u32[]{:S(2)}) collective-permute-start(bf16[24,32,384]{2,1,0:T(8,128)(2,1)} %get-tuple-element.25), channel_id=1, source_target_pairs={{0,1},{1,2},{2,3},{3,0},{4,5},{5,6},{6,7},{7,4},{8,9},{9,10},{10,1... | collective-permute-start | bytes 1769480 | tf_op jit(solution)/shard_map/ppermute | solution.py:282
  18.6 17.9 %collective-permute-start.7 = (bf16[24,32,384]{2,1,0:T(8,128)(2,1)}, bf16[24,32,384]{2,1,0:T(8,128)(2,1)S(1)}, u32[]{:S(2)}, u32[]{:S(2)}) collective-permute-start(bf16[24,32,384]{2,1,0:T(8,128)(2,1)} %get-tuple-element.26), channel_id=1, source_target_pairs={{0,3},{1,0},{2,1},{3,2},{4,7},{5,4},{6,5},{7,6},{8,11},{9,8},{10,9... | collective-permute-start | bytes 1769480 | tf_op jit(solution)/shard_map/ppermute | solution.py:283
  28.6 27.4 %collective-permute-start.2 = (bf16[24,32,640]{2,1,0:T(8,128)(2,1)}, bf16[24,32,640]{2,1,0:T(8,128)(2,1)S(1)}, u32[]{:S(2)}, u32[]{:S(2)}) collective-permute-start(bf16[24,32,640]{2,1,0:T(8,128)(2,1)} %get-tuple-element.22), channel_id=1, source_target_pairs={{0,1},{1,2},{2,3},{3,0},{4,5},{5,6},{6,7},{7,4},{8,9},{9,10},{10,1... | collective-permute-start | bytes 2949128 | tf_op jit(solution)/shard_map/ppermute | solution.py:282
  29.7 26.4 %collective-permute-start.3 = (bf16[24,32,640]{2,1,0:T(8,128)(2,1)}, bf16[24,32,640]{2,1,0:T(8,128)(2,1)S(1)}, u32[]{:S(2)}, u32[]{:S(2)}) collective-permute-start(bf16[24,32,640]{2,1,0:T(8,128)(2,1)} %get-tuple-element.23), channel_id=1, source_target_pairs={{0,3},{1,0},{2,1},{3,2},{4,7},{5,4},{6,5},{7,6},{8,11},{9,8},{10,9... | collective-permute-start | bytes 2949128 | tf_op jit(solution)/shard_map/ppermute | solution.py:283
  40.9 22.3 %all-to-all-start.1 = ((bf16[32,32,384]{2,1,0:T(8,128)(2,1)}), bf16[32,32,384]{2,1,0:T(8,128)(2,1)S(1)}, u32[]{:S(2)}, u32[]{:S(2)}) async-start(bf16[32,32,384]{2,1,0:T(8,128)(2,1)} %get-tuple-element.27), calls=%async_computation.1 | async-start | bytes 1572864 | tf_op jit(solution)/shard_map/all_to_all | solution.py:286
  63.1 27.7 %all-to-all-start = ((bf16[32,32,640]{2,1,0:T(8,128)(2,1)}), bf16[32,32,640]{2,1,0:T(8,128)(2,1)S(1)}, u32[]{:S(2)}, u32[]{:S(2)}) async-start(bf16[32,32,640]{2,1,0:T(8,128)(2,1)} %get-tuple-element.24), calls=%async_computation | async-start | bytes 2621440 | tf_op jit(solution)/shard_map/all_to_all | solution.py:286
  99.6 39.0 %all-to-all-start.2 = ((bf16[32,32,1024]{2,1,0:T(8,128)(2,1)}), bf16[32,32,1024]{2,1,0:T(8,128)(2,1)S(1)}, u32[]{:S(2)}, u32[]{:S(2)}) async-start(bf16[32,32,1024]{2,1,0:T(8,128)(2,1)} %bitcast.80), calls=%async_computation.2 | async-start | bytes 4194304 | tf_op jit(solution)/shard_map/all_to_all | solution.py:321
  113.6 40.1 %collective-permute-start.18 = (bf16[12,32,1024]{2,1,0:T(8,128)(2,1)S(1)}, bf16[12,32,1024]{2,1,0:T(8,128)(2,1)}, u32[]{:S(2)}, u32[]{:S(2)}) collective-permute-start(bf16[12,32,1024]{2,1,0:T(8,128)(2,1)S(1)} %slice.14), channel_id=1, source_target_pairs={{0,1},{1,2},{2,3},{3,0},{4,5},{5,6},{6,7},{7,4},{8,9},{9,10},{10,1... | collective-permute-start | bytes 2359304 | tf_op jit(solution)/shard_map/ppermute | solution.py:244
  114.7 52.6 %collective-permute-start.20 = (bf16[12,32,1024]{2,1,0:T(8,128)(2,1)S(1)}, bf16[12,32,1024]{2,1,0:T(8,128)(2,1)}, u32[]{:S(2)}, u32[]{:S(2)}) collective-permute-start(bf16[12,32,1024]{2,1,0:T(8,128)(2,1)S(1)} %slice.14), channel_id=1, source_target_pairs={{0,3},{1,0},{2,1},{3,2},{4,7},{5,4},{6,5},{7,6},{8,11},{9,8},{10,9... | collective-permute-start | bytes 2359304 | tf_op jit(solution)/shard_map/ppermute | solution.py:245
  118.1 12.8 %collective-permute-start.12 = (f32[2,128]{1,0:T(2,128)S(1)}, f32[2,128]{1,0:T(2,128)S(1)}, u32[]{:S(2)}, u32[]{:S(2)}) collective-permute-start(f32[2,128]{1,0:T(2,128)S(1)} %add_add_fusion.2), channel_id=1, source_target_pairs={{0,64},{32,96},{64,0},{96,32},{1,65},{33,97},{65,1},{97,33},{2,66}... | collective-permute-start | bytes 3080 | tf_op jit(solution)/shard_map/ppermute | solution.py:237
  138.0 14.2 %collective-permute-start.22 = (bf16[4,32,1024]{2,1,0:T(8,128)(2,1)S(1)}, bf16[4,32,1024]{2,1,0:T(8,128)(2,1)S(1)}, u32[]{:S(2)}, u32[]{:S(2)}) collective-permute-start(bf16[4,32,1024]{2,1,0:T(8,128)(2,1)S(1)} %slice.15), channel_id=1, source_target_pairs={{0,1},{1,2},{2,3},{3,0},{4,5},{5,6},{6,7},{7,4},{8,9},{9,10},{10,1... | collective-permute-start | bytes 786440 | tf_op jit(solution)/shard_map/ppermute | solution.py:246
  143.0 21.9 %collective-permute-start.19 = (bf16[12,32,1024]{2,1,0:T(8,128)(2,1)}, bf16[12,32,1024]{2,1,0:T(8,128)(2,1)S(1)}, u32[]{:S(2)}, u32[]{:S(2)}) collective-permute-start(bf16[12,32,1024]{2,1,0:T(8,128)(2,1)} %get-tuple-element.39), channel_id=1, source_target_pairs={{0,1},{1,2},{2,3},{3,0},{4,5},{5,6},{6,7},{7,4},{8,9},{9,10},{10,1... | collective-permute-start | bytes 2359304 | tf_op jit(solution)/shard_map/ppermute | solution.py:244
  144.4 26.2 %collective-permute-start.21 = (bf16[12,32,1024]{2,1,0:T(8,128)(2,1)}, bf16[12,32,1024]{2,1,0:T(8,128)(2,1)S(1)}, u32[]{:S(2)}, u32[]{:S(2)}) collective-permute-start(bf16[12,32,1024]{2,1,0:T(8,128)(2,1)} %get-tuple-element.39), channel_id=1, source_target_pairs={{0,3},{1,0},{2,1},{3,2},{4,7},{5,4},{6,5},{7,6},{8,11},{9,8},{10,9... | collective-permute-start | bytes 2359304 | tf_op jit(solution)/shard_map/ppermute | solution.py:245
  152.1 26.3 %collective-permute-start.24 = (bf16[4,32,1024]{2,1,0:T(8,128)(2,1)S(1)}, bf16[4,32,1024]{2,1,0:T(8,128)(2,1)S(1)}, u32[]{:S(2)}, u32[]{:S(2)}) collective-permute-start(bf16[4,32,1024]{2,1,0:T(8,128)(2,1)S(1)} %slice.15), channel_id=1, source_target_pairs={{0,3},{1,0},{2,1},{3,2},{4,7},{5,4},{6,5},{7,6},{8,11},{9,8},{10,9... | collective-permute-start | bytes 786440 | tf_op jit(solution)/shard_map/ppermute | solution.py:247
  153.7 38.1 %collective-permute-start.28 = (bf16[4,32,1024]{2,1,0:T(8,128)(2,1)S(1)}, bf16[4,32,1024]{2,1,0:T(8,128)(2,1)S(1)}, u32[]{:S(2)}, u32[]{:S(2)}) collective-permute-start(bf16[4,32,1024]{2,1,0:T(8,128)(2,1)S(1)} %collective-permute-done.22), channel_id=1, source_target_pairs={{0,1},{1,2},{2,3},{3,0},{4,5},{5,6},{6,7},{7,4},{8,9},{9,10},{10,1... | collective-permute-start | bytes 786440 | tf_op jit(solution)/shard_map/ppermute | solution.py:249
  164.9 11.2 %collective-permute-start.23 = (bf16[4,32,1024]{2,1,0:T(8,128)(2,1)}, bf16[4,32,1024]{2,1,0:T(8,128)(2,1)S(1)}, u32[]{:S(2)}, u32[]{:S(2)}) collective-permute-start(bf16[4,32,1024]{2,1,0:T(8,128)(2,1)} %get-tuple-element.40), channel_id=1, source_target_pairs={{0,1},{1,2},{2,3},{3,0},{4,5},{5,6},{6,7},{7,4},{8,9},{9,10},{10,1... | collective-permute-start | bytes 786440 | tf_op jit(solution)/shard_map/ppermute | solution.py:246
  167.3 11.9 %collective-permute-start.25 = (bf16[4,32,1024]{2,1,0:T(8,128)(2,1)}, bf16[4,32,1024]{2,1,0:T(8,128)(2,1)S(1)}, u32[]{:S(2)}, u32[]{:S(2)}) collective-permute-start(bf16[4,32,1024]{2,1,0:T(8,128)(2,1)} %get-tuple-element.40), channel_id=1, source_target_pairs={{0,3},{1,0},{2,1},{3,2},{4,7},{5,4},{6,5},{7,6},{8,11},{9,8},{10,9... | collective-permute-start | bytes 786440 | tf_op jit(solution)/shard_map/ppermute | solution.py:247
  170.5 14.9 %collective-permute-start.26 = (bf16[8,32,1024]{2,1,0:T(8,128)(2,1)}, bf16[8,32,1024]{2,1,0:T(8,128)(2,1)S(1)}, u32[]{:S(2)}, u32[]{:S(2)}) collective-permute-start(bf16[8,32,1024]{2,1,0:T(8,128)(2,1)} %get-tuple-element.41), channel_id=1, source_target_pairs={{0,1},{1,2},{2,3},{3,0},{4,5},{5,6},{6,7},{7,4},{8,9},{9,10},{10,1... | collective-permute-start | bytes 1572872 | tf_op jit(solution)/shard_map/ppermute | solution.py:331
  176.1 14.8 %collective-permute-start.27 = (bf16[8,32,1024]{2,1,0:T(8,128)(2,1)S(1)}, bf16[8,32,1024]{2,1,0:T(8,128)(2,1)S(1)}, u32[]{:S(2)}, u32[]{:S(2)}) collective-permute-start(bf16[8,32,1024]{2,1,0:T(8,128)(2,1)S(1)} %copy-done.16), channel_id=1, source_target_pairs={{0,3},{1,0},{2,1},{3,2},{4,7},{5,4},{6,5},{7,6},{8,11},{9,8},{10,9... | collective-permute-start | bytes 1572872 | tf_op jit(solution)/shard_map/ppermute | solution.py:332
  178.5 29.3 %collective-permute-start.30 = (bf16[12,32,1024]{2,1,0:T(8,128)(2,1)}, bf16[12,32,1024]{2,1,0:T(8,128)(2,1)S(1)}, u32[]{:S(2)}, u32[]{:S(2)}) collective-permute-start(bf16[12,32,1024]{2,1,0:T(8,128)(2,1)} %collective-permute-done.20), channel_id=1, source_target_pairs={{0,3},{1,0},{2,1},{3,2},{4,7},{5,4},{6,5},{7,6},{8,11},{9,8},{10,9... | collective-permute-start | bytes 2359304 | tf_op jit(solution)/shard_map/ppermute | solution.py:248
  179.2 40.7 %collective-permute-start.31 = (bf16[12,32,1024]{2,1,0:T(8,128)(2,1)S(1)}, bf16[12,32,1024]{2,1,0:T(8,128)(2,1)S(1)}, u32[]{:S(2)}, u32[]{:S(2)}) collective-permute-start(bf16[12,32,1024]{2,1,0:T(8,128)(2,1)S(1)} %collective-permute-done.21), channel_id=1, source_target_pairs={{0,3},{1,0},{2,1},{3,2},{4,7},{5,4},{6,5},{7,6},{8,11},{9,8},{10,9... | collective-permute-start | bytes 2359304 | tf_op jit(solution)/shard_map/ppermute | solution.py:248
  190.9 30.4 %collective-permute-start.32 = (bf16[8,32,1024]{2,1,0:T(8,128)(2,1)S(1)}, bf16[8,32,1024]{2,1,0:T(8,128)(2,1)S(1)}, u32[]{:S(2)}, u32[]{:S(2)}) collective-permute-start(bf16[8,32,1024]{2,1,0:T(8,128)(2,1)S(1)} %collective-permute-done.26), channel_id=1, source_target_pairs={{0,1},{1,2},{2,3},{3,0},{4,5},{5,6},{6,7},{7,4},{8,9},{9,10},{10,1... | collective-permute-start | bytes 1572872 | tf_op jit(solution)/shard_map/ppermute | solution.py:333
  (29 other events, 184.1 us)

commit v8 on v7

--- a/solution.py
+++ b/solution.py
@@ -12,7 +12,7 @@
 GROUP = ("group_0", "group_1", "group_2")
 EVERY = ("group_0", "group_1", "group_2", "rep")
 SENT = ((0, 384), (384, 640))
-RAW = (4, 12)
+RAW = 512
 
 
 step_rate = 0.5
@@ -123,14 +123,16 @@
     last = SENT[-1][0]
 
     def body(left_ref, right_ref, owned_ref, layer_ref, *rest):
-        before, (out, sums, mid) = rest[: len(earlier)], rest[len(earlier) :]
+        before, (first, second, sums, mid) = rest[: len(earlier)], rest[len(earlier) :]
         mid[:, last : last + cols] = jnp.dot(
             left_ref[...], owned_ref[...], preferred_element_type=f32
         ).astype(bf16)
         for ref, (start, size) in zip(before, SENT):
             mid[:, start : start + size] = ref[...]
-        out[...] = jnp.dot(mid[...], right_ref[...], preferred_element_type=f32).astype(bf16)
-        wide = out[...].astype(f32)
+        product = jnp.dot(mid[...], right_ref[...], preferred_element_type=f32).astype(bf16)
+        first[...] = product[:, :RAW]
+        second[...] = product[:, RAW:]
+        wide = product.astype(f32)
         squares = jnp.sum(jnp.sum(wide * wide, axis=0, keepdims=True), axis=1, keepdims=True)
 
         @pl.when(pl.program_id(0) == 0)
@@ -153,82 +155,101 @@
             row,
             *[pl.BlockSpec((tile, e.shape[1]), lambda i: (i, 0)) for e in earlier],
         ],
-        out_specs=[pl.BlockSpec((tile, order), lambda i: (i, 0)), pl.BlockSpec((2, LANES), lambda i: (0, 0))],
-        out_shape=[jax.ShapeDtypeStruct((order, order), bf16), jax.ShapeDtypeStruct((2, LANES), f32)],
+        out_specs=[
+            pl.BlockSpec((tile, RAW), lambda i: (i, 0)),
+            pl.BlockSpec((tile, order - RAW), lambda i: (i, 0)),
+            pl.BlockSpec((2, LANES), lambda i: (0, 0)),
+        ],
+        out_shape=[
+            jax.ShapeDtypeStruct((order, RAW), bf16),
+            jax.ShapeDtypeStruct((order, order - RAW), bf16),
+            jax.ShapeDtypeStruct((2, LANES), f32),
+        ],
         scratch_shapes=[pltpu.VMEM((tile, order), bf16)],
         name="products",
     )(left, right, owned, layer_row, *earlier)
 
 
-def fetch(position_ref, returned_ref, target, sems, blocks):
-    copies = []
-    for block in blocks:
-        copy = pltpu.make_async_copy(returned_ref.at[position_ref[block]], target(block), sems.at[block])
-        copy.start()
-        copies.append(copy)
-    return copies
-
-
 def pick(position, returned):
+    blocks = position.shape[0]
+    half = blocks // 2
     _, rows, cols = returned.shape
-    split, total = RAW[0], sum(RAW)
 
     def body(position_ref, returned_ref, low, high, sems):
-        def target(block):
-            return low.at[block] if block < split else high.at[block - split]
-
-        for copy in fetch(position_ref, returned_ref, target, sems, range(total)):
+        copies = []
+        for block in range(blocks):
+            out = low.at[block] if block < half else high.at[block - half]
+            copies.append(pltpu.make_async_copy(returned_ref.at[position_ref[block]], out, sems.at[block]))
+            copies[-1].start()
+        for copy in copies:
             copy.wait()
 
+    piece = pl.BlockSpec((half, rows, cols), lambda i, p: (0, 0, 0))
+    shape = jax.ShapeDtypeStruct((half, rows, cols), bf16)
     return pl.pallas_call(
         body,
         grid_spec=pltpu.PrefetchScalarGridSpec(
             num_scalar_prefetch=1,
             grid=(1,),
             in_specs=[pl.BlockSpec(memory_space=pltpu.HBM)],
-            out_specs=[pl.BlockSpec((size, rows, cols), lambda i, p: (0, 0, 0)) for size in RAW],
-            scratch_shapes=[pltpu.SemaphoreType.DMA((total,))],
-        ),
-        out_shape=[jax.ShapeDtypeStruct((size, rows, cols), bf16) for size in RAW],
+            out_specs=[piece, piece],
+            scratch_shapes=[pltpu.SemaphoreType.DMA((blocks,))],
+        ),
+        out_shape=[shape, shape],
         name="pick",
     )(position, returned)
 
 
 def update(who, position, scale, returned, params, reps):
-    blocks, rows, cols = params.shape
-    first = sum(RAW)
-
-    def body(who_ref, position_ref, scale_ref, returned_ref, params_ref, last, whole, picked, sems):
-        copies = fetch(position_ref, returned_ref, lambda block: picked.at[block], sems, range(blocks))
-        for block, copy in enumerate(copies):
-            copy.wait()
+    blocks, rows, width = params.shape
+    half = blocks // 2
+
+    def body(who_ref, position_ref, scale_ref, one, two, params_ref, low, high, whole, picked, sems):
+        copies = []
+        for block in range(blocks):
+            slot = position_ref[block]
+            pair = (
+                pltpu.make_async_copy(one.at[slot], picked.at[block, :, pl.ds(0, RAW)], sems.at[0, block]),
+                pltpu.make_async_copy(
+                    two.at[slot], picked.at[block, :, pl.ds(RAW, width - RAW)], sems.at[1, block]
+                ),
+            )
+            for copy in pair:
+                copy.start()
+            copies.append(pair)
+        for block, pair in enumerate(copies):
+            for copy in pair:
+                copy.wait()
             change = scale_ref[block] * picked[block].astype(f32)
             new = (params_ref[block].astype(f32) - change).astype(bf16)
             whole[0, block] = new
-            if block >= first:
-                last[block - first] = new
-
+            if block < half:
+                low[block] = new[:, RAW:]
+            else:
+                high[block - half] = new[:, RAW:]
+
+    hbm = pl.BlockSpec(memory_space=pltpu.HBM)
+    piece = pl.BlockSpec((half, rows, width - RAW), lambda i, w, p, s: (0, 0, 0))
+    shape = jax.ShapeDtypeStruct((half, rows, width - RAW), bf16)
     return pl.pallas_call(
         body,
         grid_spec=pltpu.PrefetchScalarGridSpec(
             num_scalar_prefetch=3,
             grid=(1,),
-            in_specs=[
-                pl.BlockSpec(memory_space=pltpu.HBM),
-                pl.BlockSpec((blocks, rows, cols), lambda i, w, p, s: (0, 0, 0)),
+            in_specs=[hbm, hbm, pl.BlockSpec((blocks, rows, width), lambda i, w, p, s: (0, 0, 0))],
+            out_specs=[
+                piece,
+                piece,
+                pl.BlockSpec((1, blocks, rows, width), lambda i, w, p, s: (w[0], 0, 0, 0)),
             ],
-            out_specs=[
-                pl.BlockSpec((blocks - first, rows, cols), lambda i, w, p, s: (0, 0, 0)),
-                pl.BlockSpec((1, blocks, rows, cols), lambda i, w, p, s: (w[0], 0, 0, 0)),
+            scratch_shapes=[
+                pltpu.VMEM((blocks, rows, width), bf16),
+                pltpu.SemaphoreType.DMA((2, blocks)),
             ],
-            scratch_shapes=[pltpu.VMEM((blocks, rows, cols), bf16), pltpu.SemaphoreType.DMA((blocks,))],
-        ),
-        out_shape=[
-            jax.ShapeDtypeStruct((blocks - first, rows, cols), bf16),
-            jax.ShapeDtypeStruct((reps, blocks, rows, cols), bf16),
-        ],
+        ),
+        out_shape=[shape, shape, jax.ShapeDtypeStruct((reps, blocks, rows, width), bf16)],
         name="update",
-    )(who, position, scale, returned, params)
+    )(who, position, scale, *returned, params)
 
 
 def everywhere(value):
@@ -241,16 +262,16 @@
 
 def spread(low, high, reps):
     up, down = ring(reps, 1), ring(reps, -1)
+    low_up = lax.ppermute(low, "rep", up)
+    high_down = lax.ppermute(high, "rep", down)
     high_up = lax.ppermute(high, "rep", up)
-    high_down = lax.ppermute(high, "rep", down)
-    low_up = lax.ppermute(low, "rep", up)
     low_down = lax.ppermute(low, "rep", down)
+    far_low = lax.ppermute(low_up, "rep", up)
     far_high = lax.ppermute(high_down, "rep", down)
-    far_low = lax.ppermute(low_up, "rep", up)
     return (
+        (3, 0, low_up),
+        (1, 1, high_down),
         (3, 1, high_up),
-        (1, 1, high_down),
-        (3, 0, low_up),
         (1, 0, low_down),
         (2, 0, far_low),
         (2, 1, far_high),
@@ -288,7 +309,7 @@
             earlier.append(left_times(left, owned))
         owned = arrived.reshape(group_size * rows, cols)
 
-    old_low, old_high = params[: RAW[0]], params[RAW[0] : sum(RAW)]
+    old_low, old_high = params[:half, :, :RAW], params[half:, :, :RAW]
     ahead = spread(old_low, old_high, reps)
 
     onehots = (layer_of[:, None] == jnp.arange(LAYERS, dtype=jnp.int32)[None, :]).astype(f32)
@@ -316,36 +337,27 @@
     graft_blocks = jnp.sum(graft * graft, axis=(1, 2))
     graft_layer = jnp.sum(onehot * graft_blocks[:, None], axis=0)
     graft_row = jnp.pad(graft_layer[None, :], ((0, 1), (0, LANES - LAYERS)))
-    precond, sums = products(left, right, owned, earlier, layer_row)
-    outgoing = precond.reshape(group_size, rows, width)
-    returned = lax.all_to_all(outgoing, GROUP, split_axis=0, concat_axis=0, tiled=True)
+    *preconds, sums = products(left, right, owned, earlier, layer_row)
+    returned = []
+    for precond in preconds:
+        outgoing = precond.reshape(group_size, rows, precond.shape[1])
+        returned.append(lax.all_to_all(outgoing, GROUP, split_axis=0, concat_axis=0, tiled=True))
     sums = everywhere(sums + graft_row)
     layer_scale = jnp.sqrt(sums[0, :LAYERS]) * lax.rsqrt(sums[1, :LAYERS] + 1e-06)
     scales = (step_rate * jnp.sum(onehots * layer_scale[None, :], axis=1)).reshape(reps, blocks)
 
-    def owner(offset):
-        return lax.rem(me + offset, reps)
-
-    changes = spread(*pick(position, returned), reps)
-    last, new_params = update(who, position, scales[me], returned, params, reps)
-    from_down = lax.ppermute(last, "rep", up)
-    from_up = lax.ppermute(last, "rep", down)
-    onward = lax.ppermute(from_down, "rep", up)
-
-    def place(whole, offset, first, piece):
-        return lax.dynamic_update_slice(whole, piece[None], (owner(offset), first, 0, 0))
-
-    pairs = list(zip(ahead, changes))
-    for group, name in ((pairs[:4], "place_near"), (pairs[4:], "place_far")):
-        for (offset, part, old), (_, _, change) in group:
-            first = RAW[0] * part
-            scale = lax.dynamic_slice(scales, (owner(offset), first), (1, RAW[part]))[0, :, None, None]
-            new = (old.astype(f32) - scale * change.astype(f32)).astype(bf16)
-            new_params = place(new_params, offset, first, new)
-        if name == "place_near":
-            new_params = place(new_params, 3, sum(RAW), from_down)
-            new_params = place(new_params, 1, sum(RAW), from_up)
-    new_params = place(new_params, 2, sum(RAW), onward)
+    changes = spread(*pick(position, returned[0]), reps)
+    low, high, new_params = update(who, position, scales[me], returned, params, reps)
+    finished = spread(low, high, reps)
+
+    for (offset, part, old), (_, _, change) in zip(ahead, changes):
+        owner = lax.rem(me + offset, reps)
+        scale = lax.dynamic_slice(scales, (owner, part * half), (1, half))[0, :, None, None]
+        new = (old.astype(f32) - scale * change.astype(f32)).astype(bf16)
+        new_params = lax.dynamic_update_slice(new_params, new[None], (owner, part * half, 0, 0))
+    for offset, part, piece in finished:
+        owner = lax.rem(me + offset, reps)
+        new_params = lax.dynamic_update_slice(new_params, piece[None], (owner, part * half, 0, RAW))
     return (new_params.reshape(reps * blocks, rows, width), new_accum)
 
 

time: 224 us -> 223 us (level)
  the two profiles are of different devices: /device:TPU:0 before, /device:TPU:30 now
where the time goes in v8:
time: 223 us; the launch traced here: 222 us
  waiting for transfers between devices  80.2 us (36%)
  starting transfers between devices  77.5 us (35%)
  Pallas kernels  34.4 us (15%)
  local copies, waits for them, and re-layouts  15.1 us (7%)
  other arithmetic  14 us (6%)
    all_to_all x4, starting transfers between devices, local(): lax.all_to_all(outgoing, GROUP, split_axis=0, concat_axis=0, tiled=True)  30.3 us
    ppermute x9, starting transfers between devices, everywhere(): lax.ppermute(value, axis, ring(4, step))  13.1 us
    all_to_all x4, waiting for transfers between devices, local(): lax.all_to_all(outgoing, GROUP, split_axis=0, concat_axis=0, tiled=True)  12.4 us
    ppermute x3, waiting for transfers between devices, spread(): far_low = lax.ppermute(low_up, 'rep', up)  9.52 us
    ppermute x2, waiting for transfers between devices, local(): near_up = lax.ppermute(to_up, 'rep', up)  9.28 us
    ppermute x9, waiting for transfers between devices, everywhere(): lax.ppermute(value, axis, ring(4, step))  9.04 us
    ppermute x3, waiting for transfers between devices, spread(): low_up = lax.ppermute(low, 'rep', up)  8.8 us
    pallas_call x2, Pallas kernels, finish(): pl.pallas_call(body, grid_spec=pltpu.PrefetchScalarGridSpec(num_scalar_pr...  8.2 us
  transfers between devices with their start and end apart: 40, of which 20 were waited for; matrix products, arithmetic and copies ran while one was open for 10% of the time, Pallas kernels for 12%

profile of v8, /device:TPU:30, one launch (start us, length us, event | category | flops | bytes accessed | tf_op | source)
XLA Modules:
  0.0 222.1 jit_solution(5253947413015741800)
XLA Ops:
  7.8 3.9 %collective-permute-done.4.from_down = bf16[12,32,384]{2,1,0:T(8,128)(2,1)S(1)} collective-permute-done((bf16[12,32,384]{2,1,0:T(8,128)(2,1)S(1)}, bf16[12,32,384]{2,1,0:T(8,128)(2,1)S(1)}, u32[]{:S(2)}, u32[]{:S(2)}) %collective-permute-start.4) | collective-permute-done | bytes 294944 | tf_op jit(solution)/shard_map/ppermute | solution.py:300
  30.9 4.0 %collective-permute-done.6.one = bf16[24,32,384]{2,1,0:T(8,128)(2,1)S(1)} collective-permute-done((bf16[24,32,384]{2,1,0:T(8,128)(2,1)}, bf16[24,32,384]{2,1,0:T(8,128)(2,1)S(1)}, u32[]{:S(2)}, u32[]{:S(2)}) %collective-permute-start.6) | collective-permute-done | bytes 589856 | tf_op jit(solution)/shard_map/ppermute | solution.py:303
  41.0 8.5 %all-to-all-start.1 = ((bf16[32,32,384]{2,1,0:T(8,128)(2,1)}), bf16[32,32,384]{2,1,0:T(8,128)(2,1)S(1)}, u32[]{:S(2)}, u32[]{:S(2)}) async-start(bf16[32,32,384]{2,1,0:T(8,128)(2,1)} %get-tuple-element.29), calls=%async_computation.1 | async-start | bytes 1572864 | tf_op jit(solution)/shard_map/all_to_all | solution.py:307
  49.5 5.3 %collective-permute-done.2.one = bf16[24,32,640]{2,1,0:T(8,128)(2,1)S(1)} collective-permute-done((bf16[24,32,640]{2,1,0:T(8,128)(2,1)}, bf16[24,32,640]{2,1,0:T(8,128)(2,1)S(1)}, u32[]{:S(2)}, u32[]{:S(2)}) %collective-permute-start.2) | collective-permute-done | bytes 983072 | tf_op jit(solution)/shard_map/ppermute | solution.py:303
  57.2 4.6 %shard_map.86 = (bf16[24,32,640]{2,1,0:T(8,128)(2,1)}, bf16[32,32,640]{2,1,0:T(8,128)(2,1)}) custom-call(s32[4]{0:T(128)} %compare_select_fusion.who_ref, s32[32]{0:T(128)} %get-tuple-element.50.table_ref, bf16[4,24,32,1024]{3,2,1,0:T(8,128)(2,1)} %bitcast.81, bf16[24,32,640]{2,1,0:T(8,128)(2,1)} %copy-done.5, bf16[24,32,640]{2,1,0:T(8,128)(2,1)} %copy-done.6), custom_call_target="tpu_custom_call" | custom-call | tf_op jit(solution)/shard_map/pallas_call | solution.py:80
  61.8 8.4 %all-to-all-start = ((bf16[32,32,640]{2,1,0:T(8,128)(2,1)}), bf16[32,32,640]{2,1,0:T(8,128)(2,1)S(1)}, u32[]{:S(2)}, u32[]{:S(2)}) async-start(bf16[32,32,640]{2,1,0:T(8,128)(2,1)} %get-tuple-element.26), calls=%async_computation | async-start | bytes 2621440 | tf_op jit(solution)/shard_map/all_to_all | solution.py:307
  72.2 3.6 %left_times.1.rest_0_ = bf16[1024,384]{1,0:T(8,128)(2,1)} custom-call(bf16[1024,1024]{1,0:T(8,128)(2,1)} %bitcast.82, bf16[1024,384]{1,0:T(8,128)(2,1)} %bitcast.85), custom_call_target="tpu_custom_call" | custom-call | tf_op jit(solution)/shard_map/left_times/pallas_call | solution.py:106
  75.9 12.4 %all-to-all-done = bf16[32,32,640]{2,1,0:T(8,128)(2,1)S(1)} async-done(((bf16[32,32,640]{2,1,0:T(8,128)(2,1)}), bf16[32,32,640]{2,1,0:T(8,128)(2,1)S(1)}, u32[]{:S(2)}, u32[]{:S(2)}) %all-to-all-start) | async-done | bytes 1310752 | tf_op jit(solution)/shard_map/all_to_all | solution.py:307
  89.3 7.7 %products.1 = (bf16[1024,512]{1,0:T(8,128)(2,1)}, bf16[1024,512]{1,0:T(8,128)(2,1)}, f32[2,128]{1,0:T(2,128)}) custom-call(bf16[1024,1024]{1,0:T(8,128)(2,1)} %bitcast.83, bf16[1024,1024]{1,0:T(8,128)(2,1)} %bitcast.86, bf16[1024,640]{1,0:T(8,128)(2,1)} %bitcast.84, f32[1,128]{1,0:T(1,128)} %pad.8.layer_ref, bf16[1024,384]{1,0:T(8,128)(2,1)} %left_times.1.rest_0_), custom_call_target="tpu_custom_call" | custom-call | tf_op jit(solution)/shard_map/products/pallas_call | solution.py:148
  97.1 5.8 %all-to-all-start.2 = ((bf16[32,32,512]{2,1,0:T(8,128)(2,1)}), bf16[32,32,512]{2,1,0:T(8,128)(2,1)S(1)}, u32[]{:S(2)}, u32[]{:S(2)}) async-start(bf16[32,32,512]{2,1,0:T(8,128)(2,1)} %bitcast.88), calls=%async_computation.2 | async-start | bytes 2097152 | tf_op jit(solution)/shard_map/all_to_all | solution.py:344
  102.9 4.6 %fusion.2 = (f32[24]{0:T(128)S(1)}, f32[24,32,1024]{2,1,0:T(8,128)}) fusion(bf16[24,32,640]{2,1,0:T(8,128)(2,1)} %get-tuple-element.38, bf16[24,32,384]{2,1,0:T(8,128)(2,1)S(1)} %copy-done.7, f32[24,32,1024]{2,1,0:T(8,128)} %param.9), kind=kLoop, calls=%fused_computation.4 | loop fusion | flops 7077864 | bytes 7864416 | tf_op jit(solution)/shard_map/reduce_sum | solution.py:337
  120.4 7.7 %all-to-all-start.3 = ((bf16[32,32,512]{2,1,0:T(8,128)(2,1)}), bf16[32,32,512]{2,1,0:T(8,128)(2,1)S(1)}, u32[]{:S(2)}, u32[]{:S(2)}) async-start(bf16[32,32,512]{2,1,0:T(8,128)(2,1)} %bitcast.87), calls=%async_computation.3 | async-start | bytes 2097152 | tf_op jit(solution)/shard_map/all_to_all | solution.py:344
  134.5 9.0 %collective-permute-done.15 = f32[2,128]{1,0:T(2,128)S(1)} collective-permute-done((f32[2,128]{1,0:T(2,128)S(1)}, f32[2,128]{1,0:T(2,128)S(1)}, u32[]{:S(2)}, u32[]{:S(2)}) %collective-permute-start.15) | collective-permute-done | bytes 1056 | tf_op jit(solution)/shard_map/ppermute | solution.py:258
  152.4 5.3 %update.1 = (bf16[12,32,512]{2,1,0:T(8,128)(2,1)}, bf16[12,32,512]{2,1,0:T(8,128)(2,1)}, bf16[4,24,32,1024]{3,2,1,0:T(8,128)(2,1)}) custom-call(s32[4]{0:T(128)} %compare_select_fusion.who_ref, s32[24]{0:T(128)} %select_reduce_fusion.position_ref, f32[24]{0:T(128)} %fusion.21.scale_ref, bf16[32,32,512]{2,1,0:T(8,128)(2,1)} %copy-done, ...), custom_call_target="tpu_custom_call" | custom-call | tf_op jit(solution)/shard_map/update/pallas_call | solution.py:234
  157.8 4.9 %collective-permute-done.19 = bf16[12,32,512]{2,1,0:T(8,128)(2,1)S(1)} collective-permute-done((bf16[12,32,512]{2,1,0:T(8,128)(2,1)}, bf16[12,32,512]{2,1,0:T(8,128)(2,1)S(1)}, u32[]{:S(2)}, u32[]{:S(2)}) %collective-permute-start.19) | collective-permute-done | bytes 393248 | tf_op jit(solution)/shard_map/ppermute | solution.py:265
  171.0 4.9 %collective-permute-done.23 = bf16[12,32,512]{2,1,0:T(8,128)(2,1)S(1)} collective-permute-done((bf16[12,32,512]{2,1,0:T(8,128)(2,1)}, bf16[12,32,512]{2,1,0:T(8,128)(2,1)S(1)}, u32[]{:S(2)}, u32[]{:S(2)}) %collective-permute-start.23) | collective-permute-done | bytes 393248 | tf_op jit(solution)/shard_map/ppermute | solution.py:267
  175.9 3.6 %collective-permute-start.27 = (bf16[12,32,512]{2,1,0:T(8,128)(2,1)S(1)}, bf16[12,32,512]{2,1,0:T(8,128)(2,1)S(1)}, u32[]{:S(2)}, u32[]{:S(2)}) collective-permute-start(bf16[12,32,512]{2,1,0:T(8,128)(2,1)S(1)} %collective-permute-done.19), channel_id=1, source_target_pairs={{0,1},{1,2},{2,3},{3,0},{4,5},{5,6},{6,7},{7,4},{8,9},{9,10},{10,1... | collective-permute-start | bytes 1179656 | tf_op jit(solution)/shard_map/ppermute | solution.py:269
  180.4 3.9 %collective-permute-done.26 = bf16[12,32,512]{2,1,0:T(8,128)(2,1)S(1)} collective-permute-done((bf16[12,32,512]{2,1,0:T(8,128)(2,1)}, bf16[12,32,512]{2,1,0:T(8,128)(2,1)S(1)}, u32[]{:S(2)}, u32[]{:S(2)}) %collective-permute-start.26) | collective-permute-done | bytes 393248 | tf_op jit(solution)/shard_map/ppermute | solution.py:269
  187.0 5.6 %collective-permute-done.27 = bf16[12,32,512]{2,1,0:T(8,128)(2,1)S(1)} collective-permute-done((bf16[12,32,512]{2,1,0:T(8,128)(2,1)S(1)}, bf16[12,32,512]{2,1,0:T(8,128)(2,1)S(1)}, u32[]{:S(2)}, u32[]{:S(2)}) %collective-permute-start.27) | collective-permute-done | bytes 393248 | tf_op jit(solution)/shard_map/ppermute | solution.py:269
  192.6 3.7 %collective-permute-start.32 = (bf16[12,32,512]{2,1,0:T(8,128)(2,1)}, bf16[12,32,512]{2,1,0:T(8,128)(2,1)S(1)}, u32[]{:S(2)}, u32[]{:S(2)}) collective-permute-start(bf16[12,32,512]{2,1,0:T(8,128)(2,1)} %get-tuple-element.45), channel_id=1, source_target_pairs={{0,1},{1,2},{2,3},{3,0},{4,5},{5,6},{6,7},{7,4},{8,9},{9,10},{10,1... | collective-permute-start | bytes 1179656 | tf_op jit(solution)/shard_map/ppermute | solution.py:267
  197.3 3.9 %collective-permute-done.30 = bf16[12,32,512]{2,1,0:T(8,128)(2,1)S(1)} collective-permute-done((bf16[12,32,512]{2,1,0:T(8,128)(2,1)}, bf16[12,32,512]{2,1,0:T(8,128)(2,1)S(1)}, u32[]{:S(2)}, u32[]{:S(2)}) %collective-permute-start.30) | collective-permute-done | bytes 393248 | tf_op jit(solution)/shard_map/ppermute | solution.py:265
  201.2 3.6 %collective-permute-start.34 = (bf16[12,32,512]{2,1,0:T(8,128)(2,1)S(1)}, bf16[12,32,512]{2,1,0:T(8,128)(2,1)S(1)}, u32[]{:S(2)}, u32[]{:S(2)}) collective-permute-start(bf16[12,32,512]{2,1,0:T(8,128)(2,1)S(1)} %collective-permute-done.30), channel_id=1, source_target_pairs={{0,1},{1,2},{2,3},{3,0},{4,5},{5,6},{6,7},{7,4},{8,9},{9,10},{10,1... | collective-permute-start | bytes 1179656 | tf_op jit(solution)/shard_map/ppermute | solution.py:269
  210.4 4.8 %collective-permute-done.33 = bf16[12,32,512]{2,1,0:T(8,128)(2,1)S(1)} collective-permute-done((bf16[12,32,512]{2,1,0:T(8,128)(2,1)}, bf16[12,32,512]{2,1,0:T(8,128)(2,1)S(1)}, u32[]{:S(2)}, u32[]{:S(2)}) %collective-permute-start.33) | collective-permute-done | bytes 393248 | tf_op jit(solution)/shard_map/ppermute | solution.py:268
  216.7 4.6 %collective-permute-done.35 = bf16[12,32,512]{2,1,0:T(8,128)(2,1)S(1)} collective-permute-done((bf16[12,32,512]{2,1,0:T(8,128)(2,1)S(1)}, bf16[12,32,512]{2,1,0:T(8,128)(2,1)S(1)}, u32[]{:S(2)}, u32[]{:S(2)}) %collective-permute-start.35) | collective-permute-done | bytes 393248 | tf_op jit(solution)/shard_map/ppermute | solution.py:270
  (134 shorter events, 86.8 us)
Async XLA Ops:
  5.1 17.1 %collective-permute-start = (bf16[12,32,640]{2,1,0:T(8,128)(2,1)S(1)}, bf16[12,32,640]{2,1,0:T(8,128)(2,1)S(1)}, u32[]{:S(2)}, u32[]{:S(2)}) collective-permute-start(bf16[12,32,640]{2,1,0:T(8,128)(2,1)S(1)} %get-tuple-element.55), channel_id=1, source_target_pairs={{0,1},{1,2},{2,3},{3,0},{4,5},{5,6},{6,7},{7,4},{8,9},{9,10},{10,1... | collective-permute-start | bytes 1474568 | tf_op jit(solution)/shard_map/ppermute | solution.py:300
  6.9 17.0 %collective-permute-start.1 = (bf16[12,32,640]{2,1,0:T(8,128)(2,1)S(1)}, bf16[12,32,640]{2,1,0:T(8,128)(2,1)S(1)}, u32[]{:S(2)}, u32[]{:S(2)}) collective-permute-start(bf16[12,32,640]{2,1,0:T(8,128)(2,1)S(1)} %get-tuple-element.54), channel_id=1, source_target_pairs={{0,3},{1,0},{2,1},{3,2},{4,7},{5,4},{6,5},{7,6},{8,11},{9,8},{10,9... | collective-permute-start | bytes 1474568 | tf_op jit(solution)/shard_map/ppermute | solution.py:301
  17.2 17.7 %collective-permute-start.6 = (bf16[24,32,384]{2,1,0:T(8,128)(2,1)}, bf16[24,32,384]{2,1,0:T(8,128)(2,1)S(1)}, u32[]{:S(2)}, u32[]{:S(2)}) collective-permute-start(bf16[24,32,384]{2,1,0:T(8,128)(2,1)} %get-tuple-element.27), channel_id=1, source_target_pairs={{0,1},{1,2},{2,3},{3,0},{4,5},{5,6},{6,7},{7,4},{8,9},{9,10},{10,1... | collective-permute-start | bytes 1769480 | tf_op jit(solution)/shard_map/ppermute | solution.py:303
  17.9 18.7 %collective-permute-start.7 = (bf16[24,32,384]{2,1,0:T(8,128)(2,1)}, bf16[24,32,384]{2,1,0:T(8,128)(2,1)S(1)}, u32[]{:S(2)}, u32[]{:S(2)}) collective-permute-start(bf16[24,32,384]{2,1,0:T(8,128)(2,1)} %get-tuple-element.28), channel_id=1, source_target_pairs={{0,3},{1,0},{2,1},{3,2},{4,7},{5,4},{6,5},{7,6},{8,11},{9,8},{10,9... | collective-permute-start | bytes 1769480 | tf_op jit(solution)/shard_map/ppermute | solution.py:304
  28.3 26.5 %collective-permute-start.2 = (bf16[24,32,640]{2,1,0:T(8,128)(2,1)}, bf16[24,32,640]{2,1,0:T(8,128)(2,1)S(1)}, u32[]{:S(2)}, u32[]{:S(2)}) collective-permute-start(bf16[24,32,640]{2,1,0:T(8,128)(2,1)} %get-tuple-element.24), channel_id=1, source_target_pairs={{0,1},{1,2},{2,3},{3,0},{4,5},{5,6},{6,7},{7,4},{8,9},{9,10},{10,1... | collective-permute-start | bytes 2949128 | tf_op jit(solution)/shard_map/ppermute | solution.py:303
  29.1 27.1 %collective-permute-start.3 = (bf16[24,32,640]{2,1,0:T(8,128)(2,1)}, bf16[24,32,640]{2,1,0:T(8,128)(2,1)S(1)}, u32[]{:S(2)}, u32[]{:S(2)}) collective-permute-start(bf16[24,32,640]{2,1,0:T(8,128)(2,1)} %get-tuple-element.25), channel_id=1, source_target_pairs={{0,3},{1,0},{2,1},{3,2},{4,7},{5,4},{6,5},{7,6},{8,11},{9,8},{10,9... | collective-permute-start | bytes 2949128 | tf_op jit(solution)/shard_map/ppermute | solution.py:304
  41.0 20.8 %all-to-all-start.1 = ((bf16[32,32,384]{2,1,0:T(8,128)(2,1)}), bf16[32,32,384]{2,1,0:T(8,128)(2,1)S(1)}, u32[]{:S(2)}, u32[]{:S(2)}) async-start(bf16[32,32,384]{2,1,0:T(8,128)(2,1)} %get-tuple-element.29), calls=%async_computation.1 | async-start | bytes 1572864 | tf_op jit(solution)/shard_map/all_to_all | solution.py:307
  61.8 26.5 %all-to-all-start = ((bf16[32,32,640]{2,1,0:T(8,128)(2,1)}), bf16[32,32,640]{2,1,0:T(8,128)(2,1)S(1)}, u32[]{:S(2)}, u32[]{:S(2)}) async-start(bf16[32,32,640]{2,1,0:T(8,128)(2,1)} %get-tuple-element.26), calls=%async_computation | async-start | bytes 2621440 | tf_op jit(solution)/shard_map/all_to_all | solution.py:307
  97.1 23.3 %all-to-all-start.2 = ((bf16[32,32,512]{2,1,0:T(8,128)(2,1)}), bf16[32,32,512]{2,1,0:T(8,128)(2,1)S(1)}, u32[]{:S(2)}, u32[]{:S(2)}) async-start(bf16[32,32,512]{2,1,0:T(8,128)(2,1)} %bitcast.88), calls=%async_computation.2 | async-start | bytes 2097152 | tf_op jit(solution)/shard_map/all_to_all | solution.py:344
  112.9 55.1 %collective-permute-start.20 = (bf16[12,32,512]{2,1,0:T(8,128)(2,1)}, bf16[12,32,512]{2,1,0:T(8,128)(2,1)S(1)}, u32[]{:S(2)}, u32[]{:S(2)}) collective-permute-start(bf16[12,32,512]{2,1,0:T(8,128)(2,1)} %get-tuple-element.56), channel_id=1, source_target_pairs={{0,3},{1,0},{2,1},{3,2},{4,7},{5,4},{6,5},{7,6},{8,11},{9,8},{10,9... | collective-permute-start | bytes 1179656 | tf_op jit(solution)/shard_map/ppermute | solution.py:266
  115.0 55.9 %collective-permute-start.22 = (bf16[12,32,512]{2,1,0:T(8,128)(2,1)}, bf16[12,32,512]{2,1,0:T(8,128)(2,1)S(1)}, u32[]{:S(2)}, u32[]{:S(2)}) collective-permute-start(bf16[12,32,512]{2,1,0:T(8,128)(2,1)} %get-tuple-element.56), channel_id=1, source_target_pairs={{0,1},{1,2},{2,3},{3,0},{4,5},{5,6},{6,7},{7,4},{8,9},{9,10},{10,1... | collective-permute-start | bytes 1179656 | tf_op jit(solution)/shard_map/ppermute | solution.py:267
  120.4 31.0 %all-to-all-start.3 = ((bf16[32,32,512]{2,1,0:T(8,128)(2,1)}), bf16[32,32,512]{2,1,0:T(8,128)(2,1)S(1)}, u32[]{:S(2)}, u32[]{:S(2)}) async-start(bf16[32,32,512]{2,1,0:T(8,128)(2,1)} %bitcast.87), calls=%async_computation.3 | async-start | bytes 2097152 | tf_op jit(solution)/shard_map/all_to_all | solution.py:344
  148.8 19.2 %collective-permute-start.21 = (bf16[12,32,512]{2,1,0:T(8,128)(2,1)}, bf16[12,32,512]{2,1,0:T(8,128)(2,1)S(1)}, u32[]{:S(2)}, u32[]{:S(2)}) collective-permute-start(bf16[12,32,512]{2,1,0:T(8,128)(2,1)} %get-tuple-element.43), channel_id=1, source_target_pairs={{0,3},{1,0},{2,1},{3,2},{4,7},{5,4},{6,5},{7,6},{8,11},{9,8},{10,9... | collective-permute-start | bytes 1179656 | tf_op jit(solution)/shard_map/ppermute | solution.py:266
  157.7 22.7 %collective-permute-start.24 = (bf16[12,32,512]{2,1,0:T(8,128)(2,1)S(1)}, bf16[12,32,512]{2,1,0:T(8,128)(2,1)S(1)}, u32[]{:S(2)}, u32[]{:S(2)}) collective-permute-start(bf16[12,32,512]{2,1,0:T(8,128)(2,1)S(1)} %get-tuple-element.57), channel_id=1, source_target_pairs={{0,3},{1,0},{2,1},{3,2},{4,7},{5,4},{6,5},{7,6},{8,11},{9,8},{10,9... | collective-permute-start | bytes 1179656 | tf_op jit(solution)/shard_map/ppermute | solution.py:268
  168.0 16.3 %collective-permute-start.26 = (bf16[12,32,512]{2,1,0:T(8,128)(2,1)}, bf16[12,32,512]{2,1,0:T(8,128)(2,1)S(1)}, u32[]{:S(2)}, u32[]{:S(2)}) collective-permute-start(bf16[12,32,512]{2,1,0:T(8,128)(2,1)} %collective-permute-done.18), channel_id=1, source_target_pairs={{0,1},{1,2},{2,3},{3,0},{4,5},{5,6},{6,7},{7,4},{8,9},{9,10},{10,1... | collective-permute-start | bytes 1179656 | tf_op jit(solution)/shard_map/ppermute | solution.py:269
  168.0 16.3 %collective-permute-start.25 = (bf16[12,32,512]{2,1,0:T(8,128)(2,1)}, bf16[12,32,512]{2,1,0:T(8,128)(2,1)S(1)}, u32[]{:S(2)}, u32[]{:S(2)}) collective-permute-start(bf16[12,32,512]{2,1,0:T(8,128)(2,1)} %get-tuple-element.42), channel_id=1, source_target_pairs={{0,3},{1,0},{2,1},{3,2},{4,7},{5,4},{6,5},{7,6},{8,11},{9,8},{10,9... | collective-permute-start | bytes 1179656 | tf_op jit(solution)/shard_map/ppermute | solution.py:268
  171.0 26.3 %collective-permute-start.28 = (bf16[12,32,512]{2,1,0:T(8,128)(2,1)S(1)}, bf16[12,32,512]{2,1,0:T(8,128)(2,1)S(1)}, u32[]{:S(2)}, u32[]{:S(2)}) collective-permute-start(bf16[12,32,512]{2,1,0:T(8,128)(2,1)S(1)} %collective-permute-done.20), channel_id=1, source_target_pairs={{0,3},{1,0},{2,1},{3,2},{4,7},{5,4},{6,5},{7,6},{8,11},{9,8},{10,9... | collective-permute-start | bytes 1179656 | tf_op jit(solution)/shard_map/ppermute | solution.py:270
  175.9 16.7 %collective-permute-start.27 = (bf16[12,32,512]{2,1,0:T(8,128)(2,1)S(1)}, bf16[12,32,512]{2,1,0:T(8,128)(2,1)S(1)}, u32[]{:S(2)}, u32[]{:S(2)}) collective-permute-start(bf16[12,32,512]{2,1,0:T(8,128)(2,1)S(1)} %collective-permute-done.19), channel_id=1, source_target_pairs={{0,1},{1,2},{2,3},{3,0},{4,5},{5,6},{6,7},{7,4},{8,9},{9,10},{10,1... | collective-permute-start | bytes 1179656 | tf_op jit(solution)/shard_map/ppermute | solution.py:269
  180.4 20.8 %collective-permute-start.30 = (bf16[12,32,512]{2,1,0:T(8,128)(2,1)}, bf16[12,32,512]{2,1,0:T(8,128)(2,1)S(1)}, u32[]{:S(2)}, u32[]{:S(2)}) collective-permute-start(bf16[12,32,512]{2,1,0:T(8,128)(2,1)} %get-tuple-element.44), channel_id=1, source_target_pairs={{0,1},{1,2},{2,3},{3,0},{4,5},{5,6},{6,7},{7,4},{8,9},{9,10},{10,1... | collective-permute-start | bytes 1179656 | tf_op jit(solution)/shard_map/ppermute | solution.py:265
  184.3 20.4 %collective-permute-start.31 = (bf16[12,32,512]{2,1,0:T(8,128)(2,1)}, bf16[12,32,512]{2,1,0:T(8,128)(2,1)S(1)}, u32[]{:S(2)}, u32[]{:S(2)}) collective-permute-start(bf16[12,32,512]{2,1,0:T(8,128)(2,1)} %get-tuple-element.45), channel_id=1, source_target_pairs={{0,3},{1,0},{2,1},{3,2},{4,7},{5,4},{6,5},{7,6},{8,11},{9,8},{10,9... | collective-permute-start | bytes 1179656 | tf_op jit(solution)/shard_map/ppermute | solution.py:266
  184.3 22.4 %collective-permute-start.29 = (bf16[12,32,512]{2,1,0:T(8,128)(2,1)S(1)}, bf16[12,32,512]{2,1,0:T(8,128)(2,1)S(1)}, u32[]{:S(2)}, u32[]{:S(2)}) collective-permute-start(bf16[12,32,512]{2,1,0:T(8,128)(2,1)S(1)} %collective-permute-done.21), channel_id=1, source_target_pairs={{0,3},{1,0},{2,1},{3,2},{4,7},{5,4},{6,5},{7,6},{8,11},{9,8},{10,9... | collective-permute-start | bytes 1179656 | tf_op jit(solution)/shard_map/ppermute | solution.py:270
  192.6 17.0 %collective-permute-start.32 = (bf16[12,32,512]{2,1,0:T(8,128)(2,1)}, bf16[12,32,512]{2,1,0:T(8,128)(2,1)S(1)}, u32[]{:S(2)}, u32[]{:S(2)}) collective-permute-start(bf16[12,32,512]{2,1,0:T(8,128)(2,1)} %get-tuple-element.45), channel_id=1, source_target_pairs={{0,1},{1,2},{2,3},{3,0},{4,5},{5,6},{6,7},{7,4},{8,9},{9,10},{10,1... | collective-permute-start | bytes 1179656 | tf_op jit(solution)/shard_map/ppermute | solution.py:267
  197.3 17.9 %collective-permute-start.33 = (bf16[12,32,512]{2,1,0:T(8,128)(2,1)}, bf16[12,32,512]{2,1,0:T(8,128)(2,1)S(1)}, u32[]{:S(2)}, u32[]{:S(2)}) collective-permute-start(bf16[12,32,512]{2,1,0:T(8,128)(2,1)} %get-tuple-element.44), channel_id=1, source_target_pairs={{0,3},{1,0},{2,1},{3,2},{4,7},{5,4},{6,5},{7,6},{8,11},{9,8},{10,9... | collective-permute-start | bytes 1179656 | tf_op jit(solution)/shard_map/ppermute | solution.py:268
  204.8 16.5 %collective-permute-start.35 = (bf16[12,32,512]{2,1,0:T(8,128)(2,1)S(1)}, bf16[12,32,512]{2,1,0:T(8,128)(2,1)S(1)}, u32[]{:S(2)}, u32[]{:S(2)}) collective-permute-start(bf16[12,32,512]{2,1,0:T(8,128)(2,1)S(1)} %collective-permute-done.31), channel_id=1, source_target_pairs={{0,3},{1,0},{2,1},{3,2},{4,7},{5,4},{6,5},{7,6},{8,11},{9,8},{10,9... | collective-permute-start | bytes 1179656 | tf_op jit(solution)/shard_map/ppermute | solution.py:270
  (33 other events, 320.4 us)

commit v9 on v8

--- a/solution.py
+++ b/solution.py
@@ -252,6 +252,55 @@
     )(who, position, scale, *returned, params)
 
 
+def place(owners, scales, whole, raw, ready):
+    half, rows, _ = raw[0][2].shape
+    blocks = 2 * half
+    pieces = len(raw) + len(ready)
+
+    def body(owners_ref, scales_ref, *refs):
+        olds, changes = refs[: len(raw)], refs[len(raw) : 2 * len(raw)]
+        values = refs[2 * len(raw) : 2 * len(raw) + len(ready)]
+        out, made, sems = refs[-3:]
+        copies = []
+        for at, (offset, part, value) in enumerate([(o, p, None) for o, p, _, _ in raw] + list(ready)):
+            owner = owners_ref[offset]
+            if at < len(raw):
+                for block in range(half):
+                    scale = scales_ref[owner * blocks + part * half + block]
+                    new = olds[at][block].astype(f32) - scale * changes[at][block].astype(f32)
+                    made[at, block] = new.astype(bf16)
+                source, columns = made.at[at], pl.ds(0, RAW)
+            else:
+                source = values[at - len(raw)]
+                columns = pl.ds(RAW, value.shape[2])
+            target = out.at[owner, pl.ds(part * half, half), :, columns]
+            copies.append(pltpu.make_async_copy(source, target, sems.at[at]))
+            copies[-1].start()
+        for copy in copies:
+            copy.wait()
+
+    def block_of(array):
+        return pl.BlockSpec(array.shape, lambda i, o, s: (0, 0, 0))
+
+    arrays = [old for _, _, old, _ in raw] + [change for _, _, _, change in raw] + [v for _, _, v in ready]
+    hbm = pl.BlockSpec(memory_space=pltpu.HBM)
+    return pl.pallas_call(
+        body,
+        grid_spec=pltpu.PrefetchScalarGridSpec(
+            num_scalar_prefetch=2,
+            grid=(1,),
+            in_specs=[*[block_of(array) for array in arrays], hbm],
+            out_specs=hbm,
+            scratch_shapes=[
+                pltpu.VMEM((len(raw), half, rows, RAW), bf16),
+                pltpu.SemaphoreType.DMA((pieces,)),
+            ],
+        ),
+        out_shape=jax.ShapeDtypeStruct(whole.shape, bf16),
+        input_output_aliases={2 + len(arrays): 0},
+    )(owners, scales, *arrays, whole)
+
+
 def everywhere(value):
     value = value + lax.ppermute(value, "group_2", [(0, 1), (1, 0)])
     for axis in ("rep", "group_0", "group_1"):
@@ -350,12 +399,11 @@
     low, high, new_params = update(who, position, scales[me], returned, params, reps)
     finished = spread(low, high, reps)
 
-    for (offset, part, old), (_, _, change) in zip(ahead, changes):
-        owner = lax.rem(me + offset, reps)
-        scale = lax.dynamic_slice(scales, (owner, part * half), (1, half))[0, :, None, None]
-        new = (old.astype(f32) - scale * change.astype(f32)).astype(bf16)
-        new_params = lax.dynamic_update_slice(new_params, new[None], (owner, part * half, 0, 0))
-    for offset, part, piece in finished:
+    raw = [(offset, part, old, change) for (offset, part, old), (_, _, change) in zip(ahead, changes)]
+    flat = scales.reshape(-1)
+    new_params = place(who, flat, new_params, raw[:4], ())
+    new_params = place(who, flat, new_params, raw[4:], finished[:4])
+    for offset, part, piece in finished[4:]:
         owner = lax.rem(me + offset, reps)
         new_params = lax.dynamic_update_slice(new_params, piece[None], (owner, part * half, 0, RAW))
     return (new_params.reshape(reps * blocks, rows, width), new_accum)

time: 223 us -> 210 us (0.942)
  the two profiles are of different devices: /device:TPU:30 before, /device:TPU:0 now
where the time goes in v9:
time: 210 us; the launch traced here: 209 us
  starting transfers between devices  75.2 us (36%)
  waiting for transfers between devices  70 us (33%)
  Pallas kernels  42.3 us (20%)
  local copies, waits for them, and re-layouts  12.8 us (6%)
  other arithmetic  7.21 us (3%)
    all_to_all x4, starting transfers between devices, local(): lax.all_to_all(outgoing, GROUP, split_axis=0, concat_axis=0, tiled=True)  24.8 us
    ppermute x9, starting transfers between devices, everywhere(): lax.ppermute(value, axis, ring(4, step))  17 us
    ppermute x3, waiting for transfers between devices, spread(): high_up = lax.ppermute(high, 'rep', up)  16.5 us
    all_to_all x4, waiting for transfers between devices, local(): lax.all_to_all(outgoing, GROUP, split_axis=0, concat_axis=0, tiled=True)  14.9 us
    ppermute x3, waiting for transfers between devices, spread(): low_up = lax.ppermute(low, 'rep', up)  12.1 us
    ppermute x2, waiting for transfers between devices, local(): near_up = lax.ppermute(to_up, 'rep', up)  10.4 us
    pallas_call x2, Pallas kernels, finish(): pl.pallas_call(body, grid_spec=pltpu.PrefetchScalarGridSpec(num_scalar_pr...  8.19 us
    pallas_call x2, Pallas kernels, place(): pl.pallas_call(body, grid_spec=pltpu.PrefetchScalarGridSpec(num_scalar_pr...  7.85 us
  transfers between devices with their start and end apart: 40, of which 19 were waited for; matrix products, arithmetic and copies ran while one was open for 5% of the time, Pallas kernels for 17%

profile of v9, /device:TPU:0, one launch (start us, length us, event | category | flops | bytes accessed | tf_op | source)
XLA Modules:
  0.0 208.5 jit_solution(15240937919117568251)
XLA Ops:
  25.0 3.6 %merge.2 = (bf16[24,32,640]{2,1,0:T(8,128)(2,1)}, bf16[24,32,640]{2,1,0:T(8,128)(2,1)}) custom-call(s32[4]{0:T(128)} %compare_select_fusion.who_ref.owners_ref, bf16[4,24,32,1024]{3,2,1,0:T(8,128)(2,1)} %bitcast.34, bf16[4,24,32,1024]{3,2,1,0:T(8,128)(2,1)} %bitcast.35, bf16[12,32,640]{2,1,0:T(8,128)(2,1)} %copy-done.10, bf16[12,32,640]{2,1,0:T(8,128)(2,1)} %copy-done.11), custom_call_target="tpu_custom_call" | custom-call | tf_op jit(solution)/shard_map/merge/pallas_call | solution.py:51
  32.4 3.7 %collective-permute-done.6.one = bf16[24,32,384]{2,1,0:T(8,128)(2,1)S(1)} collective-permute-done((bf16[24,32,384]{2,1,0:T(8,128)(2,1)}, bf16[24,32,384]{2,1,0:T(8,128)(2,1)S(1)}, u32[]{:S(2)}, u32[]{:S(2)}) %collective-permute-start.6) | collective-permute-done | bytes 589856 | tf_op jit(solution)/shard_map/ppermute | solution.py:352
  37.3 3.6 %shard_map.87 = (bf16[24,32,384]{2,1,0:T(8,128)(2,1)}, bf16[32,32,384]{2,1,0:T(8,128)(2,1)}) custom-call(s32[4]{0:T(128)} %compare_select_fusion.who_ref.owners_ref, s32[32]{0:T(128)} %get-tuple-element.50.table_ref, bf16[4,24,32,1024]{3,2,1,0:T(8,128)(2,1)} %bitcast.36, bf16[24,32,384]{2,1,0:T(8,128)(2,1)} %copy-done.8, bf16[24,32,384]{2,1,0:T(8,128)(2,1)} %copy-done.9), custom_call_target="tpu_custom_call" | custom-call | tf_op jit(solution)/shard_map/pallas_call | solution.py:80
  40.9 8.3 %all-to-all-start.1 = ((bf16[32,32,384]{2,1,0:T(8,128)(2,1)}), bf16[32,32,384]{2,1,0:T(8,128)(2,1)S(1)}, u32[]{:S(2)}, u32[]{:S(2)}) async-start(bf16[32,32,384]{2,1,0:T(8,128)(2,1)} %get-tuple-element.29), calls=%async_computation.1 | async-start | bytes 1572864 | tf_op jit(solution)/shard_map/all_to_all | solution.py:356
  49.2 6.7 %collective-permute-done.2.one = bf16[24,32,640]{2,1,0:T(8,128)(2,1)S(1)} collective-permute-done((bf16[24,32,640]{2,1,0:T(8,128)(2,1)}, bf16[24,32,640]{2,1,0:T(8,128)(2,1)S(1)}, u32[]{:S(2)}, u32[]{:S(2)}) %collective-permute-start.2) | collective-permute-done | bytes 983072 | tf_op jit(solution)/shard_map/ppermute | solution.py:352
  57.9 4.6 %shard_map.86 = (bf16[24,32,640]{2,1,0:T(8,128)(2,1)}, bf16[32,32,640]{2,1,0:T(8,128)(2,1)}) custom-call(s32[4]{0:T(128)} %compare_select_fusion.who_ref.owners_ref, s32[32]{0:T(128)} %get-tuple-element.50.table_ref, bf16[4,24,32,1024]{3,2,1,0:T(8,128)(2,1)} %bitcast.37, bf16[24,32,640]{2,1,0:T(8,128)(2,1)} %copy-done.6, bf16[24,32,640]{2,1,0:T(8,128)(2,1)} %copy-done.7), custom_call_target="tpu_custom_call" | custom-call | tf_op jit(solution)/shard_map/pallas_call | solution.py:80
  63.1 7.9 %all-to-all-start = ((bf16[32,32,640]{2,1,0:T(8,128)(2,1)}), bf16[32,32,640]{2,1,0:T(8,128)(2,1)S(1)}, u32[]{:S(2)}, u32[]{:S(2)}) async-start(bf16[32,32,640]{2,1,0:T(8,128)(2,1)} %get-tuple-element.26), calls=%async_computation | async-start | bytes 2621440 | tf_op jit(solution)/shard_map/all_to_all | solution.py:356
  73.0 3.6 %left_times.1.rest_0_ = bf16[1024,384]{1,0:T(8,128)(2,1)} custom-call(bf16[1024,1024]{1,0:T(8,128)(2,1)} %bitcast.39, bf16[1024,384]{1,0:T(8,128)(2,1)} %bitcast.42), custom_call_target="tpu_custom_call" | custom-call | tf_op jit(solution)/shard_map/left_times/pallas_call | solution.py:106
  76.6 14.2 %all-to-all-done = bf16[32,32,640]{2,1,0:T(8,128)(2,1)S(1)} async-done(((bf16[32,32,640]{2,1,0:T(8,128)(2,1)}), bf16[32,32,640]{2,1,0:T(8,128)(2,1)S(1)}, u32[]{:S(2)}, u32[]{:S(2)}) %all-to-all-start) | async-done | bytes 1310752 | tf_op jit(solution)/shard_map/all_to_all | solution.py:356
  91.9 7.8 %products.1 = (bf16[1024,512]{1,0:T(8,128)(2,1)}, bf16[1024,512]{1,0:T(8,128)(2,1)}, f32[2,128]{1,0:T(2,128)}) custom-call(bf16[1024,1024]{1,0:T(8,128)(2,1)} %bitcast.40, bf16[1024,1024]{1,0:T(8,128)(2,1)} %bitcast.43, bf16[1024,640]{1,0:T(8,128)(2,1)} %bitcast.41, f32[1,128]{1,0:T(1,128)} %pad.8.layer_ref, bf16[1024,384]{1,0:T(8,128)(2,1)} %left_times.1.rest_0_), custom_call_target="tpu_custom_call" | custom-call | tf_op jit(solution)/shard_map/products/pallas_call | solution.py:148
  99.7 3.9 %all-to-all-start.2 = ((bf16[32,32,512]{2,1,0:T(8,128)(2,1)}), bf16[32,32,512]{2,1,0:T(8,128)(2,1)S(1)}, u32[]{:S(2)}, u32[]{:S(2)}) async-start(bf16[32,32,512]{2,1,0:T(8,128)(2,1)} %bitcast.44), calls=%async_computation.2 | async-start | bytes 2097152 | tf_op jit(solution)/shard_map/all_to_all | solution.py:393
  103.7 4.6 %fusion.2 = (f32[24]{0:T(128)S(1)}, f32[24,32,1024]{2,1,0:T(8,128)}) fusion(bf16[24,32,640]{2,1,0:T(8,128)(2,1)S(1)} %copy-done.5, bf16[24,32,384]{2,1,0:T(8,128)(2,1)} %get-tuple-element.37, f32[24,32,1024]{2,1,0:T(8,128)} %param.9), kind=kLoop, calls=%fused_computation.4 | loop fusion | flops 7077864 | bytes 7864416 | tf_op jit(solution)/shard_map/reduce_sum | solution.py:386
  118.0 3.3 %collective-permute-start.12 = (f32[2,128]{1,0:T(2,128)S(1)}, f32[2,128]{1,0:T(2,128)S(1)}, u32[]{:S(2)}, u32[]{:S(2)}) collective-permute-start(f32[2,128]{1,0:T(2,128)S(1)} %add_add_fusion.2), channel_id=1, source_target_pairs={{0,64},{32,96},{64,0},{96,32},{1,65},{33,97},{65,1},{97,33},{2,66}... | collective-permute-start | bytes 3080 | tf_op jit(solution)/shard_map/ppermute | solution.py:307
  124.5 4.7 %all-to-all-start.3 = ((bf16[32,32,512]{2,1,0:T(8,128)(2,1)}), bf16[32,32,512]{2,1,0:T(8,128)(2,1)S(1)}, u32[]{:S(2)}, u32[]{:S(2)}) async-start(bf16[32,32,512]{2,1,0:T(8,128)(2,1)} %bitcast.16), calls=%async_computation.3 | async-start | bytes 2097152 | tf_op jit(solution)/shard_map/all_to_all | solution.py:393
  129.2 3.4 %collective-permute-start.15 = (f32[2,128]{1,0:T(2,128)S(1)}, f32[2,128]{1,0:T(2,128)S(1)}, u32[]{:S(2)}, u32[]{:S(2)}) collective-permute-start(f32[2,128]{1,0:T(2,128)S(1)} %add_add_fusion.1), channel_id=1, source_target_pairs={{0,16},{8,24},{16,0},{24,8},{1,17},{9,25},{17,1},{25,9},{2,18},{10... | collective-permute-start | bytes 3080 | tf_op jit(solution)/shard_map/ppermute | solution.py:307
  146.0 3.8 %collective-permute-done.30.refs_2_ = bf16[12,32,512]{2,1,0:T(8,128)(2,1)} collective-permute-done((bf16[12,32,512]{2,1,0:T(8,128)(2,1)S(1)}, bf16[12,32,512]{2,1,0:T(8,128)(2,1)}, u32[]{:S(2)}, u32[]{:S(2)}) %collective-permute-start.30) | collective-permute-done | bytes 393248 | tf_op jit(solution)/shard_map/ppermute | solution.py:316
  151.4 5.3 %update.1 = (bf16[12,32,512]{2,1,0:T(8,128)(2,1)}, bf16[12,32,512]{2,1,0:T(8,128)(2,1)}, bf16[4,24,32,1024]{3,2,1,0:T(8,128)(2,1)}) custom-call(s32[4]{0:T(128)} %compare_select_fusion.who_ref.owners_ref, s32[24]{0:T(128)} %select_reduce_fusion.position_ref, f32[24]{0:T(128)} %fusion.6.scale_ref, bf16[32,32,512]{2,1,0:T(8,128)(2,1)} %copy-done, ...), custom_call_target="tpu_custom_call" | custom-call | tf_op jit(solution)/shard_map/update/pallas_call | solution.py:234
  160.9 5.7 %collective-permute-done.22.refs_4_ = bf16[12,32,512]{2,1,0:T(8,128)(2,1)} collective-permute-done((bf16[12,32,512]{2,1,0:T(8,128)(2,1)}, bf16[12,32,512]{2,1,0:T(8,128)(2,1)}, u32[]{:S(2)}, u32[]{:S(2)}) %collective-permute-start.22) | collective-permute-done | bytes 393248 | tf_op jit(solution)/shard_map/ppermute | solution.py:314
  168.6 6.3 %collective-permute-done.32.refs_6_ = bf16[12,32,512]{2,1,0:T(8,128)(2,1)S(1)} collective-permute-done((bf16[12,32,512]{2,1,0:T(8,128)(2,1)}, bf16[12,32,512]{2,1,0:T(8,128)(2,1)S(1)}, u32[]{:S(2)}, u32[]{:S(2)}) %collective-permute-start.32) | collective-permute-done | bytes 393248 | tf_op jit(solution)/shard_map/ppermute | solution.py:316
  177.0 6.4 %collective-permute-done.26.refs_4_ = bf16[12,32,512]{2,1,0:T(8,128)(2,1)S(1)} collective-permute-done((bf16[12,32,512]{2,1,0:T(8,128)(2,1)}, bf16[12,32,512]{2,1,0:T(8,128)(2,1)S(1)}, u32[]{:S(2)}, u32[]{:S(2)}) %collective-permute-start.26) | collective-permute-done | bytes 393248 | tf_op jit(solution)/shard_map/ppermute | solution.py:314
  185.4 6.5 %collective-permute-done.28.refs_6_ = bf16[12,32,512]{2,1,0:T(8,128)(2,1)} collective-permute-done((bf16[12,32,512]{2,1,0:T(8,128)(2,1)}, bf16[12,32,512]{2,1,0:T(8,128)(2,1)}, u32[]{:S(2)}, u32[]{:S(2)}) %collective-permute-start.28) | collective-permute-done | bytes 393248 | tf_op jit(solution)/shard_map/ppermute | solution.py:316
  191.9 3.8 %shard_map.88.refs_8_ = bf16[4,24,32,1024]{3,2,1,0:T(8,128)(2,1)} custom-call(s32[4]{0:T(128)} %compare_select_fusion.who_ref.owners_ref, f32[96]{0:T(128)} %copy-done.20, bf16[12,32,512]{2,1,0:T(8,128)(2,1)} %copy-done.12, bf16[12,32,512]{2,1,0:T(8,128)(2,1)} %collective-permute-done.20.refs_1_, ...), custom_call_target="tpu_custom_call", output_to_operand_aliasing={{}: (10, {})} | custom-call | tf_op jit(solution)/shard_map/pallas_call | solution.py:287
  195.8 4.6 %collective-permute-done.23.refs_2_ = bf16[12,32,512]{2,1,0:T(8,128)(2,1)} collective-permute-done((bf16[12,32,512]{2,1,0:T(8,128)(2,1)}, bf16[12,32,512]{2,1,0:T(8,128)(2,1)}, u32[]{:S(2)}, u32[]{:S(2)}) %collective-permute-start.23) | collective-permute-done | bytes 393248 | tf_op jit(solution)/shard_map/ppermute | solution.py:318
  200.3 4.1 %shard_map.89 = bf16[4,24,32,1024]{3,2,1,0:T(8,128)(2,1)} custom-call(s32[4]{0:T(128)} %compare_select_fusion.who_ref.owners_ref, f32[96]{0:T(128)} %copy-done.20, bf16[12,32,512]{2,1,0:T(8,128)(2,1)} %collective-permute-done.19.refs_0_, bf16[12,32,512]{2,1,0:T(8,128)(2,1)} %collective-permute-done.21.refs_1_, ...), custom_call_target="tpu_custom_call", output_to_operand_aliasing={{}: (10, {})} | custom-call | tf_op jit(solution)/shard_map/pallas_call | solution.py:287
  (141 shorter events, 77.2 us)
Async XLA Ops:
  6.3 17.1 %collective-permute-start = (bf16[12,32,640]{2,1,0:T(8,128)(2,1)S(1)}, bf16[12,32,640]{2,1,0:T(8,128)(2,1)S(1)}, u32[]{:S(2)}, u32[]{:S(2)}) collective-permute-start(bf16[12,32,640]{2,1,0:T(8,128)(2,1)S(1)} %get-tuple-element.55), channel_id=1, source_target_pairs={{0,1},{1,2},{2,3},{3,0},{4,5},{5,6},{6,7},{7,4},{8,9},{9,10},{10,1... | collective-permute-start | bytes 1474568 | tf_op jit(solution)/shard_map/ppermute | solution.py:349
  6.8 17.0 %collective-permute-start.1 = (bf16[12,32,640]{2,1,0:T(8,128)(2,1)S(1)}, bf16[12,32,640]{2,1,0:T(8,128)(2,1)S(1)}, u32[]{:S(2)}, u32[]{:S(2)}) collective-permute-start(bf16[12,32,640]{2,1,0:T(8,128)(2,1)S(1)} %get-tuple-element.54), channel_id=1, source_target_pairs={{0,3},{1,0},{2,1},{3,2},{4,7},{5,4},{6,5},{7,6},{8,11},{9,8},{10,9... | collective-permute-start | bytes 1474568 | tf_op jit(solution)/shard_map/ppermute | solution.py:350
  17.4 18.7 %collective-permute-start.6 = (bf16[24,32,384]{2,1,0:T(8,128)(2,1)}, bf16[24,32,384]{2,1,0:T(8,128)(2,1)S(1)}, u32[]{:S(2)}, u32[]{:S(2)}) collective-permute-start(bf16[24,32,384]{2,1,0:T(8,128)(2,1)} %get-tuple-element.27), channel_id=1, source_target_pairs={{0,1},{1,2},{2,3},{3,0},{4,5},{5,6},{6,7},{7,4},{8,9},{9,10},{10,1... | collective-permute-start | bytes 1769480 | tf_op jit(solution)/shard_map/ppermute | solution.py:352
  18.6 17.9 %collective-permute-start.7 = (bf16[24,32,384]{2,1,0:T(8,128)(2,1)}, bf16[24,32,384]{2,1,0:T(8,128)(2,1)S(1)}, u32[]{:S(2)}, u32[]{:S(2)}) collective-permute-start(bf16[24,32,384]{2,1,0:T(8,128)(2,1)} %get-tuple-element.28), channel_id=1, source_target_pairs={{0,3},{1,0},{2,1},{3,2},{4,7},{5,4},{6,5},{7,6},{8,11},{9,8},{10,9... | collective-permute-start | bytes 1769480 | tf_op jit(solution)/shard_map/ppermute | solution.py:353
  28.6 27.3 %collective-permute-start.2 = (bf16[24,32,640]{2,1,0:T(8,128)(2,1)}, bf16[24,32,640]{2,1,0:T(8,128)(2,1)S(1)}, u32[]{:S(2)}, u32[]{:S(2)}) collective-permute-start(bf16[24,32,640]{2,1,0:T(8,128)(2,1)} %get-tuple-element.24), channel_id=1, source_target_pairs={{0,1},{1,2},{2,3},{3,0},{4,5},{5,6},{6,7},{7,4},{8,9},{9,10},{10,1... | collective-permute-start | bytes 2949128 | tf_op jit(solution)/shard_map/ppermute | solution.py:352
  29.7 26.4 %collective-permute-start.3 = (bf16[24,32,640]{2,1,0:T(8,128)(2,1)}, bf16[24,32,640]{2,1,0:T(8,128)(2,1)S(1)}, u32[]{:S(2)}, u32[]{:S(2)}) collective-permute-start(bf16[24,32,640]{2,1,0:T(8,128)(2,1)} %get-tuple-element.25), channel_id=1, source_target_pairs={{0,3},{1,0},{2,1},{3,2},{4,7},{5,4},{6,5},{7,6},{8,11},{9,8},{10,9... | collective-permute-start | bytes 2949128 | tf_op jit(solution)/shard_map/ppermute | solution.py:353
  40.9 22.3 %all-to-all-start.1 = ((bf16[32,32,384]{2,1,0:T(8,128)(2,1)}), bf16[32,32,384]{2,1,0:T(8,128)(2,1)S(1)}, u32[]{:S(2)}, u32[]{:S(2)}) async-start(bf16[32,32,384]{2,1,0:T(8,128)(2,1)} %get-tuple-element.29), calls=%async_computation.1 | async-start | bytes 1572864 | tf_op jit(solution)/shard_map/all_to_all | solution.py:356
  63.1 27.7 %all-to-all-start = ((bf16[32,32,640]{2,1,0:T(8,128)(2,1)}), bf16[32,32,640]{2,1,0:T(8,128)(2,1)S(1)}, u32[]{:S(2)}, u32[]{:S(2)}) async-start(bf16[32,32,640]{2,1,0:T(8,128)(2,1)} %get-tuple-element.26), calls=%async_computation | async-start | bytes 2621440 | tf_op jit(solution)/shard_map/all_to_all | solution.py:356
  99.7 24.8 %all-to-all-start.2 = ((bf16[32,32,512]{2,1,0:T(8,128)(2,1)}), bf16[32,32,512]{2,1,0:T(8,128)(2,1)S(1)}, u32[]{:S(2)}, u32[]{:S(2)}) async-start(bf16[32,32,512]{2,1,0:T(8,128)(2,1)} %bitcast.44), calls=%async_computation.2 | async-start | bytes 2097152 | tf_op jit(solution)/shard_map/all_to_all | solution.py:393
  113.6 22.9 %collective-permute-start.18 = (bf16[12,32,512]{2,1,0:T(8,128)(2,1)S(1)}, bf16[12,32,512]{2,1,0:T(8,128)(2,1)S(1)}, u32[]{:S(2)}, u32[]{:S(2)}) collective-permute-start(bf16[12,32,512]{2,1,0:T(8,128)(2,1)S(1)} %get-tuple-element.57), channel_id=1, source_target_pairs={{0,1},{1,2},{2,3},{3,0},{4,5},{5,6},{6,7},{7,4},{8,9},{9,10},{10,1... | collective-permute-start | bytes 1179656 | tf_op jit(solution)/shard_map/ppermute | solution.py:314
  114.7 21.8 %collective-permute-start.20 = (bf16[12,32,512]{2,1,0:T(8,128)(2,1)S(1)}, bf16[12,32,512]{2,1,0:T(8,128)(2,1)}, u32[]{:S(2)}, u32[]{:S(2)}) collective-permute-start(bf16[12,32,512]{2,1,0:T(8,128)(2,1)S(1)} %get-tuple-element.56), channel_id=1, source_target_pairs={{0,3},{1,0},{2,1},{3,2},{4,7},{5,4},{6,5},{7,6},{8,11},{9,8},{10,9... | collective-permute-start | bytes 1179656 | tf_op jit(solution)/shard_map/ppermute | solution.py:315
  124.5 25.9 %all-to-all-start.3 = ((bf16[32,32,512]{2,1,0:T(8,128)(2,1)}), bf16[32,32,512]{2,1,0:T(8,128)(2,1)S(1)}, u32[]{:S(2)}, u32[]{:S(2)}) async-start(bf16[32,32,512]{2,1,0:T(8,128)(2,1)} %bitcast.16), calls=%async_computation.3 | async-start | bytes 2097152 | tf_op jit(solution)/shard_map/all_to_all | solution.py:393
  136.5 20.3 %collective-permute-start.31 = (bf16[12,32,512]{2,1,0:T(8,128)(2,1)S(1)}, bf16[12,32,512]{2,1,0:T(8,128)(2,1)}, u32[]{:S(2)}, u32[]{:S(2)}) collective-permute-start(bf16[12,32,512]{2,1,0:T(8,128)(2,1)S(1)} %get-tuple-element.57), channel_id=1, source_target_pairs={{0,3},{1,0},{2,1},{3,2},{4,7},{5,4},{6,5},{7,6},{8,11},{9,8},{10,9... | collective-permute-start | bytes 1179656 | tf_op jit(solution)/shard_map/ppermute | solution.py:317
  139.7 19.2 %collective-permute-start.19 = (bf16[12,32,512]{2,1,0:T(8,128)(2,1)S(1)}, bf16[12,32,512]{2,1,0:T(8,128)(2,1)}, u32[]{:S(2)}, u32[]{:S(2)}) collective-permute-start(bf16[12,32,512]{2,1,0:T(8,128)(2,1)S(1)} %collective-permute-done.18.refs_0_), channel_id=1, source_target_pairs={{0,1},{1,2},{2,3},{3,0},{4,5},{5,6},{6,7},{7,4},{8,9},{9,10},{10,1... | collective-permute-start | bytes 1179656 | tf_op jit(solution)/shard_map/ppermute | solution.py:318
  139.7 20.4 %collective-permute-start.21 = (bf16[12,32,512]{2,1,0:T(8,128)(2,1)}, bf16[12,32,512]{2,1,0:T(8,128)(2,1)}, u32[]{:S(2)}, u32[]{:S(2)}) collective-permute-start(bf16[12,32,512]{2,1,0:T(8,128)(2,1)} %collective-permute-done.20.refs_1_), channel_id=1, source_target_pairs={{0,3},{1,0},{2,1},{3,2},{4,7},{5,4},{6,5},{7,6},{8,11},{9,8},{10,9... | collective-permute-start | bytes 1179656 | tf_op jit(solution)/shard_map/ppermute | solution.py:319
  145.8 20.8 %collective-permute-start.22 = (bf16[12,32,512]{2,1,0:T(8,128)(2,1)}, bf16[12,32,512]{2,1,0:T(8,128)(2,1)}, u32[]{:S(2)}, u32[]{:S(2)}) collective-permute-start(bf16[12,32,512]{2,1,0:T(8,128)(2,1)} %get-tuple-element.40), channel_id=1, source_target_pairs={{0,1},{1,2},{2,3},{3,0},{4,5},{5,6},{6,7},{7,4},{8,9},{9,10},{10,1... | collective-permute-start | bytes 1179656 | tf_op jit(solution)/shard_map/ppermute | solution.py:314
  149.8 16.9 %collective-permute-start.24 = (bf16[12,32,512]{2,1,0:T(8,128)(2,1)}, bf16[12,32,512]{2,1,0:T(8,128)(2,1)S(1)}, u32[]{:S(2)}, u32[]{:S(2)}) collective-permute-start(bf16[12,32,512]{2,1,0:T(8,128)(2,1)} %get-tuple-element.41), channel_id=1, source_target_pairs={{0,3},{1,0},{2,1},{3,2},{4,7},{5,4},{6,5},{7,6},{8,11},{9,8},{10,9... | collective-permute-start | bytes 1179656 | tf_op jit(solution)/shard_map/ppermute | solution.py:315
  156.8 18.1 %collective-permute-start.32 = (bf16[12,32,512]{2,1,0:T(8,128)(2,1)}, bf16[12,32,512]{2,1,0:T(8,128)(2,1)S(1)}, u32[]{:S(2)}, u32[]{:S(2)}) collective-permute-start(bf16[12,32,512]{2,1,0:T(8,128)(2,1)} %get-tuple-element.41), channel_id=1, source_target_pairs={{0,1},{1,2},{2,3},{3,0},{4,5},{5,6},{6,7},{7,4},{8,9},{9,10},{10,1... | collective-permute-start | bytes 1179656 | tf_op jit(solution)/shard_map/ppermute | solution.py:316
  160.1 23.3 %collective-permute-start.26 = (bf16[12,32,512]{2,1,0:T(8,128)(2,1)}, bf16[12,32,512]{2,1,0:T(8,128)(2,1)S(1)}, u32[]{:S(2)}, u32[]{:S(2)}) collective-permute-start(bf16[12,32,512]{2,1,0:T(8,128)(2,1)} %get-tuple-element.43), channel_id=1, source_target_pairs={{0,1},{1,2},{2,3},{3,0},{4,5},{5,6},{6,7},{7,4},{8,9},{9,10},{10,1... | collective-permute-start | bytes 1179656 | tf_op jit(solution)/shard_map/ppermute | solution.py:314
  166.6 25.3 %collective-permute-start.28 = (bf16[12,32,512]{2,1,0:T(8,128)(2,1)}, bf16[12,32,512]{2,1,0:T(8,128)(2,1)}, u32[]{:S(2)}, u32[]{:S(2)}) collective-permute-start(bf16[12,32,512]{2,1,0:T(8,128)(2,1)} %get-tuple-element.44), channel_id=1, source_target_pairs={{0,1},{1,2},{2,3},{3,0},{4,5},{5,6},{6,7},{7,4},{8,9},{9,10},{10,1... | collective-permute-start | bytes 1179656 | tf_op jit(solution)/shard_map/ppermute | solution.py:316
  174.9 20.8 %collective-permute-start.29 = (bf16[12,32,512]{2,1,0:T(8,128)(2,1)}, bf16[12,32,512]{2,1,0:T(8,128)(2,1)}, u32[]{:S(2)}, u32[]{:S(2)}) collective-permute-start(bf16[12,32,512]{2,1,0:T(8,128)(2,1)} %get-tuple-element.43), channel_id=1, source_target_pairs={{0,3},{1,0},{2,1},{3,2},{4,7},{5,4},{6,5},{7,6},{8,11},{9,8},{10,9... | collective-permute-start | bytes 1179656 | tf_op jit(solution)/shard_map/ppermute | solution.py:317
  174.9 25.4 %collective-permute-start.23 = (bf16[12,32,512]{2,1,0:T(8,128)(2,1)}, bf16[12,32,512]{2,1,0:T(8,128)(2,1)}, u32[]{:S(2)}, u32[]{:S(2)}) collective-permute-start(bf16[12,32,512]{2,1,0:T(8,128)(2,1)} %collective-permute-done.22.refs_4_), channel_id=1, source_target_pairs={{0,1},{1,2},{2,3},{3,0},{4,5},{5,6},{6,7},{7,4},{8,9},{9,10},{10,1... | collective-permute-start | bytes 1179656 | tf_op jit(solution)/shard_map/ppermute | solution.py:318
  183.4 17.0 %collective-permute-start.25 = (bf16[12,32,512]{2,1,0:T(8,128)(2,1)S(1)}, bf16[12,32,512]{2,1,0:T(8,128)(2,1)}, u32[]{:S(2)}, u32[]{:S(2)}) collective-permute-start(bf16[12,32,512]{2,1,0:T(8,128)(2,1)S(1)} %collective-permute-done.24.refs_5_), channel_id=1, source_target_pairs={{0,3},{1,0},{2,1},{3,2},{4,7},{5,4},{6,5},{7,6},{8,11},{9,8},{10,9... | collective-permute-start | bytes 1179656 | tf_op jit(solution)/shard_map/ppermute | solution.py:319
  183.4 23.6 %collective-permute-start.34 = (bf16[12,32,512]{2,1,0:T(8,128)(2,1)S(1)}, bf16[12,32,512]{2,1,0:T(8,128)(2,1)S(1)}, u32[]{:S(2)}, u32[]{:S(2)}) collective-permute-start(bf16[12,32,512]{2,1,0:T(8,128)(2,1)S(1)} %collective-permute-done.26.refs_4_), channel_id=1, source_target_pairs={{0,1},{1,2},{2,3},{3,0},{4,5},{5,6},{6,7},{7,4},{8,9},{9,10},{10,1... | collective-permute-start | bytes 1179656 | tf_op jit(solution)/shard_map/ppermute | solution.py:318
  (41 other events, 451.2 us)

commit v10 on v9

--- a/solution.py
+++ b/solution.py
@@ -253,7 +253,7 @@
 
 
 def place(owners, scales, whole, raw, ready):
-    half, rows, _ = raw[0][2].shape
+    half, rows, _ = (raw or ready)[0][2].shape
     blocks = 2 * half
     pieces = len(raw) + len(ready)
 
@@ -292,7 +292,7 @@
             in_specs=[*[block_of(array) for array in arrays], hbm],
             out_specs=hbm,
             scratch_shapes=[
-                pltpu.VMEM((len(raw), half, rows, RAW), bf16),
+                pltpu.VMEM((max(len(raw), 1), half, rows, RAW), bf16),
                 pltpu.SemaphoreType.DMA((pieces,)),
             ],
         ),
@@ -401,8 +401,8 @@
 
     raw = [(offset, part, old, change) for (offset, part, old), (_, _, change) in zip(ahead, changes)]
     flat = scales.reshape(-1)
-    new_params = place(who, flat, new_params, raw[:4], ())
-    new_params = place(who, flat, new_params, raw[4:], finished[:4])
+    new_params = place(who, flat, new_params, raw, ())
+    new_params = place(who, flat, new_params, (), finished[:4])
     for offset, part, piece in finished[4:]:
         owner = lax.rem(me + offset, reps)
         new_params = lax.dynamic_update_slice(new_params, piece[None], (owner, part * half, 0, RAW))

time: 210 us -> 211 us (level)
  local copies, waits for them, and re-layouts: 12.8 us -> 15.2 us
    ppermute x3, waiting for transfers between devices: 16.5 us -> 2.58 us  [spread(): high_up = lax.ppermute(high, 'rep', up)]
    ppermute x3, starting transfers between devices: 2.25 us -> 10.1 us  [spread(): high_down = lax.ppermute(high, 'rep', down)]
    ppermute x3, waiting for transfers between devices: 0.01 us -> 7.3 us  [spread(): low_down = lax.ppermute(low, 'rep', down)]
    ppermute x3, waiting for transfers between devices: 12.1 us -> 5.11 us  [spread(): low_up = lax.ppermute(low, 'rep', up)]
    ppermute x9, starting transfers between devices: 17 us -> 12.7 us  [everywhere(): lax.ppermute(value, axis, ring(4, step))]
    ppermute x3, waiting for transfers between devices: 0.01 us -> 4.08 us  [spread(): high_down = lax.ppermute(high, 'rep', down)]
    ppermute x3, starting transfers between devices: 4.11 us -> 0.09 us  [spread(): high_up = lax.ppermute(high, 'rep', up)]
    ppermute x3, waiting for transfers between devices: 7.12 us -> 10.8 us  [spread(): far_low = lax.ppermute(low_up, 'rep', up)]
  transfers between devices with their start and end apart: 40 -> 40, of which waited for: 19 -> 19; matrix products, arithmetic and copies ran while one was open for 5% -> 6% of each run, Pallas kernels for 17% -> 16%
where the time goes in v10:
time: 211 us; the launch traced here: 209 us
  starting transfers between devices  73.5 us (35%)
  waiting for transfers between devices  69.3 us (33%)
  Pallas kernels  42.1 us (20%)
  local copies, waits for them, and re-layouts  15.2 us (7%)
  other arithmetic  7.53 us (4%)
    all_to_all x4, starting transfers between devices, local(): lax.all_to_all(outgoing, GROUP, split_axis=0, concat_axis=0, tiled=True)  25.9 us
    all_to_all x4, waiting for transfers between devices, local(): lax.all_to_all(outgoing, GROUP, split_axis=0, concat_axis=0, tiled=True)  14.6 us
    ppermute x9, starting transfers between devices, everywhere(): lax.ppermute(value, axis, ring(4, step))  12.7 us
    ppermute x2, waiting for transfers between devices, local(): near_up = lax.ppermute(to_up, 'rep', up)  11.2 us
    ppermute x3, waiting for transfers between devices, spread(): far_low = lax.ppermute(low_up, 'rep', up)  10.8 us
    ppermute x3, starting transfers between devices, spread(): high_down = lax.ppermute(high, 'rep', down)  10.1 us
    unnamed x54, local copies, waits for them, and re-layouts  9.29 us
    pallas_call x2, Pallas kernels, finish(): pl.pallas_call(body, grid_spec=pltpu.PrefetchScalarGridSpec(num_scalar_pr...  8.18 us
  transfers between devices with their start and end apart: 40, of which 19 were waited for; matrix products, arithmetic and copies ran while one was open for 6% of the time, Pallas kernels for 16%

profile of v10, /device:TPU:0, one launch (start us, length us, event | category | flops | bytes accessed | tf_op | source)
XLA Modules:
  0.0 208.7 jit_solution(10119509735793251140)
XLA Ops:
  12.1 3.7 %collective-permute-done.4.from_down = bf16[12,32,384]{2,1,0:T(8,128)(2,1)S(1)} collective-permute-done((bf16[12,32,384]{2,1,0:T(8,128)(2,1)S(1)}, bf16[12,32,384]{2,1,0:T(8,128)(2,1)S(1)}, u32[]{:S(2)}, u32[]{:S(2)}) %collective-permute-start.4) | collective-permute-done | bytes 294944 | tf_op jit(solution)/shard_map/ppermute | solution.py:349
  22.8 3.5 %collective-permute-done.from_down = bf16[12,32,640]{2,1,0:T(8,128)(2,1)S(1)} collective-permute-done((bf16[12,32,640]{2,1,0:T(8,128)(2,1)S(1)}, bf16[12,32,640]{2,1,0:T(8,128)(2,1)S(1)}, u32[]{:S(2)}, u32[]{:S(2)}) %collective-permute-start) | collective-permute-done | bytes 491552 | tf_op jit(solution)/shard_map/ppermute | solution.py:349
  27.1 3.6 %merge.2 = (bf16[24,32,640]{2,1,0:T(8,128)(2,1)}, bf16[24,32,640]{2,1,0:T(8,128)(2,1)}) custom-call(s32[4]{0:T(128)} %compare_select_fusion.who_ref.owners_ref, bf16[4,24,32,1024]{3,2,1,0:T(8,128)(2,1)} %bitcast.34, bf16[4,24,32,1024]{3,2,1,0:T(8,128)(2,1)} %bitcast.35, bf16[12,32,640]{2,1,0:T(8,128)(2,1)} %copy-done.11, bf16[12,32,640]{2,1,0:T(8,128)(2,1)} %copy-done.10), custom_call_target="tpu_custom_call" | custom-call | tf_op jit(solution)/shard_map/merge/pallas_call | solution.py:51
  34.5 4.5 %collective-permute-done.6.one = bf16[24,32,384]{2,1,0:T(8,128)(2,1)S(1)} collective-permute-done((bf16[24,32,384]{2,1,0:T(8,128)(2,1)}, bf16[24,32,384]{2,1,0:T(8,128)(2,1)S(1)}, u32[]{:S(2)}, u32[]{:S(2)}) %collective-permute-start.6) | collective-permute-done | bytes 589856 | tf_op jit(solution)/shard_map/ppermute | solution.py:352
  40.0 3.6 %shard_map.87 = (bf16[24,32,384]{2,1,0:T(8,128)(2,1)}, bf16[32,32,384]{2,1,0:T(8,128)(2,1)}) custom-call(s32[4]{0:T(128)} %compare_select_fusion.who_ref.owners_ref, s32[32]{0:T(128)} %get-tuple-element.50.table_ref, bf16[4,24,32,1024]{3,2,1,0:T(8,128)(2,1)} %bitcast.36, bf16[24,32,384]{2,1,0:T(8,128)(2,1)} %copy-done.8, bf16[24,32,384]{2,1,0:T(8,128)(2,1)} %copy-done.9), custom_call_target="tpu_custom_call" | custom-call | tf_op jit(solution)/shard_map/pallas_call | solution.py:80
  43.6 8.3 %all-to-all-start.1 = ((bf16[32,32,384]{2,1,0:T(8,128)(2,1)}), bf16[32,32,384]{2,1,0:T(8,128)(2,1)S(1)}, u32[]{:S(2)}, u32[]{:S(2)}) async-start(bf16[32,32,384]{2,1,0:T(8,128)(2,1)} %get-tuple-element.29), calls=%async_computation.1 | async-start | bytes 1572864 | tf_op jit(solution)/shard_map/all_to_all | solution.py:356
  51.9 6.7 %collective-permute-done.2.one = bf16[24,32,640]{2,1,0:T(8,128)(2,1)S(1)} collective-permute-done((bf16[24,32,640]{2,1,0:T(8,128)(2,1)}, bf16[24,32,640]{2,1,0:T(8,128)(2,1)S(1)}, u32[]{:S(2)}, u32[]{:S(2)}) %collective-permute-start.2) | collective-permute-done | bytes 983072 | tf_op jit(solution)/shard_map/ppermute | solution.py:352
  60.6 4.6 %shard_map.86 = (bf16[24,32,640]{2,1,0:T(8,128)(2,1)}, bf16[32,32,640]{2,1,0:T(8,128)(2,1)}) custom-call(s32[4]{0:T(128)} %compare_select_fusion.who_ref.owners_ref, s32[32]{0:T(128)} %get-tuple-element.50.table_ref, bf16[4,24,32,1024]{3,2,1,0:T(8,128)(2,1)} %bitcast.37, bf16[24,32,640]{2,1,0:T(8,128)(2,1)} %copy-done.6, bf16[24,32,640]{2,1,0:T(8,128)(2,1)} %copy-done.7), custom_call_target="tpu_custom_call" | custom-call | tf_op jit(solution)/shard_map/pallas_call | solution.py:80
  65.8 7.7 %all-to-all-start = ((bf16[32,32,640]{2,1,0:T(8,128)(2,1)}), bf16[32,32,640]{2,1,0:T(8,128)(2,1)S(1)}, u32[]{:S(2)}, u32[]{:S(2)}) async-start(bf16[32,32,640]{2,1,0:T(8,128)(2,1)} %get-tuple-element.26), calls=%async_computation | async-start | bytes 2621440 | tf_op jit(solution)/shard_map/all_to_all | solution.py:356
  75.7 3.6 %left_times.1.rest_0_ = bf16[1024,384]{1,0:T(8,128)(2,1)} custom-call(bf16[1024,1024]{1,0:T(8,128)(2,1)} %bitcast.39, bf16[1024,384]{1,0:T(8,128)(2,1)} %bitcast.42), custom_call_target="tpu_custom_call" | custom-call | tf_op jit(solution)/shard_map/left_times/pallas_call | solution.py:106
  79.4 14.0 %all-to-all-done = bf16[32,32,640]{2,1,0:T(8,128)(2,1)S(1)} async-done(((bf16[32,32,640]{2,1,0:T(8,128)(2,1)}), bf16[32,32,640]{2,1,0:T(8,128)(2,1)S(1)}, u32[]{:S(2)}, u32[]{:S(2)}) %all-to-all-start) | async-done | bytes 1310752 | tf_op jit(solution)/shard_map/all_to_all | solution.py:356
  94.4 7.8 %products.1 = (bf16[1024,512]{1,0:T(8,128)(2,1)}, bf16[1024,512]{1,0:T(8,128)(2,1)}, f32[2,128]{1,0:T(2,128)}) custom-call(bf16[1024,1024]{1,0:T(8,128)(2,1)} %bitcast.40, bf16[1024,1024]{1,0:T(8,128)(2,1)} %bitcast.43, bf16[1024,640]{1,0:T(8,128)(2,1)} %bitcast.41, f32[1,128]{1,0:T(1,128)} %pad.8.layer_ref, bf16[1024,384]{1,0:T(8,128)(2,1)} %left_times.1.rest_0_), custom_call_target="tpu_custom_call" | custom-call | tf_op jit(solution)/shard_map/products/pallas_call | solution.py:148
  102.2 3.9 %all-to-all-start.2 = ((bf16[32,32,512]{2,1,0:T(8,128)(2,1)}), bf16[32,32,512]{2,1,0:T(8,128)(2,1)S(1)}, u32[]{:S(2)}, u32[]{:S(2)}) async-start(bf16[32,32,512]{2,1,0:T(8,128)(2,1)} %bitcast.44), calls=%async_computation.2 | async-start | bytes 2097152 | tf_op jit(solution)/shard_map/all_to_all | solution.py:393
  106.2 4.6 %fusion.2 = (f32[24]{0:T(128)S(1)}, f32[24,32,1024]{2,1,0:T(8,128)}) fusion(bf16[24,32,640]{2,1,0:T(8,128)(2,1)S(1)} %copy-done.5, bf16[24,32,384]{2,1,0:T(8,128)(2,1)} %get-tuple-element.37, f32[24,32,1024]{2,1,0:T(8,128)} %param.9), kind=kLoop, calls=%fused_computation.4 | loop fusion | flops 7077864 | bytes 7864416 | tf_op jit(solution)/shard_map/reduce_sum | solution.py:386
  124.6 5.9 %all-to-all-start.3 = ((bf16[32,32,512]{2,1,0:T(8,128)(2,1)}), bf16[32,32,512]{2,1,0:T(8,128)(2,1)S(1)}, u32[]{:S(2)}, u32[]{:S(2)}) async-start(bf16[32,32,512]{2,1,0:T(8,128)(2,1)} %bitcast.16), calls=%async_computation.3 | async-start | bytes 2097152 | tf_op jit(solution)/shard_map/all_to_all | solution.py:393
  151.6 5.3 %update.1 = (bf16[12,32,512]{2,1,0:T(8,128)(2,1)}, bf16[12,32,512]{2,1,0:T(8,128)(2,1)}, bf16[4,24,32,1024]{3,2,1,0:T(8,128)(2,1)}) custom-call(s32[4]{0:T(128)} %compare_select_fusion.who_ref.owners_ref, s32[24]{0:T(128)} %select_reduce_fusion.position_ref, f32[24]{0:T(128)} %fusion.6.scale_ref, bf16[32,32,512]{2,1,0:T(8,128)(2,1)} %copy-done, ...), custom_call_target="tpu_custom_call" | custom-call | tf_op jit(solution)/shard_map/update/pallas_call | solution.py:234
  157.8 3.8 %collective-permute-start.29 = (bf16[12,32,512]{2,1,0:T(8,128)(2,1)}, bf16[12,32,512]{2,1,0:T(8,128)(2,1)S(1)}, u32[]{:S(2)}, u32[]{:S(2)}) collective-permute-start(bf16[12,32,512]{2,1,0:T(8,128)(2,1)} %get-tuple-element.44), channel_id=1, source_target_pairs={{0,3},{1,0},{2,1},{3,2},{4,7},{5,4},{6,5},{7,6},{8,11},{9,8},{10,9... | collective-permute-start | bytes 1179656 | tf_op jit(solution)/shard_map/ppermute | solution.py:315
  161.6 4.7 %collective-permute-done.31.refs_9_ = bf16[12,32,512]{2,1,0:T(8,128)(2,1)S(1)} collective-permute-done((bf16[12,32,512]{2,1,0:T(8,128)(2,1)}, bf16[12,32,512]{2,1,0:T(8,128)(2,1)S(1)}, u32[]{:S(2)}, u32[]{:S(2)}) %collective-permute-start.31) | collective-permute-done | bytes 393248 | tf_op jit(solution)/shard_map/ppermute | solution.py:317
  167.1 3.6 %collective-permute-start.19 = (bf16[12,32,512]{2,1,0:T(8,128)(2,1)}, bf16[12,32,512]{2,1,0:T(8,128)(2,1)S(1)}, u32[]{:S(2)}, u32[]{:S(2)}) collective-permute-start(bf16[12,32,512]{2,1,0:T(8,128)(2,1)} %get-tuple-element.42), channel_id=1, source_target_pairs={{0,3},{1,0},{2,1},{3,2},{4,7},{5,4},{6,5},{7,6},{8,11},{9,8},{10,9... | collective-permute-start | bytes 1179656 | tf_op jit(solution)/shard_map/ppermute | solution.py:315
  170.7 4.1 %collective-permute-done.29.refs_7_ = bf16[12,32,512]{2,1,0:T(8,128)(2,1)S(1)} collective-permute-done((bf16[12,32,512]{2,1,0:T(8,128)(2,1)}, bf16[12,32,512]{2,1,0:T(8,128)(2,1)S(1)}, u32[]{:S(2)}, u32[]{:S(2)}) %collective-permute-start.29) | collective-permute-done | bytes 393248 | tf_op jit(solution)/shard_map/ppermute | solution.py:315
  174.7 3.6 %collective-permute-start.33 = (bf16[12,32,512]{2,1,0:T(8,128)(2,1)S(1)}, bf16[12,32,512]{2,1,0:T(8,128)(2,1)S(1)}, u32[]{:S(2)}, u32[]{:S(2)}) collective-permute-start(bf16[12,32,512]{2,1,0:T(8,128)(2,1)S(1)} %collective-permute-done.29.refs_7_), channel_id=1, source_target_pairs={{0,3},{1,0},{2,1},{3,2},{4,7},{5,4},{6,5},{7,6},{8,11},{9,8},{10,9... | collective-permute-start | bytes 1179656 | tf_op jit(solution)/shard_map/ppermute | solution.py:319
  178.4 5.1 %collective-permute-done.18.refs_0_ = bf16[12,32,512]{2,1,0:T(8,128)(2,1)S(1)} collective-permute-done((bf16[12,32,512]{2,1,0:T(8,128)(2,1)}, bf16[12,32,512]{2,1,0:T(8,128)(2,1)S(1)}, u32[]{:S(2)}, u32[]{:S(2)}) %collective-permute-start.18) | collective-permute-done | bytes 393248 | tf_op jit(solution)/shard_map/ppermute | solution.py:314
  183.6 8.4 %collective-permute-done.32.refs_10_ = bf16[12,32,512]{2,1,0:T(8,128)(2,1)} collective-permute-done((bf16[12,32,512]{2,1,0:T(8,128)(2,1)S(1)}, bf16[12,32,512]{2,1,0:T(8,128)(2,1)}, u32[]{:S(2)}, u32[]{:S(2)}) %collective-permute-start.32) | collective-permute-done | bytes 393248 | tf_op jit(solution)/shard_map/ppermute | solution.py:318
  192.9 4.5 %shard_map.88.refs_4_ = bf16[4,24,32,1024]{3,2,1,0:T(8,128)(2,1)} custom-call(s32[4]{0:T(128)} %compare_select_fusion.who_ref.owners_ref, f32[96]{0:T(128)} %copy-done.23, bf16[12,32,512]{2,1,0:T(8,128)(2,1)} %collective-permute-done.22.refs_0_, bf16[12,32,512]{2,1,0:T(8,128)(2,1)} %copy-done.16, ...), custom_call_target="tpu_custom_call", output_to_operand_aliasing={{}: (14, {})} | custom-call | tf_op jit(solution)/shard_map/pallas_call | solution.py:287
  (145 shorter events, 78.6 us)
Async XLA Ops:
  9.3 17.0 %collective-permute-start = (bf16[12,32,640]{2,1,0:T(8,128)(2,1)S(1)}, bf16[12,32,640]{2,1,0:T(8,128)(2,1)S(1)}, u32[]{:S(2)}, u32[]{:S(2)}) collective-permute-start(bf16[12,32,640]{2,1,0:T(8,128)(2,1)S(1)} %get-tuple-element.55), channel_id=1, source_target_pairs={{0,1},{1,2},{2,3},{3,0},{4,5},{5,6},{6,7},{7,4},{8,9},{9,10},{10,1... | collective-permute-start | bytes 1474568 | tf_op jit(solution)/shard_map/ppermute | solution.py:349
  19.6 19.4 %collective-permute-start.6 = (bf16[24,32,384]{2,1,0:T(8,128)(2,1)}, bf16[24,32,384]{2,1,0:T(8,128)(2,1)S(1)}, u32[]{:S(2)}, u32[]{:S(2)}) collective-permute-start(bf16[24,32,384]{2,1,0:T(8,128)(2,1)} %get-tuple-element.27), channel_id=1, source_target_pairs={{0,1},{1,2},{2,3},{3,0},{4,5},{5,6},{6,7},{7,4},{8,9},{9,10},{10,1... | collective-permute-start | bytes 1769480 | tf_op jit(solution)/shard_map/ppermute | solution.py:352
  19.6 19.4 %collective-permute-start.7 = (bf16[24,32,384]{2,1,0:T(8,128)(2,1)}, bf16[24,32,384]{2,1,0:T(8,128)(2,1)S(1)}, u32[]{:S(2)}, u32[]{:S(2)}) collective-permute-start(bf16[24,32,384]{2,1,0:T(8,128)(2,1)} %get-tuple-element.28), channel_id=1, source_target_pairs={{0,3},{1,0},{2,1},{3,2},{4,7},{5,4},{6,5},{7,6},{8,11},{9,8},{10,9... | collective-permute-start | bytes 1769480 | tf_op jit(solution)/shard_map/ppermute | solution.py:353
  30.7 27.9 %collective-permute-start.2 = (bf16[24,32,640]{2,1,0:T(8,128)(2,1)}, bf16[24,32,640]{2,1,0:T(8,128)(2,1)S(1)}, u32[]{:S(2)}, u32[]{:S(2)}) collective-permute-start(bf16[24,32,640]{2,1,0:T(8,128)(2,1)} %get-tuple-element.24), channel_id=1, source_target_pairs={{0,1},{1,2},{2,3},{3,0},{4,5},{5,6},{6,7},{7,4},{8,9},{9,10},{10,1... | collective-permute-start | bytes 2949128 | tf_op jit(solution)/shard_map/ppermute | solution.py:352
  30.7 27.9 %collective-permute-start.3 = (bf16[24,32,640]{2,1,0:T(8,128)(2,1)}, bf16[24,32,640]{2,1,0:T(8,128)(2,1)S(1)}, u32[]{:S(2)}, u32[]{:S(2)}) collective-permute-start(bf16[24,32,640]{2,1,0:T(8,128)(2,1)} %get-tuple-element.25), channel_id=1, source_target_pairs={{0,3},{1,0},{2,1},{3,2},{4,7},{5,4},{6,5},{7,6},{8,11},{9,8},{10,9... | collective-permute-start | bytes 2949128 | tf_op jit(solution)/shard_map/ppermute | solution.py:353
  43.6 22.3 %all-to-all-start.1 = ((bf16[32,32,384]{2,1,0:T(8,128)(2,1)}), bf16[32,32,384]{2,1,0:T(8,128)(2,1)S(1)}, u32[]{:S(2)}, u32[]{:S(2)}) async-start(bf16[32,32,384]{2,1,0:T(8,128)(2,1)} %get-tuple-element.29), calls=%async_computation.1 | async-start | bytes 1572864 | tf_op jit(solution)/shard_map/all_to_all | solution.py:356
  65.8 27.5 %all-to-all-start = ((bf16[32,32,640]{2,1,0:T(8,128)(2,1)}), bf16[32,32,640]{2,1,0:T(8,128)(2,1)S(1)}, u32[]{:S(2)}, u32[]{:S(2)}) async-start(bf16[32,32,640]{2,1,0:T(8,128)(2,1)} %get-tuple-element.26), calls=%async_computation | async-start | bytes 2621440 | tf_op jit(solution)/shard_map/all_to_all | solution.py:356
  102.2 22.4 %all-to-all-start.2 = ((bf16[32,32,512]{2,1,0:T(8,128)(2,1)}), bf16[32,32,512]{2,1,0:T(8,128)(2,1)S(1)}, u32[]{:S(2)}, u32[]{:S(2)}) async-start(bf16[32,32,512]{2,1,0:T(8,128)(2,1)} %bitcast.44), calls=%async_computation.2 | async-start | bytes 2097152 | tf_op jit(solution)/shard_map/all_to_all | solution.py:393
  114.3 22.3 %collective-permute-start.23 = (bf16[12,32,512]{2,1,0:T(8,128)(2,1)S(1)}, bf16[12,32,512]{2,1,0:T(8,128)(2,1)S(1)}, u32[]{:S(2)}, u32[]{:S(2)}) collective-permute-start(bf16[12,32,512]{2,1,0:T(8,128)(2,1)S(1)} %get-tuple-element.56), channel_id=1, source_target_pairs={{0,3},{1,0},{2,1},{3,2},{4,7},{5,4},{6,5},{7,6},{8,11},{9,8},{10,9... | collective-permute-start | bytes 1179656 | tf_op jit(solution)/shard_map/ppermute | solution.py:315
  117.0 19.6 %collective-permute-start.22 = (bf16[12,32,512]{2,1,0:T(8,128)(2,1)S(1)}, bf16[12,32,512]{2,1,0:T(8,128)(2,1)}, u32[]{:S(2)}, u32[]{:S(2)}) collective-permute-start(bf16[12,32,512]{2,1,0:T(8,128)(2,1)S(1)} %get-tuple-element.57), channel_id=1, source_target_pairs={{0,1},{1,2},{2,3},{3,0},{4,5},{5,6},{6,7},{7,4},{8,9},{9,10},{10,1... | collective-permute-start | bytes 1179656 | tf_op jit(solution)/shard_map/ppermute | solution.py:314
  124.6 26.0 %all-to-all-start.3 = ((bf16[32,32,512]{2,1,0:T(8,128)(2,1)}), bf16[32,32,512]{2,1,0:T(8,128)(2,1)S(1)}, u32[]{:S(2)}, u32[]{:S(2)}) async-start(bf16[32,32,512]{2,1,0:T(8,128)(2,1)} %bitcast.16), calls=%async_computation.3 | async-start | bytes 2097152 | tf_op jit(solution)/shard_map/all_to_all | solution.py:393
  136.6 20.3 %collective-permute-start.25 = (bf16[12,32,512]{2,1,0:T(8,128)(2,1)S(1)}, bf16[12,32,512]{2,1,0:T(8,128)(2,1)}, u32[]{:S(2)}, u32[]{:S(2)}) collective-permute-start(bf16[12,32,512]{2,1,0:T(8,128)(2,1)S(1)} %get-tuple-element.57), channel_id=1, source_target_pairs={{0,3},{1,0},{2,1},{3,2},{4,7},{5,4},{6,5},{7,6},{8,11},{9,8},{10,9... | collective-permute-start | bytes 1179656 | tf_op jit(solution)/shard_map/ppermute | solution.py:317
  140.1 17.7 %collective-permute-start.27 = (bf16[12,32,512]{2,1,0:T(8,128)(2,1)S(1)}, bf16[12,32,512]{2,1,0:T(8,128)(2,1)}, u32[]{:S(2)}, u32[]{:S(2)}) collective-permute-start(bf16[12,32,512]{2,1,0:T(8,128)(2,1)S(1)} %collective-permute-done.23.refs_1_), channel_id=1, source_target_pairs={{0,3},{1,0},{2,1},{3,2},{4,7},{5,4},{6,5},{7,6},{8,11},{9,8},{10,9... | collective-permute-start | bytes 1179656 | tf_op jit(solution)/shard_map/ppermute | solution.py:319
  141.4 20.2 %collective-permute-start.26 = (bf16[12,32,512]{2,1,0:T(8,128)(2,1)}, bf16[12,32,512]{2,1,0:T(8,128)(2,1)}, u32[]{:S(2)}, u32[]{:S(2)}) collective-permute-start(bf16[12,32,512]{2,1,0:T(8,128)(2,1)} %collective-permute-done.22.refs_0_), channel_id=1, source_target_pairs={{0,1},{1,2},{2,3},{3,0},{4,5},{5,6},{6,7},{7,4},{8,9},{9,10},{10,1... | collective-permute-start | bytes 1179656 | tf_op jit(solution)/shard_map/ppermute | solution.py:318
  145.0 21.3 %collective-permute-start.31 = (bf16[12,32,512]{2,1,0:T(8,128)(2,1)}, bf16[12,32,512]{2,1,0:T(8,128)(2,1)S(1)}, u32[]{:S(2)}, u32[]{:S(2)}) collective-permute-start(bf16[12,32,512]{2,1,0:T(8,128)(2,1)} %get-tuple-element.43), channel_id=1, source_target_pairs={{0,3},{1,0},{2,1},{3,2},{4,7},{5,4},{6,5},{7,6},{8,11},{9,8},{10,9... | collective-permute-start | bytes 1179656 | tf_op jit(solution)/shard_map/ppermute | solution.py:317
  149.9 20.7 %collective-permute-start.28 = (bf16[12,32,512]{2,1,0:T(8,128)(2,1)}, bf16[12,32,512]{2,1,0:T(8,128)(2,1)S(1)}, u32[]{:S(2)}, u32[]{:S(2)}) collective-permute-start(bf16[12,32,512]{2,1,0:T(8,128)(2,1)} %get-tuple-element.43), channel_id=1, source_target_pairs={{0,1},{1,2},{2,3},{3,0},{4,5},{5,6},{6,7},{7,4},{8,9},{9,10},{10,1... | collective-permute-start | bytes 1179656 | tf_op jit(solution)/shard_map/ppermute | solution.py:314
  156.9 21.4 %collective-permute-start.30 = (bf16[12,32,512]{2,1,0:T(8,128)(2,1)}, bf16[12,32,512]{2,1,0:T(8,128)(2,1)}, u32[]{:S(2)}, u32[]{:S(2)}) collective-permute-start(bf16[12,32,512]{2,1,0:T(8,128)(2,1)} %get-tuple-element.44), channel_id=1, source_target_pairs={{0,1},{1,2},{2,3},{3,0},{4,5},{5,6},{6,7},{7,4},{8,9},{9,10},{10,1... | collective-permute-start | bytes 1179656 | tf_op jit(solution)/shard_map/ppermute | solution.py:316
  157.8 17.0 %collective-permute-start.29 = (bf16[12,32,512]{2,1,0:T(8,128)(2,1)}, bf16[12,32,512]{2,1,0:T(8,128)(2,1)S(1)}, u32[]{:S(2)}, u32[]{:S(2)}) collective-permute-start(bf16[12,32,512]{2,1,0:T(8,128)(2,1)} %get-tuple-element.44), channel_id=1, source_target_pairs={{0,3},{1,0},{2,1},{3,2},{4,7},{5,4},{6,5},{7,6},{8,11},{9,8},{10,9... | collective-permute-start | bytes 1179656 | tf_op jit(solution)/shard_map/ppermute | solution.py:315
  161.6 21.9 %collective-permute-start.18 = (bf16[12,32,512]{2,1,0:T(8,128)(2,1)}, bf16[12,32,512]{2,1,0:T(8,128)(2,1)S(1)}, u32[]{:S(2)}, u32[]{:S(2)}) collective-permute-start(bf16[12,32,512]{2,1,0:T(8,128)(2,1)} %get-tuple-element.41), channel_id=1, source_target_pairs={{0,1},{1,2},{2,3},{3,0},{4,5},{5,6},{6,7},{7,4},{8,9},{9,10},{10,1... | collective-permute-start | bytes 1179656 | tf_op jit(solution)/shard_map/ppermute | solution.py:314
  170.6 21.4 %collective-permute-start.32 = (bf16[12,32,512]{2,1,0:T(8,128)(2,1)S(1)}, bf16[12,32,512]{2,1,0:T(8,128)(2,1)}, u32[]{:S(2)}, u32[]{:S(2)}) collective-permute-start(bf16[12,32,512]{2,1,0:T(8,128)(2,1)S(1)} %collective-permute-done.28.refs_6_), channel_id=1, source_target_pairs={{0,1},{1,2},{2,3},{3,0},{4,5},{5,6},{6,7},{7,4},{8,9},{9,10},{10,1... | collective-permute-start | bytes 1179656 | tf_op jit(solution)/shard_map/ppermute | solution.py:318
  174.7 17.4 %collective-permute-start.33 = (bf16[12,32,512]{2,1,0:T(8,128)(2,1)S(1)}, bf16[12,32,512]{2,1,0:T(8,128)(2,1)S(1)}, u32[]{:S(2)}, u32[]{:S(2)}) collective-permute-start(bf16[12,32,512]{2,1,0:T(8,128)(2,1)S(1)} %collective-permute-done.29.refs_7_), channel_id=1, source_target_pairs={{0,3},{1,0},{2,1},{3,2},{4,7},{5,4},{6,5},{7,6},{8,11},{9,8},{10,9... | collective-permute-start | bytes 1179656 | tf_op jit(solution)/shard_map/ppermute | solution.py:319
  178.3 21.7 %collective-permute-start.21 = (bf16[12,32,512]{2,1,0:T(8,128)(2,1)}, bf16[12,32,512]{2,1,0:T(8,128)(2,1)S(1)}, u32[]{:S(2)}, u32[]{:S(2)}) collective-permute-start(bf16[12,32,512]{2,1,0:T(8,128)(2,1)} %get-tuple-element.41), channel_id=1, source_target_pairs={{0,3},{1,0},{2,1},{3,2},{4,7},{5,4},{6,5},{7,6},{8,11},{9,8},{10,9... | collective-permute-start | bytes 1179656 | tf_op jit(solution)/shard_map/ppermute | solution.py:317
  183.5 16.9 %collective-permute-start.20 = (bf16[12,32,512]{2,1,0:T(8,128)(2,1)}, bf16[12,32,512]{2,1,0:T(8,128)(2,1)S(1)}, u32[]{:S(2)}, u32[]{:S(2)}) collective-permute-start(bf16[12,32,512]{2,1,0:T(8,128)(2,1)} %get-tuple-element.42), channel_id=1, source_target_pairs={{0,1},{1,2},{2,3},{3,0},{4,5},{5,6},{6,7},{7,4},{8,9},{9,10},{10,1... | collective-permute-start | bytes 1179656 | tf_op jit(solution)/shard_map/ppermute | solution.py:316
  183.5 23.6 %collective-permute-start.34 = (bf16[12,32,512]{2,1,0:T(8,128)(2,1)S(1)}, bf16[12,32,512]{2,1,0:T(8,128)(2,1)S(1)}, u32[]{:S(2)}, u32[]{:S(2)}) collective-permute-start(bf16[12,32,512]{2,1,0:T(8,128)(2,1)S(1)} %collective-permute-done.18.refs_0_), channel_id=1, source_target_pairs={{0,1},{1,2},{2,3},{3,0},{4,5},{5,6},{6,7},{7,4},{8,9},{9,10},{10,1... | collective-permute-start | bytes 1179656 | tf_op jit(solution)/shard_map/ppermute | solution.py:318
  (43 other events, 427.0 us)

commit v11 on v9

--- a/solution.py
+++ b/solution.py
@@ -252,48 +252,39 @@
     )(who, position, scale, *returned, params)
 
 
-def place(owners, scales, whole, raw, ready):
+def place(owners, scales, whole, raw):
     half, rows, _ = raw[0][2].shape
     blocks = 2 * half
-    pieces = len(raw) + len(ready)
 
     def body(owners_ref, scales_ref, *refs):
         olds, changes = refs[: len(raw)], refs[len(raw) : 2 * len(raw)]
-        values = refs[2 * len(raw) : 2 * len(raw) + len(ready)]
         out, made, sems = refs[-3:]
         copies = []
-        for at, (offset, part, value) in enumerate([(o, p, None) for o, p, _, _ in raw] + list(ready)):
+        for at, (offset, part, _, _) in enumerate(raw):
             owner = owners_ref[offset]
-            if at < len(raw):
-                for block in range(half):
-                    scale = scales_ref[owner * blocks + part * half + block]
-                    new = olds[at][block].astype(f32) - scale * changes[at][block].astype(f32)
-                    made[at, block] = new.astype(bf16)
-                source, columns = made.at[at], pl.ds(0, RAW)
-            else:
-                source = values[at - len(raw)]
-                columns = pl.ds(RAW, value.shape[2])
-            target = out.at[owner, pl.ds(part * half, half), :, columns]
-            copies.append(pltpu.make_async_copy(source, target, sems.at[at]))
+            for block in range(half):
+                scale = scales_ref[owner * blocks + part * half + block]
+                new = olds[at][block].astype(f32) - scale * changes[at][block].astype(f32)
+                made[at, block] = new.astype(bf16)
+            target = out.at[owner, pl.ds(part * half, half), :, pl.ds(0, RAW)]
+            copies.append(pltpu.make_async_copy(made.at[at], target, sems.at[at]))
             copies[-1].start()
         for copy in copies:
             copy.wait()
 
-    def block_of(array):
-        return pl.BlockSpec(array.shape, lambda i, o, s: (0, 0, 0))
-
-    arrays = [old for _, _, old, _ in raw] + [change for _, _, _, change in raw] + [v for _, _, v in ready]
+    arrays = [old for _, _, old, _ in raw] + [change for _, _, _, change in raw]
+    piece = pl.BlockSpec((half, rows, RAW), lambda i, o, s: (0, 0, 0))
     hbm = pl.BlockSpec(memory_space=pltpu.HBM)
     return pl.pallas_call(
         body,
         grid_spec=pltpu.PrefetchScalarGridSpec(
             num_scalar_prefetch=2,
             grid=(1,),
-            in_specs=[*[block_of(array) for array in arrays], hbm],
+            in_specs=[*[piece for _ in arrays], hbm],
             out_specs=hbm,
             scratch_shapes=[
                 pltpu.VMEM((len(raw), half, rows, RAW), bf16),
-                pltpu.SemaphoreType.DMA((pieces,)),
+                pltpu.SemaphoreType.DMA((len(raw),)),
             ],
         ),
         out_shape=jax.ShapeDtypeStruct(whole.shape, bf16),
@@ -376,16 +367,16 @@
         axis=1,
     )
 
-    owned, earlier, layer_row, onehot, gradients = lax.optimization_barrier(
-        (owned, earlier, layer_row, onehot, gradients)
-    )
-
     wide = jnp.concatenate(gradients, axis=2).astype(f32)
     new_accum = accum + wide * wide
     graft = wide * lax.rsqrt(new_accum)
     graft_blocks = jnp.sum(graft * graft, axis=(1, 2))
     graft_layer = jnp.sum(onehot * graft_blocks[:, None], axis=0)
     graft_row = jnp.pad(graft_layer[None, :], ((0, 1), (0, LANES - LAYERS)))
+    owned, earlier, layer_row, graft_row, new_accum = lax.optimization_barrier(
+        (owned, earlier, layer_row, graft_row, new_accum)
+    )
+
     *preconds, sums = products(left, right, owned, earlier, layer_row)
     returned = []
     for precond in preconds:
@@ -401,9 +392,9 @@
 
     raw = [(offset, part, old, change) for (offset, part, old), (_, _, change) in zip(ahead, changes)]
     flat = scales.reshape(-1)
-    new_params = place(who, flat, new_params, raw[:4], ())
-    new_params = place(who, flat, new_params, raw[4:], finished[:4])
-    for offset, part, piece in finished[4:]:
+    new_params = place(who, flat, new_params, raw[:4])
+    new_params = place(who, flat, new_params, raw[4:])
+    for offset, part, piece in finished:
         owner = lax.rem(me + offset, reps)
         new_params = lax.dynamic_update_slice(new_params, piece[None], (owner, part * half, 0, RAW))
     return (new_params.reshape(reps * blocks, rows, width), new_accum)

time: 210 us -> 214 us (1.019)
  the two profiles are of different devices: /device:TPU:0 before, /device:TPU:24 now
where the time goes in v11:
time: 214 us; the launch traced here: 212 us
  starting transfers between devices  74.7 us (35%)
  waiting for transfers between devices  69.1 us (32%)
  Pallas kernels  41.2 us (19%)
  local copies, waits for them, and re-layouts  18.6 us (9%)
  other arithmetic  7.92 us (4%)
    all_to_all x4, starting transfers between devices, local(): lax.all_to_all(outgoing, GROUP, split_axis=0, concat_axis=0, tiled=True)  29.4 us
    ppermute x9, starting transfers between devices, everywhere(): lax.ppermute(value, axis, ring(4, step))  13.6 us
    ppermute x3, waiting for transfers between devices, spread(): low_up = lax.ppermute(low, 'rep', up)  11.2 us
    ppermute x2, waiting for transfers between devices, local(): near_up = lax.ppermute(to_up, 'rep', up)  10.5 us
    ppermute x9, waiting for transfers between devices, everywhere(): lax.ppermute(value, axis, ring(4, step))  9.68 us
    unnamed x48, local copies, waits for them, and re-layouts  8.95 us
    all_to_all x4, waiting for transfers between devices, local(): lax.all_to_all(outgoing, GROUP, split_axis=0, concat_axis=0, tiled=True)  8.73 us
    pallas_call x2, Pallas kernels, finish(): pl.pallas_call(body, grid_spec=pltpu.PrefetchScalarGridSpec(num_scalar_pr...  8.21 us
  transfers between devices with their start and end apart: 40, of which 22 were waited for; matrix products, arithmetic and copies ran while one was open for 7% of the time, Pallas kernels for 16%

profile of v11, /device:TPU:24, one launch (start us, length us, event | category | flops | bytes accessed | tf_op | source)
XLA Modules:
  0.0 212.5 jit_solution(13768072648021195930)
XLA Ops:
  14.4 3.1 %merge.3 = (bf16[24,32,384]{2,1,0:T(8,128)(2,1)}, bf16[24,32,384]{2,1,0:T(8,128)(2,1)}) custom-call(s32[4]{0:T(128)} %compare_select_fusion.who_ref.owners_ref, bf16[4,24,32,1024]{3,2,1,0:T(8,128)(2,1)} %bitcast.40, bf16[4,24,32,1024]{3,2,1,0:T(8,128)(2,1)} %bitcast.41, bf16[12,32,384]{2,1,0:T(8,128)(2,1)} %copy-done.19, bf16[12,32,384]{2,1,0:T(8,128)(2,1)} %copy-done.20), custom_call_target="tpu_custom_call" | custom-call | tf_op jit(solution)/shard_map/merge/pallas_call | solution.py:51
  25.1 3.6 %merge.2 = (bf16[24,32,640]{2,1,0:T(8,128)(2,1)}, bf16[24,32,640]{2,1,0:T(8,128)(2,1)}) custom-call(s32[4]{0:T(128)} %compare_select_fusion.who_ref.owners_ref, bf16[4,24,32,1024]{3,2,1,0:T(8,128)(2,1)} %bitcast.42, bf16[4,24,32,1024]{3,2,1,0:T(8,128)(2,1)} %bitcast.43, bf16[12,32,640]{2,1,0:T(8,128)(2,1)} %copy-done.10, bf16[12,32,640]{2,1,0:T(8,128)(2,1)} %copy-done.11), custom_call_target="tpu_custom_call" | custom-call | tf_op jit(solution)/shard_map/merge/pallas_call | solution.py:51
  32.4 3.7 %collective-permute-done.6.one = bf16[24,32,384]{2,1,0:T(8,128)(2,1)S(1)} collective-permute-done((bf16[24,32,384]{2,1,0:T(8,128)(2,1)}, bf16[24,32,384]{2,1,0:T(8,128)(2,1)S(1)}, u32[]{:S(2)}, u32[]{:S(2)}) %collective-permute-start.6) | collective-permute-done | bytes 589856 | tf_op jit(solution)/shard_map/ppermute | solution.py:343
  37.2 3.6 %shard_map.87 = (bf16[24,32,384]{2,1,0:T(8,128)(2,1)}, bf16[32,32,384]{2,1,0:T(8,128)(2,1)}) custom-call(s32[4]{0:T(128)} %compare_select_fusion.who_ref.owners_ref, s32[32]{0:T(128)} %get-tuple-element.46.table_ref, bf16[4,24,32,1024]{3,2,1,0:T(8,128)(2,1)} %bitcast.44, bf16[24,32,384]{2,1,0:T(8,128)(2,1)} %copy-done.8, bf16[24,32,384]{2,1,0:T(8,128)(2,1)} %copy-done.9), custom_call_target="tpu_custom_call" | custom-call | tf_op jit(solution)/shard_map/pallas_call | solution.py:80
  40.8 8.5 %all-to-all-start.1 = ((bf16[32,32,384]{2,1,0:T(8,128)(2,1)}), bf16[32,32,384]{2,1,0:T(8,128)(2,1)S(1)}, u32[]{:S(2)}, u32[]{:S(2)}) async-start(bf16[32,32,384]{2,1,0:T(8,128)(2,1)} %get-tuple-element.28), calls=%async_computation.1 | async-start | bytes 1572864 | tf_op jit(solution)/shard_map/all_to_all | solution.py:347
  49.3 6.7 %collective-permute-done.2.one = bf16[24,32,640]{2,1,0:T(8,128)(2,1)S(1)} collective-permute-done((bf16[24,32,640]{2,1,0:T(8,128)(2,1)}, bf16[24,32,640]{2,1,0:T(8,128)(2,1)S(1)}, u32[]{:S(2)}, u32[]{:S(2)}) %collective-permute-start.2) | collective-permute-done | bytes 983072 | tf_op jit(solution)/shard_map/ppermute | solution.py:343
  57.9 4.6 %shard_map.86 = (bf16[24,32,640]{2,1,0:T(8,128)(2,1)}, bf16[32,32,640]{2,1,0:T(8,128)(2,1)}) custom-call(s32[4]{0:T(128)} %compare_select_fusion.who_ref.owners_ref, s32[32]{0:T(128)} %get-tuple-element.46.table_ref, bf16[4,24,32,1024]{3,2,1,0:T(8,128)(2,1)} %bitcast.45, bf16[24,32,640]{2,1,0:T(8,128)(2,1)} %copy-done.5, bf16[24,32,640]{2,1,0:T(8,128)(2,1)} %copy-done.6), custom_call_target="tpu_custom_call" | custom-call | tf_op jit(solution)/shard_map/pallas_call | solution.py:80
  63.5 8.4 %all-to-all-start = ((bf16[32,32,640]{2,1,0:T(8,128)(2,1)}), bf16[32,32,640]{2,1,0:T(8,128)(2,1)S(1)}, u32[]{:S(2)}, u32[]{:S(2)}) async-start(bf16[32,32,640]{2,1,0:T(8,128)(2,1)} %get-tuple-element.25), calls=%async_computation | async-start | bytes 2621440 | tf_op jit(solution)/shard_map/all_to_all | solution.py:347
  73.1 4.5 %fusion = (f32[24,32,1024]{2,1,0:T(8,128)}, f32[24]{0:T(128)S(1)}) fusion(f32[24,32,1024]{2,1,0:T(8,128)} %param.9, bf16[24,32,640]{2,1,0:T(8,128)(2,1)} %get-tuple-element.30, bf16[24,32,384]{2,1,0:T(8,128)(2,1)S(1)} %copy-done.7), kind=kLoop, calls=%fused_computation.2 | loop fusion | flops 7077864 | bytes 7864416 | tf_op jit(solution)/shard_map/add | solution.py:371
  78.4 3.6 %left_times.1.rest_0_ = bf16[1024,384]{1,0:T(8,128)(2,1)} custom-call(bf16[1024,1024]{1,0:T(8,128)(2,1)} %bitcast.47, bf16[1024,384]{1,0:T(8,128)(2,1)} %bitcast.50), custom_call_target="tpu_custom_call" | custom-call | tf_op jit(solution)/shard_map/left_times/pallas_call | solution.py:106
  82.0 7.9 %all-to-all-done = bf16[32,32,640]{2,1,0:T(8,128)(2,1)S(1)} async-done(((bf16[32,32,640]{2,1,0:T(8,128)(2,1)}), bf16[32,32,640]{2,1,0:T(8,128)(2,1)S(1)}, u32[]{:S(2)}, u32[]{:S(2)}) %all-to-all-start) | async-done | bytes 1310752 | tf_op jit(solution)/shard_map/all_to_all | solution.py:347
  91.0 7.8 %products.1 = (bf16[1024,512]{1,0:T(8,128)(2,1)}, bf16[1024,512]{1,0:T(8,128)(2,1)}, f32[2,128]{1,0:T(2,128)}) custom-call(bf16[1024,1024]{1,0:T(8,128)(2,1)} %bitcast.48, bf16[1024,1024]{1,0:T(8,128)(2,1)} %bitcast.51, bf16[1024,640]{1,0:T(8,128)(2,1)} %bitcast.49, f32[1,128]{1,0:T(1,128)} %pad.8.layer_ref, bf16[1024,384]{1,0:T(8,128)(2,1)} %left_times.1.rest_0_), custom_call_target="tpu_custom_call" | custom-call | tf_op jit(solution)/shard_map/products/pallas_call | solution.py:148
  98.8 5.6 %all-to-all-start.2 = ((bf16[32,32,512]{2,1,0:T(8,128)(2,1)}), bf16[32,32,512]{2,1,0:T(8,128)(2,1)S(1)}, u32[]{:S(2)}, u32[]{:S(2)}) async-start(bf16[32,32,512]{2,1,0:T(8,128)(2,1)} %bitcast.53), calls=%async_computation.2 | async-start | bytes 2097152 | tf_op jit(solution)/shard_map/all_to_all | solution.py:384
  119.6 6.9 %all-to-all-start.3 = ((bf16[32,32,512]{2,1,0:T(8,128)(2,1)}), bf16[32,32,512]{2,1,0:T(8,128)(2,1)S(1)}, u32[]{:S(2)}, u32[]{:S(2)}) async-start(bf16[32,32,512]{2,1,0:T(8,128)(2,1)} %bitcast.52), calls=%async_computation.3 | async-start | bytes 2097152 | tf_op jit(solution)/shard_map/all_to_all | solution.py:384
  126.6 3.1 %collective-permute-start.15 = (f32[2,128]{1,0:T(2,128)S(1)}, f32[2,128]{1,0:T(2,128)S(1)}, u32[]{:S(2)}, u32[]{:S(2)}) collective-permute-start(f32[2,128]{1,0:T(2,128)S(1)} %add_add_fusion.1), channel_id=1, source_target_pairs={{0,16},{8,24},{16,0},{24,8},{1,17},{9,25},{17,1},{25,9},{2,18},{10... | collective-permute-start | bytes 3080 | tf_op jit(solution)/shard_map/ppermute | solution.py:298
  134.8 7.1 %collective-permute-done.15 = f32[2,128]{1,0:T(2,128)S(1)} collective-permute-done((f32[2,128]{1,0:T(2,128)S(1)}, f32[2,128]{1,0:T(2,128)S(1)}, u32[]{:S(2)}, u32[]{:S(2)}) %collective-permute-start.15) | collective-permute-done | bytes 1056 | tf_op jit(solution)/shard_map/ppermute | solution.py:298
  150.1 3.8 %collective-permute-done.27.refs_3_ = bf16[12,32,512]{2,1,0:T(8,128)(2,1)} collective-permute-done((bf16[12,32,512]{2,1,0:T(8,128)(2,1)S(1)}, bf16[12,32,512]{2,1,0:T(8,128)(2,1)}, u32[]{:S(2)}, u32[]{:S(2)}) %collective-permute-start.27) | collective-permute-done | bytes 393248 | tf_op jit(solution)/shard_map/ppermute | solution.py:308
  157.7 5.3 %update.1 = (bf16[12,32,512]{2,1,0:T(8,128)(2,1)}, bf16[12,32,512]{2,1,0:T(8,128)(2,1)}, bf16[4,24,32,1024]{3,2,1,0:T(8,128)(2,1)}) custom-call(s32[4]{0:T(128)} %compare_select_fusion.who_ref.owners_ref, s32[24]{0:T(128)} %select_reduce_fusion.position_ref, f32[24]{0:T(128)} %fusion.6.scale_ref, bf16[32,32,512]{2,1,0:T(8,128)(2,1)} %copy-done, ...), custom_call_target="tpu_custom_call" | custom-call | tf_op jit(solution)/shard_map/update/pallas_call | solution.py:234
  163.1 8.2 %collective-permute-done.22.refs_4_ = bf16[12,32,512]{2,1,0:T(8,128)(2,1)} collective-permute-done((bf16[12,32,512]{2,1,0:T(8,128)(2,1)}, bf16[12,32,512]{2,1,0:T(8,128)(2,1)}, u32[]{:S(2)}, u32[]{:S(2)}) %collective-permute-start.22) | collective-permute-done | bytes 393248 | tf_op jit(solution)/shard_map/ppermute | solution.py:305
  171.4 3.1 %collective-permute-start.31 = (bf16[12,32,512]{2,1,0:T(8,128)(2,1)}, bf16[12,32,512]{2,1,0:T(8,128)(2,1)S(1)}, u32[]{:S(2)}, u32[]{:S(2)}) collective-permute-start(bf16[12,32,512]{2,1,0:T(8,128)(2,1)} %get-tuple-element.42), channel_id=1, source_target_pairs={{0,3},{1,0},{2,1},{3,2},{4,7},{5,4},{6,5},{7,6},{8,11},{9,8},{10,9... | collective-permute-start | bytes 1179656 | tf_op jit(solution)/shard_map/ppermute | solution.py:306
  174.6 3.2 %collective-permute-start.25 = (bf16[12,32,512]{2,1,0:T(8,128)(2,1)}, bf16[12,32,512]{2,1,0:T(8,128)(2,1)S(1)}, u32[]{:S(2)}, u32[]{:S(2)}) collective-permute-start(bf16[12,32,512]{2,1,0:T(8,128)(2,1)} %copy-done.17), channel_id=1, source_target_pairs={{0,3},{1,0},{2,1},{3,2},{4,7},{5,4},{6,5},{7,6},{8,11},{9,8},{10,9... | collective-permute-start | bytes 1179656 | tf_op jit(solution)/shard_map/ppermute | solution.py:310
  177.8 3.8 %shard_map.88.refs_4_ = bf16[4,24,32,1024]{3,2,1,0:T(8,128)(2,1)} custom-call(s32[4]{0:T(128)} %compare_select_fusion.who_ref.owners_ref, f32[96]{0:T(128)} %copy-done.21, bf16[12,32,512]{2,1,0:T(8,128)(2,1)} %copy-done.16, bf16[12,32,512]{2,1,0:T(8,128)(2,1)} %collective-permute-done.20.refs_1_, ...), custom_call_target="tpu_custom_call", output_to_operand_aliasing={{}: (10, {})} | custom-call | tf_op jit(solution)/shard_map/pallas_call | solution.py:278
  188.8 4.3 %collective-permute-done.23.refs_2_ = bf16[12,32,512]{2,1,0:T(8,128)(2,1)S(1)} collective-permute-done((bf16[12,32,512]{2,1,0:T(8,128)(2,1)}, bf16[12,32,512]{2,1,0:T(8,128)(2,1)S(1)}, u32[]{:S(2)}, u32[]{:S(2)}) %collective-permute-start.23) | collective-permute-done | bytes 393248 | tf_op jit(solution)/shard_map/ppermute | solution.py:309
  208.5 3.2 %collective-permute-done.35 = bf16[12,32,512]{2,1,0:T(8,128)(2,1)S(1)} collective-permute-done((bf16[12,32,512]{2,1,0:T(8,128)(2,1)S(1)}, bf16[12,32,512]{2,1,0:T(8,128)(2,1)S(1)}, u32[]{:S(2)}, u32[]{:S(2)}) %collective-permute-start.35) | collective-permute-done | bytes 393248 | tf_op jit(solution)/shard_map/ppermute | solution.py:310
  (143 shorter events, 87.7 us)
Async XLA Ops:
  6.3 17.1 %collective-permute-start = (bf16[12,32,640]{2,1,0:T(8,128)(2,1)S(1)}, bf16[12,32,640]{2,1,0:T(8,128)(2,1)S(1)}, u32[]{:S(2)}, u32[]{:S(2)}) collective-permute-start(bf16[12,32,640]{2,1,0:T(8,128)(2,1)S(1)} %get-tuple-element.51), channel_id=1, source_target_pairs={{0,1},{1,2},{2,3},{3,0},{4,5},{5,6},{6,7},{7,4},{8,9},{9,10},{10,1... | collective-permute-start | bytes 1474568 | tf_op jit(solution)/shard_map/ppermute | solution.py:340
  6.7 17.0 %collective-permute-start.1 = (bf16[12,32,640]{2,1,0:T(8,128)(2,1)S(1)}, bf16[12,32,640]{2,1,0:T(8,128)(2,1)S(1)}, u32[]{:S(2)}, u32[]{:S(2)}) collective-permute-start(bf16[12,32,640]{2,1,0:T(8,128)(2,1)S(1)} %get-tuple-element.50), channel_id=1, source_target_pairs={{0,3},{1,0},{2,1},{3,2},{4,7},{5,4},{6,5},{7,6},{8,11},{9,8},{10,9... | collective-permute-start | bytes 1474568 | tf_op jit(solution)/shard_map/ppermute | solution.py:341
  17.4 18.7 %collective-permute-start.6 = (bf16[24,32,384]{2,1,0:T(8,128)(2,1)}, bf16[24,32,384]{2,1,0:T(8,128)(2,1)S(1)}, u32[]{:S(2)}, u32[]{:S(2)}) collective-permute-start(bf16[24,32,384]{2,1,0:T(8,128)(2,1)} %get-tuple-element.26), channel_id=1, source_target_pairs={{0,1},{1,2},{2,3},{3,0},{4,5},{5,6},{6,7},{7,4},{8,9},{9,10},{10,1... | collective-permute-start | bytes 1769480 | tf_op jit(solution)/shard_map/ppermute | solution.py:343
  18.5 17.9 %collective-permute-start.7 = (bf16[24,32,384]{2,1,0:T(8,128)(2,1)}, bf16[24,32,384]{2,1,0:T(8,128)(2,1)S(1)}, u32[]{:S(2)}, u32[]{:S(2)}) collective-permute-start(bf16[24,32,384]{2,1,0:T(8,128)(2,1)} %get-tuple-element.27), channel_id=1, source_target_pairs={{0,3},{1,0},{2,1},{3,2},{4,7},{5,4},{6,5},{7,6},{8,11},{9,8},{10,9... | collective-permute-start | bytes 1769480 | tf_op jit(solution)/shard_map/ppermute | solution.py:344
  28.6 27.4 %collective-permute-start.2 = (bf16[24,32,640]{2,1,0:T(8,128)(2,1)}, bf16[24,32,640]{2,1,0:T(8,128)(2,1)S(1)}, u32[]{:S(2)}, u32[]{:S(2)}) collective-permute-start(bf16[24,32,640]{2,1,0:T(8,128)(2,1)} %get-tuple-element.23), channel_id=1, source_target_pairs={{0,1},{1,2},{2,3},{3,0},{4,5},{5,6},{6,7},{7,4},{8,9},{9,10},{10,1... | collective-permute-start | bytes 2949128 | tf_op jit(solution)/shard_map/ppermute | solution.py:343
  29.6 26.4 %collective-permute-start.3 = (bf16[24,32,640]{2,1,0:T(8,128)(2,1)}, bf16[24,32,640]{2,1,0:T(8,128)(2,1)S(1)}, u32[]{:S(2)}, u32[]{:S(2)}) collective-permute-start(bf16[24,32,640]{2,1,0:T(8,128)(2,1)} %get-tuple-element.24), channel_id=1, source_target_pairs={{0,3},{1,0},{2,1},{3,2},{4,7},{5,4},{6,5},{7,6},{8,11},{9,8},{10,9... | collective-permute-start | bytes 2949128 | tf_op jit(solution)/shard_map/ppermute | solution.py:344
  40.8 21.8 %all-to-all-start.1 = ((bf16[32,32,384]{2,1,0:T(8,128)(2,1)}), bf16[32,32,384]{2,1,0:T(8,128)(2,1)S(1)}, u32[]{:S(2)}, u32[]{:S(2)}) async-start(bf16[32,32,384]{2,1,0:T(8,128)(2,1)} %get-tuple-element.28), calls=%async_computation.1 | async-start | bytes 1572864 | tf_op jit(solution)/shard_map/all_to_all | solution.py:347
  63.5 26.5 %all-to-all-start = ((bf16[32,32,640]{2,1,0:T(8,128)(2,1)}), bf16[32,32,640]{2,1,0:T(8,128)(2,1)S(1)}, u32[]{:S(2)}, u32[]{:S(2)}) async-start(bf16[32,32,640]{2,1,0:T(8,128)(2,1)} %get-tuple-element.25), calls=%async_computation | async-start | bytes 2621440 | tf_op jit(solution)/shard_map/all_to_all | solution.py:347
  98.8 20.8 %all-to-all-start.2 = ((bf16[32,32,512]{2,1,0:T(8,128)(2,1)}), bf16[32,32,512]{2,1,0:T(8,128)(2,1)S(1)}, u32[]{:S(2)}, u32[]{:S(2)}) async-start(bf16[32,32,512]{2,1,0:T(8,128)(2,1)} %bitcast.53), calls=%async_computation.2 | async-start | bytes 2097152 | tf_op jit(solution)/shard_map/all_to_all | solution.py:384
  110.9 22.7 %collective-permute-start.18 = (bf16[12,32,512]{2,1,0:T(8,128)(2,1)S(1)}, bf16[12,32,512]{2,1,0:T(8,128)(2,1)S(1)}, u32[]{:S(2)}, u32[]{:S(2)}) collective-permute-start(bf16[12,32,512]{2,1,0:T(8,128)(2,1)S(1)} %get-tuple-element.55), channel_id=1, source_target_pairs={{0,1},{1,2},{2,3},{3,0},{4,5},{5,6},{6,7},{7,4},{8,9},{9,10},{10,1... | collective-permute-start | bytes 1179656 | tf_op jit(solution)/shard_map/ppermute | solution.py:305
  118.0 30.8 %collective-permute-start.20 = (bf16[12,32,512]{2,1,0:T(8,128)(2,1)}, bf16[12,32,512]{2,1,0:T(8,128)(2,1)}, u32[]{:S(2)}, u32[]{:S(2)}) collective-permute-start(bf16[12,32,512]{2,1,0:T(8,128)(2,1)} %get-tuple-element.54), channel_id=1, source_target_pairs={{0,3},{1,0},{2,1},{3,2},{4,7},{5,4},{6,5},{7,6},{8,11},{9,8},{10,9... | collective-permute-start | bytes 1179656 | tf_op jit(solution)/shard_map/ppermute | solution.py:306
  119.6 37.0 %all-to-all-start.3 = ((bf16[32,32,512]{2,1,0:T(8,128)(2,1)}), bf16[32,32,512]{2,1,0:T(8,128)(2,1)S(1)}, u32[]{:S(2)}, u32[]{:S(2)}) async-start(bf16[32,32,512]{2,1,0:T(8,128)(2,1)} %bitcast.52), calls=%async_computation.3 | async-start | bytes 2097152 | tf_op jit(solution)/shard_map/all_to_all | solution.py:384
  142.6 20.4 %collective-permute-start.19 = (bf16[12,32,512]{2,1,0:T(8,128)(2,1)S(1)}, bf16[12,32,512]{2,1,0:T(8,128)(2,1)S(1)}, u32[]{:S(2)}, u32[]{:S(2)}) collective-permute-start(bf16[12,32,512]{2,1,0:T(8,128)(2,1)S(1)} %collective-permute-done.18.refs_0_), channel_id=1, source_target_pairs={{0,1},{1,2},{2,3},{3,0},{4,5},{5,6},{6,7},{7,4},{8,9},{9,10},{10,1... | collective-permute-start | bytes 1179656 | tf_op jit(solution)/shard_map/ppermute | solution.py:309
  146.8 24.6 %collective-permute-start.24 = (bf16[12,32,512]{2,1,0:T(8,128)(2,1)}, bf16[12,32,512]{2,1,0:T(8,128)(2,1)S(1)}, u32[]{:S(2)}, u32[]{:S(2)}) collective-permute-start(bf16[12,32,512]{2,1,0:T(8,128)(2,1)} %get-tuple-element.38), channel_id=1, source_target_pairs={{0,3},{1,0},{2,1},{3,2},{4,7},{5,4},{6,5},{7,6},{8,11},{9,8},{10,9... | collective-permute-start | bytes 1179656 | tf_op jit(solution)/shard_map/ppermute | solution.py:306
  148.8 25.8 %collective-permute-start.28 = (bf16[12,32,512]{2,1,0:T(8,128)(2,1)}, bf16[12,32,512]{2,1,0:T(8,128)(2,1)}, u32[]{:S(2)}, u32[]{:S(2)}) collective-permute-start(bf16[12,32,512]{2,1,0:T(8,128)(2,1)} %get-tuple-element.38), channel_id=1, source_target_pairs={{0,1},{1,2},{2,3},{3,0},{4,5},{5,6},{6,7},{7,4},{8,9},{9,10},{10,1... | collective-permute-start | bytes 1179656 | tf_op jit(solution)/shard_map/ppermute | solution.py:307
  148.9 22.4 %collective-permute-start.22 = (bf16[12,32,512]{2,1,0:T(8,128)(2,1)}, bf16[12,32,512]{2,1,0:T(8,128)(2,1)}, u32[]{:S(2)}, u32[]{:S(2)}) collective-permute-start(bf16[12,32,512]{2,1,0:T(8,128)(2,1)} %get-tuple-element.37), channel_id=1, source_target_pairs={{0,1},{1,2},{2,3},{3,0},{4,5},{5,6},{6,7},{7,4},{8,9},{9,10},{10,1... | collective-permute-start | bytes 1179656 | tf_op jit(solution)/shard_map/ppermute | solution.py:305
  154.0 20.6 %collective-permute-start.29 = (bf16[12,32,512]{2,1,0:T(8,128)(2,1)}, bf16[12,32,512]{2,1,0:T(8,128)(2,1)S(1)}, u32[]{:S(2)}, u32[]{:S(2)}) collective-permute-start(bf16[12,32,512]{2,1,0:T(8,128)(2,1)} %get-tuple-element.37), channel_id=1, source_target_pairs={{0,3},{1,0},{2,1},{3,2},{4,7},{5,4},{6,5},{7,6},{8,11},{9,8},{10,9... | collective-permute-start | bytes 1179656 | tf_op jit(solution)/shard_map/ppermute | solution.py:308
  163.0 18.6 %collective-permute-start.21 = (bf16[12,32,512]{2,1,0:T(8,128)(2,1)}, bf16[12,32,512]{2,1,0:T(8,128)(2,1)S(1)}, u32[]{:S(2)}, u32[]{:S(2)}) collective-permute-start(bf16[12,32,512]{2,1,0:T(8,128)(2,1)} %collective-permute-done.20.refs_1_), channel_id=1, source_target_pairs={{0,3},{1,0},{2,1},{3,2},{4,7},{5,4},{6,5},{7,6},{8,11},{9,8},{10,9... | collective-permute-start | bytes 1179656 | tf_op jit(solution)/shard_map/ppermute | solution.py:310
  174.6 18.6 %collective-permute-start.23 = (bf16[12,32,512]{2,1,0:T(8,128)(2,1)}, bf16[12,32,512]{2,1,0:T(8,128)(2,1)S(1)}, u32[]{:S(2)}, u32[]{:S(2)}) collective-permute-start(bf16[12,32,512]{2,1,0:T(8,128)(2,1)} %collective-permute-done.22.refs_4_), channel_id=1, source_target_pairs={{0,1},{1,2},{2,3},{3,0},{4,5},{5,6},{6,7},{7,4},{8,9},{9,10},{10,1... | collective-permute-start | bytes 1179656 | tf_op jit(solution)/shard_map/ppermute | solution.py:309
  174.6 21.4 %collective-permute-start.25 = (bf16[12,32,512]{2,1,0:T(8,128)(2,1)}, bf16[12,32,512]{2,1,0:T(8,128)(2,1)S(1)}, u32[]{:S(2)}, u32[]{:S(2)}) collective-permute-start(bf16[12,32,512]{2,1,0:T(8,128)(2,1)} %copy-done.17), channel_id=1, source_target_pairs={{0,3},{1,0},{2,1},{3,2},{4,7},{5,4},{6,5},{7,6},{8,11},{9,8},{10,9... | collective-permute-start | bytes 1179656 | tf_op jit(solution)/shard_map/ppermute | solution.py:310
  181.6 19.9 %collective-permute-start.32 = (bf16[12,32,512]{2,1,0:T(8,128)(2,1)}, bf16[12,32,512]{2,1,0:T(8,128)(2,1)S(1)}, u32[]{:S(2)}, u32[]{:S(2)}) collective-permute-start(bf16[12,32,512]{2,1,0:T(8,128)(2,1)} %get-tuple-element.42), channel_id=1, source_target_pairs={{0,1},{1,2},{2,3},{3,0},{4,5},{5,6},{6,7},{7,4},{8,9},{9,10},{10,1... | collective-permute-start | bytes 1179656 | tf_op jit(solution)/shard_map/ppermute | solution.py:307
  184.7 19.7 %collective-permute-start.33 = (bf16[12,32,512]{2,1,0:T(8,128)(2,1)}, bf16[12,32,512]{2,1,0:T(8,128)(2,1)S(1)}, u32[]{:S(2)}, u32[]{:S(2)}) collective-permute-start(bf16[12,32,512]{2,1,0:T(8,128)(2,1)} %get-tuple-element.41), channel_id=1, source_target_pairs={{0,3},{1,0},{2,1},{3,2},{4,7},{5,4},{6,5},{7,6},{8,11},{9,8},{10,9... | collective-permute-start | bytes 1179656 | tf_op jit(solution)/shard_map/ppermute | solution.py:308
  187.6 20.1 %collective-permute-start.34 = (bf16[12,32,512]{2,1,0:T(8,128)(2,1)S(1)}, bf16[12,32,512]{2,1,0:T(8,128)(2,1)S(1)}, u32[]{:S(2)}, u32[]{:S(2)}) collective-permute-start(bf16[12,32,512]{2,1,0:T(8,128)(2,1)S(1)} %collective-permute-done.30), channel_id=1, source_target_pairs={{0,1},{1,2},{2,3},{3,0},{4,5},{5,6},{6,7},{7,4},{8,9},{9,10},{10,1... | collective-permute-start | bytes 1179656 | tf_op jit(solution)/shard_map/ppermute | solution.py:309
  193.1 18.5 %collective-permute-start.35 = (bf16[12,32,512]{2,1,0:T(8,128)(2,1)S(1)}, bf16[12,32,512]{2,1,0:T(8,128)(2,1)S(1)}, u32[]{:S(2)}, u32[]{:S(2)}) collective-permute-start(bf16[12,32,512]{2,1,0:T(8,128)(2,1)S(1)} %collective-permute-done.31), channel_id=1, source_target_pairs={{0,3},{1,0},{2,1},{3,2},{4,7},{5,4},{6,5},{7,6},{8,11},{9,8},{10,9... | collective-permute-start | bytes 1179656 | tf_op jit(solution)/shard_map/ppermute | solution.py:310
  (40 other events, 421.7 us)

commit v12 on v10

--- a/solution.py
+++ b/solution.py
@@ -376,16 +376,16 @@
         axis=1,
     )
 
-    owned, earlier, layer_row, onehot, gradients = lax.optimization_barrier(
-        (owned, earlier, layer_row, onehot, gradients)
-    )
-
     wide = jnp.concatenate(gradients, axis=2).astype(f32)
     new_accum = accum + wide * wide
     graft = wide * lax.rsqrt(new_accum)
     graft_blocks = jnp.sum(graft * graft, axis=(1, 2))
     graft_layer = jnp.sum(onehot * graft_blocks[:, None], axis=0)
     graft_row = jnp.pad(graft_layer[None, :], ((0, 1), (0, LANES - LAYERS)))
+    owned, earlier, layer_row, graft_row, new_accum = lax.optimization_barrier(
+        (owned, earlier, layer_row, graft_row, new_accum)
+    )
+
     *preconds, sums = products(left, right, owned, earlier, layer_row)
     returned = []
     for precond in preconds:
@@ -401,8 +401,8 @@
 
     raw = [(offset, part, old, change) for (offset, part, old), (_, _, change) in zip(ahead, changes)]
     flat = scales.reshape(-1)
-    new_params = place(who, flat, new_params, raw, ())
-    new_params = place(who, flat, new_params, (), finished[:4])
+    new_params = place(who, flat, new_params, raw[:4], ())
+    new_params = place(who, flat, new_params, raw[4:], finished[:4])
     for offset, part, piece in finished[4:]:
         owner = lax.rem(me + offset, reps)
         new_params = lax.dynamic_update_slice(new_params, piece[None], (owner, part * half, 0, RAW))

time: 211 us -> 206 us (0.976)
  waiting for transfers between devices: 69.3 us -> 65 us
  starting transfers between devices: 73.5 us -> 75.8 us
  local copies, waits for them, and re-layouts: 15.2 us -> 13 us
    ppermute x3, waiting for transfers between devices: 2.58 us -> 16.7 us  [spread(): high_up = lax.ppermute(high, 'rep', up)]
    ppermute x3, starting transfers between devices: 10.1 us -> 2.73 us  [spread(): high_down = lax.ppermute(high, 'rep', down)]
    ppermute x3, waiting for transfers between devices: 7.3 us -> 0.01 us  [spread(): low_down = lax.ppermute(low, 'rep', down)]
    ppermute x3, waiting for transfers between devices: 5.11 us -> 12.1 us  [spread(): low_up = lax.ppermute(low, 'rep', up)]
    reduce_sum x2 -> x0, other arithmetic: 4.76 us -> none  [the longest x1 4.57 us: local(): graft_blocks = jnp.sum(graft * graft, axis=(1, 2))]
    all_to_all x4, waiting for transfers between devices: 14.6 us -> 10.2 us  [local(): lax.all_to_all(outgoing, GROUP, split_axis=0, concat_axis=0, tiled=True)]
    add x0 -> x1, other arithmetic: none -> 4.4 us  [local(): new_accum = accum + wide * wide]
    ppermute x9, starting transfers between devices: 12.7 us -> 17 us  [everywhere(): lax.ppermute(value, axis, ring(4, step))]
  transfers between devices with their start and end apart: 40 -> 40, of which waited for: 19 -> 20; matrix products, arithmetic and copies ran while one was open for 6% -> 6% of each run, Pallas kernels for 16% -> 17%
where the time goes in v12:
time: 206 us; the launch traced here: 205 us
  starting transfers between devices  75.8 us (37%)
  waiting for transfers between devices  65 us (32%)
  Pallas kernels  42.3 us (21%)
  local copies, waits for them, and re-layouts  13 us (6%)
  other arithmetic  7.76 us (4%)
    all_to_all x4, starting transfers between devices, local(): lax.all_to_all(outgoing, GROUP, split_axis=0, concat_axis=0, tiled=True)  25.3 us
    ppermute x9, starting transfers between devices, everywhere(): lax.ppermute(value, axis, ring(4, step))  17 us
    ppermute x3, waiting for transfers between devices, spread(): high_up = lax.ppermute(high, 'rep', up)  16.7 us
    ppermute x3, waiting for transfers between devices, spread(): low_up = lax.ppermute(low, 'rep', up)  12.1 us
    ppermute x2, waiting for transfers between devices, local(): near_up = lax.ppermute(to_up, 'rep', up)  10.7 us
    all_to_all x4, waiting for transfers between devices, local(): lax.all_to_all(outgoing, GROUP, split_axis=0, concat_axis=0, tiled=True)  10.2 us
    pallas_call x2, Pallas kernels, finish(): pl.pallas_call(body, grid_spec=pltpu.PrefetchScalarGridSpec(num_scalar_pr...  8.2 us
    pallas_call x1, Pallas kernels, products(): pl.pallas_call(body, grid=(steps,), in_specs=[pl.BlockSpec((tile, order),...  7.91 us
  transfers between devices with their start and end apart: 40, of which 20 were waited for; matrix products, arithmetic and copies ran while one was open for 6% of the time, Pallas kernels for 17%

profile of v12, /device:TPU:0, one launch (start us, length us, event | category | flops | bytes accessed | tf_op | source)
XLA Modules:
  0.0 204.7 jit_solution(7098875925027535276)
XLA Ops:
  25.0 3.6 %merge.2 = (bf16[24,32,640]{2,1,0:T(8,128)(2,1)}, bf16[24,32,640]{2,1,0:T(8,128)(2,1)}) custom-call(s32[4]{0:T(128)} %compare_select_fusion.who_ref.owners_ref, bf16[4,24,32,1024]{3,2,1,0:T(8,128)(2,1)} %bitcast.34, bf16[4,24,32,1024]{3,2,1,0:T(8,128)(2,1)} %bitcast.35, bf16[12,32,640]{2,1,0:T(8,128)(2,1)} %copy-done.9, bf16[12,32,640]{2,1,0:T(8,128)(2,1)} %copy-done.10), custom_call_target="tpu_custom_call" | custom-call | tf_op jit(solution)/shard_map/merge/pallas_call | solution.py:51
  32.4 3.7 %collective-permute-done.6.one = bf16[24,32,384]{2,1,0:T(8,128)(2,1)S(1)} collective-permute-done((bf16[24,32,384]{2,1,0:T(8,128)(2,1)}, bf16[24,32,384]{2,1,0:T(8,128)(2,1)S(1)}, u32[]{:S(2)}, u32[]{:S(2)}) %collective-permute-start.6) | collective-permute-done | bytes 589856 | tf_op jit(solution)/shard_map/ppermute | solution.py:352
  36.9 3.6 %shard_map.87 = (bf16[24,32,384]{2,1,0:T(8,128)(2,1)}, bf16[32,32,384]{2,1,0:T(8,128)(2,1)}) custom-call(s32[4]{0:T(128)} %compare_select_fusion.who_ref.owners_ref, s32[32]{0:T(128)} %get-tuple-element.46.table_ref, bf16[4,24,32,1024]{3,2,1,0:T(8,128)(2,1)} %bitcast.36, bf16[24,32,384]{2,1,0:T(8,128)(2,1)} %copy-done.8, ...), custom_call_target="tpu_custom_call" | custom-call | tf_op jit(solution)/shard_map/pallas_call | solution.py:80
  40.5 8.4 %all-to-all-start.1 = ((bf16[32,32,384]{2,1,0:T(8,128)(2,1)}), bf16[32,32,384]{2,1,0:T(8,128)(2,1)S(1)}, u32[]{:S(2)}, u32[]{:S(2)}) async-start(bf16[32,32,384]{2,1,0:T(8,128)(2,1)} %get-tuple-element.28), calls=%async_computation.1 | async-start | bytes 1572864 | tf_op jit(solution)/shard_map/all_to_all | solution.py:356
  49.0 7.0 %collective-permute-done.2.one = bf16[24,32,640]{2,1,0:T(8,128)(2,1)S(1)} collective-permute-done((bf16[24,32,640]{2,1,0:T(8,128)(2,1)}, bf16[24,32,640]{2,1,0:T(8,128)(2,1)S(1)}, u32[]{:S(2)}, u32[]{:S(2)}) %collective-permute-start.2) | collective-permute-done | bytes 983072 | tf_op jit(solution)/shard_map/ppermute | solution.py:352
  57.9 4.6 %shard_map.86 = (bf16[24,32,640]{2,1,0:T(8,128)(2,1)}, bf16[32,32,640]{2,1,0:T(8,128)(2,1)}) custom-call(s32[4]{0:T(128)} %compare_select_fusion.who_ref.owners_ref, s32[32]{0:T(128)} %get-tuple-element.46.table_ref, bf16[4,24,32,1024]{3,2,1,0:T(8,128)(2,1)} %bitcast.37, bf16[24,32,640]{2,1,0:T(8,128)(2,1)} %copy-done.6, bf16[24,32,640]{2,1,0:T(8,128)(2,1)} %copy-done.7), custom_call_target="tpu_custom_call" | custom-call | tf_op jit(solution)/shard_map/pallas_call | solution.py:80
  62.9 8.3 %all-to-all-start = ((bf16[32,32,640]{2,1,0:T(8,128)(2,1)}), bf16[32,32,640]{2,1,0:T(8,128)(2,1)S(1)}, u32[]{:S(2)}, u32[]{:S(2)}) async-start(bf16[32,32,640]{2,1,0:T(8,128)(2,1)} %get-tuple-element.25), calls=%async_computation | async-start | bytes 2621440 | tf_op jit(solution)/shard_map/all_to_all | solution.py:356
  72.5 4.4 %fusion = (f32[24,32,1024]{2,1,0:T(8,128)}, f32[24]{0:T(128)S(1)}) fusion(f32[24,32,1024]{2,1,0:T(8,128)} %param.9, bf16[24,32,640]{2,1,0:T(8,128)(2,1)S(1)} %copy-done.5, bf16[24,32,384]{2,1,0:T(8,128)(2,1)} %get-tuple-element.29), kind=kLoop, calls=%fused_computation.2 | loop fusion | flops 7077864 | bytes 7864416 | tf_op jit(solution)/shard_map/add | solution.py:380
  77.6 3.6 %left_times.1.rest_0_ = bf16[1024,384]{1,0:T(8,128)(2,1)} custom-call(bf16[1024,1024]{1,0:T(8,128)(2,1)} %bitcast.39, bf16[1024,384]{1,0:T(8,128)(2,1)} %bitcast.42), custom_call_target="tpu_custom_call" | custom-call | tf_op jit(solution)/shard_map/left_times/pallas_call | solution.py:106
  81.2 9.7 %all-to-all-done = bf16[32,32,640]{2,1,0:T(8,128)(2,1)S(1)} async-done(((bf16[32,32,640]{2,1,0:T(8,128)(2,1)}), bf16[32,32,640]{2,1,0:T(8,128)(2,1)S(1)}, u32[]{:S(2)}, u32[]{:S(2)}) %all-to-all-start) | async-done | bytes 1310752 | tf_op jit(solution)/shard_map/all_to_all | solution.py:356
  92.0 7.9 %products.1 = (bf16[1024,512]{1,0:T(8,128)(2,1)}, bf16[1024,512]{1,0:T(8,128)(2,1)}, f32[2,128]{1,0:T(2,128)}) custom-call(bf16[1024,1024]{1,0:T(8,128)(2,1)} %bitcast.40, bf16[1024,1024]{1,0:T(8,128)(2,1)} %bitcast.43, bf16[1024,640]{1,0:T(8,128)(2,1)} %bitcast.41, f32[1,128]{1,0:T(1,128)} %pad.8.layer_ref, bf16[1024,384]{1,0:T(8,128)(2,1)} %left_times.1.rest_0_), custom_call_target="tpu_custom_call" | custom-call | tf_op jit(solution)/shard_map/products/pallas_call | solution.py:148
  99.9 3.9 %all-to-all-start.2 = ((bf16[32,32,512]{2,1,0:T(8,128)(2,1)}), bf16[32,32,512]{2,1,0:T(8,128)(2,1)S(1)}, u32[]{:S(2)}, u32[]{:S(2)}) async-start(bf16[32,32,512]{2,1,0:T(8,128)(2,1)} %bitcast.45), calls=%async_computation.2 | async-start | bytes 2097152 | tf_op jit(solution)/shard_map/all_to_all | solution.py:393
  114.0 3.3 %collective-permute-start.12 = (f32[2,128]{1,0:T(2,128)S(1)}, f32[2,128]{1,0:T(2,128)S(1)}, u32[]{:S(2)}, u32[]{:S(2)}) collective-permute-start(f32[2,128]{1,0:T(2,128)S(1)} %add_add_fusion.2), channel_id=1, source_target_pairs={{0,64},{32,96},{64,0},{96,32},{1,65},{33,97},{65,1},{97,33},{2,66}... | collective-permute-start | bytes 3080 | tf_op jit(solution)/shard_map/ppermute | solution.py:307
  120.6 4.6 %all-to-all-start.3 = ((bf16[32,32,512]{2,1,0:T(8,128)(2,1)}), bf16[32,32,512]{2,1,0:T(8,128)(2,1)S(1)}, u32[]{:S(2)}, u32[]{:S(2)}) async-start(bf16[32,32,512]{2,1,0:T(8,128)(2,1)} %bitcast.44), calls=%async_computation.3 | async-start | bytes 2097152 | tf_op jit(solution)/shard_map/all_to_all | solution.py:393
  125.3 3.4 %collective-permute-start.15 = (f32[2,128]{1,0:T(2,128)S(1)}, f32[2,128]{1,0:T(2,128)S(1)}, u32[]{:S(2)}, u32[]{:S(2)}) collective-permute-start(f32[2,128]{1,0:T(2,128)S(1)} %add_add_fusion.1), channel_id=1, source_target_pairs={{0,16},{8,24},{16,0},{24,8},{1,17},{9,25},{17,1},{25,9},{2,18},{10... | collective-permute-start | bytes 3080 | tf_op jit(solution)/shard_map/ppermute | solution.py:307
  142.0 3.9 %collective-permute-done.30.refs_2_ = bf16[12,32,512]{2,1,0:T(8,128)(2,1)} collective-permute-done((bf16[12,32,512]{2,1,0:T(8,128)(2,1)}, bf16[12,32,512]{2,1,0:T(8,128)(2,1)}, u32[]{:S(2)}, u32[]{:S(2)}) %collective-permute-start.30) | collective-permute-done | bytes 393248 | tf_op jit(solution)/shard_map/ppermute | solution.py:316
  148.0 5.3 %update.1 = (bf16[12,32,512]{2,1,0:T(8,128)(2,1)}, bf16[12,32,512]{2,1,0:T(8,128)(2,1)}, bf16[4,24,32,1024]{3,2,1,0:T(8,128)(2,1)}) custom-call(s32[4]{0:T(128)} %compare_select_fusion.who_ref.owners_ref, s32[24]{0:T(128)} %select_reduce_fusion.position_ref, f32[24]{0:T(128)} %fusion.6.scale_ref, bf16[32,32,512]{2,1,0:T(8,128)(2,1)} %copy-done, ...), custom_call_target="tpu_custom_call" | custom-call | tf_op jit(solution)/shard_map/update/pallas_call | solution.py:234
  157.2 5.7 %collective-permute-done.22.refs_4_ = bf16[12,32,512]{2,1,0:T(8,128)(2,1)} collective-permute-done((bf16[12,32,512]{2,1,0:T(8,128)(2,1)}, bf16[12,32,512]{2,1,0:T(8,128)(2,1)}, u32[]{:S(2)}, u32[]{:S(2)}) %collective-permute-start.22) | collective-permute-done | bytes 393248 | tf_op jit(solution)/shard_map/ppermute | solution.py:314
  164.9 6.3 %collective-permute-done.32.refs_6_ = bf16[12,32,512]{2,1,0:T(8,128)(2,1)S(1)} collective-permute-done((bf16[12,32,512]{2,1,0:T(8,128)(2,1)}, bf16[12,32,512]{2,1,0:T(8,128)(2,1)S(1)}, u32[]{:S(2)}, u32[]{:S(2)}) %collective-permute-start.32) | collective-permute-done | bytes 393248 | tf_op jit(solution)/shard_map/ppermute | solution.py:316
  173.2 6.4 %collective-permute-done.26.refs_4_ = bf16[12,32,512]{2,1,0:T(8,128)(2,1)S(1)} collective-permute-done((bf16[12,32,512]{2,1,0:T(8,128)(2,1)}, bf16[12,32,512]{2,1,0:T(8,128)(2,1)S(1)}, u32[]{:S(2)}, u32[]{:S(2)}) %collective-permute-start.26) | collective-permute-done | bytes 393248 | tf_op jit(solution)/shard_map/ppermute | solution.py:314
  181.6 6.5 %collective-permute-done.28.refs_6_ = bf16[12,32,512]{2,1,0:T(8,128)(2,1)} collective-permute-done((bf16[12,32,512]{2,1,0:T(8,128)(2,1)}, bf16[12,32,512]{2,1,0:T(8,128)(2,1)}, u32[]{:S(2)}, u32[]{:S(2)}) %collective-permute-start.28) | collective-permute-done | bytes 393248 | tf_op jit(solution)/shard_map/ppermute | solution.py:316
  188.4 3.8 %shard_map.88.refs_8_ = bf16[4,24,32,1024]{3,2,1,0:T(8,128)(2,1)} custom-call(s32[4]{0:T(128)} %compare_select_fusion.who_ref.owners_ref, f32[96]{0:T(128)} %copy-done.19, bf16[12,32,512]{2,1,0:T(8,128)(2,1)} %copy-done.11, bf16[12,32,512]{2,1,0:T(8,128)(2,1)} %copy-done.12, ...), custom_call_target="tpu_custom_call", output_to_operand_aliasing={{}: (10, {})} | custom-call | tf_op jit(solution)/shard_map/pallas_call | solution.py:287
  192.2 4.3 %collective-permute-done.23.refs_2_ = bf16[12,32,512]{2,1,0:T(8,128)(2,1)} collective-permute-done((bf16[12,32,512]{2,1,0:T(8,128)(2,1)}, bf16[12,32,512]{2,1,0:T(8,128)(2,1)}, u32[]{:S(2)}, u32[]{:S(2)}) %collective-permute-start.23) | collective-permute-done | bytes 393248 | tf_op jit(solution)/shard_map/ppermute | solution.py:318
  196.6 4.1 %shard_map.89 = bf16[4,24,32,1024]{3,2,1,0:T(8,128)(2,1)} custom-call(s32[4]{0:T(128)} %compare_select_fusion.who_ref.owners_ref, f32[96]{0:T(128)} %copy-done.19, bf16[12,32,512]{2,1,0:T(8,128)(2,1)} %collective-permute-done.19.refs_0_, bf16[12,32,512]{2,1,0:T(8,128)(2,1)} %collective-permute-done.21.refs_1_, ...), custom_call_target="tpu_custom_call", output_to_operand_aliasing={{}: (10, {})} | custom-call | tf_op jit(solution)/shard_map/pallas_call | solution.py:287
  (137 shorter events, 77.5 us)
Async XLA Ops:
  6.3 17.1 %collective-permute-start = (bf16[12,32,640]{2,1,0:T(8,128)(2,1)S(1)}, bf16[12,32,640]{2,1,0:T(8,128)(2,1)S(1)}, u32[]{:S(2)}, u32[]{:S(2)}) collective-permute-start(bf16[12,32,640]{2,1,0:T(8,128)(2,1)S(1)} %get-tuple-element.51), channel_id=1, source_target_pairs={{0,1},{1,2},{2,3},{3,0},{4,5},{5,6},{6,7},{7,4},{8,9},{9,10},{10,1... | collective-permute-start | bytes 1474568 | tf_op jit(solution)/shard_map/ppermute | solution.py:349
  6.8 17.0 %collective-permute-start.1 = (bf16[12,32,640]{2,1,0:T(8,128)(2,1)S(1)}, bf16[12,32,640]{2,1,0:T(8,128)(2,1)S(1)}, u32[]{:S(2)}, u32[]{:S(2)}) collective-permute-start(bf16[12,32,640]{2,1,0:T(8,128)(2,1)S(1)} %get-tuple-element.50), channel_id=1, source_target_pairs={{0,3},{1,0},{2,1},{3,2},{4,7},{5,4},{6,5},{7,6},{8,11},{9,8},{10,9... | collective-permute-start | bytes 1474568 | tf_op jit(solution)/shard_map/ppermute | solution.py:350
  17.4 18.7 %collective-permute-start.6 = (bf16[24,32,384]{2,1,0:T(8,128)(2,1)}, bf16[24,32,384]{2,1,0:T(8,128)(2,1)S(1)}, u32[]{:S(2)}, u32[]{:S(2)}) collective-permute-start(bf16[24,32,384]{2,1,0:T(8,128)(2,1)} %get-tuple-element.26), channel_id=1, source_target_pairs={{0,1},{1,2},{2,3},{3,0},{4,5},{5,6},{6,7},{7,4},{8,9},{9,10},{10,1... | collective-permute-start | bytes 1769480 | tf_op jit(solution)/shard_map/ppermute | solution.py:352
  18.5 18.0 %collective-permute-start.7 = (bf16[24,32,384]{2,1,0:T(8,128)(2,1)}, bf16[24,32,384]{2,1,0:T(8,128)(2,1)}, u32[]{:S(2)}, u32[]{:S(2)}) collective-permute-start(bf16[24,32,384]{2,1,0:T(8,128)(2,1)} %get-tuple-element.27), channel_id=1, source_target_pairs={{0,3},{1,0},{2,1},{3,2},{4,7},{5,4},{6,5},{7,6},{8,11},{9,8},{10,9... | collective-permute-start | bytes 1769480 | tf_op jit(solution)/shard_map/ppermute | solution.py:353
  28.6 27.3 %collective-permute-start.2 = (bf16[24,32,640]{2,1,0:T(8,128)(2,1)}, bf16[24,32,640]{2,1,0:T(8,128)(2,1)S(1)}, u32[]{:S(2)}, u32[]{:S(2)}) collective-permute-start(bf16[24,32,640]{2,1,0:T(8,128)(2,1)} %get-tuple-element.23), channel_id=1, source_target_pairs={{0,1},{1,2},{2,3},{3,0},{4,5},{5,6},{6,7},{7,4},{8,9},{9,10},{10,1... | collective-permute-start | bytes 2949128 | tf_op jit(solution)/shard_map/ppermute | solution.py:352
  29.7 26.4 %collective-permute-start.3 = (bf16[24,32,640]{2,1,0:T(8,128)(2,1)}, bf16[24,32,640]{2,1,0:T(8,128)(2,1)S(1)}, u32[]{:S(2)}, u32[]{:S(2)}) collective-permute-start(bf16[24,32,640]{2,1,0:T(8,128)(2,1)} %get-tuple-element.24), channel_id=1, source_target_pairs={{0,3},{1,0},{2,1},{3,2},{4,7},{5,4},{6,5},{7,6},{8,11},{9,8},{10,9... | collective-permute-start | bytes 2949128 | tf_op jit(solution)/shard_map/ppermute | solution.py:353
  40.5 22.4 %all-to-all-start.1 = ((bf16[32,32,384]{2,1,0:T(8,128)(2,1)}), bf16[32,32,384]{2,1,0:T(8,128)(2,1)S(1)}, u32[]{:S(2)}, u32[]{:S(2)}) async-start(bf16[32,32,384]{2,1,0:T(8,128)(2,1)} %get-tuple-element.28), calls=%async_computation.1 | async-start | bytes 1572864 | tf_op jit(solution)/shard_map/all_to_all | solution.py:356
  62.9 28.1 %all-to-all-start = ((bf16[32,32,640]{2,1,0:T(8,128)(2,1)}), bf16[32,32,640]{2,1,0:T(8,128)(2,1)S(1)}, u32[]{:S(2)}, u32[]{:S(2)}) async-start(bf16[32,32,640]{2,1,0:T(8,128)(2,1)} %get-tuple-element.25), calls=%async_computation | async-start | bytes 2621440 | tf_op jit(solution)/shard_map/all_to_all | solution.py:356
  99.9 20.7 %all-to-all-start.2 = ((bf16[32,32,512]{2,1,0:T(8,128)(2,1)}), bf16[32,32,512]{2,1,0:T(8,128)(2,1)S(1)}, u32[]{:S(2)}, u32[]{:S(2)}) async-start(bf16[32,32,512]{2,1,0:T(8,128)(2,1)} %bitcast.45), calls=%async_computation.2 | async-start | bytes 2097152 | tf_op jit(solution)/shard_map/all_to_all | solution.py:393
  110.4 22.1 %collective-permute-start.18 = (bf16[12,32,512]{2,1,0:T(8,128)(2,1)S(1)}, bf16[12,32,512]{2,1,0:T(8,128)(2,1)S(1)}, u32[]{:S(2)}, u32[]{:S(2)}) collective-permute-start(bf16[12,32,512]{2,1,0:T(8,128)(2,1)S(1)} %get-tuple-element.55), channel_id=1, source_target_pairs={{0,1},{1,2},{2,3},{3,0},{4,5},{5,6},{6,7},{7,4},{8,9},{9,10},{10,1... | collective-permute-start | bytes 1179656 | tf_op jit(solution)/shard_map/ppermute | solution.py:314
  111.4 21.1 %collective-permute-start.20 = (bf16[12,32,512]{2,1,0:T(8,128)(2,1)}, bf16[12,32,512]{2,1,0:T(8,128)(2,1)S(1)}, u32[]{:S(2)}, u32[]{:S(2)}) collective-permute-start(bf16[12,32,512]{2,1,0:T(8,128)(2,1)} %get-tuple-element.54), channel_id=1, source_target_pairs={{0,3},{1,0},{2,1},{3,2},{4,7},{5,4},{6,5},{7,6},{8,11},{9,8},{10,9... | collective-permute-start | bytes 1179656 | tf_op jit(solution)/shard_map/ppermute | solution.py:315
  120.6 26.3 %all-to-all-start.3 = ((bf16[32,32,512]{2,1,0:T(8,128)(2,1)}), bf16[32,32,512]{2,1,0:T(8,128)(2,1)S(1)}, u32[]{:S(2)}, u32[]{:S(2)}) async-start(bf16[32,32,512]{2,1,0:T(8,128)(2,1)} %bitcast.44), calls=%async_computation.3 | async-start | bytes 2097152 | tf_op jit(solution)/shard_map/all_to_all | solution.py:393
  132.5 20.8 %collective-permute-start.31 = (bf16[12,32,512]{2,1,0:T(8,128)(2,1)S(1)}, bf16[12,32,512]{2,1,0:T(8,128)(2,1)}, u32[]{:S(2)}, u32[]{:S(2)}) collective-permute-start(bf16[12,32,512]{2,1,0:T(8,128)(2,1)S(1)} %get-tuple-element.55), channel_id=1, source_target_pairs={{0,3},{1,0},{2,1},{3,2},{4,7},{5,4},{6,5},{7,6},{8,11},{9,8},{10,9... | collective-permute-start | bytes 1179656 | tf_op jit(solution)/shard_map/ppermute | solution.py:317
  135.7 19.4 %collective-permute-start.19 = (bf16[12,32,512]{2,1,0:T(8,128)(2,1)S(1)}, bf16[12,32,512]{2,1,0:T(8,128)(2,1)}, u32[]{:S(2)}, u32[]{:S(2)}) collective-permute-start(bf16[12,32,512]{2,1,0:T(8,128)(2,1)S(1)} %collective-permute-done.18.refs_0_), channel_id=1, source_target_pairs={{0,1},{1,2},{2,3},{3,0},{4,5},{5,6},{6,7},{7,4},{8,9},{9,10},{10,1... | collective-permute-start | bytes 1179656 | tf_op jit(solution)/shard_map/ppermute | solution.py:318
  135.7 20.9 %collective-permute-start.21 = (bf16[12,32,512]{2,1,0:T(8,128)(2,1)S(1)}, bf16[12,32,512]{2,1,0:T(8,128)(2,1)}, u32[]{:S(2)}, u32[]{:S(2)}) collective-permute-start(bf16[12,32,512]{2,1,0:T(8,128)(2,1)S(1)} %collective-permute-done.20.refs_1_), channel_id=1, source_target_pairs={{0,3},{1,0},{2,1},{3,2},{4,7},{5,4},{6,5},{7,6},{8,11},{9,8},{10,9... | collective-permute-start | bytes 1179656 | tf_op jit(solution)/shard_map/ppermute | solution.py:319
  141.9 21.0 %collective-permute-start.22 = (bf16[12,32,512]{2,1,0:T(8,128)(2,1)}, bf16[12,32,512]{2,1,0:T(8,128)(2,1)}, u32[]{:S(2)}, u32[]{:S(2)}) collective-permute-start(bf16[12,32,512]{2,1,0:T(8,128)(2,1)} %get-tuple-element.37), channel_id=1, source_target_pairs={{0,1},{1,2},{2,3},{3,0},{4,5},{5,6},{6,7},{7,4},{8,9},{9,10},{10,1... | collective-permute-start | bytes 1179656 | tf_op jit(solution)/shard_map/ppermute | solution.py:314
  146.0 17.1 %collective-permute-start.24 = (bf16[12,32,512]{2,1,0:T(8,128)(2,1)}, bf16[12,32,512]{2,1,0:T(8,128)(2,1)}, u32[]{:S(2)}, u32[]{:S(2)}) collective-permute-start(bf16[12,32,512]{2,1,0:T(8,128)(2,1)} %get-tuple-element.38), channel_id=1, source_target_pairs={{0,3},{1,0},{2,1},{3,2},{4,7},{5,4},{6,5},{7,6},{8,11},{9,8},{10,9... | collective-permute-start | bytes 1179656 | tf_op jit(solution)/shard_map/ppermute | solution.py:315
  153.3 17.9 %collective-permute-start.32 = (bf16[12,32,512]{2,1,0:T(8,128)(2,1)}, bf16[12,32,512]{2,1,0:T(8,128)(2,1)S(1)}, u32[]{:S(2)}, u32[]{:S(2)}) collective-permute-start(bf16[12,32,512]{2,1,0:T(8,128)(2,1)} %get-tuple-element.38), channel_id=1, source_target_pairs={{0,1},{1,2},{2,3},{3,0},{4,5},{5,6},{6,7},{7,4},{8,9},{9,10},{10,1... | collective-permute-start | bytes 1179656 | tf_op jit(solution)/shard_map/ppermute | solution.py:316
  156.6 23.0 %collective-permute-start.26 = (bf16[12,32,512]{2,1,0:T(8,128)(2,1)}, bf16[12,32,512]{2,1,0:T(8,128)(2,1)S(1)}, u32[]{:S(2)}, u32[]{:S(2)}) collective-permute-start(bf16[12,32,512]{2,1,0:T(8,128)(2,1)} %get-tuple-element.40), channel_id=1, source_target_pairs={{0,1},{1,2},{2,3},{3,0},{4,5},{5,6},{6,7},{7,4},{8,9},{9,10},{10,1... | collective-permute-start | bytes 1179656 | tf_op jit(solution)/shard_map/ppermute | solution.py:314
  162.8 17.0 %collective-permute-start.27 = (bf16[12,32,512]{2,1,0:T(8,128)(2,1)}, bf16[12,32,512]{2,1,0:T(8,128)(2,1)S(1)}, u32[]{:S(2)}, u32[]{:S(2)}) collective-permute-start(bf16[12,32,512]{2,1,0:T(8,128)(2,1)} %get-tuple-element.41), channel_id=1, source_target_pairs={{0,3},{1,0},{2,1},{3,2},{4,7},{5,4},{6,5},{7,6},{8,11},{9,8},{10,9... | collective-permute-start | bytes 1179656 | tf_op jit(solution)/shard_map/ppermute | solution.py:315
  163.1 25.0 %collective-permute-start.28 = (bf16[12,32,512]{2,1,0:T(8,128)(2,1)}, bf16[12,32,512]{2,1,0:T(8,128)(2,1)}, u32[]{:S(2)}, u32[]{:S(2)}) collective-permute-start(bf16[12,32,512]{2,1,0:T(8,128)(2,1)} %get-tuple-element.41), channel_id=1, source_target_pairs={{0,1},{1,2},{2,3},{3,0},{4,5},{5,6},{6,7},{7,4},{8,9},{9,10},{10,1... | collective-permute-start | bytes 1179656 | tf_op jit(solution)/shard_map/ppermute | solution.py:316
  171.2 21.1 %collective-permute-start.29 = (bf16[12,32,512]{2,1,0:T(8,128)(2,1)}, bf16[12,32,512]{2,1,0:T(8,128)(2,1)}, u32[]{:S(2)}, u32[]{:S(2)}) collective-permute-start(bf16[12,32,512]{2,1,0:T(8,128)(2,1)} %get-tuple-element.40), channel_id=1, source_target_pairs={{0,3},{1,0},{2,1},{3,2},{4,7},{5,4},{6,5},{7,6},{8,11},{9,8},{10,9... | collective-permute-start | bytes 1179656 | tf_op jit(solution)/shard_map/ppermute | solution.py:317
  171.4 25.1 %collective-permute-start.23 = (bf16[12,32,512]{2,1,0:T(8,128)(2,1)}, bf16[12,32,512]{2,1,0:T(8,128)(2,1)}, u32[]{:S(2)}, u32[]{:S(2)}) collective-permute-start(bf16[12,32,512]{2,1,0:T(8,128)(2,1)} %collective-permute-done.22.refs_4_), channel_id=1, source_target_pairs={{0,1},{1,2},{2,3},{3,0},{4,5},{5,6},{6,7},{7,4},{8,9},{9,10},{10,1... | collective-permute-start | bytes 1179656 | tf_op jit(solution)/shard_map/ppermute | solution.py:318
  179.9 23.3 %collective-permute-start.34 = (bf16[12,32,512]{2,1,0:T(8,128)(2,1)S(1)}, bf16[12,32,512]{2,1,0:T(8,128)(2,1)S(1)}, u32[]{:S(2)}, u32[]{:S(2)}) collective-permute-start(bf16[12,32,512]{2,1,0:T(8,128)(2,1)S(1)} %collective-permute-done.26.refs_4_), channel_id=1, source_target_pairs={{0,1},{1,2},{2,3},{3,0},{4,5},{5,6},{6,7},{7,4},{8,9},{9,10},{10,1... | collective-permute-start | bytes 1179656 | tf_op jit(solution)/shard_map/ppermute | solution.py:318
  (39 other events, 489.8 us)
